TPU v7x, 32 devices: a whole 2x2x4 slice. The times are simulated.
32 devices in a mesh: wide: 8 (over z, core), narrow: 4 (over y, x).
Axes of the slice: x: 2, y: 2, z: 4, core: 2. Of those that a mesh axis runs over, the one named last changes fastest.
Arguments:
- tokens: bfloat16 [8192, 2048], P(('wide', 'narrow')), may hold values from -6 to 6
- doc_ids: int32 [8, 1024], P('wide'), may hold values from 0 to 3, never falling along the last dimension, each value on 1 to 512 neighbouring positions
- cotangent: bfloat16 [8192, 2048], P(('wide', 'narrow')), may hold values from -6 to 6
- attn_gain: bfloat16 [2048], P('wide'), may hold values from 0.5 to 1.5
- w_query: bfloat16 [2048, 2048], P('wide', 'narrow'), may hold values from -0.125 to 0.125
- w_key: bfloat16 [2048, 1024], P('wide', 'narrow'), may hold values from -0.125 to 0.125
- w_value: bfloat16 [2048, 1024], P('wide', 'narrow'), may hold values from -0.125 to 0.125
- query_gain: bfloat16 [128], P('wide'), may hold values from 0.5 to 1.5
- key_gain: bfloat16 [128], P('wide'), may hold values from 0.5 to 1.5
- w_out: bfloat16 [2048, 2048], P('narrow', 'wide'), may hold values from -1 to 1
- mlp_gain: bfloat16 [2048], P('wide'), may hold values from 0.5 to 1.5
- w_gate: bfloat16 [2048, 6144], P('wide', 'narrow'), may hold values from -0.125 to 0.125
- w_up: bfloat16 [2048, 6144], P('wide', 'narrow'), may hold values from -0.125 to 0.125
- w_down: bfloat16 [6144, 2048], P('narrow', 'wide'), may hold values from -0.15625 to 0.15625
Outputs:
- output: bfloat16 [8192, 2048], P(('wide', 'narrow'))
- d_tokens: float32 [8192, 2048], P(('wide', 'narrow'))
- grad_attn_gain: float32 [2048], P('wide')
- grad_w_query: float32 [2048, 2048], P('wide', 'narrow')
- grad_w_key: float32 [2048, 1024], P('wide', 'narrow')
- grad_w_value: float32 [2048, 1024], P('wide', 'narrow')
- grad_query_gain: float32 [128], P('wide')
- grad_key_gain: float32 [128], P('wide')
- grad_w_out: float32 [2048, 2048], P('narrow', 'wide')
- grad_mlp_gain: float32 [2048], P('wide')
- grad_w_gate: float32 [2048, 6144], P('wide', 'narrow')
- grad_w_up: float32 [2048, 6144], P('wide', 'narrow')
- grad_w_down: float32 [6144, 2048], P('narrow', 'wide')
Inputs may be any that keep to these rules, and one draw needn't show every extreme that they name: `doc_ids`: document numbers never fall along a sequence, each of 0 to 3 appears in every sequence, every document has 1 to 512 tokens and one has exactly 512.
All inputs are finite; a program needn't handle non-finite values.
Results may differ from a plain program's by a relative error of at most 0.025.
Values may be sent and summed in bfloat16 or wider, within the bound.
A program may use at most 192 MiB of HBM per device.

v0:
```python
import jax
import jax.numpy as jnp
from jax import lax
from jax.sharding import PartitionSpec as P

H = 16
KV = 8
HD = 128


EPS = 1e-06
ROPE_BASE = 1000000.0
NEG_FILL = -1e30


def rms_apply(values, gain):
    return values * lax.rsqrt(jnp.mean(values * values, axis=-1, keepdims=True) + EPS) * gain


def rms_back(values, gain, grad):
    scale = lax.rsqrt(jnp.mean(values * values, axis=-1, keepdims=True) + EPS)
    weighted = grad * gain
    inner = jnp.mean(weighted * values, axis=-1, keepdims=True)
    d_values = scale * weighted - values * (scale * scale * scale) * inner
    return (d_values, grad * values * scale)


def rotate(values):
    half = values.shape[-1] // 2
    return jnp.concatenate([-values[..., half:], values[..., :half]], axis=-1)


def rotate_back(values):
    half = values.shape[-1] // 2
    return jnp.concatenate([values[..., half:], -values[..., :half]], axis=-1)


def rope_tables(doc_rows):
    index = lax.broadcasted_iota(jnp.int32, doc_rows.shape, 1)
    change = jnp.concatenate(
        [jnp.ones((doc_rows.shape[0], 1), jnp.bool_), doc_rows[:, 1:] != doc_rows[:, :-1]], axis=1
    )
    begin = lax.cummax(jnp.where(change, index, 0), axis=1)
    position = (index - begin).astype(jnp.float32)
    freqs = ROPE_BASE ** (-(jnp.arange(HD // 2, dtype=jnp.float32) * (2.0 / HD)))
    angle = position[..., None] * freqs
    cosine = jnp.cos(angle)
    sine = jnp.sin(angle)
    return (jnp.concatenate([cosine, cosine], axis=-1), jnp.concatenate([sine, sine], axis=-1))


def contract_rows(left, right):
    return lax.dot_general(
        left, right, (((0,), (0,)), ((), ())), preferred_element_type=jnp.float32
    )


def times_transposed(left, right):
    return lax.dot_general(
        left, right, (((1,), (1,)), ((), ())), preferred_element_type=jnp.float32
    )


def shards(
    tokens,
    doc_ids,
    cotangent,
    attn_gain,
    w_query,
    w_key,
    w_value,
    query_gain,
    key_gain,
    w_out,
    mlp_gain,
    w_gate,
    w_up,
    w_down,
):
    narrow_size = lax.axis_size("narrow")
    heads_here = H // narrow_size
    groups_here = KV // narrow_size
    repeat = H // KV
    seq_count, length = doc_ids.shape
    rows_group = seq_count * length
    scale = HD ** (-0.5)

    def fetch_attention():
        return (
            lax.all_gather(attn_gain, "wide", axis=0, tiled=True),
            lax.all_gather(w_query, "wide", axis=0, tiled=True),
            lax.all_gather(w_key, "wide", axis=0, tiled=True),
            lax.all_gather(w_value, "wide", axis=0, tiled=True),
            lax.all_gather(query_gain, "wide", axis=0, tiled=True),
            lax.all_gather(key_gain, "wide", axis=0, tiled=True),
            lax.all_gather(w_out, "wide", axis=1, tiled=True),
        )

    def fetch_mlp():
        return (
            lax.all_gather(mlp_gain, "wide", axis=0, tiled=True),
            lax.all_gather(w_gate, "wide", axis=0, tiled=True),
            lax.all_gather(w_up, "wide", axis=0, tiled=True),
            lax.all_gather(w_down, "wide", axis=1, tiled=True),
        )

    cosine, sine = rope_tables(doc_ids)
    cos_heads = cosine[:, :, None, :]
    sin_heads = sine[:, :, None, :]
    position = jnp.arange(length)
    causal = position[None, :] <= position[:, None]

    def mask_for(doc_row):
        return causal & (doc_row[None, :] == doc_row[:, None])

    attn_set = fetch_attention()
    gain_attn = attn_set[0].astype(jnp.float32)
    query_w, key_w, value_w = (attn_set[1], attn_set[2], attn_set[3])
    gain_query = attn_set[4].astype(jnp.float32)
    gain_key = attn_set[5].astype(jnp.float32)
    out_w = attn_set[6]
    inputs = tokens.astype(jnp.float32)
    normed = rms_apply(inputs, gain_attn).astype(jnp.bfloat16)
    normed_all = lax.all_gather(normed, "narrow", axis=0, tiled=True)
    q_pre = jnp.dot(normed_all, query_w, preferred_element_type=jnp.float32).reshape(
        seq_count, length, heads_here, HD
    )
    k_pre = jnp.dot(normed_all, key_w, preferred_element_type=jnp.float32).reshape(
        seq_count, length, groups_here, HD
    )
    v_use = (
        jnp.dot(normed_all, value_w, preferred_element_type=jnp.float32)
        .astype(jnp.bfloat16)
        .reshape(seq_count, length, groups_here, HD)
    )
    q_norm = rms_apply(q_pre, gain_query)
    k_norm = rms_apply(k_pre, gain_key)
    q_use = (q_norm * cos_heads + rotate(q_norm) * sin_heads).astype(jnp.bfloat16)
    k_use = (k_norm * cos_heads + rotate(k_norm) * sin_heads).astype(jnp.bfloat16)
    q_grouped = q_use.reshape(seq_count, length, groups_here, repeat, HD)

    def attend(carry, items):
        q_seq, k_seq, v_seq, doc_row = items
        allowed = mask_for(doc_row)
        scores = (
            jnp.einsum("qgrd,kgd->grqk", q_seq, k_seq, preferred_element_type=jnp.float32) * scale
        )
        scores = jnp.where(allowed, scores, NEG_FILL)
        top = jnp.max(scores, axis=-1, keepdims=True)
        weights = jnp.exp(scores - top)
        total = jnp.sum(weights, axis=-1, keepdims=True)
        probs = weights / total
        mixed = jnp.einsum(
            "grqk,kgd->qgrd", probs.astype(jnp.bfloat16), v_seq, preferred_element_type=jnp.float32
        )
        log_total = (top + jnp.log(total))[..., 0]
        return (carry, (mixed.astype(jnp.bfloat16).reshape(length, heads_here * HD), log_total))

    unused, (attended, log_totals) = lax.scan(attend, 0, (q_grouped, k_use, v_use, doc_ids))
    attended = attended.reshape(rows_group, heads_here * HD)
    resid = inputs + lax.psum_scatter(
        jnp.dot(attended, out_w, preferred_element_type=jnp.float32).astype(jnp.bfloat16),
        "narrow",
        scatter_dimension=0,
        tiled=True,
    ).astype(jnp.float32)
    mlp_set = fetch_mlp()
    gain_mlp = mlp_set[0].astype(jnp.float32)
    gate_w, up_w, down_w = (mlp_set[1], mlp_set[2], mlp_set[3])
    mlp_in = rms_apply(resid, gain_mlp).astype(jnp.bfloat16)
    mlp_all = lax.all_gather(mlp_in, "narrow", axis=0, tiled=True)
    gate = jnp.dot(mlp_all, gate_w, preferred_element_type=jnp.float32)
    up = jnp.dot(mlp_all, up_w, preferred_element_type=jnp.float32)
    sigmoid = jax.nn.sigmoid(gate)
    hidden = (gate * sigmoid * up).astype(jnp.bfloat16)
    output = (
        resid
        + lax.psum_scatter(
            jnp.dot(hidden, down_w, preferred_element_type=jnp.float32).astype(jnp.bfloat16),
            "narrow",
            scatter_dimension=0,
            tiled=True,
        ).astype(jnp.float32)
    ).astype(jnp.bfloat16)
    mlp_set = fetch_mlp()
    gain_mlp = mlp_set[0].astype(jnp.float32)
    gate_w, up_w, down_w = (mlp_set[1], mlp_set[2], mlp_set[3])
    grad_rows = lax.all_gather(cotangent, "narrow", axis=0, tiled=True)
    grad_w_down = contract_rows(hidden, grad_rows)
    d_hidden = times_transposed(grad_rows, down_w)
    d_up = (d_hidden * gate * sigmoid).astype(jnp.bfloat16)
    d_gate = (d_hidden * up * sigmoid * (1.0 + gate * (1.0 - sigmoid))).astype(jnp.bfloat16)
    grad_w_gate = contract_rows(mlp_all, d_gate)
    grad_w_up = contract_rows(mlp_all, d_up)
    d_mlp_in = lax.psum_scatter(
        (times_transposed(d_gate, gate_w) + times_transposed(d_up, up_w)).astype(jnp.bfloat16),
        "narrow",
        scatter_dimension=0,
        tiled=True,
    ).astype(jnp.float32)
    d_part, mlp_gain_terms = rms_back(resid, gain_mlp, d_mlp_in)
    grad_mlp_gain = jnp.sum(mlp_gain_terms, axis=0)
    d_resid = cotangent.astype(jnp.float32) + d_part
    attn_set = fetch_attention()
    gain_attn = attn_set[0].astype(jnp.float32)
    query_w, key_w, value_w = (attn_set[1], attn_set[2], attn_set[3])
    gain_query = attn_set[4].astype(jnp.float32)
    gain_key = attn_set[5].astype(jnp.float32)
    out_w = attn_set[6]
    branch_rows = lax.all_gather(d_resid.astype(jnp.bfloat16), "narrow", axis=0, tiled=True)
    grad_w_out = contract_rows(attended, branch_rows)
    d_attended = times_transposed(branch_rows, out_w).astype(jnp.bfloat16)
    d_grouped = d_attended.reshape(seq_count, length, groups_here, repeat, HD)

    def attend_back(carry, items):
        q_seq, k_seq, v_seq, doc_row, log_total, d_mixed = items
        allowed = mask_for(doc_row)
        scores = (
            jnp.einsum("qgrd,kgd->grqk", q_seq, k_seq, preferred_element_type=jnp.float32) * scale
        )
        probs = jnp.where(allowed, jnp.exp(scores - log_total[..., None]), 0.0)
        d_probs = jnp.einsum("qgrd,kgd->grqk", d_mixed, v_seq, preferred_element_type=jnp.float32)
        inner = jnp.sum(probs * d_probs, axis=-1, keepdims=True)
        d_scores = (probs * (d_probs - inner)).astype(jnp.bfloat16)
        d_query = (
            jnp.einsum("grqk,kgd->qgrd", d_scores, k_seq, preferred_element_type=jnp.float32)
            * scale
        )
        d_key = (
            jnp.einsum("grqk,qgrd->kgd", d_scores, q_seq, preferred_element_type=jnp.float32)
            * scale
        )
        d_value = jnp.einsum(
            "grqk,qgrd->kgd",
            probs.astype(jnp.bfloat16),
            d_mixed,
            preferred_element_type=jnp.float32,
        )
        return (carry, (d_query, d_key, d_value.astype(jnp.bfloat16)))

    unused, (d_query, d_key, d_value) = lax.scan(
        attend_back, 0, (q_grouped, k_use, v_use, doc_ids, log_totals, d_grouped)
    )
    d_query = d_query.reshape(seq_count, length, heads_here, HD)
    d_q_norm = d_query * cos_heads + rotate_back(d_query * sin_heads)
    d_k_norm = d_key * cos_heads + rotate_back(d_key * sin_heads)
    d_q_pre, query_terms = rms_back(q_pre, gain_query, d_q_norm)
    d_k_pre, key_terms = rms_back(k_pre, gain_key, d_k_norm)
    grad_query_gain = jnp.sum(query_terms, axis=(0, 1, 2))
    grad_key_gain = jnp.sum(key_terms, axis=(0, 1, 2))
    d_q_pre = d_q_pre.astype(jnp.bfloat16).reshape(rows_group, heads_here * HD)
    d_k_pre = d_k_pre.astype(jnp.bfloat16).reshape(rows_group, groups_here * HD)
    d_value = d_value.reshape(rows_group, groups_here * HD)
    grad_w_query = contract_rows(normed_all, d_q_pre)
    grad_w_key = contract_rows(normed_all, d_k_pre)
    grad_w_value = contract_rows(normed_all, d_value)
    total = times_transposed(d_q_pre, query_w)
    total = total + times_transposed(d_k_pre, key_w)
    d_normed = lax.psum_scatter(
        (total + times_transposed(d_value, value_w)).astype(jnp.bfloat16),
        "narrow",
        scatter_dimension=0,
        tiled=True,
    ).astype(jnp.float32)
    d_input_part, attn_gain_terms = rms_back(inputs, gain_attn, d_normed)
    grad_attn_gain = jnp.sum(attn_gain_terms, axis=0)
    d_tokens = d_resid + d_input_part
    every_shard = (
        lax.psum_scatter(
            grad_attn_gain.astype(jnp.bfloat16), "wide", scatter_dimension=0, tiled=True
        ).astype(jnp.float32),
        lax.psum_scatter(
            grad_w_query.astype(jnp.bfloat16), "wide", scatter_dimension=0, tiled=True
        ).astype(jnp.float32),
        lax.psum_scatter(
            grad_w_key.astype(jnp.bfloat16), "wide", scatter_dimension=0, tiled=True
        ).astype(jnp.float32),
        lax.psum_scatter(
            grad_w_value.astype(jnp.bfloat16), "wide", scatter_dimension=0, tiled=True
        ).astype(jnp.float32),
        lax.psum_scatter(
            grad_query_gain.astype(jnp.bfloat16), "wide", scatter_dimension=0, tiled=True
        ).astype(jnp.float32),
        lax.psum_scatter(
            grad_key_gain.astype(jnp.bfloat16), "wide", scatter_dimension=0, tiled=True
        ).astype(jnp.float32),
        lax.psum_scatter(
            grad_w_out.astype(jnp.bfloat16), "wide", scatter_dimension=1, tiled=True
        ).astype(jnp.float32),
        lax.psum_scatter(
            grad_mlp_gain.astype(jnp.bfloat16), "wide", scatter_dimension=0, tiled=True
        ).astype(jnp.float32),
        lax.psum_scatter(
            grad_w_gate.astype(jnp.bfloat16), "wide", scatter_dimension=0, tiled=True
        ).astype(jnp.float32),
        lax.psum_scatter(
            grad_w_up.astype(jnp.bfloat16), "wide", scatter_dimension=0, tiled=True
        ).astype(jnp.float32),
        lax.psum_scatter(
            grad_w_down.astype(jnp.bfloat16), "wide", scatter_dimension=1, tiled=True
        ).astype(jnp.float32),
    )
    attn_shards = every_shard[:7]
    mlp_shards = every_shard[7:]
    gain_totals = lax.psum(
        (attn_shards[0], attn_shards[4], attn_shards[5], mlp_shards[0]), "narrow"
    )
    return (
        output,
        d_tokens,
        gain_totals[0],
        attn_shards[1],
        attn_shards[2],
        attn_shards[3],
        gain_totals[1],
        gain_totals[2],
        attn_shards[6],
        gain_totals[3],
        mlp_shards[1],
        mlp_shards[2],
        mlp_shards[3],
    )


def solution(mesh):
    in_specs = (
        P(("wide", "narrow"), None),
        P("wide", None),
        P(("wide", "narrow"), None),
        P("wide"),
        P("wide", "narrow"),
        P("wide", "narrow"),
        P("wide", "narrow"),
        P("wide"),
        P("wide"),
        P("narrow", "wide"),
        P("wide"),
        P("wide", "narrow"),
        P("wide", "narrow"),
        P("narrow", "wide"),
    )
    out_specs = (
        P(("wide", "narrow"), None),
        P(("wide", "narrow"), None),
        P("wide"),
        P("wide", "narrow"),
        P("wide", "narrow"),
        P("wide", "narrow"),
        P("wide"),
        P("wide"),
        P("narrow", "wide"),
        P("wide"),
        P("wide", "narrow"),
        P("wide", "narrow"),
        P("narrow", "wide"),
    )
    return jax.shard_map(shards, mesh=mesh, in_specs=in_specs, out_specs=out_specs, check_vma=False)
```

profile of v0, /device:TPU:0, one launch (start us, length us, event | category | flops | bytes accessed | tf_op | source)
XLA Modules:
  0.0 1157.6 jit_solution(16592307919571008844)
XLA Ops:
  8.7 13.5 %all-gather = bf16[8,1,256]{2,1,0:T(2,128)(2,1)S(1)} all-gather(bf16[1,1,256]{2,1,0:T(2,128)(2,1)S(1)} %reshape.615), channel_id=1, replica_groups=mesh['wide'=8,'narrow'=4] {'wide'}, dimensions={0}, use_global_device_ids=true | all-gather | bytes 4608 | tf_op jit(solution)/shard_map/all_gather | solution.py:90
  30.6 13.9 %all-reduce.8 = (bf16[128]{0:T(256)(128)(2,1)S(1)}, bf16[128]{0:T(256)(128)(2,1)S(1)}) all-reduce(bf16[128]{0:T(256)(128)(2,1)S(1)} %dynamic-update-slice, bf16[128]{0:T(256)(128)(2,1)S(1)} %dynamic-update-slice.1), channel_id=1, replica_groups=mesh['wide'=8,'narrow'=4] {'wide'}, use_global_device_ids=true, to_apply=%add | all-reduce | flops 256 | bytes 1024
  49.2 40.1 %all-gather.14.cloned.1.call-done = bf16[1024,2048]{1,0:T(8,128)(2,1)} async-done(((bf16[256,2048]{1,0:T(8,128)(2,1)}), bf16[1024,2048]{1,0:T(8,128)(2,1)}) %all-gather.14.cloned.1.call-update) | async-done | bytes 4194320 | tf_op jit(solution)/shard_map/all_gather | solution.py:124
  95.3 24.8 %all-gather.20.cloned.1.call-done = bf16[2048,512]{1,0:T(8,128)(2,1)} async-done(((bf16[256,512]{1,0:T(8,128)(2,1)}), bf16[2048,512]{1,0:T(8,128)(2,1)}) %all-gather.20.cloned.1.call-update) | async-done | bytes 2097168 | tf_op jit(solution)/shard_map/all_gather | solution.py:91
  193.5 39.3 %reduce-scatter.12.cloned.1.call-done = bf16[256,2048]{1,0:T(8,128)(2,1)} async-done(((bf16[1024,2048]{1,0:T(8,128)(2,1)}), bf16[256,2048]{1,0:T(8,128)(2,1)}) %reduce-scatter.12.cloned.1.call-update) | async-done | bytes 1048592 | tf_op jit(solution)/shard_map/reduce_scatter | solution.py:161
  239.1 60.0 %all-gather.28.cloned.1.call-done = bf16[2048,1536]{1,0:T(8,128)(2,1)} async-done(((bf16[256,1536]{1,0:T(8,128)(2,1)}), bf16[2048,1536]{1,0:T(8,128)(2,1)}) %all-gather.28.cloned.1.call-update) | async-done | bytes 6291472 | tf_op jit(solution)/shard_map/all_gather | solution.py:103
  299.1 53.7 %all-gather.24.cloned.1.call-done = bf16[1024,2048]{1,0:T(8,128)(2,1)} async-done(((bf16[256,2048]{1,0:T(8,128)(2,1)}), bf16[1024,2048]{1,0:T(8,128)(2,1)}) %all-gather.24.cloned.1.call-update) | async-done | bytes 4194320 | tf_op jit(solution)/shard_map/all_gather | solution.py:171
  364.6 54.5 %all-gather.26.cloned.1.call-done = bf16[2048,1536]{1,0:T(8,128)(2,1)} async-done(((bf16[256,1536]{1,0:T(8,128)(2,1)}), bf16[2048,1536]{1,0:T(8,128)(2,1)}) %all-gather.26.cloned.1.call-update) | async-done | bytes 6291472 | tf_op jit(solution)/shard_map/all_gather | solution.py:102
  430.8 41.3 %all-gather.32.cloned.1.call-done = bf16[1024,2048]{1,0:T(8,128)(2,1)} async-done(((bf16[256,2048]{1,0:T(8,128)(2,1)}), bf16[1024,2048]{1,0:T(8,128)(2,1)}) %all-gather.32.cloned.1.call-update) | async-done | bytes 4194320 | tf_op jit(solution)/shard_map/all_gather | solution.py:188
  472.1 66.8 %all-gather.30.cloned.1.call-done = bf16[1536,2048]{1,0:T(8,128)(2,1)} async-done(((bf16[1536,256]{1,0:T(8,128)(2,1)}), bf16[1536,2048]{1,0:T(8,128)(2,1)}) %all-gather.30.cloned.1.call-update) | async-done | bytes 6291472 | tf_op jit(solution)/shard_map/all_gather | solution.py:104
  538.9 16.7 %multiply_convert_fusion = (bf16[1024,1536]{1,0:T(8,128)(2,1)}, bf16[1024,1536]{1,0:T(8,128)(2,1)S(1)}, bf16[1024,1536]{1,0:T(8,128)(2,1)}) fusion(f32[1024,1536]{1,0:T(8,128)} %fusion.63, f32[1024,1536]{1,0:T(8,128)} %fusion.64, bf16[1024,2048]{1,0:T(8,128)(2,1)} %all-gather.32.cloned.1.call-done, bf16[1536,2048]{1,0:T(8,128)(2,1)} %all-gather.30.cloned.1.call-done), kind=kOutput, calls=%fused_computation.22 | convolution fusion | flops 6467616768 | bytes 32505856 | tf_op jit(solution)/shard_map/dot_general | solution.py:59
  573.5 50.9 %reduce-scatter.16.cloned.1.call-done = bf16[256,2048]{1,0:T(8,128)(2,1)} async-done(((bf16[1024,2048]{1,0:T(8,128)(2,1)}), bf16[256,2048]{1,0:T(8,128)(2,1)}) %reduce-scatter.16.cloned.1.call-update) | async-done | bytes 1048592 | tf_op jit(solution)/shard_map/reduce_scatter | solution.py:195
  667.3 15.2 %all-gather.34.cloned.1.call-done = bf16[1024,2048]{1,0:T(8,128)(2,1)} async-done(((bf16[256,2048]{1,0:T(8,128)(2,1)}), bf16[1024,2048]{1,0:T(8,128)(2,1)}) %all-gather.34.cloned.1.call-update) | async-done | bytes 4194320 | tf_op jit(solution)/shard_map/all_gather | solution.py:210
  700.4 12.6 %fusion = (f32[2,2,1024]{2,1,0:T(2,128)S(1)}, f32[2,1024,1024,2]{2,1,3,0:T(8,128)}) fusion(f32[2,1024,1024,2]{2,1,3,0:T(8,128)} %get-tuple-element.117, f32[2,2,1024]{2,1,0:T(2,128)S(1)} %log_add_fusion, pred[1024,1024]{0,1:T(8,128)(4,1)S(1)} %copy-done.8, bf16[1024,2,128,1]{0,2,3,1:T(8,128)(2,1)} %bitcast.240, bf16[1024,2,2,128]{0,3,2,1:T(8,128)(2,1)} %bitcast.238), kind=kOutput, calls=%fused_computation.2 | convolution fusion | flops 1094709248 | bytes 36208640 | tf_op jit(solution)/shard_map/while/body/eval_jaxpr/qgrd,kgd->grqk/dot_general | solution.py:222
  713.0 12.6 %fusion.2 = bf16[2,2,1024,1024]{2,3,1,0:T(8,128)(2,1)S(1)} fusion(f32[2,1024,1024,2]{2,1,3,0:T(8,128)} %get-tuple-element.119, f32[2,1024,1024,2]{2,1,3,0:T(8,128)} %get-tuple-element.117, f32[2,2,1024]{2,1,0:T(2,128)S(1)} %get-tuple-element.118, f32[2,2,1024]{2,1,0:T(2,128)S(1)} %log_add_fusion, pred[1024,1024]{0,1:T(8,128)(4,1)S(1)} %copy-done.8), kind=kLoop, calls=%fused_computation.4 | loop fusion | flops 25165824 | bytes 43024384 | tf_op jit(solution)/shard_map/while/body/eval_jaxpr/convert_element_type | solution.py:224
  779.3 45.5 %reduce-scatter.30.cloned.1.call-done = bf16[256,1536]{1,0:T(8,128)(2,1)} async-done(((bf16[2048,1536]{1,0:T(8,128)(2,1)}), bf16[256,1536]{1,0:T(8,128)(2,1)}) %reduce-scatter.30.cloned.1.call-update) | async-done | bytes 786448 | tf_op jit(solution)/shard_map/reduce_scatter | solution.py:296
  827.2 67.9 %reduce-scatter.28.cloned.1.call-done = bf16[256,1536]{1,0:T(8,128)(2,1)} async-done(((bf16[2048,1536]{1,0:T(8,128)(2,1)}), bf16[256,1536]{1,0:T(8,128)(2,1)}) %reduce-scatter.28.cloned.1.call-update) | async-done | bytes 786448 | tf_op jit(solution)/shard_map/reduce_scatter | solution.py:293
  897.6 30.7 %reduce-scatter.24.cloned.1.call-done = bf16[256,256]{1,0:T(8,128)(2,1)} async-done(((bf16[2048,256]{1,0:T(8,128)(2,1)}), bf16[256,256]{1,0:T(8,128)(2,1)}) %reduce-scatter.24.cloned.1.call-update) | async-done | bytes 131088 | tf_op jit(solution)/shard_map/reduce_scatter | solution.py:278
  930.0 31.4 %reduce-scatter.22.cloned.1.call-done = bf16[256,256]{1,0:T(8,128)(2,1)} async-done(((bf16[2048,256]{1,0:T(8,128)(2,1)}), bf16[256,256]{1,0:T(8,128)(2,1)}) %reduce-scatter.22.cloned.1.call-update) | async-done | bytes 131088 | tf_op jit(solution)/shard_map/reduce_scatter | solution.py:275
  963.0 35.0 %reduce-scatter.26.cloned.1.call-done = bf16[512,256]{1,0:T(8,128)(2,1)} async-done(((bf16[512,2048]{1,0:T(8,128)(2,1)}), bf16[512,256]{1,0:T(8,128)(2,1)}) %reduce-scatter.26.cloned.1.call-update) | async-done | bytes 262160 | tf_op jit(solution)/shard_map/reduce_scatter | solution.py:287
  999.7 35.7 %reduce-scatter.20.cloned.1.call-done = bf16[256,512]{1,0:T(8,128)(2,1)} async-done(((bf16[2048,512]{1,0:T(8,128)(2,1)}), bf16[256,512]{1,0:T(8,128)(2,1)}) %reduce-scatter.20.cloned.1.call-update) | async-done | bytes 262160 | tf_op jit(solution)/shard_map/reduce_scatter | solution.py:272
  1037.2 52.4 %reduce-scatter.18.cloned.1.call-done = bf16[256,2048]{1,0:T(8,128)(2,1)} async-done(((bf16[1024,2048]{1,0:T(8,128)(2,1)}), bf16[256,2048]{1,0:T(8,128)(2,1)}) %reduce-scatter.18.cloned.1.call-update) | async-done | bytes 1048592 | tf_op jit(solution)/shard_map/reduce_scatter | solution.py:259
  1091.5 16.8 %all-reduce.7 = (bf16[2048]{0:T(1024)(128)(2,1)S(1)}, bf16[128]{0:T(256)(128)(2,1)S(1)}, bf16[128]{0:T(256)(128)(2,1)S(1)}, bf16[2048]{0:T(1024)(128)(2,1)S(1)}) all-reduce(bf16[2048]{0:T(1024)(128)(2,1)S(1)} %get-tuple-element.61, bf16[128]{0:T(256)(128)(2,1)S(1)} %bitcast_reduce_fusion, ...), channel_id=6, replica_groups=mesh['wide'=8,'narrow'=4] {'wide'}, use_global_device_ids=true, to_apply=%region_18.19.clone | all-reduce | flops 4352 | bytes 17408
  1118.6 26.9 %reduce-scatter.14.cloned.1.call-done = bf16[256,2048]{1,0:T(8,128)(2,1)} async-done(((bf16[1024,2048]{1,0:T(8,128)(2,1)}), bf16[256,2048]{1,0:T(8,128)(2,1)}) %reduce-scatter.14.cloned.1.call-update) | async-done | bytes 1048592 | tf_op jit(solution)/shard_map/reduce_scatter | solution.py:178
  (276 shorter events, 282.3 us)
Async XLA Ops:
  7.2 42.0 %all-gather.18.cloned.1.call-start = ((), (), s32[]{:S(2)}) async-start(), calls=%async_computation.13 | async-start | bytes 1179648 | tf_op jit(solution)/shard_map/all_gather | solution.py:92
  8.0 81.3 %all-gather.14.cloned.1.call-start = ((), (), s32[]{:S(2)}) async-start(), calls=%async_computation.11 | async-start | bytes 5242880 | tf_op jit(solution)/shard_map/all_gather | solution.py:124
  26.8 93.3 %all-gather.20.cloned.1.call-start = ((), (), s32[]{:S(2)}) async-start(), calls=%async_computation.14 | async-start | bytes 2359296 | tf_op jit(solution)/shard_map/all_gather | solution.py:91
  27.5 115.7 %all-gather.16.cloned.1.call-start = ((), (), s32[]{:S(2)}) async-start(), calls=%async_computation.12 | async-start | bytes 1179648 | tf_op jit(solution)/shard_map/all_gather | solution.py:93
  28.1 146.8 %all-gather.22.cloned.1.call-start = ((), (), s32[]{:S(2)}) async-start(), calls=%async_computation.15 | async-start | bytes 2359296 | tf_op jit(solution)/shard_map/all_gather | solution.py:96
  28.7 204.1 %reduce-scatter.12.cloned.1.call-start = ((), (), s32[]{:S(2)}) async-start(), calls=%async_computation.16 | async-start | bytes 5242880 | tf_op jit(solution)/shard_map/reduce_scatter | solution.py:161
  181.0 118.1 %all-gather.28.cloned.1.call-start = ((), (), s32[]{:S(2)}) async-start(), calls=%async_computation.19 | async-start | bytes 7077888 | tf_op jit(solution)/shard_map/all_gather | solution.py:103
  181.7 171.1 %all-gather.24.cloned.1.call-start = ((), (), s32[]{:S(2)}) async-start(), calls=%async_computation.17 | async-start | bytes 5242880 | tf_op jit(solution)/shard_map/all_gather | solution.py:171
  237.0 182.1 %all-gather.26.cloned.1.call-start = ((), (), s32[]{:S(2)}) async-start(), calls=%async_computation.18 | async-start | bytes 7077888 | tf_op jit(solution)/shard_map/all_gather | solution.py:102
  237.8 234.3 %all-gather.32.cloned.1.call-start = ((), (), s32[]{:S(2)}) async-start(), calls=%async_computation.22 | async-start | bytes 5242880 | tf_op jit(solution)/shard_map/all_gather | solution.py:188
  238.3 300.5 %all-gather.30.cloned.1.call-start = ((), (), s32[]{:S(2)}) async-start(), calls=%async_computation.20 | async-start | bytes 7077888 | tf_op jit(solution)/shard_map/all_gather | solution.py:104
  239.1 385.3 %reduce-scatter.16.cloned.1.call-start = ((), (), s32[]{:S(2)}) async-start(), calls=%async_computation.23 | async-start | bytes 5242880 | tf_op jit(solution)/shard_map/reduce_scatter | solution.py:195
  573.5 109.0 %all-gather.34.cloned.1.call-start = ((), (), s32[]{:S(2)}) async-start(), calls=%async_computation.24 | async-start | bytes 5242880 | tf_op jit(solution)/shard_map/all_gather | solution.py:210
  629.8 147.1 %reduce-scatter.32.cloned.1.call-start = ((), (), s32[]{:S(2)}) async-start(), calls=%async_computation.32 | async-start | bytes 7077888 | tf_op jit(solution)/shard_map/reduce_scatter | solution.py:299
  641.2 183.6 %reduce-scatter.30.cloned.1.call-start = ((), (), s32[]{:S(2)}) async-start(), calls=%async_computation.31 | async-start | bytes 7077888 | tf_op jit(solution)/shard_map/reduce_scatter | solution.py:296
  653.0 242.2 %reduce-scatter.28.cloned.1.call-start = ((), (), s32[]{:S(2)}) async-start(), calls=%async_computation.30 | async-start | bytes 7077888 | tf_op jit(solution)/shard_map/reduce_scatter | solution.py:293
  664.5 263.9 %reduce-scatter.24.cloned.1.call-start = ((), (), s32[]{:S(2)}) async-start(), calls=%async_computation.28 | async-start | bytes 1179648 | tf_op jit(solution)/shard_map/reduce_scatter | solution.py:278
  713.0 248.3 %reduce-scatter.22.cloned.1.call-start = ((), (), s32[]{:S(2)}) async-start(), calls=%async_computation.27 | async-start | bytes 1179648 | tf_op jit(solution)/shard_map/reduce_scatter | solution.py:275
  734.9 263.0 %reduce-scatter.26.cloned.1.call-start = ((), (), s32[]{:S(2)}) async-start(), calls=%async_computation.29 | async-start | bytes 2359296 | tf_op jit(solution)/shard_map/reduce_scatter | solution.py:287
  741.4 294.0 %reduce-scatter.20.cloned.1.call-start = ((), (), s32[]{:S(2)}) async-start(), calls=%async_computation.26 | async-start | bytes 2359296 | tf_op jit(solution)/shard_map/reduce_scatter | solution.py:272
  755.5 334.1 %reduce-scatter.18.cloned.1.call-start = ((), (), s32[]{:S(2)}) async-start(), calls=%async_computation.25 | async-start | bytes 5242880 | tf_op jit(solution)/shard_map/reduce_scatter | solution.py:259
  764.3 381.1 %reduce-scatter.14.cloned.1.call-start = ((), (), s32[]{:S(2)}) async-start(), calls=%async_computation.21 | async-start | bytes 5242880 | tf_op jit(solution)/shard_map/reduce_scatter | solution.py:178
  779.3 366.2 %copy-start.11 = (bf16[256,2048]{1,0:T(8,128)(2,1)S(1)}, bf16[256,2048]{1,0:T(8,128)(2,1)}, u32[]{:S(2)}) copy-start(bf16[256,2048]{1,0:T(8,128)(2,1)} %param.16) | copy-start | bytes 3145732
  779.3 366.2 %copy-start.47 = (f32[256]{0:T(256)S(1)}, f32[256]{0:T(256)}, u32[]{:S(2)}) copy-start(f32[256]{0:T(256)} %get-tuple-element.110) | copy-start | bytes 3076
  (61 other events, 1330.1 us)
Sparse Core Ops, SparseCore 0:
  9.6 24.9 all-gather.17
  37.0 52.2 all-gather.13
  90.9 29.1 all-gather.19
  121.5 21.6 all-gather.15
  144.7 30.1 all-gather.21
  181.1 51.6 reduce-scatter.11
  234.4 64.6 all-gather.27
  301.5 51.2 all-gather.23
  354.4 64.6 all-gather.25
  420.8 51.2 all-gather.31
  473.7 65.1 all-gather.29
  573.6 50.8 reduce-scatter.15
  629.9 52.5 all-gather.33
  684.6 69.7 reduce-scatter.31
  756.5 68.1 reduce-scatter.29
  826.9 68.1 reduce-scatter.27
  897.3 31.0 reduce-scatter.23
  930.5 30.8 reduce-scatter.21
  963.6 34.2 reduce-scatter.25
  1000.7 34.6 reduce-scatter.19
  1038.4 51.1 reduce-scatter.17
  1092.6 52.8 reduce-scatter.13
where the time goes:
time: 1170 us; the launch traced here: 1160 us
  waiting for transfers between devices  796 us (68%)
  matrix products  194 us (17%)
  other arithmetic  73.7 us (6%)
  blocking collectives  65.8 us (6%)
  between operations  17.5 us (1%)
    reduce_scatter x1, waiting for transfers between devices, shards(): lax.psum_scatter(grad_w_gate.astype(jnp.bfloat16), 'wide', scatter_dimens...  67.9 us
    all_gather x1, waiting for transfers between devices, fetch_mlp(): lax.all_gather(w_down, 'wide', axis=1, tiled=True)  66.8 us
    all_gather x1, waiting for transfers between devices, fetch_mlp(): lax.all_gather(w_up, 'wide', axis=0, tiled=True)  60 us
    all_gather x1, waiting for transfers between devices, fetch_mlp(): lax.all_gather(w_gate, 'wide', axis=0, tiled=True)  54.5 us
    all_gather x1, waiting for transfers between devices, shards(): mlp_all = lax.all_gather(mlp_in, 'narrow', axis=0, tiled=True)  53.7 us
    reduce_scatter x1, waiting for transfers between devices, shards(): lax.psum_scatter((total + times_transposed(d_value, value_w)).astype(jnp....  52.4 us
    reduce_scatter x1, waiting for transfers between devices, shards(): lax.psum_scatter((times_transposed(d_gate, gate_w) + times_transposed(d_u...  50.9 us
    dot_general x7, matrix products, contract_rows(): lax.dot_general(left, right, (((0,), (0,)), ((), ())), preferred_element_...  49.2 us
  transfers between devices with their start and end apart: 22, of which 20 were waited for; matrix products, arithmetic and copies ran while one was open for 19% of the time, Pallas kernels for 0%

commit v1 on v0

--- a/solution.py
+++ b/solution.py
@@ -11,6 +11,9 @@
 EPS = 1e-06
 ROPE_BASE = 1000000.0
 NEG_FILL = -1e30
+
+XPERM = [(0, 1), (1, 0), (2, 3), (3, 2)]
+YPERM = [(0, 2), (2, 0), (1, 3), (3, 1)]
 
 
 def rms_apply(values, gain):
@@ -59,6 +62,88 @@
     return lax.dot_general(
         left, right, (((1,), (1,)), ((), ())), preferred_element_type=jnp.float32
     )
+
+
+def place(pieces, index, axis):
+    first = jnp.stack([pieces[0], pieces[1]], axis=axis)
+    second = jnp.stack([pieces[1], pieces[0]], axis=axis)
+    return lax.select(jnp.broadcast_to(index == 0, first.shape), first, second)
+
+
+def narrow_gather(x):
+    if lax.axis_size("narrow") != 4:
+        return lax.all_gather(x, "narrow", axis=0, tiled=True)
+    n = lax.axis_index("narrow")
+    xb = n % 2
+    yb = n // 2
+    r, c = x.shape
+    h = c // 2
+    a, b = x[:, :h], x[:, h:]
+    a_x = lax.ppermute(a, "narrow", XPERM)
+    b_y = lax.ppermute(b, "narrow", YPERM)
+    a_pair = place((a, a_x), xb, 0)
+    b_pair = place((b, b_y), yb, 0)
+    a_pair_y = lax.ppermute(a_pair, "narrow", YPERM)
+    b_pair_x = lax.ppermute(b_pair, "narrow", XPERM)
+    a_full = place((a_pair, a_pair_y), yb, 0)
+    b_full = place((b_pair, b_pair_x), xb, 1)
+    return jnp.concatenate([a_full, b_full], axis=-1).reshape(4 * r, c)
+
+
+def narrow_scatter(x):
+    if lax.axis_size("narrow") != 4:
+        return lax.psum_scatter(
+            x.astype(jnp.bfloat16), "narrow", scatter_dimension=0, tiled=True
+        ).astype(jnp.float32)
+    n = lax.axis_index("narrow")
+    xb = n % 2
+    yb = n // 2
+    rows, c = x.shape
+    r = rows // 4
+    h = c // 2
+    quarters = x.reshape(2, 2, r, c)
+    a = quarters[..., :h]
+    b = quarters[..., h:]
+    a_keep = lax.dynamic_index_in_dim(a, yb, 0, keepdims=False)
+    a_send = lax.dynamic_index_in_dim(a, 1 - yb, 0, keepdims=False)
+    b_keep = lax.dynamic_index_in_dim(b, xb, 1, keepdims=False)
+    b_send = lax.dynamic_index_in_dim(b, 1 - xb, 1, keepdims=False)
+    a_got = lax.ppermute(a_send.astype(jnp.bfloat16), "narrow", YPERM)
+    b_got = lax.ppermute(b_send.astype(jnp.bfloat16), "narrow", XPERM)
+    a_sum = a_keep + a_got.astype(jnp.float32)
+    b_sum = b_keep + b_got.astype(jnp.float32)
+    a_mine = lax.dynamic_index_in_dim(a_sum, xb, 0, keepdims=False)
+    a_other = lax.dynamic_index_in_dim(a_sum, 1 - xb, 0, keepdims=False)
+    b_mine = lax.dynamic_index_in_dim(b_sum, yb, 0, keepdims=False)
+    b_other = lax.dynamic_index_in_dim(b_sum, 1 - yb, 0, keepdims=False)
+    a_got2 = lax.ppermute(a_other.astype(jnp.bfloat16), "narrow", XPERM)
+    b_got2 = lax.ppermute(b_other.astype(jnp.bfloat16), "narrow", YPERM)
+    a_fin = a_mine + a_got2.astype(jnp.float32)
+    b_fin = b_mine + b_got2.astype(jnp.float32)
+    return jnp.concatenate([a_fin, b_fin], axis=-1)
+
+
+def wide_gather(blocks):
+    widths = [blk.shape[1] for blk in blocks]
+    joined = lax.all_gather(jnp.concatenate(blocks, axis=1), "wide", axis=0, tiled=True)
+    out = []
+    start = 0
+    for w in widths:
+        out.append(joined[:, start : start + w])
+        start += w
+    return out
+
+
+def wide_scatter(blocks):
+    widths = [blk.shape[1] for blk in blocks]
+    joined = jnp.concatenate([blk.astype(jnp.bfloat16) for blk in blocks], axis=1)
+    summed = lax.psum_scatter(joined, "wide", scatter_dimension=0, tiled=True).astype(jnp.float32)
+    out = []
+    start = 0
+    for w in widths:
+        out.append(summed[:, start : start + w])
+        start += w
+    return out
 
 
 def shards(
@@ -78,31 +163,33 @@
     w_down,
 ):
     narrow_size = lax.axis_size("narrow")
+    wide_size = lax.axis_size("wide")
     heads_here = H // narrow_size
     groups_here = KV // narrow_size
     repeat = H // KV
     seq_count, length = doc_ids.shape
     rows_group = seq_count * length
     scale = HD ** (-0.5)
-
-    def fetch_attention():
-        return (
-            lax.all_gather(attn_gain, "wide", axis=0, tiled=True),
-            lax.all_gather(w_query, "wide", axis=0, tiled=True),
-            lax.all_gather(w_key, "wide", axis=0, tiled=True),
-            lax.all_gather(w_value, "wide", axis=0, tiled=True),
-            lax.all_gather(query_gain, "wide", axis=0, tiled=True),
-            lax.all_gather(key_gain, "wide", axis=0, tiled=True),
-            lax.all_gather(w_out, "wide", axis=1, tiled=True),
-        )
-
-    def fetch_mlp():
-        return (
-            lax.all_gather(mlp_gain, "wide", axis=0, tiled=True),
-            lax.all_gather(w_gate, "wide", axis=0, tiled=True),
-            lax.all_gather(w_up, "wide", axis=0, tiled=True),
-            lax.all_gather(w_down, "wide", axis=1, tiled=True),
-        )
+    d_local = attn_gain.shape[0]
+    hd_local = query_gain.shape[0]
+    q_cols = w_query.shape[1]
+    kv_cols = w_key.shape[1]
+    ff_cols = w_gate.shape[1]
+
+    gain_block = jnp.zeros((d_local, 128), jnp.bfloat16)
+    gain_block = gain_block.at[:, 0].set(attn_gain)
+    gain_block = gain_block.at[:, 1].set(mlp_gain)
+    gain_block = gain_block.at[:hd_local, 2].set(query_gain)
+    gain_block = gain_block.at[:hd_local, 3].set(key_gain)
+
+    query_w, key_w, value_w, out_wt, gains_all = wide_gather(
+        [w_query, w_key, w_value, w_out.T, gain_block]
+    )
+    gain_attn = gains_all[:, 0].astype(jnp.float32)
+    gain_mlp = gains_all[:, 1].astype(jnp.float32)
+    gain_query = gains_all.reshape(wide_size, d_local, 128)[:, :hd_local, 2].reshape(-1).astype(jnp.float32)
+    gain_key = gains_all.reshape(wide_size, d_local, 128)[:, :hd_local, 3].reshape(-1).astype(jnp.float32)
+    gate_w, up_w, down_wt = wide_gather([w_gate, w_up, w_down.T])
 
     cosine, sine = rope_tables(doc_ids)
     cos_heads = cosine[:, :, None, :]
@@ -113,15 +200,10 @@
     def mask_for(doc_row):
         return causal & (doc_row[None, :] == doc_row[:, None])
 
-    attn_set = fetch_attention()
-    gain_attn = attn_set[0].astype(jnp.float32)
-    query_w, key_w, value_w = (attn_set[1], attn_set[2], attn_set[3])
-    gain_query = attn_set[4].astype(jnp.float32)
-    gain_key = attn_set[5].astype(jnp.float32)
-    out_w = attn_set[6]
     inputs = tokens.astype(jnp.float32)
     normed = rms_apply(inputs, gain_attn).astype(jnp.bfloat16)
-    normed_all = lax.all_gather(normed, "narrow", axis=0, tiled=True)
+    normed_all = narrow_gather(normed)
+    grad_rows = narrow_gather(cotangent)
     q_pre = jnp.dot(normed_all, query_w, preferred_element_type=jnp.float32).reshape(
         seq_count, length, heads_here, HD
     )
@@ -158,58 +240,28 @@
 
     unused, (attended, log_totals) = lax.scan(attend, 0, (q_grouped, k_use, v_use, doc_ids))
     attended = attended.reshape(rows_group, heads_here * HD)
-    resid = inputs + lax.psum_scatter(
-        jnp.dot(attended, out_w, preferred_element_type=jnp.float32).astype(jnp.bfloat16),
-        "narrow",
-        scatter_dimension=0,
-        tiled=True,
-    ).astype(jnp.float32)
-    mlp_set = fetch_mlp()
-    gain_mlp = mlp_set[0].astype(jnp.float32)
-    gate_w, up_w, down_w = (mlp_set[1], mlp_set[2], mlp_set[3])
+    resid = inputs + narrow_scatter(times_transposed(attended, out_wt))
     mlp_in = rms_apply(resid, gain_mlp).astype(jnp.bfloat16)
-    mlp_all = lax.all_gather(mlp_in, "narrow", axis=0, tiled=True)
+    mlp_all = narrow_gather(mlp_in)
     gate = jnp.dot(mlp_all, gate_w, preferred_element_type=jnp.float32)
     up = jnp.dot(mlp_all, up_w, preferred_element_type=jnp.float32)
     sigmoid = jax.nn.sigmoid(gate)
     hidden = (gate * sigmoid * up).astype(jnp.bfloat16)
-    output = (
-        resid
-        + lax.psum_scatter(
-            jnp.dot(hidden, down_w, preferred_element_type=jnp.float32).astype(jnp.bfloat16),
-            "narrow",
-            scatter_dimension=0,
-            tiled=True,
-        ).astype(jnp.float32)
-    ).astype(jnp.bfloat16)
-    mlp_set = fetch_mlp()
-    gain_mlp = mlp_set[0].astype(jnp.float32)
-    gate_w, up_w, down_w = (mlp_set[1], mlp_set[2], mlp_set[3])
-    grad_rows = lax.all_gather(cotangent, "narrow", axis=0, tiled=True)
-    grad_w_down = contract_rows(hidden, grad_rows)
-    d_hidden = times_transposed(grad_rows, down_w)
+    output = (resid + narrow_scatter(times_transposed(hidden, down_wt))).astype(jnp.bfloat16)
+    grad_w_down_t = contract_rows(grad_rows, hidden)
+    d_hidden = jnp.dot(grad_rows, down_wt, preferred_element_type=jnp.float32)
     d_up = (d_hidden * gate * sigmoid).astype(jnp.bfloat16)
     d_gate = (d_hidden * up * sigmoid * (1.0 + gate * (1.0 - sigmoid))).astype(jnp.bfloat16)
     grad_w_gate = contract_rows(mlp_all, d_gate)
     grad_w_up = contract_rows(mlp_all, d_up)
-    d_mlp_in = lax.psum_scatter(
-        (times_transposed(d_gate, gate_w) + times_transposed(d_up, up_w)).astype(jnp.bfloat16),
-        "narrow",
-        scatter_dimension=0,
-        tiled=True,
-    ).astype(jnp.float32)
+    mlp_shards = wide_scatter([grad_w_gate, grad_w_up, grad_w_down_t])
+    d_mlp_in = narrow_scatter(times_transposed(d_gate, gate_w) + times_transposed(d_up, up_w))
     d_part, mlp_gain_terms = rms_back(resid, gain_mlp, d_mlp_in)
     grad_mlp_gain = jnp.sum(mlp_gain_terms, axis=0)
     d_resid = cotangent.astype(jnp.float32) + d_part
-    attn_set = fetch_attention()
-    gain_attn = attn_set[0].astype(jnp.float32)
-    query_w, key_w, value_w = (attn_set[1], attn_set[2], attn_set[3])
-    gain_query = attn_set[4].astype(jnp.float32)
-    gain_key = attn_set[5].astype(jnp.float32)
-    out_w = attn_set[6]
-    branch_rows = lax.all_gather(d_resid.astype(jnp.bfloat16), "narrow", axis=0, tiled=True)
-    grad_w_out = contract_rows(attended, branch_rows)
-    d_attended = times_transposed(branch_rows, out_w).astype(jnp.bfloat16)
+    branch_rows = narrow_gather(d_resid.astype(jnp.bfloat16))
+    grad_w_out_t = contract_rows(branch_rows, attended)
+    d_attended = jnp.dot(branch_rows, out_wt, preferred_element_type=jnp.float32).astype(jnp.bfloat16)
     d_grouped = d_attended.reshape(seq_count, length, groups_here, repeat, HD)
 
     def attend_back(carry, items):
@@ -256,69 +308,37 @@
     grad_w_value = contract_rows(normed_all, d_value)
     total = times_transposed(d_q_pre, query_w)
     total = total + times_transposed(d_k_pre, key_w)
-    d_normed = lax.psum_scatter(
-        (total + times_transposed(d_value, value_w)).astype(jnp.bfloat16),
-        "narrow",
-        scatter_dimension=0,
-        tiled=True,
-    ).astype(jnp.float32)
+    d_normed = narrow_scatter(total + times_transposed(d_value, value_w))
     d_input_part, attn_gain_terms = rms_back(inputs, gain_attn, d_normed)
     grad_attn_gain = jnp.sum(attn_gain_terms, axis=0)
     d_tokens = d_resid + d_input_part
-    every_shard = (
-        lax.psum_scatter(
-            grad_attn_gain.astype(jnp.bfloat16), "wide", scatter_dimension=0, tiled=True
-        ).astype(jnp.float32),
-        lax.psum_scatter(
-            grad_w_query.astype(jnp.bfloat16), "wide", scatter_dimension=0, tiled=True
-        ).astype(jnp.float32),
-        lax.psum_scatter(
-            grad_w_key.astype(jnp.bfloat16), "wide", scatter_dimension=0, tiled=True
-        ).astype(jnp.float32),
-        lax.psum_scatter(
-            grad_w_value.astype(jnp.bfloat16), "wide", scatter_dimension=0, tiled=True
-        ).astype(jnp.float32),
-        lax.psum_scatter(
-            grad_query_gain.astype(jnp.bfloat16), "wide", scatter_dimension=0, tiled=True
-        ).astype(jnp.float32),
-        lax.psum_scatter(
-            grad_key_gain.astype(jnp.bfloat16), "wide", scatter_dimension=0, tiled=True
-        ).astype(jnp.float32),
-        lax.psum_scatter(
-            grad_w_out.astype(jnp.bfloat16), "wide", scatter_dimension=1, tiled=True
-        ).astype(jnp.float32),
-        lax.psum_scatter(
-            grad_mlp_gain.astype(jnp.bfloat16), "wide", scatter_dimension=0, tiled=True
-        ).astype(jnp.float32),
-        lax.psum_scatter(
-            grad_w_gate.astype(jnp.bfloat16), "wide", scatter_dimension=0, tiled=True
-        ).astype(jnp.float32),
-        lax.psum_scatter(
-            grad_w_up.astype(jnp.bfloat16), "wide", scatter_dimension=0, tiled=True
-        ).astype(jnp.float32),
-        lax.psum_scatter(
-            grad_w_down.astype(jnp.bfloat16), "wide", scatter_dimension=1, tiled=True
-        ).astype(jnp.float32),
-    )
-    attn_shards = every_shard[:7]
-    mlp_shards = every_shard[7:]
-    gain_totals = lax.psum(
-        (attn_shards[0], attn_shards[4], attn_shards[5], mlp_shards[0]), "narrow"
-    )
+
+    d_full = d_local * wide_size
+    gain_grads = jnp.zeros((d_full, 128), jnp.float32)
+    gain_grads = gain_grads.at[:, 0].set(grad_attn_gain)
+    gain_grads = gain_grads.at[:, 1].set(grad_mlp_gain)
+    gain_grads = gain_grads.reshape(wide_size, d_local, 128)
+    gain_grads = gain_grads.at[:, :hd_local, 2].set(grad_query_gain.reshape(wide_size, hd_local))
+    gain_grads = gain_grads.at[:, :hd_local, 3].set(grad_key_gain.reshape(wide_size, hd_local))
+    gain_grads = gain_grads.reshape(d_full, 128)
+    g_query, g_key, g_value, g_out_t, g_gains = wide_scatter(
+        [grad_w_query, grad_w_key, grad_w_value, grad_w_out_t, gain_grads]
+    )
+    gain_totals = lax.psum(g_gains[:, :4], "narrow")
     return (
         output,
         d_tokens,
-        gain_totals[0],
-        attn_shards[1],
-        attn_shards[2],
-        attn_shards[3],
-        gain_totals[1],
-        gain_totals[2],
-        attn_shards[6],
-        gain_totals[3],
+        gain_totals[:, 0],
+        g_query,
+        g_key,
+        g_value,
+        gain_totals[:hd_local, 2],
+        gain_totals[:hd_local, 3],
+        g_out_t.T,
+        gain_totals[:, 1],
+        mlp_shards[0],
         mlp_shards[1],
-        mlp_shards[2],
-        mlp_shards[3],
+        mlp_shards[2].T,
     )
 
 

time: 1170 us -> 876 us (0.75)
  waiting for transfers between devices: 796 us -> 442 us
  local copies, waits for them, and re-layouts: 9.69 us -> 84 us
  blocking collectives: 65.8 us -> 9.85 us
  other arithmetic: 73.7 us -> 117 us
  starting transfers between devices: 1.27 us -> 37.1 us
  matrix products: 194 us -> 165 us
    all_gather x11 -> x2, waiting for transfers between devices: 375 us -> 65.3 us  [wide_gather(): lax.all_gather(jnp.concatenate(blocks, axis=1), 'wide', axis=0, tiled=True)]
    reduce_scatter x11 -> x2, waiting for transfers between devices: 416 us -> 183 us  [wide_scatter(): lax.psum_scatter(joined, 'wide', scatter_dimension=0, tiled=True)]
    ppermute x0 -> x32, waiting for transfers between devices: none -> 194 us  [the longest x4 48.2 us: narrow_scatter(): b_got = lax.ppermute(b_send.astype(jnp.bfloat16), 'narrow', XPERM)]
    ppermute x0 -> x32, starting transfers between devices: none -> 36.7 us  [the longest x4 5.96 us: narrow_scatter(): a_got = lax.ppermute(a_send.astype(jnp.bfloat16), 'narrow', YPERM)]
    concatenate x0 -> x2, other arithmetic: none -> 33.9 us  [the longest x1 31.1 us: wide_scatter(): jnp.concatenate([blk.astype(jnp.bfloat16) for blk in blocks], axis=1)]
    unnamed x2 -> x0, blocking collectives: 30.7 us -> none
    unnamed x133 -> x192, local copies, waits for them, and re-layouts: 9.4 us -> 35.4 us
    all_gather x2 -> x0, blocking collectives: 25.1 us -> none  [the longest x1 13.5 us: fetch_attention(): lax.all_gather(attn_gain, 'wide', axis=0, tiled=True)]
  transfers between devices with their start and end apart: 22 -> 36, of which waited for: 20 -> 25; matrix products, arithmetic and copies ran while one was open for 19% -> 21% of each run, Pallas kernels for 0% -> 0%
where the time goes in v1:
time: 876 us; the launch traced here: 872 us
  waiting for transfers between devices  442 us (50%)
  matrix products  165 us (19%)
  other arithmetic  117 us (13%)
  local copies, waits for them, and re-layouts  84 us (10%)
  starting transfers between devices  37.1 us (4%)
  between operations  16 us (2%)
  blocking collectives  9.85 us (1%)
    reduce_scatter x2, waiting for transfers between devices, wide_scatter(): lax.psum_scatter(joined, 'wide', scatter_dimension=0, tiled=True)  183 us
    all_gather x2, waiting for transfers between devices, wide_gather(): lax.all_gather(jnp.concatenate(blocks, axis=1), 'wide', axis=0, tiled=True)  65.3 us
    ppermute x4, waiting for transfers between devices, narrow_scatter(): b_got = lax.ppermute(b_send.astype(jnp.bfloat16), 'narrow', XPERM)  48.2 us
    ppermute x4, waiting for transfers between devices, narrow_gather(): b_pair_x = lax.ppermute(b_pair, 'narrow', XPERM)  43.8 us
    dot_general x7, matrix products, times_transposed(): lax.dot_general(left, right, (((1,), (1,)), ((), ())), preferred_element_...  41.9 us
    dot_general x7, matrix products, contract_rows(): lax.dot_general(left, right, (((0,), (0,)), ((), ())), preferred_element_...  40 us
    unnamed x192, local copies, waits for them, and re-layouts  35.4 us
    ppermute x4, waiting for transfers between devices, narrow_gather(): b_y = lax.ppermute(b, 'narrow', YPERM)  32.4 us
  transfers between devices with their start and end apart: 36, of which 25 were waited for; matrix products, arithmetic and copies ran while one was open for 21% of the time, Pallas kernels for 0%

profile of v1, /device:TPU:0, one launch (start us, length us, event | category | flops | bytes accessed | tf_op | source)
XLA Modules:
  0.0 872.2 jit_solution(11856894818581208094)
XLA Ops:
  33.9 65.3 %all-gather.3.cloned.1.call-done = bf16[2048,1664]{1,0:T(8,128)(2,1)} async-done(((bf16[256,1664]{1,0:T(8,128)(2,1)}), bf16[2048,1664]{1,0:T(8,128)(2,1)}) %all-gather.3.cloned.1.call-update) | async-done | bytes 6815760 | tf_op jit(solution)/shard_map/all_gather | solution.py:128
  107.6 10.2 %collective-permute-done.2 = bf16[256,1024]{1,0:T(8,128)(2,1)S(1)} collective-permute-done((bf16[256,1024]{1,0:T(8,128)(2,1)}, bf16[256,1024]{1,0:T(8,128)(2,1)S(1)}, u32[]{:S(2)}, u32[]{:S(2)}) %collective-permute-start.2) | collective-permute-done | bytes 524320 | tf_op jit(solution)/shard_map/ppermute | solution.py:83
  129.0 15.9 %collective-permute-done.3 = bf16[2,256,1024]{2,1,0:T(8,128)(2,1)} collective-permute-done((bf16[2,256,1024]{2,1,0:T(8,128)(2,1)}, bf16[2,256,1024]{2,1,0:T(8,128)(2,1)}, u32[]{:S(2)}, u32[]{:S(2)}) %collective-permute-start.3) | collective-permute-done | bytes 1048608 | tf_op jit(solution)/shard_map/ppermute | solution.py:87
  195.2 19.6 %collective-permute-done.6 = bf16[2,256,1024]{2,1,0:T(8,128)(2,1)} collective-permute-done((bf16[2,256,1024]{2,1,0:T(8,128)(2,1)S(1)}, bf16[2,256,1024]{2,1,0:T(8,128)(2,1)}, u32[]{:S(2)}, u32[]{:S(2)}) %collective-permute-start.6) | collective-permute-done | bytes 1048608 | tf_op jit(solution)/shard_map/ppermute | solution.py:112
  255.5 25.4 %collective-permute-done.8 = bf16[256,1024]{1,0:T(8,128)(2,1)S(1)} collective-permute-done((bf16[256,1024]{1,0:T(8,128)(2,1)S(1)}, bf16[256,1024]{1,0:T(8,128)(2,1)S(1)}, u32[]{:S(2)}, u32[]{:S(2)}) %collective-permute-start.8) | collective-permute-done | bytes 524320 | tf_op jit(solution)/shard_map/ppermute | solution.py:82
  286.7 12.4 %collective-permute-done.11 = bf16[2,256,1024]{2,1,0:T(8,128)(2,1)S(1)} collective-permute-done((bf16[2,256,1024]{2,1,0:T(8,128)(2,1)S(1)}, bf16[2,256,1024]{2,1,0:T(8,128)(2,1)S(1)}, u32[]{:S(2)}, u32[]{:S(2)}) %collective-permute-start.11) | collective-permute-done | bytes 1048608 | tf_op jit(solution)/shard_map/ppermute | solution.py:87
  302.7 12.1 %fusion.12 = f32[1024,1536]{1,0:T(8,128)} fusion(bf16[2048,4608]{0,1:T(8,128)(2,1)} %all-gather.5.cloned.1.call-done, bf16[1024,1024]{1,0:T(8,128)(2,1)} %bitcast.444, bf16[1024,1024]{1,0:T(8,128)(2,1)} %bitcast.446), kind=kOutput, calls=%fused_computation.26 | convolution fusion | flops 6450839552 | bytes 16777216 | tf_op jit(solution)/shard_map/dot_general | solution.py:252
  314.9 10.5 %fusion.18 = f32[1024,1536]{1,0:T(8,128)} fusion(bf16[2048,4608]{0,1:T(8,128)(2,1)} %all-gather.5.cloned.1.call-done, bf16[1024,1024]{1,0:T(8,128)(2,1)S(1)} %bitcast.449, bf16[1024,1024]{1,0:T(8,128)(2,1)S(1)} %bitcast.453), kind=kOutput, calls=%fused_computation.32 | convolution fusion | flops 6450839552 | bytes 16777216 | tf_op jit(solution)/shard_map/dot_general | solution.py:247
  325.3 16.9 %multiply_convert_fusion.1 = (bf16[1024,1536]{1,0:T(8,128)(2,1)}, bf16[1024,1536]{1,0:T(8,128)(2,1)}, bf16[1024,1536]{1,0:T(8,128)(2,1)}) fusion(f32[1024,1536]{1,0:T(8,128)} %fusion.12, f32[1024,1536]{1,0:T(8,128)} %fusion.18, bf16[2048,4608]{0,1:T(8,128)(2,1)} %all-gather.5.cloned.1.call-done, bf16[1024,1024]{1,0:T(8,128)(2,1)} %bitcast.448, ...), kind=kOutput, calls=%fused_computation.23 | convolution fusion | flops 6476005376 | bytes 32505856 | tf_op jit(solution)/shard_map/dot_general | solution.py:246
  342.2 9.8 %fusion.16 = f32[1024,2048]{1,0:T(8,128)S(1)} fusion(bf16[1024,1536]{1,0:T(8,128)(2,1)} %get-tuple-element.224, bf16[2048,4608]{0,1:T(8,128)(2,1)} %all-gather.5.cloned.1.call-done), kind=kOutput, calls=%fused_computation.30 | convolution fusion | flops 6442450944 | bytes 17825792 | tf_op jit(solution)/shard_map/dot_general | solution.py:62
  352.1 11.0 %fusion.25 = f32[1024,2048]{1,0:T(8,128)} fusion(f32[1024,2048]{1,0:T(8,128)S(1)} %fusion.16, bf16[1024,1536]{1,0:T(8,128)(2,1)S(1)} %copy-done.77, bf16[2048,4608]{0,1:T(8,128)(2,1)} %all-gather.5.cloned.1.call-done), kind=kOutput, calls=%fused_computation.50 | convolution fusion | flops 6444548096 | bytes 26214400 | tf_op jit(solution)/shard_map/dot_general | solution.py:62
  370.2 10.8 %fusion.14 = f32[1024,2048]{1,0:T(8,128)} fusion(bf16[1024,1536]{1,0:T(8,128)(2,1)S(1)} %copy-done.76, bf16[2048,4608]{0,1:T(8,128)(2,1)} %all-gather.5.cloned.1.call-done), kind=kOutput, calls=%fused_computation.28 | convolution fusion | flops 6442450944 | bytes 17825792 | tf_op jit(solution)/shard_map/dot_general | solution.py:62
  398.9 17.1 %collective-permute-done.14 = bf16[2,256,1024]{2,1,0:T(8,128)(2,1)S(1)} collective-permute-done((bf16[2,256,1024]{2,1,0:T(8,128)(2,1)S(1)}, bf16[2,256,1024]{2,1,0:T(8,128)(2,1)S(1)}, u32[]{:S(2)}, u32[]{:S(2)}) %collective-permute-start.14) | collective-permute-done | bytes 1048608 | tf_op jit(solution)/shard_map/ppermute | solution.py:112
  420.0 9.2 %collective-permute-done.23 = bf16[256,1024]{1,0:T(8,128)(2,1)S(1)} collective-permute-done((bf16[256,1024]{1,0:T(8,128)(2,1)S(1)}, bf16[256,1024]{1,0:T(8,128)(2,1)S(1)}, u32[]{:S(2)}, u32[]{:S(2)}) %collective-permute-start.23) | collective-permute-done | bytes 524320 | tf_op jit(solution)/shard_map/ppermute | solution.py:120
  455.1 15.4 %collective-permute-done.27 = bf16[2,256,1024]{2,1,0:T(8,128)(2,1)S(1)} collective-permute-done((bf16[2,256,1024]{2,1,0:T(8,128)(2,1)S(1)}, bf16[2,256,1024]{2,1,0:T(8,128)(2,1)S(1)}, u32[]{:S(2)}, u32[]{:S(2)}) %collective-permute-start.27) | collective-permute-done | bytes 1048608 | tf_op jit(solution)/shard_map/ppermute | solution.py:87
  477.6 12.8 %fusion = (f32[2,2,1024]{2,1,0:T(2,128)S(1)}, f32[2,1024,1024,2]{2,1,3,0:T(8,128)}) fusion(f32[2,1024,1024,2]{2,1,3,0:T(8,128)} %copy-done, f32[2,2,1024]{2,1,0:T(2,128)S(1)} %log_add_fusion, pred[1024,1024]{0,1:T(8,128)(4,1)S(1)} %copy-done.8, bf16[1024,2,128,1]{0,2,3,1:T(8,128)(2,1)S(1)} %bitcast.485, bf16[1024,2,2,128]{0,3,2,1:T(8,128)(2,1)S(1)} %bitcast.481), kind=kOutput, calls=%fused_computation.3 | convolution fusion | flops 1094709248 | bytes 36208640 | tf_op jit(solution)/shard_map/while/body/eval_jaxpr/qgrd,kgd->grqk/dot_general | solution.py:274
  490.4 12.2 %fusion.2 = bf16[2,2,1024,1024]{2,3,1,0:T(8,128)(2,1)S(1)} fusion(f32[2,1024,1024,2]{2,1,3,0:T(8,128)} %get-tuple-element.297, f32[2,1024,1024,2]{2,1,3,0:T(8,128)} %copy-done, f32[2,2,1024]{2,1,0:T(2,128)S(1)} %get-tuple-element.296, f32[2,2,1024]{2,1,0:T(2,128)S(1)} %log_add_fusion, pred[1024,1024]{0,1:T(8,128)(4,1)S(1)} %copy-done.8), kind=kLoop, calls=%fused_computation.5 | loop fusion | flops 25165824 | bytes 43024384 | tf_op jit(solution)/shard_map/while/body/eval_jaxpr/convert_element_type | solution.py:276
  553.4 9.4 %collective-permute-done.28 = bf16[2,256,1024]{2,1,0:T(8,128)(2,1)S(1)} collective-permute-done((bf16[2,256,1024]{2,1,0:T(8,128)(2,1)S(1)}, bf16[2,256,1024]{2,1,0:T(8,128)(2,1)S(1)}, u32[]{:S(2)}, u32[]{:S(2)}) %collective-permute-start.28) | collective-permute-done | bytes 1048608 | tf_op jit(solution)/shard_map/ppermute | solution.py:111
  592.6 9.9 %convolution_convert_fusion = bf16[2048,1536]{0,1:T(8,128)(2,1)S(1)} fusion(bf16[1024,1536]{1,0:T(8,128)(2,1)} %get-tuple-element.223, bf16[1024,1024]{1,0:T(8,128)(2,1)} %bitcast.445, bf16[1024,1024]{1,0:T(8,128)(2,1)} %bitcast.447), kind=kOutput, calls=%fused_computation.19 | convolution fusion | flops 6453985280 | bytes 13631488 | tf_op jit(solution)/shard_map/dot_general | solution.py:56
  609.7 9.1 %convolution_convert_fusion.2 = bf16[2048,1536]{0,1:T(8,128)(2,1)S(1)} fusion(bf16[1024,1536]{1,0:T(8,128)(2,1)} %get-tuple-element.222, bf16[1024,1024]{1,0:T(8,128)(2,1)S(1)} %bitcast.451, bf16[1024,1024]{1,0:T(8,128)(2,1)S(1)} %bitcast.455), kind=kOutput, calls=%fused_computation.21 | convolution fusion | flops 6453985280 | bytes 13631488 | tf_op jit(solution)/shard_map/dot_general | solution.py:56
  618.8 31.1 %pad_maximum_fusion = bf16[2048,4608]{0,1:T(8,128)(2,1)} fusion(bf16[2048,1536]{0,1:T(8,128)(2,1)S(1)} %convolution_convert_fusion, bf16[2048,1536]{0,1:T(8,128)(2,1)S(1)} %convolution_convert_fusion.1, bf16[2048,1536]{0,1:T(8,128)(2,1)S(1)} %convolution_convert_fusion.2), kind=kLoop, calls=%fused_computation | loop fusion | flops 56623104 | bytes 37748736 | tf_op jit(solution)/shard_map/concatenate | solution.py:139
  654.1 11.4 %reduce-scatter.3.cloned.1.call-done = bf16[256,1664]{0,1:T(8,128)(2,1)} async-done(((bf16[2048,1664]{0,1:T(8,128)(2,1)}), bf16[256,1664]{0,1:T(8,128)(2,1)}) %reduce-scatter.3.cloned.1.call-update) | async-done | bytes 851984 | tf_op jit(solution)/shard_map/reduce_scatter | solution.py:140
  670.4 9.8 %psum.7 = f32[256,4]{0,1:T(4,128)S(1)} all-reduce(f32[256,4]{0,1:T(4,128)S(1)} %slice.404), channel_id=1, replica_groups=mesh['wide'=8,'narrow'=4] {'narrow'}, use_global_device_ids=true, to_apply=%region_25.26 | all-reduce | flops 1024 | bytes 8192 | tf_op jit(solution)/shard_map/psum | solution.py:327
  682.2 171.9 %reduce-scatter.5.cloned.1.call-done = bf16[256,4608]{0,1:T(8,128)(2,1)} async-done(((bf16[2048,4608]{0,1:T(8,128)(2,1)}), bf16[256,4608]{0,1:T(8,128)(2,1)}) %reduce-scatter.5.cloned.1.call-update) | async-done | bytes 2359312 | tf_op jit(solution)/shard_map/reduce_scatter | solution.py:140
  (447 shorter events, 316.8 us)
Async XLA Ops:
  7.2 92.0 %all-gather.3.cloned.1.call-start = ((), (), s32[]{:S(2)}) async-start(), calls=%async_computation.2 | async-start | bytes 7667712 | tf_op jit(solution)/shard_map/all_gather | solution.py:128
  27.3 275.5 %all-gather.5.cloned.1.call-start = ((), (), s32[]{:S(2)}) async-start(), calls=%async_computation.3 | async-start | bytes 21233664 | tf_op jit(solution)/shard_map/all_gather | solution.py:128
  31.9 633.6 %reduce-scatter.3.cloned.1.call-start = ((), (), s32[]{:S(2)}) async-start(), calls=%async_computation.4 | async-start | bytes 7667712 | tf_op jit(solution)/shard_map/reduce_scatter | solution.py:140
  120.1 24.9 %collective-permute-start.3 = (bf16[2,256,1024]{2,1,0:T(8,128)(2,1)}, bf16[2,256,1024]{2,1,0:T(8,128)(2,1)}, u32[]{:S(2)}, u32[]{:S(2)}) collective-permute-start(bf16[2,256,1024]{2,1,0:T(8,128)(2,1)} %maximum_select_fusion.11), channel_id=1, source_target_pairs={{0,1},{1,0},{2,3},{3,2},{4,5},{5,4},{6,7},{7,6},{8,9},{9,8},{10,11... | collective-permute-start | bytes 3145736 | tf_op jit(solution)/shard_map/ppermute | solution.py:87
  125.1 24.6 %collective-permute-start.1 = (bf16[2,256,1024]{2,1,0:T(8,128)(2,1)}, bf16[2,256,1024]{2,1,0:T(8,128)(2,1)}, u32[]{:S(2)}, u32[]{:S(2)}) collective-permute-start(bf16[2,256,1024]{2,1,0:T(8,128)(2,1)} %maximum_select_fusion.9), channel_id=1, source_target_pairs={{0,2},{2,0},{1,3},{3,1},{4,6},{6,4},{5,7},{7,5},{8,10},{10,8},{9,1... | collective-permute-start | bytes 3145736 | tf_op jit(solution)/shard_map/ppermute | solution.py:86
  191.3 23.6 %collective-permute-start.6 = (bf16[2,256,1024]{2,1,0:T(8,128)(2,1)S(1)}, bf16[2,256,1024]{2,1,0:T(8,128)(2,1)}, u32[]{:S(2)}, u32[]{:S(2)}) collective-permute-start(bf16[2,256,1024]{2,1,0:T(8,128)(2,1)S(1)} %fusion.72), channel_id=1, source_target_pairs={{0,1},{1,0},{2,3},{3,2},{4,5},{5,4},{6,7},{7,6},{8,9},{9,8},{10,11... | collective-permute-start | bytes 3145736 | tf_op jit(solution)/shard_map/ppermute | solution.py:112
  193.7 25.1 %collective-permute-start.4 = (bf16[2,256,1024]{2,1,0:T(8,128)(2,1)S(1)}, bf16[2,256,1024]{2,1,0:T(8,128)(2,1)}, u32[]{:S(2)}, u32[]{:S(2)}) collective-permute-start(bf16[2,256,1024]{2,1,0:T(8,128)(2,1)S(1)} %fusion.71), channel_id=1, source_target_pairs={{0,2},{2,0},{1,3},{3,1},{4,6},{6,4},{5,7},{7,5},{8,10},{10,8},{9,1... | collective-permute-start | bytes 3145736 | tf_op jit(solution)/shard_map/ppermute | solution.py:111
  221.6 21.9 %collective-permute-start.18 = (bf16[256,1024]{1,0:T(8,128)(2,1)S(1)}, bf16[256,1024]{1,0:T(8,128)(2,1)S(1)}, u32[]{:S(2)}, u32[]{:S(2)}) collective-permute-start(bf16[256,1024]{1,0:T(8,128)(2,1)S(1)} %get-tuple-element.256), channel_id=1, source_target_pairs={{0,2},{2,0},{1,3},{3,1},{4,6},{6,4},{5,7},{7,5},{8,10},{10,8},{9,1... | collective-permute-start | bytes 1572872 | tf_op jit(solution)/shard_map/ppermute | solution.py:83
  223.1 23.3 %collective-permute-start.16 = (bf16[256,1024]{1,0:T(8,128)(2,1)S(1)}, bf16[256,1024]{1,0:T(8,128)(2,1)S(1)}, u32[]{:S(2)}, u32[]{:S(2)}) collective-permute-start(bf16[256,1024]{1,0:T(8,128)(2,1)S(1)} %get-tuple-element.257), channel_id=1, source_target_pairs={{0,1},{1,0},{2,3},{3,2},{4,5},{5,4},{6,7},{7,6},{8,9},{9,8},{10,11... | collective-permute-start | bytes 1572872 | tf_op jit(solution)/shard_map/ppermute | solution.py:82
  243.6 39.2 %collective-permute-start.19 = (bf16[2,256,1024]{2,1,0:T(8,128)(2,1)S(1)}, bf16[2,256,1024]{2,1,0:T(8,128)(2,1)S(1)}, u32[]{:S(2)}, u32[]{:S(2)}) collective-permute-start(bf16[2,256,1024]{2,1,0:T(8,128)(2,1)S(1)} %maximum_select_fusion.18), channel_id=1, source_target_pairs={{0,1},{1,0},{2,3},{3,2},{4,5},{5,4},{6,7},{7,6},{8,9},{9,8},{10,11... | collective-permute-start | bytes 3145736 | tf_op jit(solution)/shard_map/ppermute | solution.py:87
  246.6 38.1 %collective-permute-start.17 = (bf16[2,256,1024]{2,1,0:T(8,128)(2,1)S(1)}, bf16[2,256,1024]{2,1,0:T(8,128)(2,1)S(1)}, u32[]{:S(2)}, u32[]{:S(2)}) collective-permute-start(bf16[2,256,1024]{2,1,0:T(8,128)(2,1)S(1)} %maximum_select_fusion.17), channel_id=1, source_target_pairs={{0,2},{2,0},{1,3},{3,1},{4,6},{6,4},{5,7},{7,5},{8,10},{10,8},{9,1... | collective-permute-start | bytes 3145736 | tf_op jit(solution)/shard_map/ppermute | solution.py:86
  246.7 34.3 %collective-permute-start.8 = (bf16[256,1024]{1,0:T(8,128)(2,1)S(1)}, bf16[256,1024]{1,0:T(8,128)(2,1)S(1)}, u32[]{:S(2)}, u32[]{:S(2)}) collective-permute-start(bf16[256,1024]{1,0:T(8,128)(2,1)S(1)} %get-tuple-element.263), channel_id=1, source_target_pairs={{0,1},{1,0},{2,3},{3,2},{4,5},{5,4},{6,7},{7,6},{8,9},{9,8},{10,11... | collective-permute-start | bytes 1572872 | tf_op jit(solution)/shard_map/ppermute | solution.py:82
  254.9 44.3 %collective-permute-start.11 = (bf16[2,256,1024]{2,1,0:T(8,128)(2,1)S(1)}, bf16[2,256,1024]{2,1,0:T(8,128)(2,1)S(1)}, u32[]{:S(2)}, u32[]{:S(2)}) collective-permute-start(bf16[2,256,1024]{2,1,0:T(8,128)(2,1)S(1)} %maximum_select_fusion.15), channel_id=1, source_target_pairs={{0,1},{1,0},{2,3},{3,2},{4,5},{5,4},{6,7},{7,6},{8,9},{9,8},{10,11... | collective-permute-start | bytes 3145736 | tf_op jit(solution)/shard_map/ppermute | solution.py:87
  281.1 19.9 %collective-permute-start.9 = (bf16[2,256,1024]{2,1,0:T(8,128)(2,1)S(1)}, bf16[2,256,1024]{2,1,0:T(8,128)(2,1)S(1)}, u32[]{:S(2)}, u32[]{:S(2)}) collective-permute-start(bf16[2,256,1024]{2,1,0:T(8,128)(2,1)S(1)} %maximum_select_fusion.13), channel_id=1, source_target_pairs={{0,2},{2,0},{1,3},{3,1},{4,6},{6,4},{5,7},{7,5},{8,10},{10,8},{9,1... | collective-permute-start | bytes 3145736 | tf_op jit(solution)/shard_map/ppermute | solution.py:86
  367.5 26.1 %collective-permute-start.22 = (bf16[2,256,1024]{2,1,0:T(8,128)(2,1)S(1)}, bf16[2,256,1024]{2,1,0:T(8,128)(2,1)}, u32[]{:S(2)}, u32[]{:S(2)}) collective-permute-start(bf16[2,256,1024]{2,1,0:T(8,128)(2,1)S(1)} %fusion.76), channel_id=1, source_target_pairs={{0,1},{1,0},{2,3},{3,2},{4,5},{5,4},{6,7},{7,6},{8,9},{9,8},{10,11... | collective-permute-start | bytes 3145736 | tf_op jit(solution)/shard_map/ppermute | solution.py:112
  369.2 26.3 %collective-permute-start.20 = (bf16[2,256,1024]{2,1,0:T(8,128)(2,1)}, bf16[2,256,1024]{2,1,0:T(8,128)(2,1)}, u32[]{:S(2)}, u32[]{:S(2)}) collective-permute-start(bf16[2,256,1024]{2,1,0:T(8,128)(2,1)} %fusion.74), channel_id=1, source_target_pairs={{0,2},{2,0},{1,3},{3,1},{4,6},{6,4},{5,7},{7,5},{8,10},{10,8},{9,1... | collective-permute-start | bytes 3145736 | tf_op jit(solution)/shard_map/ppermute | solution.py:111
  385.5 30.5 %collective-permute-start.14 = (bf16[2,256,1024]{2,1,0:T(8,128)(2,1)S(1)}, bf16[2,256,1024]{2,1,0:T(8,128)(2,1)S(1)}, u32[]{:S(2)}, u32[]{:S(2)}) collective-permute-start(bf16[2,256,1024]{2,1,0:T(8,128)(2,1)S(1)} %fusion.77), channel_id=1, source_target_pairs={{0,1},{1,0},{2,3},{3,2},{4,5},{5,4},{6,7},{7,6},{8,9},{9,8},{10,11... | collective-permute-start | bytes 3145736 | tf_op jit(solution)/shard_map/ppermute | solution.py:112
  386.7 31.2 %collective-permute-start.12 = (bf16[2,256,1024]{2,1,0:T(8,128)(2,1)S(1)}, bf16[2,256,1024]{2,1,0:T(8,128)(2,1)S(1)}, u32[]{:S(2)}, u32[]{:S(2)}) collective-permute-start(bf16[2,256,1024]{2,1,0:T(8,128)(2,1)S(1)} %fusion.73), channel_id=1, source_target_pairs={{0,2},{2,0},{1,3},{3,1},{4,6},{6,4},{5,7},{7,5},{8,10},{10,8},{9,1... | collective-permute-start | bytes 3145736 | tf_op jit(solution)/shard_map/ppermute | solution.py:111
  395.4 33.7 %collective-permute-start.23 = (bf16[256,1024]{1,0:T(8,128)(2,1)S(1)}, bf16[256,1024]{1,0:T(8,128)(2,1)S(1)}, u32[]{:S(2)}, u32[]{:S(2)}) collective-permute-start(bf16[256,1024]{1,0:T(8,128)(2,1)S(1)} %fusion.95), channel_id=1, source_target_pairs={{0,2},{2,0},{1,3},{3,1},{4,6},{6,4},{5,7},{7,5},{8,10},{10,8},{9,1... | collective-permute-start | bytes 1572872 | tf_op jit(solution)/shard_map/ppermute | solution.py:120
  397.3 32.0 %collective-permute-start.21 = (bf16[256,1024]{1,0:T(8,128)(2,1)S(1)}, bf16[256,1024]{1,0:T(8,128)(2,1)S(1)}, u32[]{:S(2)}, u32[]{:S(2)}) collective-permute-start(bf16[256,1024]{1,0:T(8,128)(2,1)S(1)} %fusion.94), channel_id=1, source_target_pairs={{0,1},{1,0},{2,3},{3,2},{4,5},{5,4},{6,7},{7,6},{8,9},{9,8},{10,11... | collective-permute-start | bytes 1572872 | tf_op jit(solution)/shard_map/ppermute | solution.py:119
  450.0 20.5 %collective-permute-start.27 = (bf16[2,256,1024]{2,1,0:T(8,128)(2,1)S(1)}, bf16[2,256,1024]{2,1,0:T(8,128)(2,1)S(1)}, u32[]{:S(2)}, u32[]{:S(2)}) collective-permute-start(bf16[2,256,1024]{2,1,0:T(8,128)(2,1)S(1)} %maximum_select_fusion.21), channel_id=1, source_target_pairs={{0,1},{1,0},{2,3},{3,2},{4,5},{5,4},{6,7},{7,6},{8,9},{9,8},{10,11... | collective-permute-start | bytes 3145736 | tf_op jit(solution)/shard_map/ppermute | solution.py:87
  530.5 19.5 %collective-permute-start.30 = (bf16[2,256,1024]{2,1,0:T(8,128)(2,1)S(1)}, bf16[2,256,1024]{2,1,0:T(8,128)(2,1)S(1)}, u32[]{:S(2)}, u32[]{:S(2)}) collective-permute-start(bf16[2,256,1024]{2,1,0:T(8,128)(2,1)S(1)} %fusion.78), channel_id=1, source_target_pairs={{0,1},{1,0},{2,3},{3,2},{4,5},{5,4},{6,7},{7,6},{8,9},{9,8},{10,11... | collective-permute-start | bytes 3145736 | tf_op jit(solution)/shard_map/ppermute | solution.py:112
  537.3 25.6 %collective-permute-start.28 = (bf16[2,256,1024]{2,1,0:T(8,128)(2,1)S(1)}, bf16[2,256,1024]{2,1,0:T(8,128)(2,1)S(1)}, u32[]{:S(2)}, u32[]{:S(2)}) collective-permute-start(bf16[2,256,1024]{2,1,0:T(8,128)(2,1)S(1)} %fusion.75), channel_id=1, source_target_pairs={{0,2},{2,0},{1,3},{3,1},{4,6},{6,4},{5,7},{7,5},{8,10},{10,8},{9,1... | collective-permute-start | bytes 3145736 | tf_op jit(solution)/shard_map/ppermute | solution.py:111
  592.5 261.6 %reduce-scatter.5.cloned.1.call-start = ((), (), s32[]{:S(2)}) async-start(), calls=%async_computation.5 | async-start | bytes 21233664 | tf_op jit(solution)/shard_map/reduce_scatter | solution.py:140
  (101 other events, 830.8 us)
Sparse Core Ops, SparseCore 0:
  27.4 71.7 all-gather.2
  100.7 167.7 all-gather.4
  592.6 72.8 reduce-scatter.2
  667.7 186.3 reduce-scatter.4

commit v2 on v1

v2 whole, which is shorter than its diff:
```python
import jax
import jax.numpy as jnp
from jax import lax
from jax.sharding import PartitionSpec as P

H = 16
KV = 8
HD = 128


EPS = 1e-06
ROPE_BASE = 1000000.0
NEG_FILL = -1e30

XPERM = [(0, 1), (1, 0), (2, 3), (3, 2)]
YPERM = [(0, 2), (2, 0), (1, 3), (3, 1)]
BLOCK_XOR = (0, 1, 2, 3, 0, 2, 1, 3)


def rms_apply(values, gain):
    return values * lax.rsqrt(jnp.mean(values * values, axis=-1, keepdims=True) + EPS) * gain


def rms_back(values, gain, grad):
    scale = lax.rsqrt(jnp.mean(values * values, axis=-1, keepdims=True) + EPS)
    weighted = grad * gain
    inner = jnp.mean(weighted * values, axis=-1, keepdims=True)
    d_values = scale * weighted - values * (scale * scale * scale) * inner
    return (d_values, grad * values * scale)


def rotate(values):
    half = values.shape[-1] // 2
    return jnp.concatenate([-values[..., half:], values[..., :half]], axis=-1)


def rotate_back(values):
    half = values.shape[-1] // 2
    return jnp.concatenate([values[..., half:], -values[..., :half]], axis=-1)


def doc_positions(doc_rows):
    index = lax.broadcasted_iota(jnp.int32, doc_rows.shape, 1)
    change = jnp.concatenate(
        [jnp.ones((doc_rows.shape[0], 1), jnp.bool_), doc_rows[:, 1:] != doc_rows[:, :-1]], axis=1
    )
    begin = lax.cummax(jnp.where(change, index, 0), axis=1)
    return index - begin


def rope_from_positions(position):
    freqs = ROPE_BASE ** (-(jnp.arange(HD // 2, dtype=jnp.float32) * (2.0 / HD)))
    angle = position.astype(jnp.float32)[..., None] * freqs
    cosine = jnp.cos(angle)
    sine = jnp.sin(angle)
    return (jnp.concatenate([cosine, cosine], axis=-1), jnp.concatenate([sine, sine], axis=-1))


def contract_rows(left, right):
    return lax.dot_general(
        left, right, (((0,), (0,)), ((), ())), preferred_element_type=jnp.float32
    )


def times_transposed(left, right):
    return lax.dot_general(
        left, right, (((1,), (1,)), ((), ())), preferred_element_type=jnp.float32
    )


def relative_ok(seq_count):
    return lax.axis_size("narrow") == 4 and seq_count == 1


def gather_order(shard_rows):
    n = lax.axis_index("narrow")
    half = shard_rows // 2
    index = jnp.arange(4 * shard_rows, dtype=jnp.int32)
    block = index // half
    offset = index % half
    block_xor = jnp.asarray(BLOCK_XOR, jnp.int32)[block]
    shard = jnp.bitwise_xor(n, block_xor)
    return shard * shard_rows + offset + half * (block >= 4).astype(jnp.int32)


def narrow_gather(x, relative):
    if not relative:
        return lax.all_gather(x, "narrow", axis=0, tiled=True)
    half = x.shape[0] // 2
    a, b = x[:half], x[half:]
    a_x = lax.ppermute(a, "narrow", XPERM)
    b_y = lax.ppermute(b, "narrow", YPERM)
    a_pair = jnp.concatenate([a, a_x], axis=0)
    b_pair = jnp.concatenate([b, b_y], axis=0)
    a_pair_y = lax.ppermute(a_pair, "narrow", YPERM)
    b_pair_x = lax.ppermute(b_pair, "narrow", XPERM)
    return jnp.concatenate([a_pair, a_pair_y, b_pair, b_pair_x], axis=0)


def narrow_scatter(x, relative):
    if not relative:
        return lax.psum_scatter(
            x.astype(jnp.bfloat16), "narrow", scatter_dimension=0, tiled=True
        ).astype(jnp.float32)
    rows, c = x.shape
    half = rows // 8
    blocks = x.reshape(8, half, c)
    a_got = lax.ppermute(blocks[2:4].astype(jnp.bfloat16), "narrow", YPERM)
    b_got = lax.ppermute(blocks[6:8].astype(jnp.bfloat16), "narrow", XPERM)
    a_sum = blocks[0:2] + a_got.astype(jnp.float32)
    b_sum = blocks[4:6] + b_got.astype(jnp.float32)
    a_got2 = lax.ppermute(a_sum[1].astype(jnp.bfloat16), "narrow", XPERM)
    b_got2 = lax.ppermute(b_sum[1].astype(jnp.bfloat16), "narrow", YPERM)
    return jnp.concatenate(
        [a_sum[0] + a_got2.astype(jnp.float32), b_sum[0] + b_got2.astype(jnp.float32)], axis=0
    )


def split_cols(joined, widths):
    out = []
    start = 0
    for w in widths:
        out.append(joined[:, start : start + w])
        start += w
    return out


def wide_gather(blocks):
    joined = lax.all_gather(jnp.concatenate(blocks, axis=1), "wide", axis=0, tiled=True)
    return split_cols(joined, [blk.shape[1] for blk in blocks])


def wide_scatter(blocks):
    joined = jnp.concatenate([blk.astype(jnp.bfloat16) for blk in blocks], axis=1)
    summed = lax.psum_scatter(joined, "wide", scatter_dimension=0, tiled=True).astype(jnp.float32)
    return split_cols(summed, [blk.shape[1] for blk in blocks])


def shards(
    tokens,
    doc_ids,
    cotangent,
    attn_gain,
    w_query,
    w_key,
    w_value,
    query_gain,
    key_gain,
    w_out,
    mlp_gain,
    w_gate,
    w_up,
    w_down,
):
    narrow_size = lax.axis_size("narrow")
    wide_size = lax.axis_size("wide")
    heads_here = H // narrow_size
    groups_here = KV // narrow_size
    repeat = H // KV
    seq_count, length = doc_ids.shape
    rows_group = seq_count * length
    shard_rows = tokens.shape[0]
    scale = HD ** (-0.5)
    d_local = attn_gain.shape[0]
    hd_local = query_gain.shape[0]
    q_cols = w_query.shape[1]
    kv_cols = w_key.shape[1]
    ff_cols = w_gate.shape[1]
    ff_half = ff_cols // 2
    relative = relative_ok(seq_count)

    tokens_all = narrow_gather(tokens, relative)
    grad_rows = narrow_gather(cotangent, relative)

    gain_block = jnp.zeros((d_local, 128), jnp.bfloat16)
    gain_block = gain_block.at[:, 0].set(attn_gain)
    gain_block = gain_block.at[:, 1].set(mlp_gain)
    gain_block = gain_block.at[:hd_local, 2].set(query_gain)
    gain_block = gain_block.at[:hd_local, 3].set(key_gain)
    qkv_w, out_wt, gains_all = wide_gather(
        [jnp.concatenate([w_query, w_key, w_value], axis=1), w_out.T, gain_block]
    )
    gain_attn = gains_all[:, 0].astype(jnp.float32)
    gain_mlp = gains_all[:, 1].astype(jnp.float32)
    gains_split = gains_all.reshape(wide_size, d_local, 128)
    gain_query = gains_split[:, :hd_local, 2].reshape(-1).astype(jnp.float32)
    gain_key = gains_split[:, :hd_local, 3].reshape(-1).astype(jnp.float32)
    down_t = w_down.T
    mlp_sets = []
    for h in range(2):
        cols = slice(h * ff_half, (h + 1) * ff_half)
        mlp_sets.append(wide_gather([w_gate[:, cols], w_up[:, cols], down_t[:, cols]]))

    if relative:
        order = gather_order(shard_rows)
        doc_row = jnp.take(doc_ids[0], order)
        position = jnp.take(doc_positions(doc_ids)[0], order)
    else:
        order = jnp.arange(rows_group, dtype=jnp.int32)
        doc_row = doc_ids.reshape(-1)
        position = doc_positions(doc_ids).reshape(-1)
    cosine, sine = rope_from_positions(position)
    cos_heads = cosine[:, None, :]
    sin_heads = sine[:, None, :]
    allowed = (order[None, :] <= order[:, None]) & (doc_row[None, :] == doc_row[:, None])
    if not relative:
        seq_of = jnp.arange(rows_group, dtype=jnp.int32) // length
        allowed = allowed & (seq_of[None, :] == seq_of[:, None])

    inputs = tokens.astype(jnp.float32)
    normed_all = rms_apply(tokens_all.astype(jnp.float32), gain_attn).astype(jnp.bfloat16)
    qkv = jnp.dot(normed_all, qkv_w, preferred_element_type=jnp.float32)
    q_pre = qkv[:, :q_cols].reshape(rows_group, heads_here, HD)
    k_pre = qkv[:, q_cols : q_cols + kv_cols].reshape(rows_group, groups_here, HD)
    v_use = qkv[:, q_cols + kv_cols :].astype(jnp.bfloat16).reshape(rows_group, groups_here, HD)
    q_norm = rms_apply(q_pre, gain_query)
    k_norm = rms_apply(k_pre, gain_key)
    q_use = (q_norm * cos_heads + rotate(q_norm) * sin_heads).astype(jnp.bfloat16)
    k_use = (k_norm * cos_heads + rotate(k_norm) * sin_heads).astype(jnp.bfloat16)
    q_grouped = q_use.reshape(rows_group, groups_here, repeat, HD)

    scores = jnp.einsum("qgrd,kgd->grqk", q_grouped, k_use, preferred_element_type=jnp.float32) * scale
    scores = jnp.where(allowed, scores, NEG_FILL)
    top = jnp.max(scores, axis=-1, keepdims=True)
    weights = jnp.exp(scores - top)
    total = jnp.sum(weights, axis=-1, keepdims=True)
    probs = weights / total
    mixed = jnp.einsum(
        "grqk,kgd->qgrd", probs.astype(jnp.bfloat16), v_use, preferred_element_type=jnp.float32
    )
    log_totals = (top + jnp.log(total))[..., 0]
    attended = mixed.astype(jnp.bfloat16).reshape(rows_group, heads_here * HD)

    resid = inputs + narrow_scatter(times_transposed(attended, out_wt), relative)
    mlp_in = rms_apply(resid, gain_mlp).astype(jnp.bfloat16)
    mlp_all = narrow_gather(mlp_in, relative)

    down_partial = None
    d_mlp_partial = None
    mlp_grads = []
    for h in range(2):
        gate_w, up_w, down_wt = mlp_sets[h]
        gate = jnp.dot(mlp_all, gate_w, preferred_element_type=jnp.float32)
        up = jnp.dot(mlp_all, up_w, preferred_element_type=jnp.float32)
        sigmoid = jax.nn.sigmoid(gate)
        hidden = (gate * sigmoid * up).astype(jnp.bfloat16)
        part = times_transposed(hidden, down_wt)
        down_partial = part if down_partial is None else down_partial + part
        g_down_t = contract_rows(grad_rows, hidden)
        d_hidden = jnp.dot(grad_rows, down_wt, preferred_element_type=jnp.float32)
        d_up = (d_hidden * gate * sigmoid).astype(jnp.bfloat16)
        d_gate = (d_hidden * up * sigmoid * (1.0 + gate * (1.0 - sigmoid))).astype(jnp.bfloat16)
        g_gate_up = contract_rows(mlp_all, jnp.concatenate([d_gate, d_up], axis=1))
        mlp_grads.append(wide_scatter([g_gate_up, g_down_t]))
        part = times_transposed(d_gate, gate_w) + times_transposed(d_up, up_w)
        d_mlp_partial = part if d_mlp_partial is None else d_mlp_partial + part

    d_mlp_in = narrow_scatter(d_mlp_partial, relative)
    d_part, mlp_gain_terms = rms_back(resid, gain_mlp, d_mlp_in)
    grad_mlp_gain = jnp.sum(mlp_gain_terms, axis=0)
    d_resid = cotangent.astype(jnp.float32) + d_part
    branch_rows = narrow_gather(d_resid.astype(jnp.bfloat16), relative)
    (g_out_t,) = wide_scatter([contract_rows(branch_rows, attended)])
    d_attended = jnp.dot(branch_rows, out_wt, preferred_element_type=jnp.float32).astype(jnp.bfloat16)
    d_mixed = d_attended.reshape(rows_group, groups_here, repeat, HD)

    p_scores = jnp.einsum("qgrd,kgd->grqk", q_grouped, k_use, preferred_element_type=jnp.float32) * scale
    p_probs = jnp.where(allowed, jnp.exp(p_scores - log_totals[..., None]), 0.0)
    d_probs = jnp.einsum("qgrd,kgd->grqk", d_mixed, v_use, preferred_element_type=jnp.float32)
    inner = jnp.sum(p_probs * d_probs, axis=-1, keepdims=True)
    d_scores = (p_probs * (d_probs - inner)).astype(jnp.bfloat16)
    d_query = jnp.einsum("grqk,kgd->qgrd", d_scores, k_use, preferred_element_type=jnp.float32) * scale
    d_key = jnp.einsum("grqk,qgrd->kgd", d_scores, q_grouped, preferred_element_type=jnp.float32) * scale
    d_value = jnp.einsum(
        "grqk,qgrd->kgd", p_probs.astype(jnp.bfloat16), d_mixed, preferred_element_type=jnp.float32
    ).astype(jnp.bfloat16)

    d_query = d_query.reshape(rows_group, heads_here, HD)
    d_q_norm = d_query * cos_heads + rotate_back(d_query * sin_heads)
    d_k_norm = d_key * cos_heads + rotate_back(d_key * sin_heads)
    d_q_pre, query_terms = rms_back(q_pre, gain_query, d_q_norm)
    d_k_pre, key_terms = rms_back(k_pre, gain_key, d_k_norm)
    grad_query_gain = jnp.sum(query_terms, axis=(0, 1))
    grad_key_gain = jnp.sum(key_terms, axis=(0, 1))
    d_qkv = jnp.concatenate(
        [
            d_q_pre.astype(jnp.bfloat16).reshape(rows_group, heads_here * HD),
            d_k_pre.astype(jnp.bfloat16).reshape(rows_group, groups_here * HD),
            d_value.reshape(rows_group, groups_here * HD),
        ],
        axis=1,
    )
    (g_qkv,) = wide_scatter([contract_rows(normed_all, d_qkv)])
    d_normed = narrow_scatter(times_transposed(d_qkv, qkv_w), relative)
    d_input_part, attn_gain_terms = rms_back(inputs, gain_attn, d_normed)
    grad_attn_gain = jnp.sum(attn_gain_terms, axis=0)
    d_tokens = d_resid + d_input_part

    gain_grads = lax.psum(
        jnp.concatenate([grad_attn_gain, grad_mlp_gain, grad_query_gain, grad_key_gain]),
        ("wide", "narrow"),
    )
    w = lax.axis_index("wide")
    d_full = d_local * wide_size
    hd_full = hd_local * wide_size
    attn_gain_grad = lax.dynamic_slice_in_dim(gain_grads, w * d_local, d_local)
    mlp_gain_grad = lax.dynamic_slice_in_dim(gain_grads, d_full + w * d_local, d_local)
    query_gain_grad = lax.dynamic_slice_in_dim(gain_grads, 2 * d_full + w * hd_local, hd_local)
    key_gain_grad = lax.dynamic_slice_in_dim(gain_grads, 2 * d_full + hd_full + w * hd_local, hd_local)

    g_query = g_qkv[:, :q_cols]
    g_key = g_qkv[:, q_cols : q_cols + kv_cols]
    g_value = g_qkv[:, q_cols + kv_cols :]
    g_gate = jnp.concatenate([mlp_grads[h][0][:, :ff_half] for h in range(2)], axis=1)
    g_up = jnp.concatenate([mlp_grads[h][0][:, ff_half:] for h in range(2)], axis=1)
    g_down = jnp.concatenate([mlp_grads[h][1] for h in range(2)], axis=1).T
    output = (resid + narrow_scatter(down_partial, relative)).astype(jnp.bfloat16)
    return (
        output,
        d_tokens,
        attn_gain_grad,
        g_query,
        g_key,
        g_value,
        query_gain_grad,
        key_gain_grad,
        g_out_t.T,
        mlp_gain_grad,
        g_gate,
        g_up,
        g_down,
    )


def solution(mesh):
    in_specs = (
        P(("wide", "narrow"), None),
        P("wide", None),
        P(("wide", "narrow"), None),
        P("wide"),
        P("wide", "narrow"),
        P("wide", "narrow"),
        P("wide", "narrow"),
        P("wide"),
        P("wide"),
        P("narrow", "wide"),
        P("wide"),
        P("wide", "narrow"),
        P("wide", "narrow"),
        P("narrow", "wide"),
    )
    out_specs = (
        P(("wide", "narrow"), None),
        P(("wide", "narrow"), None),
        P("wide"),
        P("wide", "narrow"),
        P("wide", "narrow"),
        P("wide", "narrow"),
        P("wide"),
        P("wide"),
        P("narrow", "wide"),
        P("wide"),
        P("wide", "narrow"),
        P("wide", "narrow"),
        P("narrow", "wide"),
    )
    return jax.shard_map(shards, mesh=mesh, in_specs=in_specs, out_specs=out_specs, check_vma=False)
```

time: 876 us -> 846 us (0.966)
  waiting for transfers between devices: 442 us -> 370 us
  matrix products: 165 us -> 210 us
  blocking collectives: 9.85 us -> 40.4 us
  other arithmetic: 117 us -> 91.5 us
    reduce_scatter x2 -> x4, waiting for transfers between devices: 183 us -> 104 us  [wide_scatter(): lax.psum_scatter(joined, 'wide', scatter_dimension=0, tiled=True)]
    all_gather x2 -> x3, waiting for transfers between devices: 65.3 us -> 6.48 us  [wide_gather(): lax.all_gather(jnp.concatenate(blocks, axis=1), 'wide', axis=0, tiled=True)]
    ppermute x4, waiting for transfers between devices: 2.49 us -> 37.2 us  [narrow_gather(): a_pair_y = lax.ppermute(a_pair, 'narrow', YPERM)]
    psum x1, blocking collectives: 9.85 us -> 40.4 us  [shards(): lax.psum(jnp.concatenate([grad_attn_gain, grad_mlp_gain, grad_query_gain,...]
    dot_general x7 -> x8, matrix products: 41.9 us -> 67.2 us  [times_transposed(): lax.dot_general(left, right, (((1,), (1,)), ((), ())), preferred_element_...]
    ppermute x16, waiting for transfers between devices: 87.2 us -> 109 us  [the longest x4 54.4 us: narrow_scatter(): a_got = lax.ppermute(blocks[2:4].astype(jnp.bfloat16), 'narrow', YPERM)]
    select_n x25 -> x2, other arithmetic: 15.9 us -> 0.01 us  [the longest x1 0.01 us: shards(): doc_row = jnp.take(doc_ids[0], order)]
    ppermute x4, waiting for transfers between devices: 32.4 us -> 44.9 us  [narrow_gather(): b_y = lax.ppermute(b, 'narrow', YPERM)]
  transfers between devices with their start and end apart: 36 -> 39, of which waited for: 25 -> 26; matrix products, arithmetic and copies ran while one was open for 21% -> 29% of each run, Pallas kernels for 0% -> 0%
where the time goes in v2:
time: 846 us; the launch traced here: 842 us
  waiting for transfers between devices  370 us (44%)
  matrix products  210 us (25%)
  other arithmetic  91.5 us (11%)
  local copies, waits for them, and re-layouts  76.6 us (9%)
  blocking collectives  40.4 us (5%)
  starting transfers between devices  36.7 us (4%)
  between operations  15.9 us (2%)
    reduce_scatter x4, waiting for transfers between devices, wide_scatter(): lax.psum_scatter(joined, 'wide', scatter_dimension=0, tiled=True)  104 us
    dot_general x8, matrix products, times_transposed(): lax.dot_general(left, right, (((1,), (1,)), ((), ())), preferred_element_...  67.2 us
    ppermute x4, waiting for transfers between devices, narrow_scatter(): a_got = lax.ppermute(blocks[2:4].astype(jnp.bfloat16), 'narrow', YPERM)  54.4 us
    ppermute x4, waiting for transfers between devices, narrow_gather(): b_pair_x = lax.ppermute(b_pair, 'narrow', XPERM)  48.6 us
    dot_general x6, matrix products, contract_rows(): lax.dot_general(left, right, (((0,), (0,)), ((), ())), preferred_element_...  45.3 us
    ppermute x4, waiting for transfers between devices, narrow_gather(): b_y = lax.ppermute(b, 'narrow', YPERM)  44.9 us
    psum x1, blocking collectives, shards(): lax.psum(jnp.concatenate([grad_attn_gain, grad_mlp_gain, grad_query_gain,...  40.4 us
    ppermute x4, waiting for transfers between devices, narrow_gather(): a_pair_y = lax.ppermute(a_pair, 'narrow', YPERM)  37.2 us
  transfers between devices with their start and end apart: 39, of which 26 were waited for; matrix products, arithmetic and copies ran while one was open for 29% of the time, Pallas kernels for 0%

profile of v2, /device:TPU:0, one launch (start us, length us, event | category | flops | bytes accessed | tf_op | source)
XLA Modules:
  0.0 841.9 jit_solution(475302104918632347)
XLA Ops:
  38.5 9.2 %collective-permute-done = bf16[128,2048]{1,0:T(8,128)(2,1)S(1)} collective-permute-done((bf16[128,2048]{1,0:T(8,128)(2,1)S(1)}, bf16[128,2048]{1,0:T(8,128)(2,1)S(1)}, u32[]{:S(2)}, u32[]{:S(2)}) %collective-permute-start) | collective-permute-done | bytes 524320 | tf_op jit(solution)/shard_map/ppermute | solution.py:91
  60.6 11.8 %collective-permute-done.1 = bf16[256,2048]{1,0:T(8,128)(2,1)} collective-permute-done((bf16[256,2048]{1,0:T(8,128)(2,1)S(1)}, bf16[256,2048]{1,0:T(8,128)(2,1)}, u32[]{:S(2)}, u32[]{:S(2)}) %collective-permute-start.1) | collective-permute-done | bytes 1048608 | tf_op jit(solution)/shard_map/ppermute | solution.py:95
  77.1 10.8 %collective-permute-done.2 = bf16[128,2048]{1,0:T(8,128)(2,1)S(1)} collective-permute-done((bf16[128,2048]{1,0:T(8,128)(2,1)S(1)}, bf16[128,2048]{1,0:T(8,128)(2,1)S(1)}, u32[]{:S(2)}, u32[]{:S(2)}) %collective-permute-start.2) | collective-permute-done | bytes 524320 | tf_op jit(solution)/shard_map/ppermute | solution.py:92
  93.4 17.4 %collective-permute-done.3 = bf16[256,2048]{1,0:T(8,128)(2,1)S(1)} collective-permute-done((bf16[256,2048]{1,0:T(8,128)(2,1)S(1)}, bf16[256,2048]{1,0:T(8,128)(2,1)S(1)}, u32[]{:S(2)}, u32[]{:S(2)}) %collective-permute-start.3) | collective-permute-done | bytes 1048608 | tf_op jit(solution)/shard_map/ppermute | solution.py:96
  159.6 21.2 %collective-permute-done.4 = bf16[2,128,2048]{2,1,0:T(8,128)(2,1)S(1)} collective-permute-done((bf16[2,128,2048]{2,1,0:T(8,128)(2,1)S(1)}, bf16[2,128,2048]{2,1,0:T(8,128)(2,1)S(1)}, u32[]{:S(2)}, u32[]{:S(2)}) %collective-permute-start.4) | collective-permute-done | bytes 1048608 | tf_op jit(solution)/shard_map/ppermute | solution.py:108
  182.3 11.1 %collective-permute-done.6 = bf16[2,128,2048]{2,1,0:T(8,128)(2,1)S(1)} collective-permute-done((bf16[2,128,2048]{2,1,0:T(8,128)(2,1)S(1)}, bf16[2,128,2048]{2,1,0:T(8,128)(2,1)S(1)}, u32[]{:S(2)}, u32[]{:S(2)}) %collective-permute-start.6) | collective-permute-done | bytes 1048608 | tf_op jit(solution)/shard_map/ppermute | solution.py:109
  213.3 14.9 %collective-permute-done.17 = bf16[256,2048]{1,0:T(8,128)(2,1)S(1)} collective-permute-done((bf16[256,2048]{1,0:T(8,128)(2,1)S(1)}, bf16[256,2048]{1,0:T(8,128)(2,1)S(1)}, u32[]{:S(2)}, u32[]{:S(2)}) %collective-permute-start.17) | collective-permute-done | bytes 1048608 | tf_op jit(solution)/shard_map/ppermute | solution.py:95
  230.5 10.0 %collective-permute-done.19 = bf16[256,2048]{1,0:T(8,128)(2,1)S(1)} collective-permute-done((bf16[256,2048]{1,0:T(8,128)(2,1)S(1)}, bf16[256,2048]{1,0:T(8,128)(2,1)S(1)}, u32[]{:S(2)}, u32[]{:S(2)}) %collective-permute-start.19) | collective-permute-done | bytes 1048608 | tf_op jit(solution)/shard_map/ppermute | solution.py:96
  244.9 10.6 %collective-permute-done.9 = bf16[256,2048]{1,0:T(8,128)(2,1)S(1)} collective-permute-done((bf16[256,2048]{1,0:T(8,128)(2,1)S(1)}, bf16[256,2048]{1,0:T(8,128)(2,1)S(1)}, u32[]{:S(2)}, u32[]{:S(2)}) %collective-permute-start.9) | collective-permute-done | bytes 1048608 | tf_op jit(solution)/shard_map/ppermute | solution.py:95
  354.5 18.5 %fusion.147 = (bf16[1024,2048]{1,0:T(8,128)(2,1)}, f32[1024,2048]{1,0:T(8,128)}) fusion(f32[1024,2048]{1,0:T(8,128)} %fusion.31, bf16[1024,768]{0,1:T(8,128)(2,1)} %get-tuple-element.130, bf16[2048,2304]{0,1:T(8,128)(2,1)} %all-gather.8.cloned.1.call-done, f32[1024,2048]{1,0:T(8,128)} %fusion.43, f32[1024,2048]{1,0:T(8,128)} %fusion.39), kind=kOutput, calls=%fused_computation.340 | convolution fusion | flops 3229614080 | bytes 42467328 | tf_op jit(solution)/shard_map/dot_general | solution.py:66
  382.9 16.6 %collective-permute-done.20 = bf16[2,128,2048]{2,1,0:T(8,128)(2,1)S(1)} collective-permute-done((bf16[2,128,2048]{2,1,0:T(8,128)(2,1)S(1)}, bf16[2,128,2048]{2,1,0:T(8,128)(2,1)S(1)}, u32[]{:S(2)}, u32[]{:S(2)}) %collective-permute-start.20) | collective-permute-done | bytes 1048608 | tf_op jit(solution)/shard_map/ppermute | solution.py:108
  405.5 16.7 %collective-permute-done.21 = bf16[128,2048]{1,0:T(8,128)(2,1)S(1)} collective-permute-done((bf16[128,2048]{1,0:T(8,128)(2,1)S(1)}, bf16[128,2048]{1,0:T(8,128)(2,1)S(1)}, u32[]{:S(2)}, u32[]{:S(2)}) %collective-permute-start.21) | collective-permute-done | bytes 524320 | tf_op jit(solution)/shard_map/ppermute | solution.py:112
  428.9 10.7 %collective-permute-done.24 = bf16[128,2048]{1,0:T(8,128)(2,1)S(1)} collective-permute-done((bf16[128,2048]{1,0:T(8,128)(2,1)S(1)}, bf16[128,2048]{1,0:T(8,128)(2,1)S(1)}, u32[]{:S(2)}, u32[]{:S(2)}) %collective-permute-start.24) | collective-permute-done | bytes 524320 | tf_op jit(solution)/shard_map/ppermute | solution.py:91
  441.8 31.7 %collective-permute-done.26 = bf16[128,2048]{1,0:T(8,128)(2,1)S(1)} collective-permute-done((bf16[128,2048]{1,0:T(8,128)(2,1)S(1)}, bf16[128,2048]{1,0:T(8,128)(2,1)S(1)}, u32[]{:S(2)}, u32[]{:S(2)}) %collective-permute-start.26) | collective-permute-done | bytes 524320 | tf_op jit(solution)/shard_map/ppermute | solution.py:92
  474.2 21.1 %collective-permute-done.27 = bf16[256,2048]{1,0:T(8,128)(2,1)S(1)} collective-permute-done((bf16[256,2048]{1,0:T(8,128)(2,1)S(1)}, bf16[256,2048]{1,0:T(8,128)(2,1)S(1)}, u32[]{:S(2)}, u32[]{:S(2)}) %collective-permute-start.27) | collective-permute-done | bytes 1048608 | tf_op jit(solution)/shard_map/ppermute | solution.py:96
  506.7 12.7 %fusion = (f32[2,2,1024]{2,1,0:T(2,128)S(1)}, f32[2,1024,1024,2]{2,1,3,0:T(8,128)}) fusion(f32[2,1024,1024,2]{2,1,3,0:T(8,128)} %copy-done.1, f32[2,2,1024]{2,1,0:T(2,128)S(1)} %log_add_fusion, pred[1024,1024]{0,1:T(8,128)(4,1)S(1)} %copy-done.6, bf16[1024,2,128,1]{0,2,3,1:T(8,128)(2,1)S(1)} %bitcast.289, bf16[1024,2,2,128]{0,3,2,1:T(8,128)(2,1)S(1)} %bitcast.299), kind=kOutput, calls=%fused_computation.4 | convolution fusion | flops 1094709248 | bytes 36208640 | tf_op jit(solution)/shard_map/qgrd,kgd->grqk/dot_general | solution.py:269
  519.4 12.2 %fusion.2 = bf16[2,2,1024,1024]{2,3,1,0:T(8,128)(2,1)S(1)} fusion(f32[2,1024,1024,2]{2,1,3,0:T(8,128)} %get-tuple-element.216, f32[2,1024,1024,2]{2,1,3,0:T(8,128)} %copy-done.1, f32[2,2,1024]{2,1,0:T(2,128)S(1)} %get-tuple-element.215, f32[2,2,1024]{2,1,0:T(2,128)S(1)} %log_add_fusion, pred[1024,1024]{0,1:T(8,128)(4,1)S(1)} %copy-done.6), kind=kLoop, calls=%fused_computation.6 | loop fusion | flops 25165824 | bytes 43024384 | tf_op jit(solution)/shard_map/convert_element_type | solution.py:271
  570.8 10.6 %convolution_convert_fusion.1 = bf16[2048,1536]{0,1:T(8,128)(2,1)S(1)} fusion(bf16[1024,2048]{1,0:T(8,128)(2,1)} %constant_dynamic-update-slice_fusion.10, bf16[1024,768]{0,1:T(8,128)(2,1)S(1)} %copy-done.69, bf16[1024,768]{0,1:T(8,128)(2,1)S(1)} %copy-done.71), kind=kOutput, calls=%fused_computation.28 | convolution fusion | flops 6451888128 | bytes 13631488 | tf_op jit(solution)/shard_map/dot_general | solution.py:60
  581.4 11.5 %pad_maximum_fusion = bf16[2048,2304]{0,1:T(8,128)(2,1)} fusion(bf16[2048,768]{0,1:T(8,128)(2,1)S(1)} %convolution_convert_fusion.4, bf16[2048,1536]{0,1:T(8,128)(2,1)S(1)} %convolution_convert_fusion.1), kind=kLoop, calls=%fused_computation.17 | loop fusion | flops 18874368 | bytes 18874368 | tf_op jit(solution)/shard_map/concatenate | solution.py:134
  600.3 10.6 %convolution_convert_fusion = bf16[2048,1536]{0,1:T(8,128)(2,1)S(1)} fusion(bf16[1024,2048]{1,0:T(8,128)(2,1)} %constant_dynamic-update-slice_fusion.10, bf16[1024,768]{0,1:T(8,128)(2,1)S(1)} %copy-done.37, bf16[1024,768]{0,1:T(8,128)(2,1)S(1)} %copy-done.67), kind=kOutput, calls=%fused_computation.27 | convolution fusion | flops 6451888128 | bytes 13631488 | tf_op jit(solution)/shard_map/dot_general | solution.py:60
  611.0 11.5 %pad_maximum_fusion.1 = bf16[2048,2304]{0,1:T(8,128)(2,1)} fusion(bf16[2048,768]{0,1:T(8,128)(2,1)S(1)} %convolution_convert_fusion.3, bf16[2048,1536]{0,1:T(8,128)(2,1)S(1)} %convolution_convert_fusion), kind=kLoop, calls=%fused_computation.18 | loop fusion | flops 18874368 | bytes 18874368 | tf_op jit(solution)/shard_map/concatenate | solution.py:134
  638.7 16.5 %collective-permute-done.28 = bf16[2,128,2048]{2,1,0:T(8,128)(2,1)S(1)} collective-permute-done((bf16[2,128,2048]{2,1,0:T(8,128)(2,1)S(1)}, bf16[2,128,2048]{2,1,0:T(8,128)(2,1)S(1)}, u32[]{:S(2)}, u32[]{:S(2)}) %collective-permute-start.28) | collective-permute-done | bytes 1048608 | tf_op jit(solution)/shard_map/ppermute | solution.py:108
  669.6 40.4 %psum.7 = f32[4352]{0:T(1024)S(1)} all-reduce(f32[4352]{0:T(1024)S(1)} %pad_maximum_fusion.22), channel_id=1, replica_groups=mesh['wide'=8,'narrow'=4] {'wide','narrow'}, use_global_device_ids=true, to_apply=%region_23.25 | all-reduce | flops 4352 | bytes 34816 | tf_op jit(solution)/shard_map/psum | solution.py:299
  728.5 97.9 %reduce-scatter.11.cloned.1.call-done = bf16[256,2304]{0,1:T(8,128)(2,1)} async-done(((bf16[2048,2304]{0,1:T(8,128)(2,1)}), bf16[256,2304]{0,1:T(8,128)(2,1)}) %reduce-scatter.11.cloned.1.call-update) | async-done | bytes 1179664 | tf_op jit(solution)/shard_map/reduce_scatter | solution.py:135
  (423 shorter events, 369.6 us)
Async XLA Ops:
  7.2 106.7 %all-gather.4.cloned.1.call-start = ((), (), s32[]{:S(2)}) async-start(), calls=%async_computation.4 | async-start | bytes 7667712 | tf_op jit(solution)/shard_map/all_gather | solution.py:129
  27.1 232.3 %all-gather.6.cloned.1.call-start = ((), (), s32[]{:S(2)}) async-start(), calls=%async_computation.5 | async-start | bytes 10616832 | tf_op jit(solution)/shard_map/all_gather | solution.py:129
  31.8 250.6 %all-gather.8.cloned.1.call-start = ((), (), s32[]{:S(2)}) async-start(), calls=%async_computation.6 | async-start | bytes 10616832 | tf_op jit(solution)/shard_map/all_gather | solution.py:129
  38.2 676.5 %reduce-scatter.7.cloned.1.call-start = ((), (), s32[]{:S(2)}) async-start(), calls=%async_computation.8 | async-start | bytes 2359296 | tf_op jit(solution)/shard_map/reduce_scatter | solution.py:135
  47.8 24.6 %collective-permute-start.1 = (bf16[256,2048]{1,0:T(8,128)(2,1)S(1)}, bf16[256,2048]{1,0:T(8,128)(2,1)}, u32[]{:S(2)}, u32[]{:S(2)}) collective-permute-start(bf16[256,2048]{1,0:T(8,128)(2,1)S(1)} %pad_maximum_fusion.10), channel_id=1, source_target_pairs={{0,2},{2,0},{1,3},{3,1},{4,6},{6,4},{5,7},{7,5},{8,10},{10,8},{9,1... | collective-permute-start | bytes 3145736 | tf_op jit(solution)/shard_map/ppermute | solution.py:95
  88.0 22.8 %collective-permute-start.3 = (bf16[256,2048]{1,0:T(8,128)(2,1)S(1)}, bf16[256,2048]{1,0:T(8,128)(2,1)S(1)}, u32[]{:S(2)}, u32[]{:S(2)}) collective-permute-start(bf16[256,2048]{1,0:T(8,128)(2,1)S(1)} %pad_maximum_fusion.11), channel_id=1, source_target_pairs={{0,1},{1,0},{2,3},{3,2},{4,5},{5,4},{6,7},{7,6},{8,9},{9,8},{10,11... | collective-permute-start | bytes 3145736 | tf_op jit(solution)/shard_map/ppermute | solution.py:96
  154.7 26.1 %collective-permute-start.4 = (bf16[2,128,2048]{2,1,0:T(8,128)(2,1)S(1)}, bf16[2,128,2048]{2,1,0:T(8,128)(2,1)S(1)}, u32[]{:S(2)}, u32[]{:S(2)}) collective-permute-start(bf16[2,128,2048]{2,1,0:T(8,128)(2,1)S(1)} %bitcast.298), channel_id=1, source_target_pairs={{0,2},{2,0},{1,3},{3,1},{4,6},{6,4},{5,7},{7,5},{8,10},{10,8},{9,1... | collective-permute-start | bytes 3145736 | tf_op jit(solution)/shard_map/ppermute | solution.py:108
  156.1 38.7 %collective-permute-start.16 = (bf16[128,2048]{1,0:T(8,128)(2,1)S(1)}, bf16[128,2048]{1,0:T(8,128)(2,1)S(1)}, u32[]{:S(2)}, u32[]{:S(2)}) collective-permute-start(bf16[128,2048]{1,0:T(8,128)(2,1)S(1)} %get-tuple-element.165), channel_id=1, source_target_pairs={{0,1},{1,0},{2,3},{3,2},{4,5},{5,4},{6,7},{7,6},{8,9},{9,8},{10,11... | collective-permute-start | bytes 1572872 | tf_op jit(solution)/shard_map/ppermute | solution.py:91
  157.6 54.9 %collective-permute-start.18 = (bf16[128,2048]{1,0:T(8,128)(2,1)S(1)}, bf16[128,2048]{1,0:T(8,128)(2,1)S(1)}, u32[]{:S(2)}, u32[]{:S(2)}) collective-permute-start(bf16[128,2048]{1,0:T(8,128)(2,1)S(1)} %get-tuple-element.163), channel_id=1, source_target_pairs={{0,2},{2,0},{1,3},{3,1},{4,6},{6,4},{5,7},{7,5},{8,10},{10,8},{9,1... | collective-permute-start | bytes 1572872 | tf_op jit(solution)/shard_map/ppermute | solution.py:92
  158.5 34.9 %collective-permute-start.6 = (bf16[2,128,2048]{2,1,0:T(8,128)(2,1)S(1)}, bf16[2,128,2048]{2,1,0:T(8,128)(2,1)S(1)}, u32[]{:S(2)}, u32[]{:S(2)}) collective-permute-start(bf16[2,128,2048]{2,1,0:T(8,128)(2,1)S(1)} %bitcast.296), channel_id=1, source_target_pairs={{0,1},{1,0},{2,3},{3,2},{4,5},{5,4},{6,7},{7,6},{8,9},{9,8},{10,11... | collective-permute-start | bytes 3145736 | tf_op jit(solution)/shard_map/ppermute | solution.py:109
  194.8 33.3 %collective-permute-start.17 = (bf16[256,2048]{1,0:T(8,128)(2,1)S(1)}, bf16[256,2048]{1,0:T(8,128)(2,1)S(1)}, u32[]{:S(2)}, u32[]{:S(2)}) collective-permute-start(bf16[256,2048]{1,0:T(8,128)(2,1)S(1)} %pad_maximum_fusion.14), channel_id=1, source_target_pairs={{0,2},{2,0},{1,3},{3,1},{4,6},{6,4},{5,7},{7,5},{8,10},{10,8},{9,1... | collective-permute-start | bytes 3145736 | tf_op jit(solution)/shard_map/ppermute | solution.py:95
  212.6 27.9 %collective-permute-start.19 = (bf16[256,2048]{1,0:T(8,128)(2,1)S(1)}, bf16[256,2048]{1,0:T(8,128)(2,1)S(1)}, u32[]{:S(2)}, u32[]{:S(2)}) collective-permute-start(bf16[256,2048]{1,0:T(8,128)(2,1)S(1)} %pad_maximum_fusion.15), channel_id=1, source_target_pairs={{0,1},{1,0},{2,3},{3,2},{4,5},{5,4},{6,7},{7,6},{8,9},{9,8},{10,11... | collective-permute-start | bytes 3145736 | tf_op jit(solution)/shard_map/ppermute | solution.py:96
  229.3 26.2 %collective-permute-start.9 = (bf16[256,2048]{1,0:T(8,128)(2,1)S(1)}, bf16[256,2048]{1,0:T(8,128)(2,1)S(1)}, u32[]{:S(2)}, u32[]{:S(2)}) collective-permute-start(bf16[256,2048]{1,0:T(8,128)(2,1)S(1)} %pad_maximum_fusion.12), channel_id=1, source_target_pairs={{0,2},{2,0},{1,3},{3,1},{4,6},{6,4},{5,7},{7,5},{8,10},{10,8},{9,1... | collective-permute-start | bytes 3145736 | tf_op jit(solution)/shard_map/ppermute | solution.py:95
  328.3 51.4 %collective-permute-start.12 = (bf16[2,128,2048]{2,1,0:T(8,128)(2,1)}, bf16[2,128,2048]{2,1,0:T(8,128)(2,1)}, u32[]{:S(2)}, u32[]{:S(2)}) collective-permute-start(bf16[2,128,2048]{2,1,0:T(8,128)(2,1)} %bitcast.36), channel_id=1, source_target_pairs={{0,2},{2,0},{1,3},{3,1},{4,6},{6,4},{5,7},{7,5},{8,10},{10,8},{9,1... | collective-permute-start | bytes 3145736 | tf_op jit(solution)/shard_map/ppermute | solution.py:108
  329.8 73.4 %collective-permute-start.14 = (bf16[2,128,2048]{2,1,0:T(8,128)(2,1)}, bf16[2,128,2048]{2,1,0:T(8,128)(2,1)}, u32[]{:S(2)}, u32[]{:S(2)}) collective-permute-start(bf16[2,128,2048]{2,1,0:T(8,128)(2,1)} %bitcast.40), channel_id=1, source_target_pairs={{0,1},{1,0},{2,3},{3,2},{4,5},{5,4},{6,7},{7,6},{8,9},{9,8},{10,11... | collective-permute-start | bytes 3145736 | tf_op jit(solution)/shard_map/ppermute | solution.py:109
  374.7 24.8 %collective-permute-start.20 = (bf16[2,128,2048]{2,1,0:T(8,128)(2,1)S(1)}, bf16[2,128,2048]{2,1,0:T(8,128)(2,1)S(1)}, u32[]{:S(2)}, u32[]{:S(2)}) collective-permute-start(bf16[2,128,2048]{2,1,0:T(8,128)(2,1)S(1)} %bitcast.297), channel_id=1, source_target_pairs={{0,2},{2,0},{1,3},{3,1},{4,6},{6,4},{5,7},{7,5},{8,10},{10,8},{9,1... | collective-permute-start | bytes 3145736 | tf_op jit(solution)/shard_map/ppermute | solution.py:108
  375.3 26.0 %collective-permute-start.22 = (bf16[2,128,2048]{2,1,0:T(8,128)(2,1)S(1)}, bf16[2,128,2048]{2,1,0:T(8,128)(2,1)S(1)}, u32[]{:S(2)}, u32[]{:S(2)}) collective-permute-start(bf16[2,128,2048]{2,1,0:T(8,128)(2,1)S(1)} %bitcast.295), channel_id=1, source_target_pairs={{0,1},{1,0},{2,3},{3,2},{4,5},{5,4},{6,7},{7,6},{8,9},{9,8},{10,11... | collective-permute-start | bytes 3145736 | tf_op jit(solution)/shard_map/ppermute | solution.py:109
  381.4 41.8 %collective-permute-start.13 = (bf16[128,2048]{1,0:T(8,128)(2,1)S(1)}, bf16[128,2048]{1,0:T(8,128)(2,1)S(1)}, u32[]{:S(2)}, u32[]{:S(2)}) collective-permute-start(bf16[128,2048]{1,0:T(8,128)(2,1)S(1)} %fusion.94), channel_id=1, source_target_pairs={{0,1},{1,0},{2,3},{3,2},{4,5},{5,4},{6,7},{7,6},{8,9},{9,8},{10,11... | collective-permute-start | bytes 1572872 | tf_op jit(solution)/shard_map/ppermute | solution.py:112
  439.6 34.3 %collective-permute-start.25 = (bf16[256,2048]{1,0:T(8,128)(2,1)S(1)}, bf16[256,2048]{1,0:T(8,128)(2,1)S(1)}, u32[]{:S(2)}, u32[]{:S(2)}) collective-permute-start(bf16[256,2048]{1,0:T(8,128)(2,1)S(1)} %pad_maximum_fusion.16), channel_id=1, source_target_pairs={{0,2},{2,0},{1,3},{3,1},{4,6},{6,4},{5,7},{7,5},{8,10},{10,8},{9,1... | collective-permute-start | bytes 3145736 | tf_op jit(solution)/shard_map/ppermute | solution.py:95
  441.2 32.3 %collective-permute-start.26 = (bf16[128,2048]{1,0:T(8,128)(2,1)S(1)}, bf16[128,2048]{1,0:T(8,128)(2,1)S(1)}, u32[]{:S(2)}, u32[]{:S(2)}) collective-permute-start(bf16[128,2048]{1,0:T(8,128)(2,1)S(1)} %get-tuple-element.160), channel_id=1, source_target_pairs={{0,2},{2,0},{1,3},{3,1},{4,6},{6,4},{5,7},{7,5},{8,10},{10,8},{9,1... | collective-permute-start | bytes 1572872 | tf_op jit(solution)/shard_map/ppermute | solution.py:92
  539.7 177.0 %reduce-scatter.5.cloned.1.call-start = ((), (), s32[]{:S(2)}) async-start(), calls=%async_computation.7 | async-start | bytes 4718592 | tf_op jit(solution)/shard_map/reduce_scatter | solution.py:135
  564.2 162.0 %reduce-scatter.9.cloned.1.call-start = ((), (), s32[]{:S(2)}) async-start(), calls=%async_computation.9 | async-start | bytes 10616832 | tf_op jit(solution)/shard_map/reduce_scatter | solution.py:135
  593.0 233.4 %reduce-scatter.11.cloned.1.call-start = ((), (), s32[]{:S(2)}) async-start(), calls=%async_computation.10 | async-start | bytes 10616832 | tf_op jit(solution)/shard_map/reduce_scatter | solution.py:135
  635.4 23.9 %collective-permute-start.30 = (bf16[2,128,2048]{2,1,0:T(8,128)(2,1)S(1)}, bf16[2,128,2048]{2,1,0:T(8,128)(2,1)S(1)}, u32[]{:S(2)}, u32[]{:S(2)}) collective-permute-start(bf16[2,128,2048]{2,1,0:T(8,128)(2,1)S(1)} %bitcast.293), channel_id=1, source_target_pairs={{0,1},{1,0},{2,3},{3,2},{4,5},{5,4},{6,7},{7,6},{8,9},{9,8},{10,11... | collective-permute-start | bytes 3145736 | tf_op jit(solution)/shard_map/ppermute | solution.py:109
  (93 other events, 788.3 us)
Sparse Core Ops, SparseCore 0:
  27.2 72.1 all-gather.3
  101.6 89.3 all-gather.5
  193.1 89.3 all-gather.7
  539.9 34.4 reduce-scatter.6
  576.5 48.4 reduce-scatter.4
  627.2 98.9 reduce-scatter.8
  728.5 97.8 reduce-scatter.10

commit v3 on v2

--- a/solution.py
+++ b/solution.py
@@ -72,15 +72,22 @@
     return lax.axis_size("narrow") == 4 and seq_count == 1
 
 
-def gather_order(shard_rows):
+def relative_rows(vec):
     n = lax.axis_index("narrow")
-    half = shard_rows // 2
-    index = jnp.arange(4 * shard_rows, dtype=jnp.int32)
-    block = index // half
-    offset = index % half
-    block_xor = jnp.asarray(BLOCK_XOR, jnp.int32)[block]
-    shard = jnp.bitwise_xor(n, block_xor)
-    return shard * shard_rows + offset + half * (block >= 4).astype(jnp.int32)
+    half = vec.shape[0] // 8
+    split = vec.reshape(4, 2, half)
+    pieces = []
+    for blk, flip in enumerate(BLOCK_XOR):
+        source = split[:, 1 if blk >= 4 else 0]
+        pieces.append(lax.dynamic_index_in_dim(source, jnp.bitwise_xor(n, flip), 0, keepdims=False))
+    return jnp.concatenate(pieces)
+
+
+def narrow_allreduce(v):
+    if lax.axis_size("narrow") != 4:
+        return lax.psum(v, "narrow")
+    v = v + lax.ppermute(v, "narrow", XPERM)
+    return v + lax.ppermute(v, "narrow", YPERM)
 
 
 def narrow_gather(x, relative):
@@ -192,9 +199,9 @@
         mlp_sets.append(wide_gather([w_gate[:, cols], w_up[:, cols], down_t[:, cols]]))
 
     if relative:
-        order = gather_order(shard_rows)
-        doc_row = jnp.take(doc_ids[0], order)
-        position = jnp.take(doc_positions(doc_ids)[0], order)
+        order = relative_rows(jnp.arange(rows_group, dtype=jnp.int32))
+        doc_row = relative_rows(doc_ids[0])
+        position = relative_rows(doc_positions(doc_ids)[0])
     else:
         order = jnp.arange(rows_group, dtype=jnp.int32)
         doc_row = doc_ids.reshape(-1)
@@ -251,9 +258,15 @@
         d_up = (d_hidden * gate * sigmoid).astype(jnp.bfloat16)
         d_gate = (d_hidden * up * sigmoid * (1.0 + gate * (1.0 - sigmoid))).astype(jnp.bfloat16)
         g_gate_up = contract_rows(mlp_all, jnp.concatenate([d_gate, d_up], axis=1))
-        mlp_grads.append(wide_scatter([g_gate_up, g_down_t]))
         part = times_transposed(d_gate, gate_w) + times_transposed(d_up, up_w)
         d_mlp_partial = part if d_mlp_partial is None else d_mlp_partial + part
+        joined = jnp.concatenate([g_gate_up.astype(jnp.bfloat16), g_down_t.astype(jnp.bfloat16)], axis=1)
+        if h == 0:
+            joined, mlp_sets[1] = lax.optimization_barrier((joined, mlp_sets[1]))
+        else:
+            joined, d_mlp_partial = lax.optimization_barrier((joined, d_mlp_partial))
+        summed = lax.psum_scatter(joined, "wide", scatter_dimension=0, tiled=True).astype(jnp.float32)
+        mlp_grads.append(split_cols(summed, [2 * ff_half, ff_half]))
 
     d_mlp_in = narrow_scatter(d_mlp_partial, relative)
     d_part, mlp_gain_terms = rms_back(resid, gain_mlp, d_mlp_in)
@@ -290,23 +303,37 @@
         ],
         axis=1,
     )
-    (g_qkv,) = wide_scatter([contract_rows(normed_all, d_qkv)])
-    d_normed = narrow_scatter(times_transposed(d_qkv, qkv_w), relative)
-    d_input_part, attn_gain_terms = rms_back(inputs, gain_attn, d_normed)
-    grad_attn_gain = jnp.sum(attn_gain_terms, axis=0)
-    d_tokens = d_resid + d_input_part
-
-    gain_grads = lax.psum(
-        jnp.concatenate([grad_attn_gain, grad_mlp_gain, grad_query_gain, grad_key_gain]),
-        ("wide", "narrow"),
-    )
-    w = lax.axis_index("wide")
+    d_normed_partial = times_transposed(d_qkv, qkv_w)
+    tokens_all_f = tokens_all.astype(jnp.float32)
+    scale_all = lax.rsqrt(jnp.mean(tokens_all_f * tokens_all_f, axis=-1, keepdims=True) + EPS)
+    attn_gain_part = jnp.sum(d_normed_partial * tokens_all_f * scale_all, axis=0)
+    gain_parts = narrow_allreduce(
+        jnp.concatenate([attn_gain_part, grad_mlp_gain, grad_query_gain, grad_key_gain])
+    )
     d_full = d_local * wide_size
     hd_full = hd_local * wide_size
-    attn_gain_grad = lax.dynamic_slice_in_dim(gain_grads, w * d_local, d_local)
-    mlp_gain_grad = lax.dynamic_slice_in_dim(gain_grads, d_full + w * d_local, d_local)
-    query_gain_grad = lax.dynamic_slice_in_dim(gain_grads, 2 * d_full + w * hd_local, hd_local)
-    key_gain_grad = lax.dynamic_slice_in_dim(gain_grads, 2 * d_full + hd_full + w * hd_local, hd_local)
+
+    def by_chunk(vec, size):
+        return jnp.pad(vec.reshape(wide_size, size), ((0, 0), (0, d_local - size)))
+
+    gain_block = jnp.stack(
+        [
+            by_chunk(gain_parts[:d_full], d_local),
+            by_chunk(gain_parts[d_full : 2 * d_full], d_local),
+            by_chunk(gain_parts[2 * d_full : 2 * d_full + hd_full], hd_local),
+            by_chunk(gain_parts[2 * d_full + hd_full :], hd_local),
+        ],
+        axis=-1,
+    ).reshape(d_full, 4)
+    gain_block = jnp.pad(gain_block, ((0, 0), (0, 124)))
+    g_qkv, g_gains = wide_scatter([contract_rows(normed_all, d_qkv), gain_block])
+    d_normed = narrow_scatter(d_normed_partial, relative)
+    d_input_part, unused_terms = rms_back(inputs, gain_attn, d_normed)
+    d_tokens = d_resid + d_input_part
+    attn_gain_grad = g_gains[:, 0]
+    mlp_gain_grad = g_gains[:, 1]
+    query_gain_grad = g_gains[:hd_local, 2]
+    key_gain_grad = g_gains[:hd_local, 3]
 
     g_query = g_qkv[:, :q_cols]
     g_key = g_qkv[:, q_cols : q_cols + kv_cols]

time: 846 us -> 871 us (1.030)
  waiting for transfers between devices: 370 us -> 474 us
  blocking collectives: 40.4 us -> 0 us
  matrix products: 210 us -> 180 us
  local copies, waits for them, and re-layouts: 76.6 us -> 67.8 us
    reduce_scatter x0 -> x2, waiting for transfers between devices: none -> 192 us  [shards(): lax.psum_scatter(joined, 'wide', scatter_dimension=0, tiled=True)]
    reduce_scatter x4 -> x2, waiting for transfers between devices: 104 us -> 20.2 us  [wide_scatter(): lax.psum_scatter(joined, 'wide', scatter_dimension=0, tiled=True)]
    psum x1 -> x0, blocking collectives: 40.4 us -> none  [shards(): lax.psum(jnp.concatenate([grad_attn_gain, grad_mlp_gain, grad_query_gain,...]
    ppermute x4, waiting for transfers between devices: 15.6 us -> 49.1 us  [narrow_scatter(): b_got = lax.ppermute(blocks[6:8].astype(jnp.bfloat16), 'narrow', XPERM)]
    concatenate x1 -> x3, other arithmetic: 0.01 us -> 22.8 us  [the longest x2 22.8 us: shards(): jnp.concatenate([g_gate_up.astype(jnp.bfloat16), g_down_t.astype(jnp.bflo...]
    ppermute x4, waiting for transfers between devices: 54.4 us -> 35.7 us  [narrow_scatter(): a_got = lax.ppermute(blocks[2:4].astype(jnp.bfloat16), 'narrow', YPERM)]
    concatenate x2 -> x1, other arithmetic: 23.1 us -> 5.01 us  [wide_scatter(): jnp.concatenate([blk.astype(jnp.bfloat16) for blk in blocks], axis=1)]
    dot_general x8, matrix products: 67.2 us -> 55.8 us  [times_transposed(): lax.dot_general(left, right, (((1,), (1,)), ((), ())), preferred_element_...]
  transfers between devices with their start and end apart: 39 -> 41, of which waited for: 26 -> 28; matrix products, arithmetic and copies ran while one was open for 29% -> 19% of each run, Pallas kernels for 0% -> 0%
where the time goes in v3:
time: 871 us; the launch traced here: 866 us
  waiting for transfers between devices  474 us (54%)
  matrix products  180 us (21%)
  other arithmetic  85.5 us (10%)
  local copies, waits for them, and re-layouts  67.8 us (8%)
  starting transfers between devices  42.3 us (5%)
  between operations  16.7 us (2%)
    reduce_scatter x2, waiting for transfers between devices, shards(): lax.psum_scatter(joined, 'wide', scatter_dimension=0, tiled=True)  192 us
    dot_general x8, matrix products, times_transposed(): lax.dot_general(left, right, (((1,), (1,)), ((), ())), preferred_element_...  55.8 us
    ppermute x4, waiting for transfers between devices, narrow_scatter(): b_got = lax.ppermute(blocks[6:8].astype(jnp.bfloat16), 'narrow', XPERM)  49.1 us
    ppermute x4, waiting for transfers between devices, narrow_gather(): a_pair_y = lax.ppermute(a_pair, 'narrow', YPERM)  46.1 us
    ppermute x4, waiting for transfers between devices, narrow_gather(): b_pair_x = lax.ppermute(b_pair, 'narrow', XPERM)  41.3 us
    dot_general x6, matrix products, contract_rows(): lax.dot_general(left, right, (((0,), (0,)), ((), ())), preferred_element_...  41 us
    ppermute x4, waiting for transfers between devices, narrow_scatter(): a_got = lax.ppermute(blocks[2:4].astype(jnp.bfloat16), 'narrow', YPERM)  35.7 us
    ppermute x4, waiting for transfers between devices, narrow_gather(): b_y = lax.ppermute(b, 'narrow', YPERM)  34.9 us
  transfers between devices with their start and end apart: 41, of which 28 were waited for; matrix products, arithmetic and copies ran while one was open for 19% of the time, Pallas kernels for 0%

profile of v3, /device:TPU:0, one launch (start us, length us, event | category | flops | bytes accessed | tf_op | source)
XLA Modules:
  0.0 866.3 jit_solution(8422641194619796897)
XLA Ops:
  50.0 21.7 %collective-permute-done.1 = bf16[256,2048]{1,0:T(8,128)(2,1)S(1)} collective-permute-done((bf16[256,2048]{1,0:T(8,128)(2,1)S(1)}, bf16[256,2048]{1,0:T(8,128)(2,1)S(1)}, u32[]{:S(2)}, u32[]{:S(2)}) %collective-permute-start.1) | collective-permute-done | bytes 1048608 | tf_op jit(solution)/shard_map/ppermute | solution.py:102
  75.2 10.9 %collective-permute-done.2 = bf16[128,2048]{1,0:T(8,128)(2,1)S(1)} collective-permute-done((bf16[128,2048]{1,0:T(8,128)(2,1)S(1)}, bf16[128,2048]{1,0:T(8,128)(2,1)S(1)}, u32[]{:S(2)}, u32[]{:S(2)}) %collective-permute-start.2) | collective-permute-done | bytes 524320 | tf_op jit(solution)/shard_map/ppermute | solution.py:99
  91.8 17.4 %collective-permute-done.3 = bf16[256,2048]{1,0:T(8,128)(2,1)S(1)} collective-permute-done((bf16[256,2048]{1,0:T(8,128)(2,1)S(1)}, bf16[256,2048]{1,0:T(8,128)(2,1)S(1)}, u32[]{:S(2)}, u32[]{:S(2)}) %collective-permute-start.3) | collective-permute-done | bytes 1048608 | tf_op jit(solution)/shard_map/ppermute | solution.py:103
  154.4 21.2 %collective-permute-done.4 = bf16[2,128,2048]{2,1,0:T(8,128)(2,1)S(1)} collective-permute-done((bf16[2,128,2048]{2,1,0:T(8,128)(2,1)S(1)}, bf16[2,128,2048]{2,1,0:T(8,128)(2,1)S(1)}, u32[]{:S(2)}, u32[]{:S(2)}) %collective-permute-start.4) | collective-permute-done | bytes 1048608 | tf_op jit(solution)/shard_map/ppermute | solution.py:115
  177.2 12.0 %collective-permute-done.6 = bf16[2,128,2048]{2,1,0:T(8,128)(2,1)S(1)} collective-permute-done((bf16[2,128,2048]{2,1,0:T(8,128)(2,1)S(1)}, bf16[2,128,2048]{2,1,0:T(8,128)(2,1)S(1)}, u32[]{:S(2)}, u32[]{:S(2)}) %collective-permute-start.6) | collective-permute-done | bytes 1048608 | tf_op jit(solution)/shard_map/ppermute | solution.py:116
  208.9 14.9 %collective-permute-done.13 = bf16[256,2048]{1,0:T(8,128)(2,1)S(1)} collective-permute-done((bf16[256,2048]{1,0:T(8,128)(2,1)S(1)}, bf16[256,2048]{1,0:T(8,128)(2,1)S(1)}, u32[]{:S(2)}, u32[]{:S(2)}) %collective-permute-start.13) | collective-permute-done | bytes 1048608 | tf_op jit(solution)/shard_map/ppermute | solution.py:102
  226.3 9.8 %collective-permute-done.15 = bf16[256,2048]{1,0:T(8,128)(2,1)S(1)} collective-permute-done((bf16[256,2048]{1,0:T(8,128)(2,1)S(1)}, bf16[256,2048]{1,0:T(8,128)(2,1)S(1)}, u32[]{:S(2)}, u32[]{:S(2)}) %collective-permute-start.15) | collective-permute-done | bytes 1048608 | tf_op jit(solution)/shard_map/ppermute | solution.py:103
  241.3 9.5 %collective-permute-done.9 = bf16[256,2048]{1,0:T(8,128)(2,1)S(1)} collective-permute-done((bf16[256,2048]{1,0:T(8,128)(2,1)S(1)}, bf16[256,2048]{1,0:T(8,128)(2,1)S(1)}, u32[]{:S(2)}, u32[]{:S(2)}) %collective-permute-start.9) | collective-permute-done | bytes 1048608 | tf_op jit(solution)/shard_map/ppermute | solution.py:102
  277.7 10.6 %convolution_convert_fusion.1 = bf16[2048,1536]{0,1:T(8,128)(2,1)S(1)} fusion(bf16[1024,2048]{1,0:T(8,128)(2,1)} %constant_dynamic-update-slice_fusion.13, bf16[1024,768]{0,1:T(8,128)(2,1)S(1)} %get-tuple-element.147, bf16[1024,768]{0,1:T(8,128)(2,1)S(1)} %get-tuple-element.145), kind=kOutput, calls=%fused_computation.29 | convolution fusion | flops 6451888128 | bytes 13631488 | tf_op jit(solution)/shard_map/dot_general | solution.py:60
  288.3 11.5 %pad_maximum_fusion = bf16[2048,2304]{0,1:T(8,128)(2,1)} fusion(bf16[2048,768]{0,1:T(8,128)(2,1)S(1)} %convolution_convert_fusion.4, bf16[2048,1536]{0,1:T(8,128)(2,1)S(1)} %convolution_convert_fusion.1), kind=kLoop, calls=%fused_computation.16 | loop fusion | flops 18874368 | bytes 18874368 | tf_op jit(solution)/shard_map/concatenate | solution.py:263
  329.8 11.1 %convolution_convert_fusion = bf16[2048,1536]{0,1:T(8,128)(2,1)S(1)} fusion(bf16[1024,2048]{1,0:T(8,128)(2,1)} %constant_dynamic-update-slice_fusion.13, bf16[1024,768]{0,1:T(8,128)(2,1)S(1)} %get-tuple-element.144, bf16[1024,768]{0,1:T(8,128)(2,1)S(1)} %get-tuple-element.142), kind=kOutput, calls=%fused_computation.28 | convolution fusion | flops 6451888128 | bytes 13631488 | tf_op jit(solution)/shard_map/dot_general | solution.py:60
  354.0 11.3 %pad_maximum_fusion.1 = bf16[2048,2304]{0,1:T(8,128)(2,1)} fusion(bf16[2048,768]{0,1:T(8,128)(2,1)S(1)} %convolution_convert_fusion.3, bf16[2048,1536]{0,1:T(8,128)(2,1)S(1)} %convolution_convert_fusion), kind=kLoop, calls=%fused_computation.17 | loop fusion | flops 18874368 | bytes 18874368 | tf_op jit(solution)/shard_map/concatenate | solution.py:263
  365.3 9.2 %fusion.35 = f32[1024,2048]{1,0:T(8,128)} fusion(bf16[1024,768]{0,1:T(8,128)(2,1)} %copy-done.68, bf16[2048,2304]{0,1:T(8,128)(2,1)} %all-gather.6.cloned.1.call-done), kind=kOutput, calls=%fused_computation.69 | convolution fusion | flops 3221225472 | bytes 13107200 | tf_op jit(solution)/shard_map/dot_general | solution.py:66
  382.2 10.9 %add_add_fusion = f32[1024,2048]{1,0:T(8,128)S(1)} fusion(f32[1024,2048]{1,0:T(8,128)} %fusion.165, f32[1024,2048]{1,0:T(8,128)} %fusion.35, f32[1024,2048]{1,0:T(8,128)} %fusion.31, bf16[1024,768]{0,1:T(8,128)(2,1)S(1)} %copy-done.33, bf16[2048,768]{0,1:T(8,128)(2,1)S(1)} %get-tuple-element.68), kind=kOutput, calls=%fused_computation.24 | convolution fusion | flops 3227516928 | bytes 38273024 | tf_op jit(solution)/shard_map/dot_general | solution.py:66
  399.7 37.1 %collective-permute-done.22 = bf16[2,128,2048]{2,1,0:T(8,128)(2,1)S(1)} collective-permute-done((bf16[2,128,2048]{2,1,0:T(8,128)(2,1)S(1)}, bf16[2,128,2048]{2,1,0:T(8,128)(2,1)S(1)}, u32[]{:S(2)}, u32[]{:S(2)}) %collective-permute-start.22) | collective-permute-done | bytes 1048608 | tf_op jit(solution)/shard_map/ppermute | solution.py:116
  452.1 9.1 %collective-permute-done.17 = bf16[128,2048]{1,0:T(8,128)(2,1)S(1)} collective-permute-done((bf16[128,2048]{1,0:T(8,128)(2,1)S(1)}, bf16[128,2048]{1,0:T(8,128)(2,1)S(1)}, u32[]{:S(2)}, u32[]{:S(2)}) %collective-permute-start.17) | collective-permute-done | bytes 524320 | tf_op jit(solution)/shard_map/ppermute | solution.py:119
  475.0 21.5 %collective-permute-done.26 = bf16[128,2048]{1,0:T(8,128)(2,1)S(1)} collective-permute-done((bf16[128,2048]{1,0:T(8,128)(2,1)S(1)}, bf16[128,2048]{1,0:T(8,128)(2,1)S(1)}, u32[]{:S(2)}, u32[]{:S(2)}) %collective-permute-start.26) | collective-permute-done | bytes 524320 | tf_op jit(solution)/shard_map/ppermute | solution.py:99
  497.4 13.9 %collective-permute-done.27 = bf16[256,2048]{1,0:T(8,128)(2,1)S(1)} collective-permute-done((bf16[256,2048]{1,0:T(8,128)(2,1)S(1)}, bf16[256,2048]{1,0:T(8,128)(2,1)S(1)}, u32[]{:S(2)}, u32[]{:S(2)}) %collective-permute-start.27) | collective-permute-done | bytes 1048608 | tf_op jit(solution)/shard_map/ppermute | solution.py:103
  531.5 12.2 %fusion = (f32[2,2,1024]{2,1,0:T(2,128)S(1)}, f32[2,1024,1024,2]{2,1,3,0:T(8,128)}) fusion(f32[2,1024,1024,2]{2,1,3,0:T(8,128)} %copy-done, f32[2,2,1024]{2,1,0:T(2,128)S(1)} %log_add_fusion, pred[1024,1024]{0,1:T(8,128)(4,1)S(1)} %copy-done.7, bf16[1024,2,128,1]{0,2,3,1:T(8,128)(2,1)S(1)} %bitcast.401, bf16[1024,2,2,128]{0,3,2,1:T(8,128)(2,1)S(1)} %bitcast.416), kind=kOutput, calls=%fused_computation.2 | convolution fusion | flops 1094709248 | bytes 36208640 | tf_op jit(solution)/shard_map/qgrd,kgd->grqk/dot_general | solution.py:282
  543.8 12.3 %fusion.2 = bf16[2,2,1024,1024]{2,3,1,0:T(8,128)(2,1)S(1)} fusion(f32[2,1024,1024,2]{2,1,3,0:T(8,128)} %get-tuple-element.235, f32[2,1024,1024,2]{2,1,3,0:T(8,128)} %copy-done, f32[2,2,1024]{2,1,0:T(2,128)S(1)} %get-tuple-element.234, f32[2,2,1024]{2,1,0:T(2,128)S(1)} %log_add_fusion, pred[1024,1024]{0,1:T(8,128)(4,1)S(1)} %copy-done.7), kind=kLoop, calls=%fused_computation.4 | loop fusion | flops 25165824 | bytes 43024384 | tf_op jit(solution)/shard_map/convert_element_type | solution.py:284
  600.5 14.1 %collective-permute-done.28 = bf16[2,128,2048]{2,1,0:T(8,128)(2,1)S(1)} collective-permute-done((bf16[2,128,2048]{2,1,0:T(8,128)(2,1)S(1)}, bf16[2,128,2048]{2,1,0:T(8,128)(2,1)S(1)}, u32[]{:S(2)}, u32[]{:S(2)}) %collective-permute-start.28) | collective-permute-done | bytes 1048608 | tf_op jit(solution)/shard_map/ppermute | solution.py:115
  630.1 20.2 %reduce-scatter.5.cloned.1.call-done = bf16[256,1152]{0,1:T(8,128)(2,1)} async-done(((bf16[2048,1152]{0,1:T(8,128)(2,1)}), bf16[256,1152]{0,1:T(8,128)(2,1)}) %reduce-scatter.5.cloned.1.call-update) | async-done | bytes 589840 | tf_op jit(solution)/shard_map/reduce_scatter | solution.py:142
  656.2 94.1 %reduce-scatter.9.cloned.1.call-done = bf16[256,2304]{0,1:T(8,128)(2,1)} async-done(((bf16[2048,2304]{0,1:T(8,128)(2,1)}), bf16[256,2304]{0,1:T(8,128)(2,1)}) %reduce-scatter.9.cloned.1.call-update) | async-done | bytes 1179664 | tf_op jit(solution)/shard_map/reduce_scatter | solution.py:268
  752.7 97.9 %reduce-scatter.11.cloned.1.call-done = bf16[256,2304]{0,1:T(8,128)(2,1)} async-done(((bf16[2048,2304]{0,1:T(8,128)(2,1)}), bf16[256,2304]{0,1:T(8,128)(2,1)}) %reduce-scatter.11.cloned.1.call-update) | async-done | bytes 1179664 | tf_op jit(solution)/shard_map/reduce_scatter | solution.py:268
  (477 shorter events, 335.1 us)
Async XLA Ops:
  7.2 105.0 %all-gather.4.cloned.1.call-start = ((), (), s32[]{:S(2)}) async-start(), calls=%async_computation.4 | async-start | bytes 7667712 | tf_op jit(solution)/shard_map/all_gather | solution.py:136
  26.4 228.4 %all-gather.6.cloned.1.call-start = ((), (), s32[]{:S(2)}) async-start(), calls=%async_computation.5 | async-start | bytes 10616832 | tf_op jit(solution)/shard_map/all_gather | solution.py:136
  31.2 268.7 %all-gather.8.cloned.1.call-start = ((), (), s32[]{:S(2)}) async-start(), calls=%async_computation.6 | async-start | bytes 10616832 | tf_op jit(solution)/shard_map/all_gather | solution.py:136
  37.7 590.4 %reduce-scatter.7.cloned.1.call-start = ((), (), s32[]{:S(2)}) async-start(), calls=%async_computation.8 | async-start | bytes 2359296 | tf_op jit(solution)/shard_map/reduce_scatter | solution.py:142
  47.2 24.5 %collective-permute-start.1 = (bf16[256,2048]{1,0:T(8,128)(2,1)S(1)}, bf16[256,2048]{1,0:T(8,128)(2,1)S(1)}, u32[]{:S(2)}, u32[]{:S(2)}) collective-permute-start(bf16[256,2048]{1,0:T(8,128)(2,1)S(1)} %pad_maximum_fusion.10), channel_id=1, source_target_pairs={{0,2},{2,0},{1,3},{3,1},{4,6},{6,4},{5,7},{7,5},{8,10},{10,8},{9,1... | collective-permute-start | bytes 3145736 | tf_op jit(solution)/shard_map/ppermute | solution.py:102
  86.2 23.0 %collective-permute-start.3 = (bf16[256,2048]{1,0:T(8,128)(2,1)S(1)}, bf16[256,2048]{1,0:T(8,128)(2,1)S(1)}, u32[]{:S(2)}, u32[]{:S(2)}) collective-permute-start(bf16[256,2048]{1,0:T(8,128)(2,1)S(1)} %pad_maximum_fusion.11), channel_id=1, source_target_pairs={{0,1},{1,0},{2,3},{3,2},{4,5},{5,4},{6,7},{7,6},{8,9},{9,8},{10,11... | collective-permute-start | bytes 3145736 | tf_op jit(solution)/shard_map/ppermute | solution.py:103
  149.5 26.1 %collective-permute-start.4 = (bf16[2,128,2048]{2,1,0:T(8,128)(2,1)S(1)}, bf16[2,128,2048]{2,1,0:T(8,128)(2,1)S(1)}, u32[]{:S(2)}, u32[]{:S(2)}) collective-permute-start(bf16[2,128,2048]{2,1,0:T(8,128)(2,1)S(1)} %bitcast.411), channel_id=1, source_target_pairs={{0,2},{2,0},{1,3},{3,1},{4,6},{6,4},{5,7},{7,5},{8,10},{10,8},{9,1... | collective-permute-start | bytes 3145736 | tf_op jit(solution)/shard_map/ppermute | solution.py:115
  150.9 57.3 %collective-permute-start.14 = (bf16[128,2048]{1,0:T(8,128)(2,1)S(1)}, bf16[128,2048]{1,0:T(8,128)(2,1)S(1)}, u32[]{:S(2)}, u32[]{:S(2)}) collective-permute-start(bf16[128,2048]{1,0:T(8,128)(2,1)S(1)} %get-tuple-element.176), channel_id=1, source_target_pairs={{0,2},{2,0},{1,3},{3,1},{4,6},{6,4},{5,7},{7,5},{8,10},{10,8},{9,1... | collective-permute-start | bytes 1572872 | tf_op jit(solution)/shard_map/ppermute | solution.py:99
  151.9 38.8 %collective-permute-start.12 = (bf16[128,2048]{1,0:T(8,128)(2,1)S(1)}, bf16[128,2048]{1,0:T(8,128)(2,1)S(1)}, u32[]{:S(2)}, u32[]{:S(2)}) collective-permute-start(bf16[128,2048]{1,0:T(8,128)(2,1)S(1)} %get-tuple-element.178), channel_id=1, source_target_pairs={{0,1},{1,0},{2,3},{3,2},{4,5},{5,4},{6,7},{7,6},{8,9},{9,8},{10,11... | collective-permute-start | bytes 1572872 | tf_op jit(solution)/shard_map/ppermute | solution.py:98
  153.4 35.8 %collective-permute-start.6 = (bf16[2,128,2048]{2,1,0:T(8,128)(2,1)S(1)}, bf16[2,128,2048]{2,1,0:T(8,128)(2,1)S(1)}, u32[]{:S(2)}, u32[]{:S(2)}) collective-permute-start(bf16[2,128,2048]{2,1,0:T(8,128)(2,1)S(1)} %bitcast.409), channel_id=1, source_target_pairs={{0,1},{1,0},{2,3},{3,2},{4,5},{5,4},{6,7},{7,6},{8,9},{9,8},{10,11... | collective-permute-start | bytes 3145736 | tf_op jit(solution)/shard_map/ppermute | solution.py:116
  176.0 20.0 %collective-permute-start.5 = (bf16[128,2048]{1,0:T(8,128)(2,1)S(1)}, bf16[128,2048]{1,0:T(8,128)(2,1)S(1)}, u32[]{:S(2)}, u32[]{:S(2)}) collective-permute-start(bf16[128,2048]{1,0:T(8,128)(2,1)S(1)} %fusion.86), channel_id=1, source_target_pairs={{0,1},{1,0},{2,3},{3,2},{4,5},{5,4},{6,7},{7,6},{8,9},{9,8},{10,11... | collective-permute-start | bytes 1572872 | tf_op jit(solution)/shard_map/ppermute | solution.py:119
  190.8 33.1 %collective-permute-start.13 = (bf16[256,2048]{1,0:T(8,128)(2,1)S(1)}, bf16[256,2048]{1,0:T(8,128)(2,1)S(1)}, u32[]{:S(2)}, u32[]{:S(2)}) collective-permute-start(bf16[256,2048]{1,0:T(8,128)(2,1)S(1)} %pad_maximum_fusion.14), channel_id=1, source_target_pairs={{0,2},{2,0},{1,3},{3,1},{4,6},{6,4},{5,7},{7,5},{8,10},{10,8},{9,1... | collective-permute-start | bytes 3145736 | tf_op jit(solution)/shard_map/ppermute | solution.py:102
  208.3 27.8 %collective-permute-start.15 = (bf16[256,2048]{1,0:T(8,128)(2,1)S(1)}, bf16[256,2048]{1,0:T(8,128)(2,1)S(1)}, u32[]{:S(2)}, u32[]{:S(2)}) collective-permute-start(bf16[256,2048]{1,0:T(8,128)(2,1)S(1)} %pad_maximum_fusion.15), channel_id=1, source_target_pairs={{0,1},{1,0},{2,3},{3,2},{4,5},{5,4},{6,7},{7,6},{8,9},{9,8},{10,11... | collective-permute-start | bytes 3145736 | tf_op jit(solution)/shard_map/ppermute | solution.py:103
  225.3 25.6 %collective-permute-start.9 = (bf16[256,2048]{1,0:T(8,128)(2,1)S(1)}, bf16[256,2048]{1,0:T(8,128)(2,1)S(1)}, u32[]{:S(2)}, u32[]{:S(2)}) collective-permute-start(bf16[256,2048]{1,0:T(8,128)(2,1)S(1)} %pad_maximum_fusion.12), channel_id=1, source_target_pairs={{0,2},{2,0},{1,3},{3,1},{4,6},{6,4},{5,7},{7,5},{8,10},{10,8},{9,1... | collective-permute-start | bytes 3145736 | tf_op jit(solution)/shard_map/ppermute | solution.py:102
  393.1 49.5 %collective-permute-start.18 = (bf16[2,128,2048]{2,1,0:T(8,128)(2,1)}, bf16[2,128,2048]{2,1,0:T(8,128)(2,1)S(1)}, u32[]{:S(2)}, u32[]{:S(2)}) collective-permute-start(bf16[2,128,2048]{2,1,0:T(8,128)(2,1)} %bitcast.61), channel_id=1, source_target_pairs={{0,1},{1,0},{2,3},{3,2},{4,5},{5,4},{6,7},{7,6},{8,9},{9,8},{10,11... | collective-permute-start | bytes 3145736 | tf_op jit(solution)/shard_map/ppermute | solution.py:116
  394.9 47.4 %collective-permute-start.16 = (bf16[2,128,2048]{2,1,0:T(8,128)(2,1)}, bf16[2,128,2048]{2,1,0:T(8,128)(2,1)S(1)}, u32[]{:S(2)}, u32[]{:S(2)}) collective-permute-start(bf16[2,128,2048]{2,1,0:T(8,128)(2,1)} %bitcast.57), channel_id=1, source_target_pairs={{0,2},{2,0},{1,3},{3,1},{4,6},{6,4},{5,7},{7,5},{8,10},{10,8},{9,1... | collective-permute-start | bytes 3145736 | tf_op jit(solution)/shard_map/ppermute | solution.py:115
  396.5 40.3 %collective-permute-start.22 = (bf16[2,128,2048]{2,1,0:T(8,128)(2,1)S(1)}, bf16[2,128,2048]{2,1,0:T(8,128)(2,1)S(1)}, u32[]{:S(2)}, u32[]{:S(2)}) collective-permute-start(bf16[2,128,2048]{2,1,0:T(8,128)(2,1)S(1)} %bitcast.413), channel_id=1, source_target_pairs={{0,1},{1,0},{2,3},{3,2},{4,5},{5,4},{6,7},{7,6},{8,9},{9,8},{10,11... | collective-permute-start | bytes 3145736 | tf_op jit(solution)/shard_map/ppermute | solution.py:116
  397.4 42.8 %collective-permute-start.20 = (bf16[2,128,2048]{2,1,0:T(8,128)(2,1)S(1)}, bf16[2,128,2048]{2,1,0:T(8,128)(2,1)S(1)}, u32[]{:S(2)}, u32[]{:S(2)}) collective-permute-start(bf16[2,128,2048]{2,1,0:T(8,128)(2,1)S(1)} %bitcast.410), channel_id=1, source_target_pairs={{0,2},{2,0},{1,3},{3,1},{4,6},{6,4},{5,7},{7,5},{8,10},{10,8},{9,1... | collective-permute-start | bytes 3145736 | tf_op jit(solution)/shard_map/ppermute | solution.py:115
  472.8 24.4 %collective-permute-start.25 = (bf16[256,2048]{1,0:T(8,128)(2,1)S(1)}, bf16[256,2048]{1,0:T(8,128)(2,1)S(1)}, u32[]{:S(2)}, u32[]{:S(2)}) collective-permute-start(bf16[256,2048]{1,0:T(8,128)(2,1)S(1)} %pad_maximum_fusion.16), channel_id=1, source_target_pairs={{0,2},{2,0},{1,3},{3,1},{4,6},{6,4},{5,7},{7,5},{8,10},{10,8},{9,1... | collective-permute-start | bytes 3145736 | tf_op jit(solution)/shard_map/ppermute | solution.py:102
  474.5 22.0 %collective-permute-start.26 = (bf16[128,2048]{1,0:T(8,128)(2,1)S(1)}, bf16[128,2048]{1,0:T(8,128)(2,1)S(1)}, u32[]{:S(2)}, u32[]{:S(2)}) collective-permute-start(bf16[128,2048]{1,0:T(8,128)(2,1)S(1)} %get-tuple-element.173), channel_id=1, source_target_pairs={{0,2},{2,0},{1,3},{3,1},{4,6},{6,4},{5,7},{7,5},{8,10},{10,8},{9,1... | collective-permute-start | bytes 1572872 | tf_op jit(solution)/shard_map/ppermute | solution.py:99
  543.7 106.6 %reduce-scatter.5.cloned.1.call-start = ((), (), s32[]{:S(2)}) async-start(), calls=%async_computation.7 | async-start | bytes 5308416 | tf_op jit(solution)/shard_map/reduce_scatter | solution.py:142
  592.9 157.5 %reduce-scatter.9.cloned.1.call-start = ((), (), s32[]{:S(2)}) async-start(), calls=%async_computation.9 | async-start | bytes 10616832 | tf_op jit(solution)/shard_map/reduce_scatter | solution.py:268
  593.5 257.1 %reduce-scatter.11.cloned.1.call-start = ((), (), s32[]{:S(2)}) async-start(), calls=%async_computation.10 | async-start | bytes 10616832 | tf_op jit(solution)/shard_map/reduce_scatter | solution.py:268
  595.9 18.7 %collective-permute-start.28 = (bf16[2,128,2048]{2,1,0:T(8,128)(2,1)S(1)}, bf16[2,128,2048]{2,1,0:T(8,128)(2,1)S(1)}, u32[]{:S(2)}, u32[]{:S(2)}) collective-permute-start(bf16[2,128,2048]{2,1,0:T(8,128)(2,1)S(1)} %bitcast.414), channel_id=1, source_target_pairs={{0,2},{2,0},{1,3},{3,1},{4,6},{6,4},{5,7},{7,5},{8,10},{10,8},{9,1... | collective-permute-start | bytes 3145736 | tf_op jit(solution)/shard_map/ppermute | solution.py:115
  (97 other events, 866.0 us)
Sparse Core Ops, SparseCore 0:
  26.6 72.1 all-gather.3
  101.0 89.3 all-gather.5
  192.5 89.3 all-gather.7
  543.8 37.4 reduce-scatter.6
  593.0 57.2 reduce-scatter.4
  652.5 97.8 reduce-scatter.8
  752.7 97.8 reduce-scatter.10

commit v4 on v3

--- a/solution.py
+++ b/solution.py
@@ -265,15 +265,17 @@
             joined, mlp_sets[1] = lax.optimization_barrier((joined, mlp_sets[1]))
         else:
             joined, d_mlp_partial = lax.optimization_barrier((joined, d_mlp_partial))
-        summed = lax.psum_scatter(joined, "wide", scatter_dimension=0, tiled=True).astype(jnp.float32)
-        mlp_grads.append(split_cols(summed, [2 * ff_half, ff_half]))
+        mlp_grads.append(lax.psum_scatter(joined, "wide", scatter_dimension=0, tiled=True))
 
     d_mlp_in = narrow_scatter(d_mlp_partial, relative)
     d_part, mlp_gain_terms = rms_back(resid, gain_mlp, d_mlp_in)
     grad_mlp_gain = jnp.sum(mlp_gain_terms, axis=0)
     d_resid = cotangent.astype(jnp.float32) + d_part
     branch_rows = narrow_gather(d_resid.astype(jnp.bfloat16), relative)
-    (g_out_t,) = wide_scatter([contract_rows(branch_rows, attended)])
+    out_grad = contract_rows(branch_rows, attended).astype(jnp.bfloat16)
+    mlp_grads, out_grad = lax.optimization_barrier((mlp_grads, out_grad))
+    mlp_grads = [split_cols(g.astype(jnp.float32), [2 * ff_half, ff_half]) for g in mlp_grads]
+    g_out_t = lax.psum_scatter(out_grad, "wide", scatter_dimension=0, tiled=True).astype(jnp.float32)
     d_attended = jnp.dot(branch_rows, out_wt, preferred_element_type=jnp.float32).astype(jnp.bfloat16)
     d_mixed = d_attended.reshape(rows_group, groups_here, repeat, HD)
 
@@ -326,7 +328,14 @@
         axis=-1,
     ).reshape(d_full, 4)
     gain_block = jnp.pad(gain_block, ((0, 0), (0, 124)))
-    g_qkv, g_gains = wide_scatter([contract_rows(normed_all, d_qkv), gain_block])
+    qkv_grad = jnp.concatenate(
+        [contract_rows(normed_all, d_qkv).astype(jnp.bfloat16), gain_block.astype(jnp.bfloat16)], axis=1
+    )
+    g_out_t, qkv_grad = lax.optimization_barrier((g_out_t, qkv_grad))
+    g_qkv, g_gains = split_cols(
+        lax.psum_scatter(qkv_grad, "wide", scatter_dimension=0, tiled=True).astype(jnp.float32),
+        [q_cols + 2 * kv_cols, 128],
+    )
     d_normed = narrow_scatter(d_normed_partial, relative)
     d_input_part, unused_terms = rms_back(inputs, gain_attn, d_normed)
     d_tokens = d_resid + d_input_part

time: 871 us -> 682 us (0.78)
  waiting for transfers between devices: 474 us -> 272 us
    reduce_scatter x2, waiting for transfers between devices: 192 us -> 0.01 us  [shards(): lax.psum_scatter(joined, 'wide', scatter_dimension=0, tiled=True)]
    reduce_scatter x2, waiting for transfers between devices: 20.2 us -> 9.91 us  [the longest x1 5.19 us: shards(): lax.psum_scatter(qkv_grad, 'wide', scatter_dimension=0, tiled=True)]
    unnamed x211 -> x239, local copies, waits for them, and re-layouts: 32.8 us -> 32.7 us
  transfers between devices with their start and end apart: 41 -> 41, of which waited for: 28 -> 26; matrix products, arithmetic and copies ran while one was open for 19% -> 45% of each run, Pallas kernels for 0% -> 0%
where the time goes in v4:
time: 682 us; the launch traced here: 677 us
  waiting for transfers between devices  272 us (40%)
  matrix products  186 us (27%)
  other arithmetic  90.2 us (13%)
  local copies, waits for them, and re-layouts  72 us (11%)
  starting transfers between devices  40.9 us (6%)
  between operations  16.7 us (2%)
    dot_general x8, matrix products, times_transposed(): lax.dot_general(left, right, (((1,), (1,)), ((), ())), preferred_element_...  60.3 us
    ppermute x4, waiting for transfers between devices, narrow_gather(): a_pair_y = lax.ppermute(a_pair, 'narrow', YPERM)  46.1 us
    ppermute x4, waiting for transfers between devices, narrow_scatter(): b_got = lax.ppermute(blocks[6:8].astype(jnp.bfloat16), 'narrow', XPERM)  44.2 us
    ppermute x4, waiting for transfers between devices, narrow_gather(): b_pair_x = lax.ppermute(b_pair, 'narrow', XPERM)  41.3 us
    dot_general x6, matrix products, contract_rows(): lax.dot_general(left, right, (((0,), (0,)), ((), ())), preferred_element_...  40.6 us
    ppermute x4, waiting for transfers between devices, narrow_scatter(): a_got = lax.ppermute(blocks[2:4].astype(jnp.bfloat16), 'narrow', YPERM)  37.9 us
    ppermute x4, waiting for transfers between devices, narrow_gather(): b_y = lax.ppermute(b, 'narrow', YPERM)  35.6 us
    unnamed x239, local copies, waits for them, and re-layouts  32.7 us
  transfers between devices with their start and end apart: 41, of which 26 were waited for; matrix products, arithmetic and copies ran while one was open for 45% of the time, Pallas kernels for 0%

profile of v4, /device:TPU:0, one launch (start us, length us, event | category | flops | bytes accessed | tf_op | source)
XLA Modules:
  0.0 677.3 jit_solution(16055563237938505900)
XLA Ops:
  50.1 21.7 %collective-permute-done.1 = bf16[256,2048]{1,0:T(8,128)(2,1)S(1)} collective-permute-done((bf16[256,2048]{1,0:T(8,128)(2,1)S(1)}, bf16[256,2048]{1,0:T(8,128)(2,1)S(1)}, u32[]{:S(2)}, u32[]{:S(2)}) %collective-permute-start.1) | collective-permute-done | bytes 1048608 | tf_op jit(solution)/shard_map/ppermute | solution.py:102
  75.3 10.9 %collective-permute-done.2 = bf16[128,2048]{1,0:T(8,128)(2,1)S(1)} collective-permute-done((bf16[128,2048]{1,0:T(8,128)(2,1)S(1)}, bf16[128,2048]{1,0:T(8,128)(2,1)S(1)}, u32[]{:S(2)}, u32[]{:S(2)}) %collective-permute-start.2) | collective-permute-done | bytes 524320 | tf_op jit(solution)/shard_map/ppermute | solution.py:99
  91.8 17.4 %collective-permute-done.3 = bf16[256,2048]{1,0:T(8,128)(2,1)S(1)} collective-permute-done((bf16[256,2048]{1,0:T(8,128)(2,1)S(1)}, bf16[256,2048]{1,0:T(8,128)(2,1)S(1)}, u32[]{:S(2)}, u32[]{:S(2)}) %collective-permute-start.3) | collective-permute-done | bytes 1048608 | tf_op jit(solution)/shard_map/ppermute | solution.py:103
  154.2 21.2 %collective-permute-done.4 = bf16[2,128,2048]{2,1,0:T(8,128)(2,1)S(1)} collective-permute-done((bf16[2,128,2048]{2,1,0:T(8,128)(2,1)S(1)}, bf16[2,128,2048]{2,1,0:T(8,128)(2,1)S(1)}, u32[]{:S(2)}, u32[]{:S(2)}) %collective-permute-start.4) | collective-permute-done | bytes 1048608 | tf_op jit(solution)/shard_map/ppermute | solution.py:115
  176.9 12.0 %collective-permute-done.6 = bf16[2,128,2048]{2,1,0:T(8,128)(2,1)S(1)} collective-permute-done((bf16[2,128,2048]{2,1,0:T(8,128)(2,1)S(1)}, bf16[2,128,2048]{2,1,0:T(8,128)(2,1)S(1)}, u32[]{:S(2)}, u32[]{:S(2)}) %collective-permute-start.6) | collective-permute-done | bytes 1048608 | tf_op jit(solution)/shard_map/ppermute | solution.py:116
  208.7 14.9 %collective-permute-done.13 = bf16[256,2048]{1,0:T(8,128)(2,1)S(1)} collective-permute-done((bf16[256,2048]{1,0:T(8,128)(2,1)S(1)}, bf16[256,2048]{1,0:T(8,128)(2,1)S(1)}, u32[]{:S(2)}, u32[]{:S(2)}) %collective-permute-start.13) | collective-permute-done | bytes 1048608 | tf_op jit(solution)/shard_map/ppermute | solution.py:102
  226.1 9.8 %collective-permute-done.15 = bf16[256,2048]{1,0:T(8,128)(2,1)S(1)} collective-permute-done((bf16[256,2048]{1,0:T(8,128)(2,1)S(1)}, bf16[256,2048]{1,0:T(8,128)(2,1)S(1)}, u32[]{:S(2)}, u32[]{:S(2)}) %collective-permute-start.15) | collective-permute-done | bytes 1048608 | tf_op jit(solution)/shard_map/ppermute | solution.py:103
  241.1 9.5 %collective-permute-done.9 = bf16[256,2048]{1,0:T(8,128)(2,1)S(1)} collective-permute-done((bf16[256,2048]{1,0:T(8,128)(2,1)S(1)}, bf16[256,2048]{1,0:T(8,128)(2,1)S(1)}, u32[]{:S(2)}, u32[]{:S(2)}) %collective-permute-start.9) | collective-permute-done | bytes 1048608 | tf_op jit(solution)/shard_map/ppermute | solution.py:102
  277.8 10.6 %convolution_convert_fusion.1 = bf16[2048,1536]{0,1:T(8,128)(2,1)S(1)} fusion(bf16[1024,2048]{1,0:T(8,128)(2,1)} %constant_dynamic-update-slice_fusion.13, bf16[1024,768]{0,1:T(8,128)(2,1)S(1)} %get-tuple-element.157, bf16[1024,768]{0,1:T(8,128)(2,1)S(1)} %get-tuple-element.155), kind=kOutput, calls=%fused_computation.29 | convolution fusion | flops 6451888128 | bytes 13631488 | tf_op jit(solution)/shard_map/dot_general | solution.py:60
  288.4 11.6 %pad_maximum_fusion = bf16[2048,2304]{0,1:T(8,128)(2,1)} fusion(bf16[2048,768]{0,1:T(8,128)(2,1)S(1)} %convolution_convert_fusion.4, bf16[2048,1536]{0,1:T(8,128)(2,1)S(1)} %convolution_convert_fusion.1), kind=kLoop, calls=%fused_computation.16 | loop fusion | flops 18874368 | bytes 18874368 | tf_op jit(solution)/shard_map/concatenate | solution.py:263
  347.3 10.7 %convolution_convert_fusion = bf16[2048,1536]{0,1:T(8,128)(2,1)S(1)} fusion(bf16[1024,2048]{1,0:T(8,128)(2,1)} %constant_dynamic-update-slice_fusion.13, bf16[1024,768]{0,1:T(8,128)(2,1)S(1)} %get-tuple-element.154, bf16[1024,768]{0,1:T(8,128)(2,1)S(1)} %copy-done.83), kind=kOutput, calls=%fused_computation.28 | convolution fusion | flops 6451888128 | bytes 13631488 | tf_op jit(solution)/shard_map/dot_general | solution.py:60
  357.9 11.5 %pad_maximum_fusion.1 = bf16[2048,2304]{0,1:T(8,128)(2,1)} fusion(bf16[2048,768]{0,1:T(8,128)(2,1)S(1)} %convolution_convert_fusion.3, bf16[2048,1536]{0,1:T(8,128)(2,1)S(1)} %convolution_convert_fusion), kind=kLoop, calls=%fused_computation.17 | loop fusion | flops 18874368 | bytes 18874368 | tf_op jit(solution)/shard_map/concatenate | solution.py:263
  369.5 11.3 %add_add_fusion = f32[1024,2048]{1,0:T(8,128)S(1)} fusion(f32[1024,2048]{1,0:T(8,128)} %fusion.165, f32[1024,2048]{1,0:T(8,128)} %fusion.35, f32[1024,2048]{1,0:T(8,128)} %fusion.31, bf16[1024,768]{0,1:T(8,128)(2,1)} %copy-done.40, bf16[2048,768]{0,1:T(8,128)(2,1)S(1)} %get-tuple-element.73), kind=kOutput, calls=%fused_computation.24 | convolution fusion | flops 3227516928 | bytes 38273024 | tf_op jit(solution)/shard_map/dot_general | solution.py:66
  380.8 9.0 %fusion.29 = f32[1024,2048]{1,0:T(8,128)S(1)} fusion(bf16[1024,768]{0,1:T(8,128)(2,1)} %copy-done.77, bf16[2048,2304]{0,1:T(8,128)(2,1)} %all-gather.6.cloned.1.call-done), kind=kOutput, calls=%fused_computation.63 | convolution fusion | flops 3221225472 | bytes 13107200 | tf_op jit(solution)/shard_map/dot_general | solution.py:66
  409.0 31.2 %collective-permute-done.22 = bf16[2,128,2048]{2,1,0:T(8,128)(2,1)} collective-permute-done((bf16[2,128,2048]{2,1,0:T(8,128)(2,1)}, bf16[2,128,2048]{2,1,0:T(8,128)(2,1)}, u32[]{:S(2)}, u32[]{:S(2)}) %collective-permute-start.22) | collective-permute-done | bytes 1048608 | tf_op jit(solution)/shard_map/ppermute | solution.py:116
  455.6 9.7 %collective-permute-done.17 = bf16[128,2048]{1,0:T(8,128)(2,1)S(1)} collective-permute-done((bf16[128,2048]{1,0:T(8,128)(2,1)S(1)}, bf16[128,2048]{1,0:T(8,128)(2,1)S(1)}, u32[]{:S(2)}, u32[]{:S(2)}) %collective-permute-start.17) | collective-permute-done | bytes 524320 | tf_op jit(solution)/shard_map/ppermute | solution.py:119
  479.1 22.2 %collective-permute-done.26 = bf16[128,2048]{1,0:T(8,128)(2,1)S(1)} collective-permute-done((bf16[128,2048]{1,0:T(8,128)(2,1)S(1)}, bf16[128,2048]{1,0:T(8,128)(2,1)S(1)}, u32[]{:S(2)}, u32[]{:S(2)}) %collective-permute-start.26) | collective-permute-done | bytes 524320 | tf_op jit(solution)/shard_map/ppermute | solution.py:99
  502.4 13.8 %collective-permute-done.27 = bf16[256,2048]{1,0:T(8,128)(2,1)S(1)} collective-permute-done((bf16[256,2048]{1,0:T(8,128)(2,1)S(1)}, bf16[256,2048]{1,0:T(8,128)(2,1)S(1)}, u32[]{:S(2)}, u32[]{:S(2)}) %collective-permute-start.27) | collective-permute-done | bytes 1048608 | tf_op jit(solution)/shard_map/ppermute | solution.py:103
  518.9 12.7 %fusion = (f32[2,2,1024]{2,1,0:T(2,128)S(1)}, f32[2,1024,1024,2]{2,1,3,0:T(8,128)}) fusion(f32[2,1024,1024,2]{2,1,3,0:T(8,128)} %copy-done, f32[2,2,1024]{2,1,0:T(2,128)S(1)} %log_add_fusion, pred[1024,1024]{0,1:T(8,128)(4,1)S(1)} %copy-done.9, bf16[1024,2,128,1]{0,2,3,1:T(8,128)(2,1)S(1)} %bitcast.398, bf16[1024,2,2,128]{0,3,2,1:T(8,128)(2,1)S(1)} %bitcast.411), kind=kOutput, calls=%fused_computation.2 | convolution fusion | flops 1094709248 | bytes 36208640 | tf_op jit(solution)/shard_map/qgrd,kgd->grqk/dot_general | solution.py:284
  531.6 12.4 %fusion.2 = bf16[2,2,1024,1024]{2,3,1,0:T(8,128)(2,1)S(1)} fusion(f32[2,1024,1024,2]{2,1,3,0:T(8,128)} %get-tuple-element.245, f32[2,1024,1024,2]{2,1,3,0:T(8,128)} %copy-done, f32[2,2,1024]{2,1,0:T(2,128)S(1)} %get-tuple-element.244, f32[2,2,1024]{2,1,0:T(2,128)S(1)} %log_add_fusion, pred[1024,1024]{0,1:T(8,128)(4,1)S(1)} %copy-done.9), kind=kLoop, calls=%fused_computation.4 | loop fusion | flops 25165824 | bytes 43024384 | tf_op jit(solution)/shard_map/convert_element_type | solution.py:286
  560.6 10.9 %fusion.66 = bf16[2,128,1024]{2,1,0:T(8,128)(2,1)} fusion(bf16[1024,2,2,128]{0,3,2,1:T(8,128)(2,1)} %bitcast.412, f32[2,1024,1024,2]{2,1,3,0:T(8,128)} %copy-done, f32[2,2,1024]{2,1,0:T(2,128)S(1)} %log_add_fusion, pred[1024,1024]{0,1:T(8,128)(4,1)S(1)} %copy-done.9), kind=kOutput, calls=%fused_computation.127 | convolution fusion | flops 1090781184 | bytes 19415040 | tf_op jit(solution)/shard_map/grqk,qgrd->kgd/dot_general | solution.py:289
  571.7 13.9 %fusion.12 = (f32[2048]{0:T(1024)S(1)}, bf16[1024,2048]{1,0:T(8,128)(2,1)}, f32[1024,2048]{1,0:T(8,128)}) fusion(bf16[1024,2048]{1,0:T(8,128)(2,1)} %copy-done.21, f32[1024]{0:T(1024)S(1)} %copy-done.74, bf16[2048,1664]{0,1:T(8,128)(2,1)} %all-gather.4.cloned.1.call-done, bf16[1024,256]{0,1:T(8,128)(2,1)} %bitcast.433, bf16[1024,256]{0,1:T(8,128)(2,1)} %bitcast.415, ...), kind=kOutput, calls=%fused_computation.23 | convolution fusion | flops 4311742464 | bytes 23080960 | tf_op jit(solution)/shard_map/dot_general | solution.py:66
  617.7 16.7 %collective-permute-done.28 = bf16[2,128,2048]{2,1,0:T(8,128)(2,1)S(1)} collective-permute-done((bf16[2,128,2048]{2,1,0:T(8,128)(2,1)S(1)}, bf16[2,128,2048]{2,1,0:T(8,128)(2,1)S(1)}, u32[]{:S(2)}, u32[]{:S(2)}) %collective-permute-start.28) | collective-permute-done | bytes 1048608 | tf_op jit(solution)/shard_map/ppermute | solution.py:115
  638.0 8.7 %collective-permute-done.29 = bf16[128,2048]{1,0:T(8,128)(2,1)S(1)} collective-permute-done((bf16[128,2048]{1,0:T(8,128)(2,1)S(1)}, bf16[128,2048]{1,0:T(8,128)(2,1)S(1)}, u32[]{:S(2)}, u32[]{:S(2)}) %collective-permute-start.29) | collective-permute-done | bytes 524320 | tf_op jit(solution)/shard_map/ppermute | solution.py:119
  (505 shorter events, 326.3 us)
Async XLA Ops:
  7.2 105.1 %all-gather.4.cloned.1.call-start = ((), (), s32[]{:S(2)}) async-start(), calls=%async_computation.4 | async-start | bytes 7667712 | tf_op jit(solution)/shard_map/all_gather | solution.py:136
  26.4 228.2 %all-gather.6.cloned.1.call-start = ((), (), s32[]{:S(2)}) async-start(), calls=%async_computation.5 | async-start | bytes 10616832 | tf_op jit(solution)/shard_map/all_gather | solution.py:136
  31.2 268.7 %all-gather.8.cloned.1.call-start = ((), (), s32[]{:S(2)}) async-start(), calls=%async_computation.6 | async-start | bytes 10616832 | tf_op jit(solution)/shard_map/all_gather | solution.py:136
  37.7 533.8 %reduce-scatter.5.cloned.1.call-start = ((), (), s32[]{:S(2)}) async-start(), calls=%async_computation.7 | async-start | bytes 10616832 | tf_op jit(solution)/shard_map/reduce_scatter | solution.py:268
  47.2 24.5 %collective-permute-start.1 = (bf16[256,2048]{1,0:T(8,128)(2,1)S(1)}, bf16[256,2048]{1,0:T(8,128)(2,1)S(1)}, u32[]{:S(2)}, u32[]{:S(2)}) collective-permute-start(bf16[256,2048]{1,0:T(8,128)(2,1)S(1)} %pad_maximum_fusion.10), channel_id=1, source_target_pairs={{0,2},{2,0},{1,3},{3,1},{4,6},{6,4},{5,7},{7,5},{8,10},{10,8},{9,1... | collective-permute-start | bytes 3145736 | tf_op jit(solution)/shard_map/ppermute | solution.py:102
  86.2 23.0 %collective-permute-start.3 = (bf16[256,2048]{1,0:T(8,128)(2,1)S(1)}, bf16[256,2048]{1,0:T(8,128)(2,1)S(1)}, u32[]{:S(2)}, u32[]{:S(2)}) collective-permute-start(bf16[256,2048]{1,0:T(8,128)(2,1)S(1)} %pad_maximum_fusion.11), channel_id=1, source_target_pairs={{0,1},{1,0},{2,3},{3,2},{4,5},{5,4},{6,7},{7,6},{8,9},{9,8},{10,11... | collective-permute-start | bytes 3145736 | tf_op jit(solution)/shard_map/ppermute | solution.py:103
  149.3 26.1 %collective-permute-start.4 = (bf16[2,128,2048]{2,1,0:T(8,128)(2,1)S(1)}, bf16[2,128,2048]{2,1,0:T(8,128)(2,1)S(1)}, u32[]{:S(2)}, u32[]{:S(2)}) collective-permute-start(bf16[2,128,2048]{2,1,0:T(8,128)(2,1)S(1)} %bitcast.408), channel_id=1, source_target_pairs={{0,2},{2,0},{1,3},{3,1},{4,6},{6,4},{5,7},{7,5},{8,10},{10,8},{9,1... | collective-permute-start | bytes 3145736 | tf_op jit(solution)/shard_map/ppermute | solution.py:115
  150.7 57.3 %collective-permute-start.14 = (bf16[128,2048]{1,0:T(8,128)(2,1)S(1)}, bf16[128,2048]{1,0:T(8,128)(2,1)S(1)}, u32[]{:S(2)}, u32[]{:S(2)}) collective-permute-start(bf16[128,2048]{1,0:T(8,128)(2,1)S(1)} %get-tuple-element.186), channel_id=1, source_target_pairs={{0,2},{2,0},{1,3},{3,1},{4,6},{6,4},{5,7},{7,5},{8,10},{10,8},{9,1... | collective-permute-start | bytes 1572872 | tf_op jit(solution)/shard_map/ppermute | solution.py:99
  151.7 38.8 %collective-permute-start.12 = (bf16[128,2048]{1,0:T(8,128)(2,1)S(1)}, bf16[128,2048]{1,0:T(8,128)(2,1)S(1)}, u32[]{:S(2)}, u32[]{:S(2)}) collective-permute-start(bf16[128,2048]{1,0:T(8,128)(2,1)S(1)} %get-tuple-element.188), channel_id=1, source_target_pairs={{0,1},{1,0},{2,3},{3,2},{4,5},{5,4},{6,7},{7,6},{8,9},{9,8},{10,11... | collective-permute-start | bytes 1572872 | tf_op jit(solution)/shard_map/ppermute | solution.py:98
  153.2 35.8 %collective-permute-start.6 = (bf16[2,128,2048]{2,1,0:T(8,128)(2,1)S(1)}, bf16[2,128,2048]{2,1,0:T(8,128)(2,1)S(1)}, u32[]{:S(2)}, u32[]{:S(2)}) collective-permute-start(bf16[2,128,2048]{2,1,0:T(8,128)(2,1)S(1)} %bitcast.407), channel_id=1, source_target_pairs={{0,1},{1,0},{2,3},{3,2},{4,5},{5,4},{6,7},{7,6},{8,9},{9,8},{10,11... | collective-permute-start | bytes 3145736 | tf_op jit(solution)/shard_map/ppermute | solution.py:116
  190.6 33.1 %collective-permute-start.13 = (bf16[256,2048]{1,0:T(8,128)(2,1)S(1)}, bf16[256,2048]{1,0:T(8,128)(2,1)S(1)}, u32[]{:S(2)}, u32[]{:S(2)}) collective-permute-start(bf16[256,2048]{1,0:T(8,128)(2,1)S(1)} %pad_maximum_fusion.14), channel_id=1, source_target_pairs={{0,2},{2,0},{1,3},{3,1},{4,6},{6,4},{5,7},{7,5},{8,10},{10,8},{9,1... | collective-permute-start | bytes 3145736 | tf_op jit(solution)/shard_map/ppermute | solution.py:102
  208.1 27.8 %collective-permute-start.15 = (bf16[256,2048]{1,0:T(8,128)(2,1)S(1)}, bf16[256,2048]{1,0:T(8,128)(2,1)S(1)}, u32[]{:S(2)}, u32[]{:S(2)}) collective-permute-start(bf16[256,2048]{1,0:T(8,128)(2,1)S(1)} %pad_maximum_fusion.15), channel_id=1, source_target_pairs={{0,1},{1,0},{2,3},{3,2},{4,5},{5,4},{6,7},{7,6},{8,9},{9,8},{10,11... | collective-permute-start | bytes 3145736 | tf_op jit(solution)/shard_map/ppermute | solution.py:103
  225.0 25.5 %collective-permute-start.9 = (bf16[256,2048]{1,0:T(8,128)(2,1)S(1)}, bf16[256,2048]{1,0:T(8,128)(2,1)S(1)}, u32[]{:S(2)}, u32[]{:S(2)}) collective-permute-start(bf16[256,2048]{1,0:T(8,128)(2,1)S(1)} %pad_maximum_fusion.12), channel_id=1, source_target_pairs={{0,2},{2,0},{1,3},{3,1},{4,6},{6,4},{5,7},{7,5},{8,10},{10,8},{9,1... | collective-permute-start | bytes 3145736 | tf_op jit(solution)/shard_map/ppermute | solution.py:102
  306.0 265.5 %reduce-scatter.7.cloned.1.call-start = ((), (), s32[]{:S(2)}) async-start(), calls=%async_computation.8 | async-start | bytes 10616832 | tf_op jit(solution)/shard_map/reduce_scatter | solution.py:268
  397.8 48.1 %collective-permute-start.18 = (bf16[2,128,2048]{2,1,0:T(8,128)(2,1)}, bf16[2,128,2048]{2,1,0:T(8,128)(2,1)S(1)}, u32[]{:S(2)}, u32[]{:S(2)}) collective-permute-start(bf16[2,128,2048]{2,1,0:T(8,128)(2,1)} %bitcast.61), channel_id=1, source_target_pairs={{0,1},{1,0},{2,3},{3,2},{4,5},{5,4},{6,7},{7,6},{8,9},{9,8},{10,11... | collective-permute-start | bytes 3145736 | tf_op jit(solution)/shard_map/ppermute | solution.py:116
  399.5 46.0 %collective-permute-start.16 = (bf16[2,128,2048]{2,1,0:T(8,128)(2,1)}, bf16[2,128,2048]{2,1,0:T(8,128)(2,1)S(1)}, u32[]{:S(2)}, u32[]{:S(2)}) collective-permute-start(bf16[2,128,2048]{2,1,0:T(8,128)(2,1)} %bitcast.57), channel_id=1, source_target_pairs={{0,2},{2,0},{1,3},{3,1},{4,6},{6,4},{5,7},{7,5},{8,10},{10,8},{9,1... | collective-permute-start | bytes 3145736 | tf_op jit(solution)/shard_map/ppermute | solution.py:115
  402.2 38.1 %collective-permute-start.22 = (bf16[2,128,2048]{2,1,0:T(8,128)(2,1)}, bf16[2,128,2048]{2,1,0:T(8,128)(2,1)}, u32[]{:S(2)}, u32[]{:S(2)}) collective-permute-start(bf16[2,128,2048]{2,1,0:T(8,128)(2,1)} %bitcast.69), channel_id=1, source_target_pairs={{0,1},{1,0},{2,3},{3,2},{4,5},{5,4},{6,7},{7,6},{8,9},{9,8},{10,11... | collective-permute-start | bytes 3145736 | tf_op jit(solution)/shard_map/ppermute | solution.py:116
  403.1 41.2 %collective-permute-start.20 = (bf16[2,128,2048]{2,1,0:T(8,128)(2,1)}, bf16[2,128,2048]{2,1,0:T(8,128)(2,1)S(1)}, u32[]{:S(2)}, u32[]{:S(2)}) collective-permute-start(bf16[2,128,2048]{2,1,0:T(8,128)(2,1)} %bitcast.65), channel_id=1, source_target_pairs={{0,2},{2,0},{1,3},{3,1},{4,6},{6,4},{5,7},{7,5},{8,10},{10,8},{9,1... | collective-permute-start | bytes 3145736 | tf_op jit(solution)/shard_map/ppermute | solution.py:115
  404.0 204.5 %reduce-scatter.9.cloned.1.call-start = ((), (), s32[]{:S(2)}) async-start(), calls=%async_computation.9 | async-start | bytes 2359296 | tf_op jit(solution)/shard_map/reduce_scatter | solution.py:278
  476.9 25.3 %collective-permute-start.25 = (bf16[256,2048]{1,0:T(8,128)(2,1)S(1)}, bf16[256,2048]{1,0:T(8,128)(2,1)S(1)}, u32[]{:S(2)}, u32[]{:S(2)}) collective-permute-start(bf16[256,2048]{1,0:T(8,128)(2,1)S(1)} %pad_maximum_fusion.16), channel_id=1, source_target_pairs={{0,2},{2,0},{1,3},{3,1},{4,6},{6,4},{5,7},{7,5},{8,10},{10,8},{9,1... | collective-permute-start | bytes 3145736 | tf_op jit(solution)/shard_map/ppermute | solution.py:102
  477.7 23.5 %collective-permute-start.26 = (bf16[128,2048]{1,0:T(8,128)(2,1)S(1)}, bf16[128,2048]{1,0:T(8,128)(2,1)S(1)}, u32[]{:S(2)}, u32[]{:S(2)}) collective-permute-start(bf16[128,2048]{1,0:T(8,128)(2,1)S(1)} %get-tuple-element.183), channel_id=1, source_target_pairs={{0,2},{2,0},{1,3},{3,1},{4,6},{6,4},{5,7},{7,5},{8,10},{10,8},{9,1... | collective-permute-start | bytes 1572872 | tf_op jit(solution)/shard_map/ppermute | solution.py:99
  571.6 92.8 %reduce-scatter.11.cloned.1.call-start = ((), (), s32[]{:S(2)}) async-start(), calls=%async_computation.10 | async-start | bytes 5308416 | tf_op jit(solution)/shard_map/reduce_scatter | solution.py:336
  612.0 22.4 %collective-permute-start.28 = (bf16[2,128,2048]{2,1,0:T(8,128)(2,1)S(1)}, bf16[2,128,2048]{2,1,0:T(8,128)(2,1)S(1)}, u32[]{:S(2)}, u32[]{:S(2)}) collective-permute-start(bf16[2,128,2048]{2,1,0:T(8,128)(2,1)S(1)} %bitcast.410), channel_id=1, source_target_pairs={{0,2},{2,0},{1,3},{3,1},{4,6},{6,4},{5,7},{7,5},{8,10},{10,8},{9,1... | collective-permute-start | bytes 3145736 | tf_op jit(solution)/shard_map/ppermute | solution.py:115
  613.7 23.3 %collective-permute-start.30 = (bf16[2,128,2048]{2,1,0:T(8,128)(2,1)S(1)}, bf16[2,128,2048]{2,1,0:T(8,128)(2,1)S(1)}, u32[]{:S(2)}, u32[]{:S(2)}) collective-permute-start(bf16[2,128,2048]{2,1,0:T(8,128)(2,1)S(1)} %bitcast.409), channel_id=1, source_target_pairs={{0,1},{1,0},{2,3},{3,2},{4,5},{5,4},{6,7},{7,6},{8,9},{9,8},{10,11... | collective-permute-start | bytes 3145736 | tf_op jit(solution)/shard_map/ppermute | solution.py:116
  (111 other events, 1157.6 us)
Sparse Core Ops, SparseCore 0:
  26.6 72.2 all-gather.3
  101.0 89.2 all-gather.5
  192.5 89.3 all-gather.7
  306.1 99.9 reduce-scatter.4
  408.3 97.8 reduce-scatter.6
  571.7 36.7 reduce-scatter.8
  610.8 53.5 reduce-scatter.10

commit v5 on v4

--- a/solution.py
+++ b/solution.py
@@ -179,11 +179,13 @@
     tokens_all = narrow_gather(tokens, relative)
     grad_rows = narrow_gather(cotangent, relative)
 
-    gain_block = jnp.zeros((d_local, 128), jnp.bfloat16)
-    gain_block = gain_block.at[:, 0].set(attn_gain)
-    gain_block = gain_block.at[:, 1].set(mlp_gain)
-    gain_block = gain_block.at[:hd_local, 2].set(query_gain)
-    gain_block = gain_block.at[:hd_local, 3].set(key_gain)
+    pad_hd = ((0, d_local - hd_local),)
+    gain_block = jnp.pad(
+        jnp.stack(
+            [attn_gain, mlp_gain, jnp.pad(query_gain, pad_hd), jnp.pad(key_gain, pad_hd)], axis=1
+        ),
+        ((0, 0), (0, 124)),
+    )
     qkv_w, out_wt, gains_all = wide_gather(
         [jnp.concatenate([w_query, w_key, w_value], axis=1), w_out.T, gain_block]
     )
@@ -263,15 +265,21 @@
         joined = jnp.concatenate([g_gate_up.astype(jnp.bfloat16), g_down_t.astype(jnp.bfloat16)], axis=1)
         if h == 0:
             joined, mlp_sets[1] = lax.optimization_barrier((joined, mlp_sets[1]))
+            mlp_grads.append(lax.psum_scatter(joined, "wide", scatter_dimension=0, tiled=True))
         else:
-            joined, d_mlp_partial = lax.optimization_barrier((joined, d_mlp_partial))
-        mlp_grads.append(lax.psum_scatter(joined, "wide", scatter_dimension=0, tiled=True))
+            last_joined = joined
 
     d_mlp_in = narrow_scatter(d_mlp_partial, relative)
     d_part, mlp_gain_terms = rms_back(resid, gain_mlp, d_mlp_in)
     grad_mlp_gain = jnp.sum(mlp_gain_terms, axis=0)
     d_resid = cotangent.astype(jnp.float32) + d_part
-    branch_rows = narrow_gather(d_resid.astype(jnp.bfloat16), relative)
+    p_scores = jnp.einsum("qgrd,kgd->grqk", q_grouped, k_use, preferred_element_type=jnp.float32) * scale
+    p_probs = jnp.where(allowed, jnp.exp(p_scores - log_totals[..., None]), 0.0)
+    d_resid_low, p_probs, last_joined = lax.optimization_barrier(
+        (d_resid.astype(jnp.bfloat16), p_probs, last_joined)
+    )
+    mlp_grads.append(lax.psum_scatter(last_joined, "wide", scatter_dimension=0, tiled=True))
+    branch_rows = narrow_gather(d_resid_low, relative)
     out_grad = contract_rows(branch_rows, attended).astype(jnp.bfloat16)
     mlp_grads, out_grad = lax.optimization_barrier((mlp_grads, out_grad))
     mlp_grads = [split_cols(g.astype(jnp.float32), [2 * ff_half, ff_half]) for g in mlp_grads]
@@ -279,8 +287,6 @@
     d_attended = jnp.dot(branch_rows, out_wt, preferred_element_type=jnp.float32).astype(jnp.bfloat16)
     d_mixed = d_attended.reshape(rows_group, groups_here, repeat, HD)
 
-    p_scores = jnp.einsum("qgrd,kgd->grqk", q_grouped, k_use, preferred_element_type=jnp.float32) * scale
-    p_probs = jnp.where(allowed, jnp.exp(p_scores - log_totals[..., None]), 0.0)
     d_probs = jnp.einsum("qgrd,kgd->grqk", d_mixed, v_use, preferred_element_type=jnp.float32)
     inner = jnp.sum(p_probs * d_probs, axis=-1, keepdims=True)
     d_scores = (p_probs * (d_probs - inner)).astype(jnp.bfloat16)

time: 682 us -> 650 us (0.953)
  waiting for transfers between devices: 272 us -> 218 us
  local copies, waits for them, and re-layouts: 72 us -> 84.3 us
  matrix products: 186 us -> 198 us
    ppermute x4, waiting for transfers between devices: 44.2 us -> 10.4 us  [narrow_scatter(): b_got = lax.ppermute(blocks[6:8].astype(jnp.bfloat16), 'narrow', XPERM)]
    ppermute x4, waiting for transfers between devices: 46.1 us -> 30.9 us  [narrow_gather(): a_pair_y = lax.ppermute(a_pair, 'narrow', YPERM)]
    another operation x12 -> x3, other arithmetic: 11.1 us -> 0.47 us
    unnamed x239 -> x233, local copies, waits for them, and re-layouts: 32.7 us -> 41 us
    ppermute x4, waiting for transfers between devices: 37.9 us -> 30.3 us  [narrow_scatter(): a_got = lax.ppermute(blocks[2:4].astype(jnp.bfloat16), 'narrow', YPERM)]
    select_n x0 -> x1, other arithmetic: none -> 6.97 us  [shards(): p_probs = jnp.where(allowed, jnp.exp(p_scores - log_totals[..., None]), 0.0)]
  transfers between devices with their start and end apart: 41 -> 41, of which waited for: 26 -> 25; matrix products, arithmetic and copies ran while one was open for 45% -> 52% of each run, Pallas kernels for 0% -> 0%
where the time goes in v5:
time: 650 us; the launch traced here: 645 us
  waiting for transfers between devices  218 us (34%)
  matrix products  198 us (30%)
  other arithmetic  89.9 us (14%)
  local copies, waits for them, and re-layouts  84.3 us (13%)
  starting transfers between devices  39.2 us (6%)
  between operations  16.4 us (3%)
    dot_general x8, matrix products, times_transposed(): lax.dot_general(left, right, (((1,), (1,)), ((), ())), preferred_element_...  59.3 us
    dot_general x6, matrix products, contract_rows(): lax.dot_general(left, right, (((0,), (0,)), ((), ())), preferred_element_...  46.9 us
    unnamed x233, local copies, waits for them, and re-layouts  41 us
    ppermute x4, waiting for transfers between devices, narrow_gather(): b_y = lax.ppermute(b, 'narrow', YPERM)  38.9 us
    ppermute x4, waiting for transfers between devices, narrow_gather(): b_pair_x = lax.ppermute(b_pair, 'narrow', XPERM)  38.9 us
    ppermute x4, waiting for transfers between devices, narrow_gather(): a_pair_y = lax.ppermute(a_pair, 'narrow', YPERM)  30.9 us
    ppermute x4, waiting for transfers between devices, narrow_scatter(): a_got = lax.ppermute(blocks[2:4].astype(jnp.bfloat16), 'narrow', YPERM)  30.3 us
    ppermute x4, waiting for transfers between devices, narrow_scatter(): a_got2 = lax.ppermute(a_sum[1].astype(jnp.bfloat16), 'narrow', XPERM)  25.6 us
  transfers between devices with their start and end apart: 41, of which 25 were waited for; matrix products, arithmetic and copies ran while one was open for 52% of the time, Pallas kernels for 0%

profile of v5, /device:TPU:0, one launch (start us, length us, event | category | flops | bytes accessed | tf_op | source)
XLA Modules:
  0.0 645.0 jit_solution(15216649246104085683)
XLA Ops:
  39.5 21.4 %collective-permute-done.1 = bf16[256,2048]{1,0:T(8,128)(2,1)S(1)} collective-permute-done((bf16[256,2048]{1,0:T(8,128)(2,1)S(1)}, bf16[256,2048]{1,0:T(8,128)(2,1)S(1)}, u32[]{:S(2)}, u32[]{:S(2)}) %collective-permute-start.1) | collective-permute-done | bytes 1048608 | tf_op jit(solution)/shard_map/ppermute | solution.py:102
  67.3 8.0 %collective-permute-done.2 = bf16[128,2048]{1,0:T(8,128)(2,1)S(1)} collective-permute-done((bf16[128,2048]{1,0:T(8,128)(2,1)S(1)}, bf16[128,2048]{1,0:T(8,128)(2,1)S(1)}, u32[]{:S(2)}, u32[]{:S(2)}) %collective-permute-start.2) | collective-permute-done | bytes 524320 | tf_op jit(solution)/shard_map/ppermute | solution.py:99
  84.8 16.6 %collective-permute-done.3 = bf16[256,2048]{1,0:T(8,128)(2,1)S(1)} collective-permute-done((bf16[256,2048]{1,0:T(8,128)(2,1)S(1)}, bf16[256,2048]{1,0:T(8,128)(2,1)S(1)}, u32[]{:S(2)}, u32[]{:S(2)}) %collective-permute-start.3) | collective-permute-done | bytes 1048608 | tf_op jit(solution)/shard_map/ppermute | solution.py:103
  105.5 7.8 %fusion.17 = f32[1024,1024]{0,1:T(8,128)S(1)} fusion(bf16[2048,1664]{0,1:T(8,128)(2,1)} %all-gather.4.cloned.1.call-done, bf16[1024,2048]{1,0:T(8,128)(2,1)} %copy-done.23, f32[2048]{0:T(1024)S(1)} %bitcast.403, f32[1024]{0:T(1024)S(1)} %add_rsqrt_fusion.2), kind=kOutput, calls=%fused_computation.35 | convolution fusion | flops 4303355904 | bytes 12595200 | tf_op jit(solution)/shard_map/dot_general | solution.py:221
  145.5 13.7 %collective-permute-done.4 = bf16[2,128,2048]{2,1,0:T(8,128)(2,1)S(1)} collective-permute-done((bf16[2,128,2048]{2,1,0:T(8,128)(2,1)S(1)}, bf16[2,128,2048]{2,1,0:T(8,128)(2,1)S(1)}, u32[]{:S(2)}, u32[]{:S(2)}) %collective-permute-start.4) | collective-permute-done | bytes 1048608 | tf_op jit(solution)/shard_map/ppermute | solution.py:115
  160.0 9.1 %collective-permute-done.6 = bf16[2,128,2048]{2,1,0:T(8,128)(2,1)S(1)} collective-permute-done((bf16[2,128,2048]{2,1,0:T(8,128)(2,1)S(1)}, bf16[2,128,2048]{2,1,0:T(8,128)(2,1)S(1)}, u32[]{:S(2)}, u32[]{:S(2)}) %collective-permute-start.6) | collective-permute-done | bytes 1048608 | tf_op jit(solution)/shard_map/ppermute | solution.py:116
  202.9 9.5 %collective-permute-done.9 = bf16[256,2048]{1,0:T(8,128)(2,1)S(1)} collective-permute-done((bf16[256,2048]{1,0:T(8,128)(2,1)S(1)}, bf16[256,2048]{1,0:T(8,128)(2,1)S(1)}, u32[]{:S(2)}, u32[]{:S(2)}) %collective-permute-start.9) | collective-permute-done | bytes 1048608 | tf_op jit(solution)/shard_map/ppermute | solution.py:102
  244.1 10.6 %convolution_convert_fusion.1 = bf16[2048,1536]{0,1:T(8,128)(2,1)S(1)} fusion(bf16[1024,2048]{1,0:T(8,128)(2,1)} %constant_dynamic-update-slice_fusion.13, bf16[1024,768]{0,1:T(8,128)(2,1)S(1)} %get-tuple-element.109, bf16[1024,768]{0,1:T(8,128)(2,1)S(1)} %get-tuple-element.107), kind=kOutput, calls=%fused_computation.28 | convolution fusion | flops 6451888128 | bytes 13631488 | tf_op jit(solution)/shard_map/dot_general | solution.py:60
  254.8 11.5 %pad_maximum_fusion = bf16[2048,2304]{0,1:T(8,128)(2,1)} fusion(bf16[2048,768]{0,1:T(8,128)(2,1)S(1)} %convolution_convert_fusion.4, bf16[2048,1536]{0,1:T(8,128)(2,1)S(1)} %convolution_convert_fusion.1), kind=kLoop, calls=%fused_computation.16 | loop fusion | flops 18874368 | bytes 18874368 | tf_op jit(solution)/shard_map/concatenate | solution.py:265
  276.6 7.9 %fusion.165 = f32[1024,768]{0,1:T(8,128)S(1)} fusion(bf16[1024,2048]{1,0:T(8,128)(2,1)} %constant_dynamic-update-slice_fusion.13, bf16[2048,768]{0,1:T(8,128)(2,1)} %get-tuple-element.25), kind=kOutput, calls=%fused_computation.381 | convolution fusion | flops 3221225472 | bytes 10485760 | tf_op jit(solution)/shard_map/dot_general | solution.py:252
  290.2 8.4 %multiply_convert_fusion = (bf16[1024,768]{0,1:T(8,128)(2,1)}, bf16[1024,768]{0,1:T(8,128)(2,1)S(1)}, bf16[1024,768]{0,1:T(8,128)(2,1)}) fusion(f32[1024,768]{0,1:T(8,128)S(1)} %fusion.165, f32[1024,768]{0,1:T(8,128)S(1)} %fusion.166, bf16[1024,2048]{1,0:T(8,128)(2,1)} %constant_dynamic-update-slice_fusion.19, bf16[2048,768]{0,1:T(8,128)(2,1)S(1)} %get-tuple-element.27), kind=kOutput, calls=%fused_computation.51 | convolution fusion | flops 3233808384 | bytes 18350080 | tf_op jit(solution)/shard_map/dot_general | solution.py:259
  315.7 12.7 %fusion.163 = (bf16[1024,2048]{1,0:T(8,128)(2,1)}, f32[1024,2048]{1,0:T(8,128)S(1)}) fusion(f32[1024,2048]{1,0:T(8,128)} %fusion.167, bf16[1024,768]{0,1:T(8,128)(2,1)} %get-tuple-element.104, bf16[2048,768]{0,1:T(8,128)(2,1)S(1)} %copy-done.13, f32[1024,2048]{1,0:T(8,128)} %fusion.33, f32[1024,2048]{1,0:T(8,128)} %fusion.29), kind=kOutput, calls=%fused_computation.379 | convolution fusion | flops 3229614080 | bytes 42467328 | tf_op jit(solution)/shard_map/dot_general | solution.py:66
  357.6 10.9 %convolution_convert_fusion = bf16[2048,1536]{0,1:T(8,128)(2,1)S(1)} fusion(bf16[1024,2048]{1,0:T(8,128)(2,1)} %constant_dynamic-update-slice_fusion.13, bf16[1024,768]{0,1:T(8,128)(2,1)S(1)} %copy-done.41, bf16[1024,768]{0,1:T(8,128)(2,1)S(1)} %copy-done.74), kind=kOutput, calls=%fused_computation.27 | convolution fusion | flops 6451888128 | bytes 13631488 | tf_op jit(solution)/shard_map/dot_general | solution.py:60
  370.2 11.3 %pad_maximum_fusion.1 = bf16[2048,2304]{0,1:T(8,128)(2,1)} fusion(bf16[2048,768]{0,1:T(8,128)(2,1)S(1)} %convolution_convert_fusion.3, bf16[2048,1536]{0,1:T(8,128)(2,1)S(1)} %convolution_convert_fusion), kind=kLoop, calls=%fused_computation.17 | loop fusion | flops 18874368 | bytes 18874368 | tf_op jit(solution)/shard_map/concatenate | solution.py:265
  415.3 11.1 %collective-permute-done.24 = bf16[128,2048]{1,0:T(8,128)(2,1)S(1)} collective-permute-done((bf16[128,2048]{1,0:T(8,128)(2,1)S(1)}, bf16[128,2048]{1,0:T(8,128)(2,1)S(1)}, u32[]{:S(2)}, u32[]{:S(2)}) %collective-permute-start.24) | collective-permute-done | bytes 524320 | tf_op jit(solution)/shard_map/ppermute | solution.py:98
  429.2 30.9 %collective-permute-done.26 = bf16[128,2048]{1,0:T(8,128)(2,1)S(1)} collective-permute-done((bf16[128,2048]{1,0:T(8,128)(2,1)S(1)}, bf16[128,2048]{1,0:T(8,128)(2,1)S(1)}, u32[]{:S(2)}, u32[]{:S(2)}) %collective-permute-start.26) | collective-permute-done | bytes 524320 | tf_op jit(solution)/shard_map/ppermute | solution.py:99
  460.9 21.0 %collective-permute-done.27 = bf16[256,2048]{1,0:T(8,128)(2,1)S(1)} collective-permute-done((bf16[256,2048]{1,0:T(8,128)(2,1)S(1)}, bf16[256,2048]{1,0:T(8,128)(2,1)S(1)}, u32[]{:S(2)}, u32[]{:S(2)}) %collective-permute-start.27) | collective-permute-done | bytes 1048608 | tf_op jit(solution)/shard_map/ppermute | solution.py:103
  488.5 14.1 %fusion = (f32[2,2,1024]{2,1,0:T(2,128)S(1)}, f32[2,1024,1024,2]{2,1,3,0:T(8,128)}) fusion(f32[2,2,1024,1024]{2,3,1,0:T(8,128)} %fusion.4, bf16[1024,2,128,1]{0,2,3,1:T(8,128)(2,1)S(1)} %bitcast.385, bf16[1024,2,2,128]{0,3,2,1:T(8,128)(2,1)} %bitcast.380), kind=kOutput, calls=%fused_computation.2 | convolution fusion | flops 1082126336 | bytes 35143680 | tf_op jit(solution)/shard_map/qgrd,kgd->grqk/dot_general | solution.py:290
  505.4 8.4 %fusion.2 = bf16[2,2,1024,1024]{2,3,1,0:T(8,128)(2,1)S(1)} fusion(f32[2,2,1024,1024]{2,3,1,0:T(8,128)S(1)} %bitcast.367, f32[2,1024,1024,2]{2,1,3,0:T(8,128)} %get-tuple-element.195, f32[2,2,1024]{2,1,0:T(2,128)S(1)} %get-tuple-element.194), kind=kLoop, calls=%fused_computation.4 | loop fusion | flops 12582912 | bytes 41959424 | tf_op jit(solution)/shard_map/convert_element_type | solution.py:292
  532.0 9.0 %fusion.64 = bf16[2,128,1024]{2,1,0:T(8,128)(2,1)S(1)} fusion(bf16[1024,2,2,128]{0,3,2,1:T(8,128)(2,1)} %bitcast.381, f32[2,2,1024,1024]{2,3,1,0:T(8,128)} %fusion.4), kind=kOutput, calls=%fused_computation.126 | convolution fusion | flops 1078198272 | bytes 18350080 | tf_op jit(solution)/shard_map/grqk,qgrd->kgd/dot_general | solution.py:295
  541.4 13.7 %fusion.11 = (f32[2048]{0:T(1024)S(1)}, bf16[1024,2048]{1,0:T(8,128)(2,1)}, f32[1024,2048]{1,0:T(8,128)}) fusion(bf16[1024,2048]{1,0:T(8,128)(2,1)} %copy-done.23, f32[1024]{0:T(1024)S(1)} %copy-done.69, bf16[2048,1664]{0,1:T(8,128)(2,1)} %all-gather.4.cloned.1.call-done, bf16[1024,256]{0,1:T(8,128)(2,1)S(1)} %bitcast.396, ...), kind=kOutput, calls=%fused_computation.22 | convolution fusion | flops 4311742464 | bytes 23080960 | tf_op jit(solution)/shard_map/dot_general | solution.py:66
  560.8 8.0 %convolution_convert_fusion.2 = bf16[2048,1024]{0,1:T(8,128)(2,1)} fusion(bf16[1024,2048]{1,0:T(8,128)(2,1)S(1)} %copy-done.24, f32[2048]{0:T(1024)S(1)} %bitcast.404, f32[1024]{0:T(1024)S(1)} %copy-done.69, bf16[1024,256]{0,1:T(8,128)(2,1)S(1)} %bitcast.397, bf16[1024,256]{0,1:T(8,128)(2,1)S(1)} %bitcast.399, bf16[1024,512]{0,1:T(8,128)(2,1)S(1)} %copy-done.43), kind=kOutput, calls=%fused_computation.32 | convolution fusion | flops 4311744512 | bytes 10498048 | tf_op jit(solution)/shard_map/dot_general | solution.py:60
  585.5 16.6 %collective-permute-done.28 = bf16[2,128,2048]{2,1,0:T(8,128)(2,1)S(1)} collective-permute-done((bf16[2,128,2048]{2,1,0:T(8,128)(2,1)S(1)}, bf16[2,128,2048]{2,1,0:T(8,128)(2,1)S(1)}, u32[]{:S(2)}, u32[]{:S(2)}) %collective-permute-start.28) | collective-permute-done | bytes 1048608 | tf_op jit(solution)/shard_map/ppermute | solution.py:115
  605.7 8.7 %collective-permute-done.29 = bf16[128,2048]{1,0:T(8,128)(2,1)S(1)} collective-permute-done((bf16[128,2048]{1,0:T(8,128)(2,1)S(1)}, bf16[128,2048]{1,0:T(8,128)(2,1)S(1)}, u32[]{:S(2)}, u32[]{:S(2)}) %collective-permute-start.29) | collective-permute-done | bytes 524320 | tf_op jit(solution)/shard_map/ppermute | solution.py:119
  (489 shorter events, 327.7 us)
Async XLA Ops:
  7.2 97.4 %all-gather.4.cloned.1.call-start = ((), (), s32[]{:S(2)}) async-start(), calls=%async_computation.4 | async-start | bytes 7667712 | tf_op jit(solution)/shard_map/all_gather | solution.py:136
  15.1 202.5 %all-gather.6.cloned.1.call-start = ((), (), s32[]{:S(2)}) async-start(), calls=%async_computation.5 | async-start | bytes 10616832 | tf_op jit(solution)/shard_map/all_gather | solution.py:136
  19.5 251.0 %all-gather.8.cloned.1.call-start = ((), (), s32[]{:S(2)}) async-start(), calls=%async_computation.6 | async-start | bytes 10616832 | tf_op jit(solution)/shard_map/all_gather | solution.py:136
  24.8 55.6 %collective-permute-start.14 = (bf16[128,2048]{1,0:T(8,128)(2,1)}, bf16[128,2048]{1,0:T(8,128)(2,1)}, u32[]{:S(2)}, u32[]{:S(2)}) collective-permute-start(bf16[128,2048]{1,0:T(8,128)(2,1)} %get-tuple-element.138), channel_id=1, source_target_pairs={{0,2},{2,0},{1,3},{3,1},{4,6},{6,4},{5,7},{7,5},{8,10},{10,8},{9,1... | collective-permute-start | bytes 1572872 | tf_op jit(solution)/shard_map/ppermute | solution.py:99
  26.3 50.8 %collective-permute-start.12 = (bf16[128,2048]{1,0:T(8,128)(2,1)}, bf16[128,2048]{1,0:T(8,128)(2,1)}, u32[]{:S(2)}, u32[]{:S(2)}) collective-permute-start(bf16[128,2048]{1,0:T(8,128)(2,1)} %get-tuple-element.140), channel_id=1, source_target_pairs={{0,1},{1,0},{2,3},{3,2},{4,5},{5,4},{6,7},{7,6},{8,9},{9,8},{10,11... | collective-permute-start | bytes 1572872 | tf_op jit(solution)/shard_map/ppermute | solution.py:98
  30.3 510.7 %reduce-scatter.5.cloned.1.call-start = ((), (), s32[]{:S(2)}) async-start(), calls=%async_computation.7 | async-start | bytes 10616832 | tf_op jit(solution)/shard_map/reduce_scatter | solution.py:268
  36.4 24.5 %collective-permute-start.1 = (bf16[256,2048]{1,0:T(8,128)(2,1)S(1)}, bf16[256,2048]{1,0:T(8,128)(2,1)S(1)}, u32[]{:S(2)}, u32[]{:S(2)}) collective-permute-start(bf16[256,2048]{1,0:T(8,128)(2,1)S(1)} %pad_maximum_fusion.10), channel_id=1, source_target_pairs={{0,2},{2,0},{1,3},{3,1},{4,6},{6,4},{5,7},{7,5},{8,10},{10,8},{9,1... | collective-permute-start | bytes 3145736 | tf_op jit(solution)/shard_map/ppermute | solution.py:102
  75.4 26.1 %collective-permute-start.3 = (bf16[256,2048]{1,0:T(8,128)(2,1)S(1)}, bf16[256,2048]{1,0:T(8,128)(2,1)S(1)}, u32[]{:S(2)}, u32[]{:S(2)}) collective-permute-start(bf16[256,2048]{1,0:T(8,128)(2,1)S(1)} %pad_maximum_fusion.11), channel_id=1, source_target_pairs={{0,1},{1,0},{2,3},{3,2},{4,5},{5,4},{6,7},{7,6},{8,9},{9,8},{10,11... | collective-permute-start | bytes 3145736 | tf_op jit(solution)/shard_map/ppermute | solution.py:103
  79.4 63.3 %collective-permute-start.13 = (bf16[256,2048]{1,0:T(8,128)(2,1)}, bf16[256,2048]{1,0:T(8,128)(2,1)}, u32[]{:S(2)}, u32[]{:S(2)}) collective-permute-start(bf16[256,2048]{1,0:T(8,128)(2,1)} %pad_maximum_fusion.14), channel_id=1, source_target_pairs={{0,2},{2,0},{1,3},{3,1},{4,6},{6,4},{5,7},{7,5},{8,10},{10,8},{9,1... | collective-permute-start | bytes 3145736 | tf_op jit(solution)/shard_map/ppermute | solution.py:102
  82.7 101.4 %collective-permute-start.15 = (bf16[256,2048]{1,0:T(8,128)(2,1)}, bf16[256,2048]{1,0:T(8,128)(2,1)}, u32[]{:S(2)}, u32[]{:S(2)}) collective-permute-start(bf16[256,2048]{1,0:T(8,128)(2,1)} %pad_maximum_fusion.15), channel_id=1, source_target_pairs={{0,1},{1,0},{2,3},{3,2},{4,5},{5,4},{6,7},{7,6},{8,9},{9,8},{10,11... | collective-permute-start | bytes 3145736 | tf_op jit(solution)/shard_map/ppermute | solution.py:103
  145.1 24.0 %collective-permute-start.6 = (bf16[2,128,2048]{2,1,0:T(8,128)(2,1)S(1)}, bf16[2,128,2048]{2,1,0:T(8,128)(2,1)S(1)}, u32[]{:S(2)}, u32[]{:S(2)}) collective-permute-start(bf16[2,128,2048]{2,1,0:T(8,128)(2,1)S(1)} %bitcast.390), channel_id=1, source_target_pairs={{0,1},{1,0},{2,3},{3,2},{4,5},{5,4},{6,7},{7,6},{8,9},{9,8},{10,11... | collective-permute-start | bytes 3145736 | tf_op jit(solution)/shard_map/ppermute | solution.py:116
  191.5 21.0 %collective-permute-start.9 = (bf16[256,2048]{1,0:T(8,128)(2,1)S(1)}, bf16[256,2048]{1,0:T(8,128)(2,1)S(1)}, u32[]{:S(2)}, u32[]{:S(2)}) collective-permute-start(bf16[256,2048]{1,0:T(8,128)(2,1)S(1)} %pad_maximum_fusion.12), channel_id=1, source_target_pairs={{0,2},{2,0},{1,3},{3,1},{4,6},{6,4},{5,7},{7,5},{8,10},{10,8},{9,1... | collective-permute-start | bytes 3145736 | tf_op jit(solution)/shard_map/ppermute | solution.py:102
  276.6 264.5 %reduce-scatter.7.cloned.1.call-start = ((), (), s32[]{:S(2)}) async-start(), calls=%async_computation.8 | async-start | bytes 10616832 | tf_op jit(solution)/shard_map/reduce_scatter | solution.py:281
  331.6 53.6 %collective-permute-start.22 = (bf16[2,128,2048]{2,1,0:T(8,128)(2,1)}, bf16[2,128,2048]{2,1,0:T(8,128)(2,1)}, u32[]{:S(2)}, u32[]{:S(2)}) collective-permute-start(bf16[2,128,2048]{2,1,0:T(8,128)(2,1)} %bitcast.63), channel_id=1, source_target_pairs={{0,1},{1,0},{2,3},{3,2},{4,5},{5,4},{6,7},{7,6},{8,9},{9,8},{10,11... | collective-permute-start | bytes 3145736 | tf_op jit(solution)/shard_map/ppermute | solution.py:116
  333.0 48.5 %collective-permute-start.20 = (bf16[2,128,2048]{2,1,0:T(8,128)(2,1)}, bf16[2,128,2048]{2,1,0:T(8,128)(2,1)}, u32[]{:S(2)}, u32[]{:S(2)}) collective-permute-start(bf16[2,128,2048]{2,1,0:T(8,128)(2,1)} %bitcast.59), channel_id=1, source_target_pairs={{0,2},{2,0},{1,3},{3,1},{4,6},{6,4},{5,7},{7,5},{8,10},{10,8},{9,1... | collective-permute-start | bytes 3145736 | tf_op jit(solution)/shard_map/ppermute | solution.py:115
  347.6 42.6 %collective-permute-start.18 = (bf16[2,128,2048]{2,1,0:T(8,128)(2,1)}, bf16[2,128,2048]{2,1,0:T(8,128)(2,1)S(1)}, u32[]{:S(2)}, u32[]{:S(2)}) collective-permute-start(bf16[2,128,2048]{2,1,0:T(8,128)(2,1)} %bitcast.55), channel_id=1, source_target_pairs={{0,1},{1,0},{2,3},{3,2},{4,5},{5,4},{6,7},{7,6},{8,9},{9,8},{10,11... | collective-permute-start | bytes 3145736 | tf_op jit(solution)/shard_map/ppermute | solution.py:116
  348.2 40.3 %collective-permute-start.16 = (bf16[2,128,2048]{2,1,0:T(8,128)(2,1)}, bf16[2,128,2048]{2,1,0:T(8,128)(2,1)}, u32[]{:S(2)}, u32[]{:S(2)}) collective-permute-start(bf16[2,128,2048]{2,1,0:T(8,128)(2,1)} %bitcast.51), channel_id=1, source_target_pairs={{0,2},{2,0},{1,3},{3,1},{4,6},{6,4},{5,7},{7,5},{8,10},{10,8},{9,1... | collective-permute-start | bytes 3145736 | tf_op jit(solution)/shard_map/ppermute | solution.py:115
  413.2 163.1 %reduce-scatter.9.cloned.1.call-start = ((), (), s32[]{:S(2)}) async-start(), calls=%async_computation.9 | async-start | bytes 2359296 | tf_op jit(solution)/shard_map/reduce_scatter | solution.py:286
  426.5 34.2 %collective-permute-start.25 = (bf16[256,2048]{1,0:T(8,128)(2,1)S(1)}, bf16[256,2048]{1,0:T(8,128)(2,1)S(1)}, u32[]{:S(2)}, u32[]{:S(2)}) collective-permute-start(bf16[256,2048]{1,0:T(8,128)(2,1)S(1)} %pad_maximum_fusion.16), channel_id=1, source_target_pairs={{0,2},{2,0},{1,3},{3,1},{4,6},{6,4},{5,7},{7,5},{8,10},{10,8},{9,1... | collective-permute-start | bytes 3145736 | tf_op jit(solution)/shard_map/ppermute | solution.py:102
  428.3 31.8 %collective-permute-start.26 = (bf16[128,2048]{1,0:T(8,128)(2,1)S(1)}, bf16[128,2048]{1,0:T(8,128)(2,1)S(1)}, u32[]{:S(2)}, u32[]{:S(2)}) collective-permute-start(bf16[128,2048]{1,0:T(8,128)(2,1)S(1)} %get-tuple-element.135), channel_id=1, source_target_pairs={{0,2},{2,0},{1,3},{3,1},{4,6},{6,4},{5,7},{7,5},{8,10},{10,8},{9,1... | collective-permute-start | bytes 1572872 | tf_op jit(solution)/shard_map/ppermute | solution.py:99
  460.2 21.6 %collective-permute-start.27 = (bf16[256,2048]{1,0:T(8,128)(2,1)S(1)}, bf16[256,2048]{1,0:T(8,128)(2,1)S(1)}, u32[]{:S(2)}, u32[]{:S(2)}) collective-permute-start(bf16[256,2048]{1,0:T(8,128)(2,1)S(1)} %pad_maximum_fusion.17), channel_id=1, source_target_pairs={{0,1},{1,0},{2,3},{3,2},{4,5},{5,4},{6,7},{7,6},{8,9},{9,8},{10,11... | collective-permute-start | bytes 3145736 | tf_op jit(solution)/shard_map/ppermute | solution.py:103
  541.1 91.0 %reduce-scatter.11.cloned.1.call-start = ((), (), s32[]{:S(2)}) async-start(), calls=%async_computation.10 | async-start | bytes 5308416 | tf_op jit(solution)/shard_map/reduce_scatter | solution.py:342
  579.9 22.2 %collective-permute-start.28 = (bf16[2,128,2048]{2,1,0:T(8,128)(2,1)S(1)}, bf16[2,128,2048]{2,1,0:T(8,128)(2,1)S(1)}, u32[]{:S(2)}, u32[]{:S(2)}) collective-permute-start(bf16[2,128,2048]{2,1,0:T(8,128)(2,1)S(1)} %bitcast.393), channel_id=1, source_target_pairs={{0,2},{2,0},{1,3},{3,1},{4,6},{6,4},{5,7},{7,5},{8,10},{10,8},{9,1... | collective-permute-start | bytes 3145736 | tf_op jit(solution)/shard_map/ppermute | solution.py:115
  581.2 23.9 %collective-permute-start.30 = (bf16[2,128,2048]{2,1,0:T(8,128)(2,1)S(1)}, bf16[2,128,2048]{2,1,0:T(8,128)(2,1)S(1)}, u32[]{:S(2)}, u32[]{:S(2)}) collective-permute-start(bf16[2,128,2048]{2,1,0:T(8,128)(2,1)S(1)} %bitcast.392), channel_id=1, source_target_pairs={{0,1},{1,0},{2,3},{3,2},{4,5},{5,4},{6,7},{7,6},{8,9},{9,8},{10,11... | collective-permute-start | bytes 3145736 | tf_op jit(solution)/shard_map/ppermute | solution.py:116
  (108 other events, 985.8 us)
Sparse Core Ops, SparseCore 0:
  15.2 72.1 all-gather.3
  89.6 89.3 all-gather.5
  181.2 89.3 all-gather.7
  276.7 97.6 reduce-scatter.4
  413.4 97.6 reduce-scatter.6
  541.2 35.0 reduce-scatter.8
  578.7 53.3 reduce-scatter.10

commit v6 on v5

--- a/solution.py
+++ b/solution.py
@@ -2,6 +2,7 @@
 import jax.numpy as jnp
 from jax import lax
 from jax.sharding import PartitionSpec as P
+
 
 H = 16
 KV = 8
@@ -137,13 +138,11 @@
     return split_cols(joined, [blk.shape[1] for blk in blocks])
 
 
-def wide_scatter(blocks):
-    joined = jnp.concatenate([blk.astype(jnp.bfloat16) for blk in blocks], axis=1)
-    summed = lax.psum_scatter(joined, "wide", scatter_dimension=0, tiled=True).astype(jnp.float32)
-    return split_cols(summed, [blk.shape[1] for blk in blocks])
-
-
-def shards(
+def qkv_scatter(grad):
+    return lax.psum_scatter(grad, "wide", scatter_dimension=0, tiled=True)
+
+
+def shards_body(
     tokens,
     doc_ids,
     cotangent,
@@ -166,7 +165,6 @@
     repeat = H // KV
     seq_count, length = doc_ids.shape
     rows_group = seq_count * length
-    shard_rows = tokens.shape[0]
     scale = HD ** (-0.5)
     d_local = attn_gain.shape[0]
     hd_local = query_gain.shape[0]
@@ -248,26 +246,26 @@
     d_mlp_partial = None
     mlp_grads = []
     for h in range(2):
-        gate_w, up_w, down_wt = mlp_sets[h]
-        gate = jnp.dot(mlp_all, gate_w, preferred_element_type=jnp.float32)
-        up = jnp.dot(mlp_all, up_w, preferred_element_type=jnp.float32)
-        sigmoid = jax.nn.sigmoid(gate)
-        hidden = (gate * sigmoid * up).astype(jnp.bfloat16)
-        part = times_transposed(hidden, down_wt)
-        down_partial = part if down_partial is None else down_partial + part
-        g_down_t = contract_rows(grad_rows, hidden)
-        d_hidden = jnp.dot(grad_rows, down_wt, preferred_element_type=jnp.float32)
-        d_up = (d_hidden * gate * sigmoid).astype(jnp.bfloat16)
-        d_gate = (d_hidden * up * sigmoid * (1.0 + gate * (1.0 - sigmoid))).astype(jnp.bfloat16)
-        g_gate_up = contract_rows(mlp_all, jnp.concatenate([d_gate, d_up], axis=1))
-        part = times_transposed(d_gate, gate_w) + times_transposed(d_up, up_w)
-        d_mlp_partial = part if d_mlp_partial is None else d_mlp_partial + part
-        joined = jnp.concatenate([g_gate_up.astype(jnp.bfloat16), g_down_t.astype(jnp.bfloat16)], axis=1)
-        if h == 0:
-            joined, mlp_sets[1] = lax.optimization_barrier((joined, mlp_sets[1]))
-            mlp_grads.append(lax.psum_scatter(joined, "wide", scatter_dimension=0, tiled=True))
-        else:
-            last_joined = joined
+      gate_w, up_w, down_wt = mlp_sets[h]
+      gate = jnp.dot(mlp_all, gate_w, preferred_element_type=jnp.float32)
+      up = jnp.dot(mlp_all, up_w, preferred_element_type=jnp.float32)
+      sigmoid = jax.nn.sigmoid(gate)
+      hidden = (gate * sigmoid * up).astype(jnp.bfloat16)
+      part = times_transposed(hidden, down_wt)
+      down_partial = part if down_partial is None else down_partial + part
+      g_down_t = contract_rows(grad_rows, hidden)
+      d_hidden = jnp.dot(grad_rows, down_wt, preferred_element_type=jnp.float32)
+      d_up = (d_hidden * gate * sigmoid).astype(jnp.bfloat16)
+      d_gate = (d_hidden * up * sigmoid * (1.0 + gate * (1.0 - sigmoid))).astype(jnp.bfloat16)
+      g_gate_up = contract_rows(mlp_all, jnp.concatenate([d_gate, d_up], axis=1))
+      part = times_transposed(d_gate, gate_w) + times_transposed(d_up, up_w)
+      d_mlp_partial = part if d_mlp_partial is None else d_mlp_partial + part
+      joined = jnp.concatenate([g_gate_up.astype(jnp.bfloat16), g_down_t.astype(jnp.bfloat16)], axis=1)
+      if h == 0:
+          joined, mlp_sets[1] = lax.optimization_barrier((joined, mlp_sets[1]))
+          mlp_grads.append(lax.psum_scatter(joined, "wide", scatter_dimension=0, tiled=True))
+      else:
+          last_joined = joined
 
     d_mlp_in = narrow_scatter(d_mlp_partial, relative)
     d_part, mlp_gain_terms = rms_back(resid, gain_mlp, d_mlp_in)
@@ -281,9 +279,7 @@
     mlp_grads.append(lax.psum_scatter(last_joined, "wide", scatter_dimension=0, tiled=True))
     branch_rows = narrow_gather(d_resid_low, relative)
     out_grad = contract_rows(branch_rows, attended).astype(jnp.bfloat16)
-    mlp_grads, out_grad = lax.optimization_barrier((mlp_grads, out_grad))
-    mlp_grads = [split_cols(g.astype(jnp.float32), [2 * ff_half, ff_half]) for g in mlp_grads]
-    g_out_t = lax.psum_scatter(out_grad, "wide", scatter_dimension=0, tiled=True).astype(jnp.float32)
+    g_out_t = lax.psum_scatter(out_grad, "wide", scatter_dimension=0, tiled=True)
     d_attended = jnp.dot(branch_rows, out_wt, preferred_element_type=jnp.float32).astype(jnp.bfloat16)
     d_mixed = d_attended.reshape(rows_group, groups_here, repeat, HD)
 
@@ -337,13 +333,14 @@
     qkv_grad = jnp.concatenate(
         [contract_rows(normed_all, d_qkv).astype(jnp.bfloat16), gain_block.astype(jnp.bfloat16)], axis=1
     )
-    g_out_t, qkv_grad = lax.optimization_barrier((g_out_t, qkv_grad))
+    g_out_t = g_out_t.astype(jnp.float32)
+    mlp_grads = [split_cols(g.astype(jnp.float32), [2 * ff_half, ff_half]) for g in mlp_grads]
     g_qkv, g_gains = split_cols(
-        lax.psum_scatter(qkv_grad, "wide", scatter_dimension=0, tiled=True).astype(jnp.float32),
+        qkv_scatter(qkv_grad).astype(jnp.float32),
         [q_cols + 2 * kv_cols, 128],
     )
     d_normed = narrow_scatter(d_normed_partial, relative)
-    d_input_part, unused_terms = rms_back(inputs, gain_attn, d_normed)
+    d_input_part, _ = rms_back(inputs, gain_attn, d_normed)
     d_tokens = d_resid + d_input_part
     attn_gain_grad = g_gains[:, 0]
     mlp_gain_grad = g_gains[:, 1]
@@ -406,4 +403,4 @@
         P("wide", "narrow"),
         P("narrow", "wide"),
     )
-    return jax.shard_map(shards, mesh=mesh, in_specs=in_specs, out_specs=out_specs, check_vma=False)
+    return jax.shard_map(shards_body, mesh=mesh, in_specs=in_specs, out_specs=out_specs, check_vma=False)

time: 650 us -> 862 us (1.33)
  waiting for transfers between devices: 218 us -> 434 us
    reduce_scatter x4, waiting for transfers between devices: 7.2 us -> 204 us  [the longest x1 97.9 us: shards_body(): lax.psum_scatter(last_joined, 'wide', scatter_dimension=0, tiled=True)]
    ppermute x4, waiting for transfers between devices: 30.3 us -> 51.6 us  [narrow_scatter(): a_got = lax.ppermute(blocks[2:4].astype(jnp.bfloat16), 'narrow', YPERM)]
    unnamed x233 -> x213, local copies, waits for them, and re-layouts: 41 us -> 38.6 us
  transfers between devices with their start and end apart: 41 -> 41, of which waited for: 25 -> 29; matrix products, arithmetic and copies ran while one was open for 52% -> 25% of each run, Pallas kernels for 0% -> 0%
where the time goes in v6:
time: 862 us; the launch traced here: 857 us
  waiting for transfers between devices  434 us (50%)
  matrix products  190 us (22%)
  other arithmetic  90.9 us (11%)
  local copies, waits for them, and re-layouts  83.9 us (10%)
  starting transfers between devices  40.8 us (5%)
  between operations  16.5 us (2%)
    reduce_scatter x1, waiting for transfers between devices, shards_body(): lax.psum_scatter(last_joined, 'wide', scatter_dimension=0, tiled=True)  97.9 us
    reduce_scatter x1, waiting for transfers between devices, shards_body(): lax.psum_scatter(joined, 'wide', scatter_dimension=0, tiled=True)  94.1 us
    dot_general x8, matrix products, times_transposed(): lax.dot_general(left, right, (((1,), (1,)), ((), ())), preferred_element_...  56.7 us
    ppermute x4, waiting for transfers between devices, narrow_scatter(): a_got = lax.ppermute(blocks[2:4].astype(jnp.bfloat16), 'narrow', YPERM)  51.6 us
    dot_general x6, matrix products, contract_rows(): lax.dot_general(left, right, (((0,), (0,)), ((), ())), preferred_element_...  50.7 us
    ppermute x4, waiting for transfers between devices, narrow_gather(): b_y = lax.ppermute(b, 'narrow', YPERM)  39.9 us
    ppermute x4, waiting for transfers between devices, narrow_gather(): b_pair_x = lax.ppermute(b_pair, 'narrow', XPERM)  39.6 us
    unnamed x213, local copies, waits for them, and re-layouts  38.6 us
  transfers between devices with their start and end apart: 41, of which 29 were waited for; matrix products, arithmetic and copies ran while one was open for 25% of the time, Pallas kernels for 0%

profile of v6, /device:TPU:0, one launch (start us, length us, event | category | flops | bytes accessed | tf_op | source)
XLA Modules:
  0.0 856.5 jit_solution(17875934480851913663)
XLA Ops:
  39.4 21.4 %collective-permute-done.1 = bf16[256,2048]{1,0:T(8,128)(2,1)S(1)} collective-permute-done((bf16[256,2048]{1,0:T(8,128)(2,1)S(1)}, bf16[256,2048]{1,0:T(8,128)(2,1)S(1)}, u32[]{:S(2)}, u32[]{:S(2)}) %collective-permute-start.1) | collective-permute-done | bytes 1048608 | tf_op jit(solution)/shard_map/ppermute | solution.py:103
  84.5 16.9 %collective-permute-done.3 = bf16[256,2048]{1,0:T(8,128)(2,1)S(1)} collective-permute-done((bf16[256,2048]{1,0:T(8,128)(2,1)S(1)}, bf16[256,2048]{1,0:T(8,128)(2,1)S(1)}, u32[]{:S(2)}, u32[]{:S(2)}) %collective-permute-start.3) | collective-permute-done | bytes 1048608 | tf_op jit(solution)/shard_map/ppermute | solution.py:104
  145.7 13.7 %collective-permute-done.4 = bf16[2,128,2048]{2,1,0:T(8,128)(2,1)S(1)} collective-permute-done((bf16[2,128,2048]{2,1,0:T(8,128)(2,1)S(1)}, bf16[2,128,2048]{2,1,0:T(8,128)(2,1)S(1)}, u32[]{:S(2)}, u32[]{:S(2)}) %collective-permute-start.4) | collective-permute-done | bytes 1048608 | tf_op jit(solution)/shard_map/ppermute | solution.py:116
  160.2 9.1 %collective-permute-done.6 = bf16[2,128,2048]{2,1,0:T(8,128)(2,1)S(1)} collective-permute-done((bf16[2,128,2048]{2,1,0:T(8,128)(2,1)S(1)}, bf16[2,128,2048]{2,1,0:T(8,128)(2,1)S(1)}, u32[]{:S(2)}, u32[]{:S(2)}) %collective-permute-start.6) | collective-permute-done | bytes 1048608 | tf_op jit(solution)/shard_map/ppermute | solution.py:117
  203.1 9.6 %collective-permute-done.9 = bf16[256,2048]{1,0:T(8,128)(2,1)S(1)} collective-permute-done((bf16[256,2048]{1,0:T(8,128)(2,1)S(1)}, bf16[256,2048]{1,0:T(8,128)(2,1)S(1)}, u32[]{:S(2)}, u32[]{:S(2)}) %collective-permute-start.9) | collective-permute-done | bytes 1048608 | tf_op jit(solution)/shard_map/ppermute | solution.py:103
  244.3 10.6 %convolution_convert_fusion.1 = bf16[2048,1536]{0,1:T(8,128)(2,1)S(1)} fusion(bf16[1024,2048]{1,0:T(8,128)(2,1)} %constant_dynamic-update-slice_fusion.13, bf16[1024,768]{0,1:T(8,128)(2,1)S(1)} %get-tuple-element.99, bf16[1024,768]{0,1:T(8,128)(2,1)S(1)} %get-tuple-element.97), kind=kOutput, calls=%fused_computation.28 | convolution fusion | flops 6451888128 | bytes 13631488 | tf_op jit(solution)/shard_map/dot_general | solution.py:61
  254.9 11.5 %pad_maximum_fusion = bf16[2048,2304]{0,1:T(8,128)(2,1)} fusion(bf16[2048,768]{0,1:T(8,128)(2,1)S(1)} %convolution_convert_fusion.4, bf16[2048,1536]{0,1:T(8,128)(2,1)S(1)} %convolution_convert_fusion.1), kind=kLoop, calls=%fused_computation.16 | loop fusion | flops 18874368 | bytes 18874368 | tf_op jit(solution)/shard_map/concatenate | solution.py:263
  292.7 8.1 convolution_convert_fusion.3
  306.6 12.6 %convolution_convert_fusion = bf16[2048,1536]{0,1:T(8,128)(2,1)} fusion(bf16[1024,2048]{1,0:T(8,128)(2,1)} %constant_dynamic-update-slice_fusion.13, bf16[1024,768]{0,1:T(8,128)(2,1)S(1)} %get-tuple-element.94, bf16[1024,768]{0,1:T(8,128)(2,1)S(1)} %get-tuple-element.95), kind=kOutput, calls=%fused_computation.27 | convolution fusion | flops 6451888128 | bytes 13631488 | tf_op jit(solution)/shard_map/dot_general | solution.py:61
  345.8 13.7 %fusion.163 = (bf16[1024,2048]{1,0:T(8,128)(2,1)}, f32[1024,2048]{1,0:T(8,128)}) fusion(f32[1024,2048]{1,0:T(8,128)} %fusion.167, bf16[1024,768]{0,1:T(8,128)(2,1)} %copy-done.35, bf16[2048,768]{0,1:T(8,128)(2,1)S(1)} %get-tuple-element.21, f32[1024,2048]{1,0:T(8,128)} %fusion.33, f32[1024,2048]{1,0:T(8,128)} %fusion.29), kind=kOutput, calls=%fused_computation.380 | convolution fusion | flops 3229614080 | bytes 42467328 | tf_op jit(solution)/shard_map/dot_general | solution.py:67
  374.7 11.2 %pad_maximum_fusion.1 = bf16[2048,2304]{0,1:T(8,128)(2,1)} fusion(bf16[2048,768]{0,1:T(8,128)(2,1)S(1)} %copy-done.23, bf16[2048,1536]{0,1:T(8,128)(2,1)S(1)} %bitcast.380), kind=kLoop, calls=%fused_computation.17 | loop fusion | flops 18874368 | bytes 18874368 | tf_op jit(solution)/shard_map/concatenate | solution.py:263
  396.7 16.1 %collective-permute-done.16 = bf16[2,128,2048]{2,1,0:T(8,128)(2,1)} collective-permute-done((bf16[2,128,2048]{2,1,0:T(8,128)(2,1)}, bf16[2,128,2048]{2,1,0:T(8,128)(2,1)}, u32[]{:S(2)}, u32[]{:S(2)}) %collective-permute-start.16) | collective-permute-done | bytes 1048608 | tf_op jit(solution)/shard_map/ppermute | solution.py:116
  424.8 8.3 collective-permute-done.17
  437.0 12.4 %collective-permute-done.24 = bf16[128,2048]{1,0:T(8,128)(2,1)S(1)} collective-permute-done((bf16[128,2048]{1,0:T(8,128)(2,1)S(1)}, bf16[128,2048]{1,0:T(8,128)(2,1)S(1)}, u32[]{:S(2)}, u32[]{:S(2)}) %collective-permute-start.24) | collective-permute-done | bytes 524320 | tf_op jit(solution)/shard_map/ppermute | solution.py:99
  452.1 31.9 %collective-permute-done.26 = bf16[128,2048]{1,0:T(8,128)(2,1)S(1)} collective-permute-done((bf16[128,2048]{1,0:T(8,128)(2,1)S(1)}, bf16[128,2048]{1,0:T(8,128)(2,1)S(1)}, u32[]{:S(2)}, u32[]{:S(2)}) %collective-permute-start.26) | collective-permute-done | bytes 524320 | tf_op jit(solution)/shard_map/ppermute | solution.py:100
  485.2 21.4 %collective-permute-done.27 = bf16[256,2048]{1,0:T(8,128)(2,1)S(1)} collective-permute-done((bf16[256,2048]{1,0:T(8,128)(2,1)S(1)}, bf16[256,2048]{1,0:T(8,128)(2,1)S(1)}, u32[]{:S(2)}, u32[]{:S(2)}) %collective-permute-start.27) | collective-permute-done | bytes 1048608 | tf_op jit(solution)/shard_map/ppermute | solution.py:104
  518.9 9.9 %fusion.64 = bf16[2,128,1024]{2,1,0:T(8,128)(2,1)} fusion(bf16[1024,2,2,128]{0,3,2,1:T(8,128)(2,1)} %bitcast.381, f32[2,2,1024,1024]{2,3,1,0:T(8,128)} %fusion.4), kind=kOutput, calls=%fused_computation.126 | convolution fusion | flops 1078198272 | bytes 18350080 | tf_op jit(solution)/shard_map/grqk,qgrd->kgd/dot_general | solution.py:291
  528.8 8.6 %fusion = (f32[2,2,1024]{2,1,0:T(2,128)S(1)}, f32[2,1024,1024,2]{2,1,3,0:T(8,128)}) fusion(f32[2,2,1024,1024]{2,3,1,0:T(8,128)S(1)} %bitcast.368, bf16[1024,2,128,1]{0,2,3,1:T(8,128)(2,1)S(1)} %bitcast.386, bf16[1024,2,2,128]{0,3,2,1:T(8,128)(2,1)} %bitcast.382), kind=kOutput, calls=%fused_computation.2 | convolution fusion | flops 1082126336 | bytes 35143680 | tf_op jit(solution)/shard_map/qgrd,kgd->grqk/dot_general | solution.py:286
  537.5 12.3 %fusion.2 = bf16[2,2,1024,1024]{2,3,1,0:T(8,128)(2,1)S(1)} fusion(f32[2,2,1024,1024]{2,3,1,0:T(8,128)} %fusion.4, f32[2,1024,1024,2]{2,1,3,0:T(8,128)} %get-tuple-element.185, f32[2,2,1024]{2,1,0:T(2,128)S(1)} %get-tuple-element.184), kind=kLoop, calls=%fused_computation.4 | loop fusion | flops 12582912 | bytes 41959424 | tf_op jit(solution)/shard_map/convert_element_type | solution.py:288
  560.2 8.3 fusion.11
  594.6 17.4 %collective-permute-done.28 = bf16[2,128,2048]{2,1,0:T(8,128)(2,1)S(1)} collective-permute-done((bf16[2,128,2048]{2,1,0:T(8,128)(2,1)S(1)}, bf16[2,128,2048]{2,1,0:T(8,128)(2,1)S(1)}, u32[]{:S(2)}, u32[]{:S(2)}) %collective-permute-start.28) | collective-permute-done | bytes 1048608 | tf_op jit(solution)/shard_map/ppermute | solution.py:116
  628.5 12.0 %reduce-scatter.5.cloned.1.call-done = bf16[256,1152]{0,1:T(8,128)(2,1)} async-done(((bf16[2048,1152]{0,1:T(8,128)(2,1)}), bf16[256,1152]{0,1:T(8,128)(2,1)}) %reduce-scatter.5.cloned.1.call-update) | async-done | bytes 589840 | tf_op jit(solution)/shard_map/reduce_scatter | solution.py:142
  646.5 94.1 %reduce-scatter.9.cloned.1.call-done = bf16[256,2304]{0,1:T(8,128)(2,1)} async-done(((bf16[2048,2304]{0,1:T(8,128)(2,1)}), bf16[256,2304]{0,1:T(8,128)(2,1)}) %reduce-scatter.9.cloned.1.call-update) | async-done | bytes 1179664 | tf_op jit(solution)/shard_map/reduce_scatter | solution.py:266
  742.9 97.9 %reduce-scatter.11.cloned.1.call-done = bf16[256,2304]{0,1:T(8,128)(2,1)} async-done(((bf16[2048,2304]{0,1:T(8,128)(2,1)}), bf16[256,2304]{0,1:T(8,128)(2,1)}) %reduce-scatter.11.cloned.1.call-update) | async-done | bytes 1179664 | tf_op jit(solution)/shard_map/reduce_scatter | solution.py:279
  (469 shorter events, 351.1 us)
Async XLA Ops:
  7.2 97.4 %all-gather.4.cloned.1.call-start = ((), (), s32[]{:S(2)}) async-start(), calls=%async_computation.4 | async-start | bytes 7667712 | tf_op jit(solution)/shard_map/all_gather | solution.py:137
  15.1 202.7 %all-gather.6.cloned.1.call-start = ((), (), s32[]{:S(2)}) async-start(), calls=%async_computation.5 | async-start | bytes 10616832 | tf_op jit(solution)/shard_map/all_gather | solution.py:137
  19.5 251.0 %all-gather.8.cloned.1.call-start = ((), (), s32[]{:S(2)}) async-start(), calls=%async_computation.6 | async-start | bytes 10616832 | tf_op jit(solution)/shard_map/all_gather | solution.py:137
  24.8 55.3 %collective-permute-start.14 = (bf16[128,2048]{1,0:T(8,128)(2,1)}, bf16[128,2048]{1,0:T(8,128)(2,1)}, u32[]{:S(2)}, u32[]{:S(2)}) collective-permute-start(bf16[128,2048]{1,0:T(8,128)(2,1)} %get-tuple-element.128), channel_id=1, source_target_pairs={{0,2},{2,0},{1,3},{3,1},{4,6},{6,4},{5,7},{7,5},{8,10},{10,8},{9,1... | collective-permute-start | bytes 1572872 | tf_op jit(solution)/shard_map/ppermute | solution.py:100
  26.3 50.5 %collective-permute-start.12 = (bf16[128,2048]{1,0:T(8,128)(2,1)}, bf16[128,2048]{1,0:T(8,128)(2,1)}, u32[]{:S(2)}, u32[]{:S(2)}) collective-permute-start(bf16[128,2048]{1,0:T(8,128)(2,1)} %get-tuple-element.130), channel_id=1, source_target_pairs={{0,1},{1,0},{2,3},{3,2},{4,5},{5,4},{6,7},{7,6},{8,9},{9,8},{10,11... | collective-permute-start | bytes 1572872 | tf_op jit(solution)/shard_map/ppermute | solution.py:99
  30.3 596.2 %reduce-scatter.7.cloned.1.call-start = ((), (), s32[]{:S(2)}) async-start(), calls=%async_computation.8 | async-start | bytes 2359296 | tf_op jit(solution)/shard_map/reduce_scatter | solution.py:282
  36.4 24.5 %collective-permute-start.1 = (bf16[256,2048]{1,0:T(8,128)(2,1)S(1)}, bf16[256,2048]{1,0:T(8,128)(2,1)S(1)}, u32[]{:S(2)}, u32[]{:S(2)}) collective-permute-start(bf16[256,2048]{1,0:T(8,128)(2,1)S(1)} %pad_maximum_fusion.10), channel_id=1, source_target_pairs={{0,2},{2,0},{1,3},{3,1},{4,6},{6,4},{5,7},{7,5},{8,10},{10,8},{9,1... | collective-permute-start | bytes 3145736 | tf_op jit(solution)/shard_map/ppermute | solution.py:103
  75.3 26.1 %collective-permute-start.3 = (bf16[256,2048]{1,0:T(8,128)(2,1)S(1)}, bf16[256,2048]{1,0:T(8,128)(2,1)S(1)}, u32[]{:S(2)}, u32[]{:S(2)}) collective-permute-start(bf16[256,2048]{1,0:T(8,128)(2,1)S(1)} %pad_maximum_fusion.11), channel_id=1, source_target_pairs={{0,1},{1,0},{2,3},{3,2},{4,5},{5,4},{6,7},{7,6},{8,9},{9,8},{10,11... | collective-permute-start | bytes 3145736 | tf_op jit(solution)/shard_map/ppermute | solution.py:104
  79.1 63.8 %collective-permute-start.13 = (bf16[256,2048]{1,0:T(8,128)(2,1)}, bf16[256,2048]{1,0:T(8,128)(2,1)}, u32[]{:S(2)}, u32[]{:S(2)}) collective-permute-start(bf16[256,2048]{1,0:T(8,128)(2,1)} %pad_maximum_fusion.14), channel_id=1, source_target_pairs={{0,2},{2,0},{1,3},{3,1},{4,6},{6,4},{5,7},{7,5},{8,10},{10,8},{9,1... | collective-permute-start | bytes 3145736 | tf_op jit(solution)/shard_map/ppermute | solution.py:103
  82.4 101.9 %collective-permute-start.15 = (bf16[256,2048]{1,0:T(8,128)(2,1)}, bf16[256,2048]{1,0:T(8,128)(2,1)}, u32[]{:S(2)}, u32[]{:S(2)}) collective-permute-start(bf16[256,2048]{1,0:T(8,128)(2,1)} %pad_maximum_fusion.15), channel_id=1, source_target_pairs={{0,1},{1,0},{2,3},{3,2},{4,5},{5,4},{6,7},{7,6},{8,9},{9,8},{10,11... | collective-permute-start | bytes 3145736 | tf_op jit(solution)/shard_map/ppermute | solution.py:104
  145.3 24.0 %collective-permute-start.6 = (bf16[2,128,2048]{2,1,0:T(8,128)(2,1)S(1)}, bf16[2,128,2048]{2,1,0:T(8,128)(2,1)S(1)}, u32[]{:S(2)}, u32[]{:S(2)}) collective-permute-start(bf16[2,128,2048]{2,1,0:T(8,128)(2,1)S(1)} %bitcast.392), channel_id=1, source_target_pairs={{0,1},{1,0},{2,3},{3,2},{4,5},{5,4},{6,7},{7,6},{8,9},{9,8},{10,11... | collective-permute-start | bytes 3145736 | tf_op jit(solution)/shard_map/ppermute | solution.py:117
  362.6 30.8 %collective-permute-start.22 = (bf16[2,128,2048]{2,1,0:T(8,128)(2,1)}, bf16[2,128,2048]{2,1,0:T(8,128)(2,1)}, u32[]{:S(2)}, u32[]{:S(2)}) collective-permute-start(bf16[2,128,2048]{2,1,0:T(8,128)(2,1)} %bitcast.63), channel_id=1, source_target_pairs={{0,1},{1,0},{2,3},{3,2},{4,5},{5,4},{6,7},{7,6},{8,9},{9,8},{10,11... | collective-permute-start | bytes 3145736 | tf_op jit(solution)/shard_map/ppermute | solution.py:117
  364.0 26.3 %collective-permute-start.20 = (bf16[2,128,2048]{2,1,0:T(8,128)(2,1)}, bf16[2,128,2048]{2,1,0:T(8,128)(2,1)}, u32[]{:S(2)}, u32[]{:S(2)}) collective-permute-start(bf16[2,128,2048]{2,1,0:T(8,128)(2,1)} %bitcast.59), channel_id=1, source_target_pairs={{0,2},{2,0},{1,3},{3,1},{4,6},{6,4},{5,7},{7,5},{8,10},{10,8},{9,1... | collective-permute-start | bytes 3145736 | tf_op jit(solution)/shard_map/ppermute | solution.py:116
  365.5 49.0 %collective-permute-start.18 = (bf16[2,128,2048]{2,1,0:T(8,128)(2,1)}, bf16[2,128,2048]{2,1,0:T(8,128)(2,1)S(1)}, u32[]{:S(2)}, u32[]{:S(2)}) collective-permute-start(bf16[2,128,2048]{2,1,0:T(8,128)(2,1)} %bitcast.55), channel_id=1, source_target_pairs={{0,1},{1,0},{2,3},{3,2},{4,5},{5,4},{6,7},{7,6},{8,9},{9,8},{10,11... | collective-permute-start | bytes 3145736 | tf_op jit(solution)/shard_map/ppermute | solution.py:117
  366.1 46.8 %collective-permute-start.16 = (bf16[2,128,2048]{2,1,0:T(8,128)(2,1)}, bf16[2,128,2048]{2,1,0:T(8,128)(2,1)}, u32[]{:S(2)}, u32[]{:S(2)}) collective-permute-start(bf16[2,128,2048]{2,1,0:T(8,128)(2,1)} %bitcast.51), channel_id=1, source_target_pairs={{0,2},{2,0},{1,3},{3,1},{4,6},{6,4},{5,7},{7,5},{8,10},{10,8},{9,1... | collective-permute-start | bytes 3145736 | tf_op jit(solution)/shard_map/ppermute | solution.py:116
  392.7 29.8 %collective-permute-start.21 = (bf16[128,2048]{1,0:T(8,128)(2,1)S(1)}, bf16[128,2048]{1,0:T(8,128)(2,1)S(1)}, u32[]{:S(2)}, u32[]{:S(2)}) collective-permute-start(bf16[128,2048]{1,0:T(8,128)(2,1)S(1)} %fusion.88), channel_id=1, source_target_pairs={{0,1},{1,0},{2,3},{3,2},{4,5},{5,4},{6,7},{7,6},{8,9},{9,8},{10,11... | collective-permute-start | bytes 1572872 | tf_op jit(solution)/shard_map/ppermute | solution.py:120
  395.2 28.8 %collective-permute-start.23 = (bf16[128,2048]{1,0:T(8,128)(2,1)S(1)}, bf16[128,2048]{1,0:T(8,128)(2,1)S(1)}, u32[]{:S(2)}, u32[]{:S(2)}) collective-permute-start(bf16[128,2048]{1,0:T(8,128)(2,1)S(1)} %fusion.89), channel_id=1, source_target_pairs={{0,2},{2,0},{1,3},{3,1},{4,6},{6,4},{5,7},{7,5},{8,10},{10,8},{9,1... | collective-permute-start | bytes 1572872 | tf_op jit(solution)/shard_map/ppermute | solution.py:121
  449.4 35.7 %collective-permute-start.25 = (bf16[256,2048]{1,0:T(8,128)(2,1)S(1)}, bf16[256,2048]{1,0:T(8,128)(2,1)S(1)}, u32[]{:S(2)}, u32[]{:S(2)}) collective-permute-start(bf16[256,2048]{1,0:T(8,128)(2,1)S(1)} %pad_maximum_fusion.16), channel_id=1, source_target_pairs={{0,2},{2,0},{1,3},{3,1},{4,6},{6,4},{5,7},{7,5},{8,10},{10,8},{9,1... | collective-permute-start | bytes 3145736 | tf_op jit(solution)/shard_map/ppermute | solution.py:103
  450.9 33.1 %collective-permute-start.26 = (bf16[128,2048]{1,0:T(8,128)(2,1)S(1)}, bf16[128,2048]{1,0:T(8,128)(2,1)S(1)}, u32[]{:S(2)}, u32[]{:S(2)}) collective-permute-start(bf16[128,2048]{1,0:T(8,128)(2,1)S(1)} %get-tuple-element.125), channel_id=1, source_target_pairs={{0,2},{2,0},{1,3},{3,1},{4,6},{6,4},{5,7},{7,5},{8,10},{10,8},{9,1... | collective-permute-start | bytes 1572872 | tf_op jit(solution)/shard_map/ppermute | solution.py:100
  484.1 22.5 %collective-permute-start.27 = (bf16[256,2048]{1,0:T(8,128)(2,1)S(1)}, bf16[256,2048]{1,0:T(8,128)(2,1)S(1)}, u32[]{:S(2)}, u32[]{:S(2)}) collective-permute-start(bf16[256,2048]{1,0:T(8,128)(2,1)S(1)} %pad_maximum_fusion.17), channel_id=1, source_target_pairs={{0,1},{1,0},{2,3},{3,2},{4,5},{5,4},{6,7},{7,6},{8,9},{9,8},{10,11... | collective-permute-start | bytes 3145736 | tf_op jit(solution)/shard_map/ppermute | solution.py:104
  537.4 103.1 %reduce-scatter.5.cloned.1.call-start = ((), (), s32[]{:S(2)}) async-start(), calls=%async_computation.7 | async-start | bytes 5308416 | tf_op jit(solution)/shard_map/reduce_scatter | solution.py:142
  587.5 153.1 %reduce-scatter.9.cloned.1.call-start = ((), (), s32[]{:S(2)}) async-start(), calls=%async_computation.9 | async-start | bytes 10616832 | tf_op jit(solution)/shard_map/reduce_scatter | solution.py:266
  588.1 252.7 %reduce-scatter.11.cloned.1.call-start = ((), (), s32[]{:S(2)}) async-start(), calls=%async_computation.10 | async-start | bytes 10616832 | tf_op jit(solution)/shard_map/reduce_scatter | solution.py:279
  591.2 22.8 %collective-permute-start.30 = (bf16[2,128,2048]{2,1,0:T(8,128)(2,1)S(1)}, bf16[2,128,2048]{2,1,0:T(8,128)(2,1)S(1)}, u32[]{:S(2)}, u32[]{:S(2)}) collective-permute-start(bf16[2,128,2048]{2,1,0:T(8,128)(2,1)S(1)} %bitcast.394), channel_id=1, source_target_pairs={{0,1},{1,0},{2,3},{3,2},{4,5},{5,4},{6,7},{7,6},{8,9},{9,8},{10,11... | collective-permute-start | bytes 3145736 | tf_op jit(solution)/shard_map/ppermute | solution.py:117
  (98 other events, 870.4 us)
Sparse Core Ops, SparseCore 0:
  15.2 72.1 all-gather.3
  89.6 89.3 all-gather.5
  181.2 89.3 all-gather.7
  537.6 34.4 reduce-scatter.6
  587.6 52.8 reduce-scatter.4
  642.7 97.8 reduce-scatter.8
  742.9 97.8 reduce-scatter.10

commit v7 on v5

--- a/solution.py
+++ b/solution.py
@@ -2,6 +2,7 @@
 import jax.numpy as jnp
 from jax import lax
 from jax.sharding import PartitionSpec as P
+
 
 H = 16
 KV = 8
@@ -137,13 +138,7 @@
     return split_cols(joined, [blk.shape[1] for blk in blocks])
 
 
-def wide_scatter(blocks):
-    joined = jnp.concatenate([blk.astype(jnp.bfloat16) for blk in blocks], axis=1)
-    summed = lax.psum_scatter(joined, "wide", scatter_dimension=0, tiled=True).astype(jnp.float32)
-    return split_cols(summed, [blk.shape[1] for blk in blocks])
-
-
-def shards(
+def shards_body(
     tokens,
     doc_ids,
     cotangent,
@@ -166,7 +161,6 @@
     repeat = H // KV
     seq_count, length = doc_ids.shape
     rows_group = seq_count * length
-    shard_rows = tokens.shape[0]
     scale = HD ** (-0.5)
     d_local = attn_gain.shape[0]
     hd_local = query_gain.shape[0]
@@ -255,14 +249,16 @@
         hidden = (gate * sigmoid * up).astype(jnp.bfloat16)
         part = times_transposed(hidden, down_wt)
         down_partial = part if down_partial is None else down_partial + part
-        g_down_t = contract_rows(grad_rows, hidden)
         d_hidden = jnp.dot(grad_rows, down_wt, preferred_element_type=jnp.float32)
         d_up = (d_hidden * gate * sigmoid).astype(jnp.bfloat16)
         d_gate = (d_hidden * up * sigmoid * (1.0 + gate * (1.0 - sigmoid))).astype(jnp.bfloat16)
-        g_gate_up = contract_rows(mlp_all, jnp.concatenate([d_gate, d_up], axis=1))
         part = times_transposed(d_gate, gate_w) + times_transposed(d_up, up_w)
         d_mlp_partial = part if d_mlp_partial is None else d_mlp_partial + part
-        joined = jnp.concatenate([g_gate_up.astype(jnp.bfloat16), g_down_t.astype(jnp.bfloat16)], axis=1)
+        g_down_t = contract_rows(grad_rows, hidden)
+        g_gate_up = contract_rows(mlp_all, jnp.concatenate([d_gate, d_up], axis=1))
+        joined = jnp.concatenate(
+            [g_gate_up.astype(jnp.bfloat16), g_down_t.astype(jnp.bfloat16)], axis=1
+        )
         if h == 0:
             joined, mlp_sets[1] = lax.optimization_barrier((joined, mlp_sets[1]))
             mlp_grads.append(lax.psum_scatter(joined, "wide", scatter_dimension=0, tiled=True))
@@ -273,11 +269,11 @@
     d_part, mlp_gain_terms = rms_back(resid, gain_mlp, d_mlp_in)
     grad_mlp_gain = jnp.sum(mlp_gain_terms, axis=0)
     d_resid = cotangent.astype(jnp.float32) + d_part
-    p_scores = jnp.einsum("qgrd,kgd->grqk", q_grouped, k_use, preferred_element_type=jnp.float32) * scale
+    p_scores = (
+        jnp.einsum("qgrd,kgd->grqk", q_grouped, k_use, preferred_element_type=jnp.float32) * scale
+    )
     p_probs = jnp.where(allowed, jnp.exp(p_scores - log_totals[..., None]), 0.0)
-    d_resid_low, p_probs, last_joined = lax.optimization_barrier(
-        (d_resid.astype(jnp.bfloat16), p_probs, last_joined)
-    )
+    d_resid_low, last_joined = lax.optimization_barrier((d_resid.astype(jnp.bfloat16), last_joined))
     mlp_grads.append(lax.psum_scatter(last_joined, "wide", scatter_dimension=0, tiled=True))
     branch_rows = narrow_gather(d_resid_low, relative)
     out_grad = contract_rows(branch_rows, attended).astype(jnp.bfloat16)
@@ -343,7 +339,7 @@
         [q_cols + 2 * kv_cols, 128],
     )
     d_normed = narrow_scatter(d_normed_partial, relative)
-    d_input_part, unused_terms = rms_back(inputs, gain_attn, d_normed)
+    d_input_part, _ = rms_back(inputs, gain_attn, d_normed)
     d_tokens = d_resid + d_input_part
     attn_gain_grad = g_gains[:, 0]
     mlp_gain_grad = g_gains[:, 1]
@@ -406,4 +402,4 @@
         P("wide", "narrow"),
         P("narrow", "wide"),
     )
-    return jax.shard_map(shards, mesh=mesh, in_specs=in_specs, out_specs=out_specs, check_vma=False)
+    return jax.shard_map(shards_body, mesh=mesh, in_specs=in_specs, out_specs=out_specs, check_vma=False)

time: 650 us -> 640 us (0.985)
  waiting for transfers between devices: 218 us -> 235 us
  local copies, waits for them, and re-layouts: 84.3 us -> 72.4 us
  matrix products: 198 us -> 187 us
  other arithmetic: 89.9 us -> 82.8 us
    ppermute x4, waiting for transfers between devices: 30.9 us -> 46.3 us  [narrow_gather(): a_pair_y = lax.ppermute(a_pair, 'narrow', YPERM)]
    unnamed x233 -> x241, local copies, waits for them, and re-layouts: 41 us -> 33.3 us
    ppermute x4, waiting for transfers between devices: 30.3 us -> 37.8 us  [narrow_scatter(): a_got = lax.ppermute(blocks[2:4].astype(jnp.bfloat16), 'narrow', YPERM)]
    select_n x1 -> x0, other arithmetic: 6.97 us -> none  [shards(): p_probs = jnp.where(allowed, jnp.exp(p_scores - log_totals[..., None]), 0.0)]
  transfers between devices with their start and end apart: 41 -> 41, of which waited for: 25 -> 24; matrix products, arithmetic and copies ran while one was open for 52% -> 48% of each run, Pallas kernels for 0% -> 0%
where the time goes in v7:
time: 640 us; the launch traced here: 635 us
  waiting for transfers between devices  235 us (37%)
  matrix products  187 us (29%)
  other arithmetic  82.8 us (13%)
  local copies, waits for them, and re-layouts  72.4 us (11%)
  starting transfers between devices  41.2 us (6%)
  between operations  16.6 us (3%)
    dot_general x8, matrix products, times_transposed(): lax.dot_general(left, right, (((1,), (1,)), ((), ())), preferred_element_...  57.8 us
    ppermute x4, waiting for transfers between devices, narrow_gather(): a_pair_y = lax.ppermute(a_pair, 'narrow', YPERM)  46.3 us
    dot_general x6, matrix products, contract_rows(): lax.dot_general(left, right, (((0,), (0,)), ((), ())), preferred_element_...  40.8 us
    ppermute x4, waiting for transfers between devices, narrow_gather(): b_pair_x = lax.ppermute(b_pair, 'narrow', XPERM)  40.5 us
    ppermute x4, waiting for transfers between devices, narrow_scatter(): a_got = lax.ppermute(blocks[2:4].astype(jnp.bfloat16), 'narrow', YPERM)  37.8 us
    ppermute x4, waiting for transfers between devices, narrow_gather(): b_y = lax.ppermute(b, 'narrow', YPERM)  35.9 us
    unnamed x241, local copies, waits for them, and re-layouts  33.3 us
    concatenate x2, other arithmetic, shards_body(): jnp.concatenate([g_gate_up.astype(jnp.bfloat16), g_down_t.astype(jnp.bflo...  22.8 us
  transfers between devices with their start and end apart: 41, of which 24 were waited for; matrix products, arithmetic and copies ran while one was open for 48% of the time, Pallas kernels for 0%

profile of v7, /device:TPU:0, one launch (start us, length us, event | category | flops | bytes accessed | tf_op | source)
XLA Modules:
  0.0 635.1 jit_solution(11897084425980093312)
XLA Ops:
  27.7 8.0 %collective-permute-done = bf16[128,2048]{1,0:T(8,128)(2,1)S(1)} collective-permute-done((bf16[128,2048]{1,0:T(8,128)(2,1)S(1)}, bf16[128,2048]{1,0:T(8,128)(2,1)S(1)}, u32[]{:S(2)}, u32[]{:S(2)}) %collective-permute-start) | collective-permute-done | bytes 524320 | tf_op jit(solution)/shard_map/ppermute | solution.py:99
  38.6 21.6 %collective-permute-done.1 = bf16[256,2048]{1,0:T(8,128)(2,1)S(1)} collective-permute-done((bf16[256,2048]{1,0:T(8,128)(2,1)S(1)}, bf16[256,2048]{1,0:T(8,128)(2,1)S(1)}, u32[]{:S(2)}, u32[]{:S(2)}) %collective-permute-start.1) | collective-permute-done | bytes 1048608 | tf_op jit(solution)/shard_map/ppermute | solution.py:103
  63.8 10.9 %collective-permute-done.2 = bf16[128,2048]{1,0:T(8,128)(2,1)S(1)} collective-permute-done((bf16[128,2048]{1,0:T(8,128)(2,1)S(1)}, bf16[128,2048]{1,0:T(8,128)(2,1)S(1)}, u32[]{:S(2)}, u32[]{:S(2)}) %collective-permute-start.2) | collective-permute-done | bytes 524320 | tf_op jit(solution)/shard_map/ppermute | solution.py:100
  80.3 17.4 %collective-permute-done.3 = bf16[256,2048]{1,0:T(8,128)(2,1)S(1)} collective-permute-done((bf16[256,2048]{1,0:T(8,128)(2,1)S(1)}, bf16[256,2048]{1,0:T(8,128)(2,1)S(1)}, u32[]{:S(2)}, u32[]{:S(2)}) %collective-permute-start.3) | collective-permute-done | bytes 1048608 | tf_op jit(solution)/shard_map/ppermute | solution.py:104
  142.9 21.2 %collective-permute-done.4 = bf16[2,128,2048]{2,1,0:T(8,128)(2,1)S(1)} collective-permute-done((bf16[2,128,2048]{2,1,0:T(8,128)(2,1)S(1)}, bf16[2,128,2048]{2,1,0:T(8,128)(2,1)S(1)}, u32[]{:S(2)}, u32[]{:S(2)}) %collective-permute-start.4) | collective-permute-done | bytes 1048608 | tf_op jit(solution)/shard_map/ppermute | solution.py:116
  165.6 12.0 %collective-permute-done.6 = bf16[2,128,2048]{2,1,0:T(8,128)(2,1)S(1)} collective-permute-done((bf16[2,128,2048]{2,1,0:T(8,128)(2,1)S(1)}, bf16[2,128,2048]{2,1,0:T(8,128)(2,1)S(1)}, u32[]{:S(2)}, u32[]{:S(2)}) %collective-permute-start.6) | collective-permute-done | bytes 1048608 | tf_op jit(solution)/shard_map/ppermute | solution.py:117
  184.6 8.2 %collective-permute-done.7 = bf16[128,2048]{1,0:T(8,128)(2,1)S(1)} collective-permute-done((bf16[128,2048]{1,0:T(8,128)(2,1)S(1)}, bf16[128,2048]{1,0:T(8,128)(2,1)S(1)}, u32[]{:S(2)}, u32[]{:S(2)}) %collective-permute-start.7) | collective-permute-done | bytes 524320 | tf_op jit(solution)/shard_map/ppermute | solution.py:121
  197.4 15.0 %collective-permute-done.13 = bf16[256,2048]{1,0:T(8,128)(2,1)S(1)} collective-permute-done((bf16[256,2048]{1,0:T(8,128)(2,1)S(1)}, bf16[256,2048]{1,0:T(8,128)(2,1)S(1)}, u32[]{:S(2)}, u32[]{:S(2)}) %collective-permute-start.13) | collective-permute-done | bytes 1048608 | tf_op jit(solution)/shard_map/ppermute | solution.py:103
  214.8 9.8 %collective-permute-done.15 = bf16[256,2048]{1,0:T(8,128)(2,1)S(1)} collective-permute-done((bf16[256,2048]{1,0:T(8,128)(2,1)S(1)}, bf16[256,2048]{1,0:T(8,128)(2,1)S(1)}, u32[]{:S(2)}, u32[]{:S(2)}) %collective-permute-start.15) | collective-permute-done | bytes 1048608 | tf_op jit(solution)/shard_map/ppermute | solution.py:104
  229.8 9.7 %collective-permute-done.9 = bf16[256,2048]{1,0:T(8,128)(2,1)S(1)} collective-permute-done((bf16[256,2048]{1,0:T(8,128)(2,1)S(1)}, bf16[256,2048]{1,0:T(8,128)(2,1)S(1)}, u32[]{:S(2)}, u32[]{:S(2)}) %collective-permute-start.9) | collective-permute-done | bytes 1048608 | tf_op jit(solution)/shard_map/ppermute | solution.py:103
  266.5 10.6 %convolution_convert_fusion.1 = bf16[2048,1536]{0,1:T(8,128)(2,1)S(1)} fusion(bf16[1024,2048]{1,0:T(8,128)(2,1)} %constant_dynamic-update-slice_fusion.13, bf16[1024,768]{0,1:T(8,128)(2,1)S(1)} %get-tuple-element.107, bf16[1024,768]{0,1:T(8,128)(2,1)S(1)} %get-tuple-element.105), kind=kOutput, calls=%fused_computation.29 | convolution fusion | flops 6451888128 | bytes 13631488 | tf_op jit(solution)/shard_map/dot_general | solution.py:61
  277.1 11.5 %pad_maximum_fusion = bf16[2048,2304]{0,1:T(8,128)(2,1)} fusion(bf16[2048,768]{0,1:T(8,128)(2,1)S(1)} %convolution_convert_fusion.4, bf16[2048,1536]{0,1:T(8,128)(2,1)S(1)} %convolution_convert_fusion.1), kind=kLoop, calls=%fused_computation.16 | loop fusion | flops 18874368 | bytes 18874368 | tf_op jit(solution)/shard_map/concatenate | solution.py:259
  331.0 12.7 %fusion.167 = (bf16[1024,2048]{1,0:T(8,128)(2,1)}, f32[1024,2048]{1,0:T(8,128)S(1)}) fusion(f32[1024,2048]{1,0:T(8,128)} %fusion.171, bf16[1024,768]{0,1:T(8,128)(2,1)} %get-tuple-element.102, bf16[2048,768]{0,1:T(8,128)(2,1)S(1)} %copy-done.15, f32[1024,2048]{1,0:T(8,128)} %fusion.35, f32[1024,2048]{1,0:T(8,128)} %fusion.31), kind=kOutput, calls=%fused_computation.382 | convolution fusion | flops 3229614080 | bytes 42467328 | tf_op jit(solution)/shard_map/dot_general | solution.py:67
  372.0 11.1 %convolution_convert_fusion = bf16[2048,1536]{0,1:T(8,128)(2,1)S(1)} fusion(bf16[1024,2048]{1,0:T(8,128)(2,1)} %constant_dynamic-update-slice_fusion.13, bf16[1024,768]{0,1:T(8,128)(2,1)S(1)} %copy-done.41, bf16[1024,768]{0,1:T(8,128)(2,1)S(1)} %copy-done.82), kind=kOutput, calls=%fused_computation.28 | convolution fusion | flops 6451888128 | bytes 13631488 | tf_op jit(solution)/shard_map/dot_general | solution.py:61
  384.8 11.3 %pad_maximum_fusion.1 = bf16[2048,2304]{0,1:T(8,128)(2,1)} fusion(bf16[2048,768]{0,1:T(8,128)(2,1)S(1)} %convolution_convert_fusion.3, bf16[2048,1536]{0,1:T(8,128)(2,1)S(1)} %convolution_convert_fusion), kind=kLoop, calls=%fused_computation.17 | loop fusion | flops 18874368 | bytes 18874368 | tf_op jit(solution)/shard_map/concatenate | solution.py:259
  423.0 8.3 %collective-permute-done.24 = bf16[128,2048]{1,0:T(8,128)(2,1)S(1)} collective-permute-done((bf16[128,2048]{1,0:T(8,128)(2,1)S(1)}, bf16[128,2048]{1,0:T(8,128)(2,1)S(1)}, u32[]{:S(2)}, u32[]{:S(2)}) %collective-permute-start.24) | collective-permute-done | bytes 524320 | tf_op jit(solution)/shard_map/ppermute | solution.py:99
  433.5 22.4 %collective-permute-done.26 = bf16[128,2048]{1,0:T(8,128)(2,1)S(1)} collective-permute-done((bf16[128,2048]{1,0:T(8,128)(2,1)S(1)}, bf16[128,2048]{1,0:T(8,128)(2,1)S(1)}, u32[]{:S(2)}, u32[]{:S(2)}) %collective-permute-start.26) | collective-permute-done | bytes 524320 | tf_op jit(solution)/shard_map/ppermute | solution.py:100
  457.6 13.3 %collective-permute-done.27 = bf16[256,2048]{1,0:T(8,128)(2,1)S(1)} collective-permute-done((bf16[256,2048]{1,0:T(8,128)(2,1)S(1)}, bf16[256,2048]{1,0:T(8,128)(2,1)S(1)}, u32[]{:S(2)}, u32[]{:S(2)}) %collective-permute-start.27) | collective-permute-done | bytes 1048608 | tf_op jit(solution)/shard_map/ppermute | solution.py:104
  476.6 12.7 %fusion = (f32[2,2,1024]{2,1,0:T(2,128)S(1)}, f32[2,1024,1024,2]{2,1,3,0:T(8,128)}) fusion(f32[2,1024,1024,2]{2,1,3,0:T(8,128)} %copy-done, f32[2,2,1024]{2,1,0:T(2,128)S(1)} %log_add_fusion, pred[1024,1024]{0,1:T(8,128)(4,1)S(1)} %copy-done.8, bf16[1024,2,128,1]{0,2,3,1:T(8,128)(2,1)S(1)} %bitcast.390, bf16[1024,2,2,128]{0,3,2,1:T(8,128)(2,1)S(1)} %bitcast.401), kind=kOutput, calls=%fused_computation.2 | convolution fusion | flops 1094709248 | bytes 36208640 | tf_op jit(solution)/shard_map/qgrd,kgd->grqk/dot_general | solution.py:286
  489.3 12.7 %fusion.2 = bf16[2,2,1024,1024]{2,3,1,0:T(8,128)(2,1)S(1)} fusion(f32[2,1024,1024,2]{2,1,3,0:T(8,128)} %get-tuple-element.193, f32[2,1024,1024,2]{2,1,3,0:T(8,128)} %copy-done, f32[2,2,1024]{2,1,0:T(2,128)S(1)} %get-tuple-element.192, f32[2,2,1024]{2,1,0:T(2,128)S(1)} %log_add_fusion, pred[1024,1024]{0,1:T(8,128)(4,1)S(1)} %copy-done.8), kind=kLoop, calls=%fused_computation.4 | loop fusion | flops 25165824 | bytes 43024384 | tf_op jit(solution)/shard_map/convert_element_type | solution.py:288
  518.8 11.0 %fusion.66 = bf16[2,128,1024]{2,1,0:T(8,128)(2,1)} fusion(bf16[1024,2,2,128]{0,3,2,1:T(8,128)(2,1)} %bitcast.402, f32[2,1024,1024,2]{2,1,3,0:T(8,128)} %copy-done, f32[2,2,1024]{2,1,0:T(2,128)S(1)} %log_add_fusion, pred[1024,1024]{0,1:T(8,128)(4,1)S(1)} %copy-done.8), kind=kOutput, calls=%fused_computation.127 | convolution fusion | flops 1090781184 | bytes 19415040 | tf_op jit(solution)/shard_map/grqk,qgrd->kgd/dot_general | solution.py:291
  530.0 14.0 %fusion.12 = (f32[2048]{0:T(1024)S(1)}, bf16[1024,2048]{1,0:T(8,128)(2,1)}, f32[1024,2048]{1,0:T(8,128)}) fusion(bf16[1024,2048]{1,0:T(8,128)(2,1)} %copy-done.23, f32[1024]{0:T(1024)S(1)} %copy-done.76, bf16[2048,1664]{0,1:T(8,128)(2,1)} %all-gather.4.cloned.1.call-done, bf16[1024,256]{0,1:T(8,128)(2,1)} %bitcast.423, bf16[1024,256]{0,1:T(8,128)(2,1)} %bitcast.405, ...), kind=kOutput, calls=%fused_computation.23 | convolution fusion | flops 4311742464 | bytes 23080960 | tf_op jit(solution)/shard_map/dot_general | solution.py:67
  575.5 16.5 %collective-permute-done.28 = bf16[2,128,2048]{2,1,0:T(8,128)(2,1)S(1)} collective-permute-done((bf16[2,128,2048]{2,1,0:T(8,128)(2,1)S(1)}, bf16[2,128,2048]{2,1,0:T(8,128)(2,1)S(1)}, u32[]{:S(2)}, u32[]{:S(2)}) %collective-permute-start.28) | collective-permute-done | bytes 1048608 | tf_op jit(solution)/shard_map/ppermute | solution.py:116
  595.8 8.6 %collective-permute-done.29 = bf16[128,2048]{1,0:T(8,128)(2,1)S(1)} collective-permute-done((bf16[128,2048]{1,0:T(8,128)(2,1)S(1)}, bf16[128,2048]{1,0:T(8,128)(2,1)S(1)}, u32[]{:S(2)}, u32[]{:S(2)}) %collective-permute-start.29) | collective-permute-done | bytes 524320 | tf_op jit(solution)/shard_map/ppermute | solution.py:120
  (495 shorter events, 307.9 us)
Async XLA Ops:
  7.2 93.8 %all-gather.4.cloned.1.call-start = ((), (), s32[]{:S(2)}) async-start(), calls=%async_computation.4 | async-start | bytes 7667712 | tf_op jit(solution)/shard_map/all_gather | solution.py:137
  15.1 228.3 %all-gather.6.cloned.1.call-start = ((), (), s32[]{:S(2)}) async-start(), calls=%async_computation.5 | async-start | bytes 10616832 | tf_op jit(solution)/shard_map/all_gather | solution.py:137
  19.8 268.8 %all-gather.8.cloned.1.call-start = ((), (), s32[]{:S(2)}) async-start(), calls=%async_computation.6 | async-start | bytes 10616832 | tf_op jit(solution)/shard_map/all_gather | solution.py:137
  26.3 503.6 %reduce-scatter.5.cloned.1.call-start = ((), (), s32[]{:S(2)}) async-start(), calls=%async_computation.7 | async-start | bytes 10616832 | tf_op jit(solution)/shard_map/reduce_scatter | solution.py:264
  35.8 24.5 %collective-permute-start.1 = (bf16[256,2048]{1,0:T(8,128)(2,1)S(1)}, bf16[256,2048]{1,0:T(8,128)(2,1)S(1)}, u32[]{:S(2)}, u32[]{:S(2)}) collective-permute-start(bf16[256,2048]{1,0:T(8,128)(2,1)S(1)} %pad_maximum_fusion.10), channel_id=1, source_target_pairs={{0,2},{2,0},{1,3},{3,1},{4,6},{6,4},{5,7},{7,5},{8,10},{10,8},{9,1... | collective-permute-start | bytes 3145736 | tf_op jit(solution)/shard_map/ppermute | solution.py:103
  74.8 23.0 %collective-permute-start.3 = (bf16[256,2048]{1,0:T(8,128)(2,1)S(1)}, bf16[256,2048]{1,0:T(8,128)(2,1)S(1)}, u32[]{:S(2)}, u32[]{:S(2)}) collective-permute-start(bf16[256,2048]{1,0:T(8,128)(2,1)S(1)} %pad_maximum_fusion.11), channel_id=1, source_target_pairs={{0,1},{1,0},{2,3},{3,2},{4,5},{5,4},{6,7},{7,6},{8,9},{9,8},{10,11... | collective-permute-start | bytes 3145736 | tf_op jit(solution)/shard_map/ppermute | solution.py:104
  138.0 26.1 %collective-permute-start.4 = (bf16[2,128,2048]{2,1,0:T(8,128)(2,1)S(1)}, bf16[2,128,2048]{2,1,0:T(8,128)(2,1)S(1)}, u32[]{:S(2)}, u32[]{:S(2)}) collective-permute-start(bf16[2,128,2048]{2,1,0:T(8,128)(2,1)S(1)} %bitcast.398), channel_id=1, source_target_pairs={{0,2},{2,0},{1,3},{3,1},{4,6},{6,4},{5,7},{7,5},{8,10},{10,8},{9,1... | collective-permute-start | bytes 3145736 | tf_op jit(solution)/shard_map/ppermute | solution.py:116
  139.4 57.2 %collective-permute-start.14 = (bf16[128,2048]{1,0:T(8,128)(2,1)S(1)}, bf16[128,2048]{1,0:T(8,128)(2,1)S(1)}, u32[]{:S(2)}, u32[]{:S(2)}) collective-permute-start(bf16[128,2048]{1,0:T(8,128)(2,1)S(1)} %get-tuple-element.136), channel_id=1, source_target_pairs={{0,2},{2,0},{1,3},{3,1},{4,6},{6,4},{5,7},{7,5},{8,10},{10,8},{9,1... | collective-permute-start | bytes 1572872 | tf_op jit(solution)/shard_map/ppermute | solution.py:100
  140.4 38.8 %collective-permute-start.12 = (bf16[128,2048]{1,0:T(8,128)(2,1)S(1)}, bf16[128,2048]{1,0:T(8,128)(2,1)S(1)}, u32[]{:S(2)}, u32[]{:S(2)}) collective-permute-start(bf16[128,2048]{1,0:T(8,128)(2,1)S(1)} %get-tuple-element.138), channel_id=1, source_target_pairs={{0,1},{1,0},{2,3},{3,2},{4,5},{5,4},{6,7},{7,6},{8,9},{9,8},{10,11... | collective-permute-start | bytes 1572872 | tf_op jit(solution)/shard_map/ppermute | solution.py:99
  141.8 35.8 %collective-permute-start.6 = (bf16[2,128,2048]{2,1,0:T(8,128)(2,1)S(1)}, bf16[2,128,2048]{2,1,0:T(8,128)(2,1)S(1)}, u32[]{:S(2)}, u32[]{:S(2)}) collective-permute-start(bf16[2,128,2048]{2,1,0:T(8,128)(2,1)S(1)} %bitcast.397), channel_id=1, source_target_pairs={{0,1},{1,0},{2,3},{3,2},{4,5},{5,4},{6,7},{7,6},{8,9},{9,8},{10,11... | collective-permute-start | bytes 3145736 | tf_op jit(solution)/shard_map/ppermute | solution.py:117
  179.2 33.1 %collective-permute-start.13 = (bf16[256,2048]{1,0:T(8,128)(2,1)S(1)}, bf16[256,2048]{1,0:T(8,128)(2,1)S(1)}, u32[]{:S(2)}, u32[]{:S(2)}) collective-permute-start(bf16[256,2048]{1,0:T(8,128)(2,1)S(1)} %pad_maximum_fusion.14), channel_id=1, source_target_pairs={{0,2},{2,0},{1,3},{3,1},{4,6},{6,4},{5,7},{7,5},{8,10},{10,8},{9,1... | collective-permute-start | bytes 3145736 | tf_op jit(solution)/shard_map/ppermute | solution.py:103
  196.7 27.8 %collective-permute-start.15 = (bf16[256,2048]{1,0:T(8,128)(2,1)S(1)}, bf16[256,2048]{1,0:T(8,128)(2,1)S(1)}, u32[]{:S(2)}, u32[]{:S(2)}) collective-permute-start(bf16[256,2048]{1,0:T(8,128)(2,1)S(1)} %pad_maximum_fusion.15), channel_id=1, source_target_pairs={{0,1},{1,0},{2,3},{3,2},{4,5},{5,4},{6,7},{7,6},{8,9},{9,8},{10,11... | collective-permute-start | bytes 3145736 | tf_op jit(solution)/shard_map/ppermute | solution.py:104
  213.7 25.7 %collective-permute-start.9 = (bf16[256,2048]{1,0:T(8,128)(2,1)S(1)}, bf16[256,2048]{1,0:T(8,128)(2,1)S(1)}, u32[]{:S(2)}, u32[]{:S(2)}) collective-permute-start(bf16[256,2048]{1,0:T(8,128)(2,1)S(1)} %pad_maximum_fusion.12), channel_id=1, source_target_pairs={{0,2},{2,0},{1,3},{3,1},{4,6},{6,4},{5,7},{7,5},{8,10},{10,8},{9,1... | collective-permute-start | bytes 3145736 | tf_op jit(solution)/shard_map/ppermute | solution.py:103
  294.6 235.2 %reduce-scatter.7.cloned.1.call-start = ((), (), s32[]{:S(2)}) async-start(), calls=%async_computation.8 | async-start | bytes 10616832 | tf_op jit(solution)/shard_map/reduce_scatter | solution.py:277
  347.0 53.3 %collective-permute-start.22 = (bf16[2,128,2048]{2,1,0:T(8,128)(2,1)}, bf16[2,128,2048]{2,1,0:T(8,128)(2,1)}, u32[]{:S(2)}, u32[]{:S(2)}) collective-permute-start(bf16[2,128,2048]{2,1,0:T(8,128)(2,1)} %bitcast.63), channel_id=1, source_target_pairs={{0,1},{1,0},{2,3},{3,2},{4,5},{5,4},{6,7},{7,6},{8,9},{9,8},{10,11... | collective-permute-start | bytes 3145736 | tf_op jit(solution)/shard_map/ppermute | solution.py:117
  348.6 47.6 %collective-permute-start.20 = (bf16[2,128,2048]{2,1,0:T(8,128)(2,1)}, bf16[2,128,2048]{2,1,0:T(8,128)(2,1)}, u32[]{:S(2)}, u32[]{:S(2)}) collective-permute-start(bf16[2,128,2048]{2,1,0:T(8,128)(2,1)} %bitcast.59), channel_id=1, source_target_pairs={{0,2},{2,0},{1,3},{3,1},{4,6},{6,4},{5,7},{7,5},{8,10},{10,8},{9,1... | collective-permute-start | bytes 3145736 | tf_op jit(solution)/shard_map/ppermute | solution.py:116
  362.9 42.0 %collective-permute-start.18 = (bf16[2,128,2048]{2,1,0:T(8,128)(2,1)}, bf16[2,128,2048]{2,1,0:T(8,128)(2,1)S(1)}, u32[]{:S(2)}, u32[]{:S(2)}) collective-permute-start(bf16[2,128,2048]{2,1,0:T(8,128)(2,1)} %bitcast.55), channel_id=1, source_target_pairs={{0,1},{1,0},{2,3},{3,2},{4,5},{5,4},{6,7},{7,6},{8,9},{9,8},{10,11... | collective-permute-start | bytes 3145736 | tf_op jit(solution)/shard_map/ppermute | solution.py:117
  363.6 39.6 %collective-permute-start.16 = (bf16[2,128,2048]{2,1,0:T(8,128)(2,1)}, bf16[2,128,2048]{2,1,0:T(8,128)(2,1)}, u32[]{:S(2)}, u32[]{:S(2)}) collective-permute-start(bf16[2,128,2048]{2,1,0:T(8,128)(2,1)} %bitcast.51), channel_id=1, source_target_pairs={{0,2},{2,0},{1,3},{3,1},{4,6},{6,4},{5,7},{7,5},{8,10},{10,8},{9,1... | collective-permute-start | bytes 3145736 | tf_op jit(solution)/shard_map/ppermute | solution.py:116
  421.9 144.4 %reduce-scatter.9.cloned.1.call-start = ((), (), s32[]{:S(2)}) async-start(), calls=%async_computation.9 | async-start | bytes 2359296 | tf_op jit(solution)/shard_map/reduce_scatter | solution.py:282
  431.4 26.0 %collective-permute-start.25 = (bf16[256,2048]{1,0:T(8,128)(2,1)S(1)}, bf16[256,2048]{1,0:T(8,128)(2,1)S(1)}, u32[]{:S(2)}, u32[]{:S(2)}) collective-permute-start(bf16[256,2048]{1,0:T(8,128)(2,1)S(1)} %pad_maximum_fusion.16), channel_id=1, source_target_pairs={{0,2},{2,0},{1,3},{3,1},{4,6},{6,4},{5,7},{7,5},{8,10},{10,8},{9,1... | collective-permute-start | bytes 3145736 | tf_op jit(solution)/shard_map/ppermute | solution.py:103
  432.6 23.3 %collective-permute-start.26 = (bf16[128,2048]{1,0:T(8,128)(2,1)S(1)}, bf16[128,2048]{1,0:T(8,128)(2,1)S(1)}, u32[]{:S(2)}, u32[]{:S(2)}) collective-permute-start(bf16[128,2048]{1,0:T(8,128)(2,1)S(1)} %get-tuple-element.133), channel_id=1, source_target_pairs={{0,2},{2,0},{1,3},{3,1},{4,6},{6,4},{5,7},{7,5},{8,10},{10,8},{9,1... | collective-permute-start | bytes 1572872 | tf_op jit(solution)/shard_map/ppermute | solution.py:100
  529.9 92.2 %reduce-scatter.11.cloned.1.call-start = ((), (), s32[]{:S(2)}) async-start(), calls=%async_computation.10 | async-start | bytes 5308416 | tf_op jit(solution)/shard_map/reduce_scatter | solution.py:338
  569.8 22.2 %collective-permute-start.28 = (bf16[2,128,2048]{2,1,0:T(8,128)(2,1)S(1)}, bf16[2,128,2048]{2,1,0:T(8,128)(2,1)S(1)}, u32[]{:S(2)}, u32[]{:S(2)}) collective-permute-start(bf16[2,128,2048]{2,1,0:T(8,128)(2,1)S(1)} %bitcast.400), channel_id=1, source_target_pairs={{0,2},{2,0},{1,3},{3,1},{4,6},{6,4},{5,7},{7,5},{8,10},{10,8},{9,1... | collective-permute-start | bytes 3145736 | tf_op jit(solution)/shard_map/ppermute | solution.py:116
  571.4 23.6 %collective-permute-start.30 = (bf16[2,128,2048]{2,1,0:T(8,128)(2,1)S(1)}, bf16[2,128,2048]{2,1,0:T(8,128)(2,1)S(1)}, u32[]{:S(2)}, u32[]{:S(2)}) collective-permute-start(bf16[2,128,2048]{2,1,0:T(8,128)(2,1)S(1)} %bitcast.399), channel_id=1, source_target_pairs={{0,1},{1,0},{2,3},{3,2},{4,5},{5,4},{6,7},{7,6},{8,9},{9,8},{10,11... | collective-permute-start | bytes 3145736 | tf_op jit(solution)/shard_map/ppermute | solution.py:117
  (112 other events, 1001.4 us)
Sparse Core Ops, SparseCore 0:
  15.2 72.1 all-gather.3
  89.6 89.3 all-gather.5
  181.1 89.3 all-gather.7
  294.7 100.0 reduce-scatter.4
  422.0 98.8 reduce-scatter.6
  530.0 36.2 reduce-scatter.8
  568.6 53.5 reduce-scatter.10

commit v8 on v7

--- a/solution.py
+++ b/solution.py
@@ -277,9 +277,6 @@
     mlp_grads.append(lax.psum_scatter(last_joined, "wide", scatter_dimension=0, tiled=True))
     branch_rows = narrow_gather(d_resid_low, relative)
     out_grad = contract_rows(branch_rows, attended).astype(jnp.bfloat16)
-    mlp_grads, out_grad = lax.optimization_barrier((mlp_grads, out_grad))
-    mlp_grads = [split_cols(g.astype(jnp.float32), [2 * ff_half, ff_half]) for g in mlp_grads]
-    g_out_t = lax.psum_scatter(out_grad, "wide", scatter_dimension=0, tiled=True).astype(jnp.float32)
     d_attended = jnp.dot(branch_rows, out_wt, preferred_element_type=jnp.float32).astype(jnp.bfloat16)
     d_mixed = d_attended.reshape(rows_group, groups_here, repeat, HD)
 
@@ -331,12 +328,18 @@
     ).reshape(d_full, 4)
     gain_block = jnp.pad(gain_block, ((0, 0), (0, 124)))
     qkv_grad = jnp.concatenate(
-        [contract_rows(normed_all, d_qkv).astype(jnp.bfloat16), gain_block.astype(jnp.bfloat16)], axis=1
-    )
-    g_out_t, qkv_grad = lax.optimization_barrier((g_out_t, qkv_grad))
-    g_qkv, g_gains = split_cols(
-        lax.psum_scatter(qkv_grad, "wide", scatter_dimension=0, tiled=True).astype(jnp.float32),
-        [q_cols + 2 * kv_cols, 128],
+        [
+            out_grad,
+            contract_rows(normed_all, d_qkv).astype(jnp.bfloat16),
+            gain_block.astype(jnp.bfloat16),
+        ],
+        axis=1,
+    )
+    mlp_grads, qkv_grad = lax.optimization_barrier((mlp_grads, qkv_grad))
+    mlp_grads = [split_cols(g.astype(jnp.float32), [2 * ff_half, ff_half]) for g in mlp_grads]
+    last_grads = lax.psum_scatter(qkv_grad, "wide", scatter_dimension=0, tiled=True)
+    g_out_t, g_qkv, g_gains = split_cols(
+        last_grads.astype(jnp.float32), [q_cols, q_cols + 2 * kv_cols, 128]
     )
     d_normed = narrow_scatter(d_normed_partial, relative)
     d_input_part, _ = rms_back(inputs, gain_attn, d_normed)

time: 640 us -> 644 us (level)
  waiting for transfers between devices: 235 us -> 252 us
    reduce_scatter x1, waiting for transfers between devices: 5.26 us -> 30.5 us  [shards_body(): lax.psum_scatter(qkv_grad, 'wide', scatter_dimension=0, tiled=True)]
    unnamed x241 -> x230, local copies, waits for them, and re-layouts: 33.3 us -> 31.5 us
  transfers between devices with their start and end apart: 41 -> 40, of which waited for: 24 -> 22; matrix products, arithmetic and copies ran while one was open for 48% -> 47% of each run, Pallas kernels for 0% -> 0%
where the time goes in v8:
time: 644 us; the launch traced here: 640 us
  waiting for transfers between devices  252 us (39%)
  matrix products  181 us (28%)
  other arithmetic  81.6 us (13%)
  local copies, waits for them, and re-layouts  69.1 us (11%)
  starting transfers between devices  40.1 us (6%)
  between operations  16.6 us (3%)
    dot_general x8, matrix products, times_transposed(): lax.dot_general(left, right, (((1,), (1,)), ((), ())), preferred_element_...  54.5 us
    ppermute x4, waiting for transfers between devices, narrow_gather(): a_pair_y = lax.ppermute(a_pair, 'narrow', YPERM)  46.3 us
    ppermute x4, waiting for transfers between devices, narrow_gather(): b_pair_x = lax.ppermute(b_pair, 'narrow', XPERM)  40.5 us
    dot_general x6, matrix products, contract_rows(): lax.dot_general(left, right, (((0,), (0,)), ((), ())), preferred_element_...  40.4 us
    ppermute x4, waiting for transfers between devices, narrow_scatter(): a_got = lax.ppermute(blocks[2:4].astype(jnp.bfloat16), 'narrow', YPERM)  37.1 us
    ppermute x4, waiting for transfers between devices, narrow_gather(): b_y = lax.ppermute(b, 'narrow', YPERM)  35.9 us
    unnamed x230, local copies, waits for them, and re-layouts  31.5 us
    reduce_scatter x1, waiting for transfers between devices, shards_body(): lax.psum_scatter(qkv_grad, 'wide', scatter_dimension=0, tiled=True)  30.5 us
  transfers between devices with their start and end apart: 40, of which 22 were waited for; matrix products, arithmetic and copies ran while one was open for 47% of the time, Pallas kernels for 0%

profile of v8, /device:TPU:0, one launch (start us, length us, event | category | flops | bytes accessed | tf_op | source)
XLA Modules:
  0.0 640.0 jit_solution(5884479680046738847)
XLA Ops:
  27.7 8.0 %collective-permute-done = bf16[128,2048]{1,0:T(8,128)(2,1)S(1)} collective-permute-done((bf16[128,2048]{1,0:T(8,128)(2,1)S(1)}, bf16[128,2048]{1,0:T(8,128)(2,1)S(1)}, u32[]{:S(2)}, u32[]{:S(2)}) %collective-permute-start) | collective-permute-done | bytes 524320 | tf_op jit(solution)/shard_map/ppermute | solution.py:99
  38.6 21.7 %collective-permute-done.1 = bf16[256,2048]{1,0:T(8,128)(2,1)S(1)} collective-permute-done((bf16[256,2048]{1,0:T(8,128)(2,1)S(1)}, bf16[256,2048]{1,0:T(8,128)(2,1)S(1)}, u32[]{:S(2)}, u32[]{:S(2)}) %collective-permute-start.1) | collective-permute-done | bytes 1048608 | tf_op jit(solution)/shard_map/ppermute | solution.py:103
  63.8 10.9 %collective-permute-done.2 = bf16[128,2048]{1,0:T(8,128)(2,1)S(1)} collective-permute-done((bf16[128,2048]{1,0:T(8,128)(2,1)S(1)}, bf16[128,2048]{1,0:T(8,128)(2,1)S(1)}, u32[]{:S(2)}, u32[]{:S(2)}) %collective-permute-start.2) | collective-permute-done | bytes 524320 | tf_op jit(solution)/shard_map/ppermute | solution.py:100
  80.3 17.4 %collective-permute-done.3 = bf16[256,2048]{1,0:T(8,128)(2,1)S(1)} collective-permute-done((bf16[256,2048]{1,0:T(8,128)(2,1)S(1)}, bf16[256,2048]{1,0:T(8,128)(2,1)S(1)}, u32[]{:S(2)}, u32[]{:S(2)}) %collective-permute-start.3) | collective-permute-done | bytes 1048608 | tf_op jit(solution)/shard_map/ppermute | solution.py:104
  142.9 21.2 %collective-permute-done.4 = bf16[2,128,2048]{2,1,0:T(8,128)(2,1)S(1)} collective-permute-done((bf16[2,128,2048]{2,1,0:T(8,128)(2,1)S(1)}, bf16[2,128,2048]{2,1,0:T(8,128)(2,1)S(1)}, u32[]{:S(2)}, u32[]{:S(2)}) %collective-permute-start.4) | collective-permute-done | bytes 1048608 | tf_op jit(solution)/shard_map/ppermute | solution.py:116
  165.6 12.0 %collective-permute-done.6 = bf16[2,128,2048]{2,1,0:T(8,128)(2,1)S(1)} collective-permute-done((bf16[2,128,2048]{2,1,0:T(8,128)(2,1)S(1)}, bf16[2,128,2048]{2,1,0:T(8,128)(2,1)S(1)}, u32[]{:S(2)}, u32[]{:S(2)}) %collective-permute-start.6) | collective-permute-done | bytes 1048608 | tf_op jit(solution)/shard_map/ppermute | solution.py:117
  184.6 8.2 %collective-permute-done.7 = bf16[128,2048]{1,0:T(8,128)(2,1)S(1)} collective-permute-done((bf16[128,2048]{1,0:T(8,128)(2,1)S(1)}, bf16[128,2048]{1,0:T(8,128)(2,1)S(1)}, u32[]{:S(2)}, u32[]{:S(2)}) %collective-permute-start.7) | collective-permute-done | bytes 524320 | tf_op jit(solution)/shard_map/ppermute | solution.py:121
  197.4 14.9 %collective-permute-done.13 = bf16[256,2048]{1,0:T(8,128)(2,1)S(1)} collective-permute-done((bf16[256,2048]{1,0:T(8,128)(2,1)S(1)}, bf16[256,2048]{1,0:T(8,128)(2,1)S(1)}, u32[]{:S(2)}, u32[]{:S(2)}) %collective-permute-start.13) | collective-permute-done | bytes 1048608 | tf_op jit(solution)/shard_map/ppermute | solution.py:103
  214.8 9.8 %collective-permute-done.15 = bf16[256,2048]{1,0:T(8,128)(2,1)S(1)} collective-permute-done((bf16[256,2048]{1,0:T(8,128)(2,1)S(1)}, bf16[256,2048]{1,0:T(8,128)(2,1)S(1)}, u32[]{:S(2)}, u32[]{:S(2)}) %collective-permute-start.15) | collective-permute-done | bytes 1048608 | tf_op jit(solution)/shard_map/ppermute | solution.py:104
  229.8 9.7 %collective-permute-done.9 = bf16[256,2048]{1,0:T(8,128)(2,1)S(1)} collective-permute-done((bf16[256,2048]{1,0:T(8,128)(2,1)S(1)}, bf16[256,2048]{1,0:T(8,128)(2,1)S(1)}, u32[]{:S(2)}, u32[]{:S(2)}) %collective-permute-start.9) | collective-permute-done | bytes 1048608 | tf_op jit(solution)/shard_map/ppermute | solution.py:103
  266.5 10.6 %convolution_convert_fusion.1 = bf16[2048,1536]{0,1:T(8,128)(2,1)S(1)} fusion(bf16[1024,2048]{1,0:T(8,128)(2,1)} %constant_dynamic-update-slice_fusion.13, bf16[1024,768]{0,1:T(8,128)(2,1)S(1)} %get-tuple-element.103, bf16[1024,768]{0,1:T(8,128)(2,1)S(1)} %get-tuple-element.101), kind=kOutput, calls=%fused_computation.29 | convolution fusion | flops 6451888128 | bytes 13631488 | tf_op jit(solution)/shard_map/dot_general | solution.py:61
  277.1 11.5 %pad_maximum_fusion = bf16[2048,2304]{0,1:T(8,128)(2,1)} fusion(bf16[2048,768]{0,1:T(8,128)(2,1)S(1)} %convolution_convert_fusion.4, bf16[2048,1536]{0,1:T(8,128)(2,1)S(1)} %convolution_convert_fusion.1), kind=kLoop, calls=%fused_computation.16 | loop fusion | flops 18874368 | bytes 18874368 | tf_op jit(solution)/shard_map/concatenate | solution.py:259
  331.3 12.7 %fusion.167 = (bf16[1024,2048]{1,0:T(8,128)(2,1)}, f32[1024,2048]{1,0:T(8,128)S(1)}) fusion(f32[1024,2048]{1,0:T(8,128)} %fusion.171, bf16[1024,768]{0,1:T(8,128)(2,1)} %get-tuple-element.98, bf16[2048,768]{0,1:T(8,128)(2,1)S(1)} %copy-done.15, f32[1024,2048]{1,0:T(8,128)} %fusion.35, f32[1024,2048]{1,0:T(8,128)} %fusion.31), kind=kOutput, calls=%fused_computation.383 | convolution fusion | flops 3229614080 | bytes 42467328 | tf_op jit(solution)/shard_map/dot_general | solution.py:67
  372.3 11.0 %convolution_convert_fusion = bf16[2048,1536]{0,1:T(8,128)(2,1)S(1)} fusion(bf16[1024,2048]{1,0:T(8,128)(2,1)} %constant_dynamic-update-slice_fusion.13, bf16[1024,768]{0,1:T(8,128)(2,1)S(1)} %copy-done.40, bf16[1024,768]{0,1:T(8,128)(2,1)S(1)} %copy-done.77), kind=kOutput, calls=%fused_computation.28 | convolution fusion | flops 6451888128 | bytes 13631488 | tf_op jit(solution)/shard_map/dot_general | solution.py:61
  385.0 11.3 %pad_maximum_fusion.1 = bf16[2048,2304]{0,1:T(8,128)(2,1)} fusion(bf16[2048,768]{0,1:T(8,128)(2,1)S(1)} %convolution_convert_fusion.3, bf16[2048,1536]{0,1:T(8,128)(2,1)S(1)} %convolution_convert_fusion), kind=kLoop, calls=%fused_computation.17 | loop fusion | flops 18874368 | bytes 18874368 | tf_op jit(solution)/shard_map/concatenate | solution.py:259
  423.3 8.2 %collective-permute-done.24 = bf16[128,2048]{1,0:T(8,128)(2,1)S(1)} collective-permute-done((bf16[128,2048]{1,0:T(8,128)(2,1)S(1)}, bf16[128,2048]{1,0:T(8,128)(2,1)S(1)}, u32[]{:S(2)}, u32[]{:S(2)}) %collective-permute-start.24) | collective-permute-done | bytes 524320 | tf_op jit(solution)/shard_map/ppermute | solution.py:99
  433.8 22.4 %collective-permute-done.26 = bf16[128,2048]{1,0:T(8,128)(2,1)S(1)} collective-permute-done((bf16[128,2048]{1,0:T(8,128)(2,1)S(1)}, bf16[128,2048]{1,0:T(8,128)(2,1)S(1)}, u32[]{:S(2)}, u32[]{:S(2)}) %collective-permute-start.26) | collective-permute-done | bytes 524320 | tf_op jit(solution)/shard_map/ppermute | solution.py:100
  457.9 13.3 %collective-permute-done.27 = bf16[256,2048]{1,0:T(8,128)(2,1)S(1)} collective-permute-done((bf16[256,2048]{1,0:T(8,128)(2,1)S(1)}, bf16[256,2048]{1,0:T(8,128)(2,1)S(1)}, u32[]{:S(2)}, u32[]{:S(2)}) %collective-permute-start.27) | collective-permute-done | bytes 1048608 | tf_op jit(solution)/shard_map/ppermute | solution.py:104
  476.9 12.4 %fusion = (f32[2,2,1024]{2,1,0:T(2,128)S(1)}, f32[2,1024,1024,2]{2,1,3,0:T(8,128)}) fusion(f32[2,1024,1024,2]{2,1,3,0:T(8,128)} %copy-done, f32[2,2,1024]{2,1,0:T(2,128)S(1)} %log_add_fusion, pred[1024,1024]{0,1:T(8,128)(4,1)S(1)} %copy-done.8, bf16[1024,2,128,1]{0,2,3,1:T(8,128)(2,1)S(1)} %bitcast.391, bf16[1024,2,2,128]{0,3,2,1:T(8,128)(2,1)S(1)} %bitcast.401), kind=kOutput, calls=%fused_computation.2 | convolution fusion | flops 1094709248 | bytes 36208640 | tf_op jit(solution)/shard_map/qgrd,kgd->grqk/dot_general | solution.py:283
  489.3 12.5 %fusion.2 = bf16[2,2,1024,1024]{2,3,1,0:T(8,128)(2,1)S(1)} fusion(f32[2,1024,1024,2]{2,1,3,0:T(8,128)} %get-tuple-element.189, f32[2,1024,1024,2]{2,1,3,0:T(8,128)} %copy-done, f32[2,2,1024]{2,1,0:T(2,128)S(1)} %get-tuple-element.188, f32[2,2,1024]{2,1,0:T(2,128)S(1)} %log_add_fusion, pred[1024,1024]{0,1:T(8,128)(4,1)S(1)} %copy-done.8), kind=kLoop, calls=%fused_computation.4 | loop fusion | flops 25165824 | bytes 43024384 | tf_op jit(solution)/shard_map/convert_element_type | solution.py:285
  512.3 8.4 %fusion.66 = bf16[2,128,1024]{2,1,0:T(8,128)(2,1)S(1)} fusion(bf16[1024,2,2,128]{0,3,2,1:T(8,128)(2,1)S(1)} %bitcast.402, f32[2,1024,1024,2]{2,1,3,0:T(8,128)} %copy-done, f32[2,2,1024]{2,1,0:T(2,128)S(1)} %log_add_fusion, pred[1024,1024]{0,1:T(8,128)(4,1)S(1)} %copy-done.8), kind=kOutput, calls=%fused_computation.127 | convolution fusion | flops 1090781184 | bytes 19415040 | tf_op jit(solution)/shard_map/grqk,qgrd->kgd/dot_general | solution.py:288
  520.7 10.4 %fusion.12 = (f32[2048]{0:T(1024)S(1)}, bf16[1024,2048]{1,0:T(8,128)(2,1)}, f32[1024,2048]{1,0:T(8,128)}) fusion(bf16[1024,2048]{1,0:T(8,128)(2,1)S(1)} %copy-done.24, f32[1024]{0:T(1024)S(1)} %copy-done.72, bf16[2048,1664]{0,1:T(8,128)(2,1)} %all-gather.4.cloned.1.call-done, bf16[1024,256]{0,1:T(8,128)(2,1)S(1)} %bitcast.423, ...), kind=kOutput, calls=%fused_computation.23 | convolution fusion | flops 4311742464 | bytes 23080960 | tf_op jit(solution)/shard_map/dot_general | solution.py:67
  557.9 15.9 %collective-permute-done.28 = bf16[2,128,2048]{2,1,0:T(8,128)(2,1)S(1)} collective-permute-done((bf16[2,128,2048]{2,1,0:T(8,128)(2,1)S(1)}, bf16[2,128,2048]{2,1,0:T(8,128)(2,1)S(1)}, u32[]{:S(2)}, u32[]{:S(2)}) %collective-permute-start.28) | collective-permute-done | bytes 1048608 | tf_op jit(solution)/shard_map/ppermute | solution.py:116
  596.3 30.5 %reduce-scatter.8.cloned.1.call-done = bf16[256,1664]{0,1:T(8,128)(2,1)} async-done(((bf16[2048,1664]{0,1:T(8,128)(2,1)}), bf16[256,1664]{0,1:T(8,128)(2,1)}) %reduce-scatter.8.cloned.1.call-update) | async-done | bytes 851984 | tf_op jit(solution)/shard_map/reduce_scatter | solution.py:340
  (481 shorter events, 298.3 us)
Async XLA Ops:
  7.2 93.7 %all-gather.4.cloned.1.call-start = ((), (), s32[]{:S(2)}) async-start(), calls=%async_computation.3 | async-start | bytes 7667712 | tf_op jit(solution)/shard_map/all_gather | solution.py:137
  15.1 228.3 %all-gather.6.cloned.1.call-start = ((), (), s32[]{:S(2)}) async-start(), calls=%async_computation.4 | async-start | bytes 10616832 | tf_op jit(solution)/shard_map/all_gather | solution.py:137
  19.8 268.8 %all-gather.8.cloned.1.call-start = ((), (), s32[]{:S(2)}) async-start(), calls=%async_computation.5 | async-start | bytes 10616832 | tf_op jit(solution)/shard_map/all_gather | solution.py:137
  26.3 525.2 %reduce-scatter.4.cloned.1.call-start = ((), (), s32[]{:S(2)}) async-start(), calls=%async_computation.6 | async-start | bytes 10616832 | tf_op jit(solution)/shard_map/reduce_scatter | solution.py:264
  35.8 24.5 %collective-permute-start.1 = (bf16[256,2048]{1,0:T(8,128)(2,1)S(1)}, bf16[256,2048]{1,0:T(8,128)(2,1)S(1)}, u32[]{:S(2)}, u32[]{:S(2)}) collective-permute-start(bf16[256,2048]{1,0:T(8,128)(2,1)S(1)} %pad_maximum_fusion.10), channel_id=1, source_target_pairs={{0,2},{2,0},{1,3},{3,1},{4,6},{6,4},{5,7},{7,5},{8,10},{10,8},{9,1... | collective-permute-start | bytes 3145736 | tf_op jit(solution)/shard_map/ppermute | solution.py:103
  74.8 23.0 %collective-permute-start.3 = (bf16[256,2048]{1,0:T(8,128)(2,1)S(1)}, bf16[256,2048]{1,0:T(8,128)(2,1)S(1)}, u32[]{:S(2)}, u32[]{:S(2)}) collective-permute-start(bf16[256,2048]{1,0:T(8,128)(2,1)S(1)} %pad_maximum_fusion.11), channel_id=1, source_target_pairs={{0,1},{1,0},{2,3},{3,2},{4,5},{5,4},{6,7},{7,6},{8,9},{9,8},{10,11... | collective-permute-start | bytes 3145736 | tf_op jit(solution)/shard_map/ppermute | solution.py:104
  138.0 26.1 %collective-permute-start.4 = (bf16[2,128,2048]{2,1,0:T(8,128)(2,1)S(1)}, bf16[2,128,2048]{2,1,0:T(8,128)(2,1)S(1)}, u32[]{:S(2)}, u32[]{:S(2)}) collective-permute-start(bf16[2,128,2048]{2,1,0:T(8,128)(2,1)S(1)} %bitcast.398), channel_id=1, source_target_pairs={{0,2},{2,0},{1,3},{3,1},{4,6},{6,4},{5,7},{7,5},{8,10},{10,8},{9,1... | collective-permute-start | bytes 3145736 | tf_op jit(solution)/shard_map/ppermute | solution.py:116
  139.4 57.3 %collective-permute-start.14 = (bf16[128,2048]{1,0:T(8,128)(2,1)S(1)}, bf16[128,2048]{1,0:T(8,128)(2,1)S(1)}, u32[]{:S(2)}, u32[]{:S(2)}) collective-permute-start(bf16[128,2048]{1,0:T(8,128)(2,1)S(1)} %get-tuple-element.132), channel_id=1, source_target_pairs={{0,2},{2,0},{1,3},{3,1},{4,6},{6,4},{5,7},{7,5},{8,10},{10,8},{9,1... | collective-permute-start | bytes 1572872 | tf_op jit(solution)/shard_map/ppermute | solution.py:100
  140.3 38.8 %collective-permute-start.12 = (bf16[128,2048]{1,0:T(8,128)(2,1)S(1)}, bf16[128,2048]{1,0:T(8,128)(2,1)S(1)}, u32[]{:S(2)}, u32[]{:S(2)}) collective-permute-start(bf16[128,2048]{1,0:T(8,128)(2,1)S(1)} %get-tuple-element.134), channel_id=1, source_target_pairs={{0,1},{1,0},{2,3},{3,2},{4,5},{5,4},{6,7},{7,6},{8,9},{9,8},{10,11... | collective-permute-start | bytes 1572872 | tf_op jit(solution)/shard_map/ppermute | solution.py:99
  141.8 35.8 %collective-permute-start.6 = (bf16[2,128,2048]{2,1,0:T(8,128)(2,1)S(1)}, bf16[2,128,2048]{2,1,0:T(8,128)(2,1)S(1)}, u32[]{:S(2)}, u32[]{:S(2)}) collective-permute-start(bf16[2,128,2048]{2,1,0:T(8,128)(2,1)S(1)} %bitcast.397), channel_id=1, source_target_pairs={{0,1},{1,0},{2,3},{3,2},{4,5},{5,4},{6,7},{7,6},{8,9},{9,8},{10,11... | collective-permute-start | bytes 3145736 | tf_op jit(solution)/shard_map/ppermute | solution.py:117
  164.4 20.0 %collective-permute-start.5 = (bf16[128,2048]{1,0:T(8,128)(2,1)S(1)}, bf16[128,2048]{1,0:T(8,128)(2,1)S(1)}, u32[]{:S(2)}, u32[]{:S(2)}) collective-permute-start(bf16[128,2048]{1,0:T(8,128)(2,1)S(1)} %fusion.86), channel_id=1, source_target_pairs={{0,1},{1,0},{2,3},{3,2},{4,5},{5,4},{6,7},{7,6},{8,9},{9,8},{10,11... | collective-permute-start | bytes 1572872 | tf_op jit(solution)/shard_map/ppermute | solution.py:120
  179.2 33.1 %collective-permute-start.13 = (bf16[256,2048]{1,0:T(8,128)(2,1)S(1)}, bf16[256,2048]{1,0:T(8,128)(2,1)S(1)}, u32[]{:S(2)}, u32[]{:S(2)}) collective-permute-start(bf16[256,2048]{1,0:T(8,128)(2,1)S(1)} %pad_maximum_fusion.14), channel_id=1, source_target_pairs={{0,2},{2,0},{1,3},{3,1},{4,6},{6,4},{5,7},{7,5},{8,10},{10,8},{9,1... | collective-permute-start | bytes 3145736 | tf_op jit(solution)/shard_map/ppermute | solution.py:103
  196.7 27.8 %collective-permute-start.15 = (bf16[256,2048]{1,0:T(8,128)(2,1)S(1)}, bf16[256,2048]{1,0:T(8,128)(2,1)S(1)}, u32[]{:S(2)}, u32[]{:S(2)}) collective-permute-start(bf16[256,2048]{1,0:T(8,128)(2,1)S(1)} %pad_maximum_fusion.15), channel_id=1, source_target_pairs={{0,1},{1,0},{2,3},{3,2},{4,5},{5,4},{6,7},{7,6},{8,9},{9,8},{10,11... | collective-permute-start | bytes 3145736 | tf_op jit(solution)/shard_map/ppermute | solution.py:104
  213.7 25.7 %collective-permute-start.9 = (bf16[256,2048]{1,0:T(8,128)(2,1)S(1)}, bf16[256,2048]{1,0:T(8,128)(2,1)S(1)}, u32[]{:S(2)}, u32[]{:S(2)}) collective-permute-start(bf16[256,2048]{1,0:T(8,128)(2,1)S(1)} %pad_maximum_fusion.12), channel_id=1, source_target_pairs={{0,2},{2,0},{1,3},{3,1},{4,6},{6,4},{5,7},{7,5},{8,10},{10,8},{9,1... | collective-permute-start | bytes 3145736 | tf_op jit(solution)/shard_map/ppermute | solution.py:103
  294.6 256.9 %reduce-scatter.6.cloned.1.call-start = ((), (), s32[]{:S(2)}) async-start(), calls=%async_computation.7 | async-start | bytes 10616832 | tf_op jit(solution)/shard_map/reduce_scatter | solution.py:277
  347.2 53.2 %collective-permute-start.22 = (bf16[2,128,2048]{2,1,0:T(8,128)(2,1)}, bf16[2,128,2048]{2,1,0:T(8,128)(2,1)}, u32[]{:S(2)}, u32[]{:S(2)}) collective-permute-start(bf16[2,128,2048]{2,1,0:T(8,128)(2,1)} %bitcast.63), channel_id=1, source_target_pairs={{0,1},{1,0},{2,3},{3,2},{4,5},{5,4},{6,7},{7,6},{8,9},{9,8},{10,11... | collective-permute-start | bytes 3145736 | tf_op jit(solution)/shard_map/ppermute | solution.py:117
  348.9 47.4 %collective-permute-start.20 = (bf16[2,128,2048]{2,1,0:T(8,128)(2,1)}, bf16[2,128,2048]{2,1,0:T(8,128)(2,1)}, u32[]{:S(2)}, u32[]{:S(2)}) collective-permute-start(bf16[2,128,2048]{2,1,0:T(8,128)(2,1)} %bitcast.59), channel_id=1, source_target_pairs={{0,2},{2,0},{1,3},{3,1},{4,6},{6,4},{5,7},{7,5},{8,10},{10,8},{9,1... | collective-permute-start | bytes 3145736 | tf_op jit(solution)/shard_map/ppermute | solution.py:116
  363.2 41.9 %collective-permute-start.18 = (bf16[2,128,2048]{2,1,0:T(8,128)(2,1)}, bf16[2,128,2048]{2,1,0:T(8,128)(2,1)S(1)}, u32[]{:S(2)}, u32[]{:S(2)}) collective-permute-start(bf16[2,128,2048]{2,1,0:T(8,128)(2,1)} %bitcast.55), channel_id=1, source_target_pairs={{0,1},{1,0},{2,3},{3,2},{4,5},{5,4},{6,7},{7,6},{8,9},{9,8},{10,11... | collective-permute-start | bytes 3145736 | tf_op jit(solution)/shard_map/ppermute | solution.py:117
  364.0 39.5 %collective-permute-start.16 = (bf16[2,128,2048]{2,1,0:T(8,128)(2,1)}, bf16[2,128,2048]{2,1,0:T(8,128)(2,1)}, u32[]{:S(2)}, u32[]{:S(2)}) collective-permute-start(bf16[2,128,2048]{2,1,0:T(8,128)(2,1)} %bitcast.51), channel_id=1, source_target_pairs={{0,2},{2,0},{1,3},{3,1},{4,6},{6,4},{5,7},{7,5},{8,10},{10,8},{9,1... | collective-permute-start | bytes 3145736 | tf_op jit(solution)/shard_map/ppermute | solution.py:116
  422.1 204.7 %reduce-scatter.8.cloned.1.call-start = ((), (), s32[]{:S(2)}) async-start(), calls=%async_computation.8 | async-start | bytes 7667712 | tf_op jit(solution)/shard_map/reduce_scatter | solution.py:340
  431.7 26.1 %collective-permute-start.25 = (bf16[256,2048]{1,0:T(8,128)(2,1)S(1)}, bf16[256,2048]{1,0:T(8,128)(2,1)S(1)}, u32[]{:S(2)}, u32[]{:S(2)}) collective-permute-start(bf16[256,2048]{1,0:T(8,128)(2,1)S(1)} %pad_maximum_fusion.16), channel_id=1, source_target_pairs={{0,2},{2,0},{1,3},{3,1},{4,6},{6,4},{5,7},{7,5},{8,10},{10,8},{9,1... | collective-permute-start | bytes 3145736 | tf_op jit(solution)/shard_map/ppermute | solution.py:103
  432.9 23.4 %collective-permute-start.26 = (bf16[128,2048]{1,0:T(8,128)(2,1)S(1)}, bf16[128,2048]{1,0:T(8,128)(2,1)S(1)}, u32[]{:S(2)}, u32[]{:S(2)}) collective-permute-start(bf16[128,2048]{1,0:T(8,128)(2,1)S(1)} %get-tuple-element.129), channel_id=1, source_target_pairs={{0,2},{2,0},{1,3},{3,1},{4,6},{6,4},{5,7},{7,5},{8,10},{10,8},{9,1... | collective-permute-start | bytes 1572872 | tf_op jit(solution)/shard_map/ppermute | solution.py:100
  553.3 20.5 %collective-permute-start.28 = (bf16[2,128,2048]{2,1,0:T(8,128)(2,1)S(1)}, bf16[2,128,2048]{2,1,0:T(8,128)(2,1)S(1)}, u32[]{:S(2)}, u32[]{:S(2)}) collective-permute-start(bf16[2,128,2048]{2,1,0:T(8,128)(2,1)S(1)} %bitcast.400), channel_id=1, source_target_pairs={{0,2},{2,0},{1,3},{3,1},{4,6},{6,4},{5,7},{7,5},{8,10},{10,8},{9,1... | collective-permute-start | bytes 3145736 | tf_op jit(solution)/shard_map/ppermute | solution.py:116
  554.7 20.8 %collective-permute-start.30 = (bf16[2,128,2048]{2,1,0:T(8,128)(2,1)S(1)}, bf16[2,128,2048]{2,1,0:T(8,128)(2,1)S(1)}, u32[]{:S(2)}, u32[]{:S(2)}) collective-permute-start(bf16[2,128,2048]{2,1,0:T(8,128)(2,1)S(1)} %bitcast.399), channel_id=1, source_target_pairs={{0,1},{1,0},{2,3},{3,2},{4,5},{5,4},{6,7},{7,6},{8,9},{9,8},{10,11... | collective-permute-start | bytes 3145736 | tf_op jit(solution)/shard_map/ppermute | solution.py:117
  (106 other events, 898.4 us)
Sparse Core Ops, SparseCore 0:
  15.2 72.2 all-gather.3
  89.6 89.2 all-gather.5
  181.1 89.3 all-gather.7
  294.8 99.9 reduce-scatter.3
  422.2 99.0 reduce-scatter.5
  551.7 75.1 reduce-scatter.7

commit v9 on v7

--- a/solution.py
+++ b/solution.py
@@ -192,7 +192,9 @@
     mlp_sets = []
     for h in range(2):
         cols = slice(h * ff_half, (h + 1) * ff_half)
-        mlp_sets.append(wide_gather([w_gate[:, cols], w_up[:, cols], down_t[:, cols]]))
+        mlp_sets.append(
+            wide_gather([jnp.concatenate([w_gate[:, cols], w_up[:, cols]], axis=1), down_t[:, cols]])
+        )
 
     if relative:
         order = relative_rows(jnp.arange(rows_group, dtype=jnp.int32))
@@ -242,9 +244,10 @@
     d_mlp_partial = None
     mlp_grads = []
     for h in range(2):
-        gate_w, up_w, down_wt = mlp_sets[h]
-        gate = jnp.dot(mlp_all, gate_w, preferred_element_type=jnp.float32)
-        up = jnp.dot(mlp_all, up_w, preferred_element_type=jnp.float32)
+        gate_up_w, down_wt = mlp_sets[h]
+        gate_up = jnp.dot(mlp_all, gate_up_w, preferred_element_type=jnp.float32)
+        gate = gate_up[:, :ff_half]
+        up = gate_up[:, ff_half:]
         sigmoid = jax.nn.sigmoid(gate)
         hidden = (gate * sigmoid * up).astype(jnp.bfloat16)
         part = times_transposed(hidden, down_wt)
@@ -252,10 +255,11 @@
         d_hidden = jnp.dot(grad_rows, down_wt, preferred_element_type=jnp.float32)
         d_up = (d_hidden * gate * sigmoid).astype(jnp.bfloat16)
         d_gate = (d_hidden * up * sigmoid * (1.0 + gate * (1.0 - sigmoid))).astype(jnp.bfloat16)
-        part = times_transposed(d_gate, gate_w) + times_transposed(d_up, up_w)
+        d_gate_up = jnp.concatenate([d_gate, d_up], axis=1)
+        part = times_transposed(d_gate_up, gate_up_w)
         d_mlp_partial = part if d_mlp_partial is None else d_mlp_partial + part
         g_down_t = contract_rows(grad_rows, hidden)
-        g_gate_up = contract_rows(mlp_all, jnp.concatenate([d_gate, d_up], axis=1))
+        g_gate_up = contract_rows(mlp_all, d_gate_up)
         joined = jnp.concatenate(
             [g_gate_up.astype(jnp.bfloat16), g_down_t.astype(jnp.bfloat16)], axis=1
         )

time: 640 us -> 622 us (0.972)
  matrix products: 187 us -> 168 us
    dot_general x8 -> x6, matrix products: 57.8 us -> 46.8 us  [times_transposed(): lax.dot_general(left, right, (((1,), (1,)), ((), ())), preferred_element_...]
    dot_general x4 -> x2, matrix products: 25.8 us -> 21.2 us  [shards_body(): gate_up = jnp.dot(mlp_all, gate_up_w, preferred_element_type=jnp.float32)]
    unnamed x241 -> x227, local copies, waits for them, and re-layouts: 33.3 us -> 31.7 us
  transfers between devices with their start and end apart: 41 -> 41, of which waited for: 24 -> 26; matrix products, arithmetic and copies ran while one was open for 48% -> 47% of each run, Pallas kernels for 0% -> 0%
where the time goes in v9:
time: 622 us; the launch traced here: 618 us
  waiting for transfers between devices  237 us (38%)
  matrix products  168 us (27%)
  other arithmetic  83 us (13%)
  local copies, waits for them, and re-layouts  73.6 us (12%)
  starting transfers between devices  39.4 us (6%)
  between operations  16.6 us (3%)
    dot_general x6, matrix products, times_transposed(): lax.dot_general(left, right, (((1,), (1,)), ((), ())), preferred_element_...  46.8 us
    ppermute x4, waiting for transfers between devices, narrow_gather(): a_pair_y = lax.ppermute(a_pair, 'narrow', YPERM)  46 us
    ppermute x4, waiting for transfers between devices, narrow_gather(): b_pair_x = lax.ppermute(b_pair, 'narrow', XPERM)  41.3 us
    dot_general x6, matrix products, contract_rows(): lax.dot_general(left, right, (((0,), (0,)), ((), ())), preferred_element_...  38.9 us
    ppermute x4, waiting for transfers between devices, narrow_scatter(): a_got = lax.ppermute(blocks[2:4].astype(jnp.bfloat16), 'narrow', YPERM)  37.7 us
    ppermute x4, waiting for transfers between devices, narrow_gather(): b_y = lax.ppermute(b, 'narrow', YPERM)  36.2 us
    unnamed x227, local copies, waits for them, and re-layouts  31.7 us
    concatenate x2, other arithmetic, shards_body(): jnp.concatenate([g_gate_up.astype(jnp.bfloat16), g_down_t.astype(jnp.bflo...  23 us
  transfers between devices with their start and end apart: 41, of which 26 were waited for; matrix products, arithmetic and copies ran while one was open for 47% of the time, Pallas kernels for 0%

profile of v9, /device:TPU:0, one launch (start us, length us, event | category | flops | bytes accessed | tf_op | source)
XLA Modules:
  0.0 617.6 jit_solution(8046907940381134474)
XLA Ops:
  38.6 21.7 %collective-permute-done.1 = bf16[256,2048]{1,0:T(8,128)(2,1)S(1)} collective-permute-done((bf16[256,2048]{1,0:T(8,128)(2,1)S(1)}, bf16[256,2048]{1,0:T(8,128)(2,1)S(1)}, u32[]{:S(2)}, u32[]{:S(2)}) %collective-permute-start.1) | collective-permute-done | bytes 1048608 | tf_op jit(solution)/shard_map/ppermute | solution.py:103
  63.8 10.9 %collective-permute-done.2 = bf16[128,2048]{1,0:T(8,128)(2,1)S(1)} collective-permute-done((bf16[128,2048]{1,0:T(8,128)(2,1)S(1)}, bf16[128,2048]{1,0:T(8,128)(2,1)S(1)}, u32[]{:S(2)}, u32[]{:S(2)}) %collective-permute-start.2) | collective-permute-done | bytes 524320 | tf_op jit(solution)/shard_map/ppermute | solution.py:100
  80.3 17.5 %collective-permute-done.3 = bf16[256,2048]{1,0:T(8,128)(2,1)S(1)} collective-permute-done((bf16[256,2048]{1,0:T(8,128)(2,1)S(1)}, bf16[256,2048]{1,0:T(8,128)(2,1)S(1)}, u32[]{:S(2)}, u32[]{:S(2)}) %collective-permute-start.3) | collective-permute-done | bytes 1048608 | tf_op jit(solution)/shard_map/ppermute | solution.py:104
  142.8 21.2 %collective-permute-done.4 = bf16[2,128,2048]{2,1,0:T(8,128)(2,1)S(1)} collective-permute-done((bf16[2,128,2048]{2,1,0:T(8,128)(2,1)S(1)}, bf16[2,128,2048]{2,1,0:T(8,128)(2,1)S(1)}, u32[]{:S(2)}, u32[]{:S(2)}) %collective-permute-start.4) | collective-permute-done | bytes 1048608 | tf_op jit(solution)/shard_map/ppermute | solution.py:116
  165.5 12.0 %collective-permute-done.6 = bf16[2,128,2048]{2,1,0:T(8,128)(2,1)S(1)} collective-permute-done((bf16[2,128,2048]{2,1,0:T(8,128)(2,1)S(1)}, bf16[2,128,2048]{2,1,0:T(8,128)(2,1)S(1)}, u32[]{:S(2)}, u32[]{:S(2)}) %collective-permute-start.6) | collective-permute-done | bytes 1048608 | tf_op jit(solution)/shard_map/ppermute | solution.py:117
  197.3 14.9 %collective-permute-done.13 = bf16[256,2048]{1,0:T(8,128)(2,1)S(1)} collective-permute-done((bf16[256,2048]{1,0:T(8,128)(2,1)S(1)}, bf16[256,2048]{1,0:T(8,128)(2,1)S(1)}, u32[]{:S(2)}, u32[]{:S(2)}) %collective-permute-start.13) | collective-permute-done | bytes 1048608 | tf_op jit(solution)/shard_map/ppermute | solution.py:103
  214.7 9.8 %collective-permute-done.15 = bf16[256,2048]{1,0:T(8,128)(2,1)S(1)} collective-permute-done((bf16[256,2048]{1,0:T(8,128)(2,1)S(1)}, bf16[256,2048]{1,0:T(8,128)(2,1)S(1)}, u32[]{:S(2)}, u32[]{:S(2)}) %collective-permute-start.15) | collective-permute-done | bytes 1048608 | tf_op jit(solution)/shard_map/ppermute | solution.py:104
  229.7 9.4 %collective-permute-done.9 = bf16[256,2048]{1,0:T(8,128)(2,1)S(1)} collective-permute-done((bf16[256,2048]{1,0:T(8,128)(2,1)S(1)}, bf16[256,2048]{1,0:T(8,128)(2,1)S(1)}, u32[]{:S(2)}, u32[]{:S(2)}) %collective-permute-start.9) | collective-permute-done | bytes 1048608 | tf_op jit(solution)/shard_map/ppermute | solution.py:103
  243.2 10.8 %fusion.19 = f32[1024,1536]{1,0:T(8,128)S(1)} fusion(bf16[1024,2048]{1,0:T(8,128)(2,1)} %constant_dynamic-update-slice_fusion.13, bf16[2048,2304]{0,1:T(8,128)(2,1)} %all-gather.6.cloned.1.call-done), kind=kOutput, calls=%fused_computation.31 | convolution fusion | flops 6442450944 | bytes 16777216 | tf_op jit(solution)/shard_map/dot_general | solution.py:248
  264.3 9.7 %convolution_convert_fusion.1 = bf16[2048,1536]{0,1:T(8,128)(2,1)S(1)} fusion(bf16[1024,2048]{1,0:T(8,128)(2,1)} %constant_dynamic-update-slice_fusion.13, bf16[1024,768]{1,0:T(8,128)(2,1)S(1)} %get-tuple-element.86, bf16[1024,768]{1,0:T(8,128)(2,1)S(1)} %get-tuple-element.85), kind=kOutput, calls=%fused_computation.28 | convolution fusion | flops 6451888128 | bytes 13631488 | tf_op jit(solution)/shard_map/dot_general | solution.py:61
  274.0 11.3 %pad_maximum_fusion = bf16[2048,2304]{0,1:T(8,128)(2,1)} fusion(bf16[2048,768]{0,1:T(8,128)(2,1)S(1)} %convolution_convert_fusion.4, bf16[2048,1536]{0,1:T(8,128)(2,1)S(1)} %convolution_convert_fusion.1), kind=kLoop, calls=%fused_computation.16 | loop fusion | flops 18874368 | bytes 18874368 | tf_op jit(solution)/shard_map/concatenate | solution.py:263
  294.0 10.4 %fusion.164 = f32[1024,1536]{1,0:T(8,128)S(1)} fusion(bf16[1024,2048]{1,0:T(8,128)(2,1)} %constant_dynamic-update-slice_fusion.13, bf16[2048,1536]{0,1:T(8,128)(2,1)} %slice.566), kind=kOutput, calls=%fused_computation.378 | convolution fusion | flops 6442450944 | bytes 16777216 | tf_op jit(solution)/shard_map/dot_general | solution.py:248
  308.9 8.9 %fusion.48 = f32[1024,2048]{1,0:T(8,128)} fusion(bf16[2048,1536]{0,1:T(8,128)(2,1)S(1)} %bitcast.380, bf16[1024,768]{1,0:T(8,128)(2,1)S(1)} %get-tuple-element.84, bf16[1024,768]{1,0:T(8,128)(2,1)S(1)} %get-tuple-element.83), kind=kOutput, calls=%fused_computation.107 | convolution fusion | flops 6448742400 | bytes 17825792 | tf_op jit(solution)/shard_map/dot_general | solution.py:67
  317.8 12.7 %fusion.162 = (bf16[1024,2048]{1,0:T(8,128)(2,1)S(1)}, f32[1024,2048]{1,0:T(8,128)}) fusion(f32[1024,2048]{1,0:T(8,128)} %fusion.48, bf16[2048,2304]{0,1:T(8,128)(2,1)} %all-gather.6.cloned.1.call-done, bf16[1024,768]{1,0:T(8,128)(2,1)} %copy-done.80, bf16[1024,768]{1,0:T(8,128)(2,1)S(1)} %copy-done.79), kind=kOutput, calls=%fused_computation.376 | convolution fusion | flops 6452936704 | bytes 30408704 | tf_op jit(solution)/shard_map/dot_general | solution.py:67
  355.2 9.8 %convolution_convert_fusion = bf16[2048,1536]{0,1:T(8,128)(2,1)S(1)} fusion(bf16[1024,2048]{1,0:T(8,128)(2,1)} %constant_dynamic-update-slice_fusion.13, bf16[1024,768]{1,0:T(8,128)(2,1)S(1)} %copy-done.77, bf16[1024,768]{1,0:T(8,128)(2,1)S(1)} %copy-done.75), kind=kOutput, calls=%fused_computation.27 | convolution fusion | flops 6451888128 | bytes 13631488 | tf_op jit(solution)/shard_map/dot_general | solution.py:61
  366.8 11.7 %pad_maximum_fusion.1 = bf16[2048,2304]{0,1:T(8,128)(2,1)} fusion(bf16[2048,768]{0,1:T(8,128)(2,1)S(1)} %convolution_convert_fusion.3, bf16[2048,1536]{0,1:T(8,128)(2,1)S(1)} %convolution_convert_fusion), kind=kLoop, calls=%fused_computation.17 | loop fusion | flops 18874368 | bytes 18874368 | tf_op jit(solution)/shard_map/concatenate | solution.py:263
  415.8 22.8 %collective-permute-done.26 = bf16[128,2048]{1,0:T(8,128)(2,1)S(1)} collective-permute-done((bf16[128,2048]{1,0:T(8,128)(2,1)S(1)}, bf16[128,2048]{1,0:T(8,128)(2,1)S(1)}, u32[]{:S(2)}, u32[]{:S(2)}) %collective-permute-start.26) | collective-permute-done | bytes 524320 | tf_op jit(solution)/shard_map/ppermute | solution.py:100
  439.8 13.8 %collective-permute-done.27 = bf16[256,2048]{1,0:T(8,128)(2,1)S(1)} collective-permute-done((bf16[256,2048]{1,0:T(8,128)(2,1)S(1)}, bf16[256,2048]{1,0:T(8,128)(2,1)S(1)}, u32[]{:S(2)}, u32[]{:S(2)}) %collective-permute-start.27) | collective-permute-done | bytes 1048608 | tf_op jit(solution)/shard_map/ppermute | solution.py:104
  459.3 12.7 %fusion = (f32[2,2,1024]{2,1,0:T(2,128)S(1)}, f32[2,1024,1024,2]{2,1,3,0:T(8,128)}) fusion(f32[2,1024,1024,2]{2,1,3,0:T(8,128)} %copy-done, f32[2,2,1024]{2,1,0:T(2,128)S(1)} %log_add_fusion, pred[1024,1024]{0,1:T(8,128)(4,1)S(1)} %copy-done.8, bf16[1024,2,128,1]{0,2,3,1:T(8,128)(2,1)S(1)} %bitcast.384, bf16[1024,2,2,128]{0,3,2,1:T(8,128)(2,1)S(1)} %bitcast.395), kind=kOutput, calls=%fused_computation.2 | convolution fusion | flops 1094709248 | bytes 36208640 | tf_op jit(solution)/shard_map/qgrd,kgd->grqk/dot_general | solution.py:290
  472.0 12.7 %fusion.2 = bf16[2,2,1024,1024]{2,3,1,0:T(8,128)(2,1)S(1)} fusion(f32[2,1024,1024,2]{2,1,3,0:T(8,128)} %get-tuple-element.188, f32[2,1024,1024,2]{2,1,3,0:T(8,128)} %copy-done, f32[2,2,1024]{2,1,0:T(2,128)S(1)} %get-tuple-element.187, f32[2,2,1024]{2,1,0:T(2,128)S(1)} %log_add_fusion, pred[1024,1024]{0,1:T(8,128)(4,1)S(1)} %copy-done.8), kind=kLoop, calls=%fused_computation.4 | loop fusion | flops 25165824 | bytes 43024384 | tf_op jit(solution)/shard_map/convert_element_type | solution.py:292
  501.5 11.0 %fusion.60 = bf16[2,128,1024]{2,1,0:T(8,128)(2,1)} fusion(bf16[1024,2,2,128]{0,3,2,1:T(8,128)(2,1)} %bitcast.396, f32[2,1024,1024,2]{2,1,3,0:T(8,128)} %copy-done, f32[2,2,1024]{2,1,0:T(2,128)S(1)} %log_add_fusion, pred[1024,1024]{0,1:T(8,128)(4,1)S(1)} %copy-done.8), kind=kOutput, calls=%fused_computation.120 | convolution fusion | flops 1090781184 | bytes 19415040 | tf_op jit(solution)/shard_map/grqk,qgrd->kgd/dot_general | solution.py:295
  512.7 14.0 %fusion.12 = (f32[2048]{0:T(1024)S(1)}, bf16[1024,2048]{1,0:T(8,128)(2,1)}, f32[1024,2048]{1,0:T(8,128)}) fusion(bf16[1024,2048]{1,0:T(8,128)(2,1)} %copy-done.20, f32[1024]{0:T(1024)S(1)} %copy-done.70, bf16[2048,1664]{0,1:T(8,128)(2,1)} %all-gather.4.cloned.1.call-done, bf16[1024,256]{0,1:T(8,128)(2,1)} %bitcast.415, bf16[1024,256]{0,1:T(8,128)(2,1)} %bitcast.399, ...), kind=kOutput, calls=%fused_computation.23 | convolution fusion | flops 4311742464 | bytes 23080960 | tf_op jit(solution)/shard_map/dot_general | solution.py:67
  558.0 16.5 %collective-permute-done.28 = bf16[2,128,2048]{2,1,0:T(8,128)(2,1)S(1)} collective-permute-done((bf16[2,128,2048]{2,1,0:T(8,128)(2,1)S(1)}, bf16[2,128,2048]{2,1,0:T(8,128)(2,1)S(1)}, u32[]{:S(2)}, u32[]{:S(2)}) %collective-permute-start.28) | collective-permute-done | bytes 1048608 | tf_op jit(solution)/shard_map/ppermute | solution.py:116
  578.3 8.7 %collective-permute-done.29 = bf16[128,2048]{1,0:T(8,128)(2,1)S(1)} collective-permute-done((bf16[128,2048]{1,0:T(8,128)(2,1)S(1)}, bf16[128,2048]{1,0:T(8,128)(2,1)S(1)}, u32[]{:S(2)}, u32[]{:S(2)}) %collective-permute-start.29) | collective-permute-done | bytes 524320 | tf_op jit(solution)/shard_map/ppermute | solution.py:120
  (478 shorter events, 286.2 us)
Async XLA Ops:
  7.2 93.6 %all-gather.4.cloned.1.call-start = ((), (), s32[]{:S(2)}) async-start(), calls=%async_computation.4 | async-start | bytes 7667712 | tf_op jit(solution)/shard_map/all_gather | solution.py:137
  15.0 228.2 %all-gather.6.cloned.1.call-start = ((), (), s32[]{:S(2)}) async-start(), calls=%async_computation.5 | async-start | bytes 10616832 | tf_op jit(solution)/shard_map/all_gather | solution.py:137
  19.8 265.5 %all-gather.8.cloned.1.call-start = ((), (), s32[]{:S(2)}) async-start(), calls=%async_computation.6 | async-start | bytes 10616832 | tf_op jit(solution)/shard_map/all_gather | solution.py:137
  26.3 486.2 %reduce-scatter.5.cloned.1.call-start = ((), (), s32[]{:S(2)}) async-start(), calls=%async_computation.7 | async-start | bytes 10616832 | tf_op jit(solution)/shard_map/reduce_scatter | solution.py:268
  35.8 24.5 %collective-permute-start.1 = (bf16[256,2048]{1,0:T(8,128)(2,1)S(1)}, bf16[256,2048]{1,0:T(8,128)(2,1)S(1)}, u32[]{:S(2)}, u32[]{:S(2)}) collective-permute-start(bf16[256,2048]{1,0:T(8,128)(2,1)S(1)} %pad_maximum_fusion.16), channel_id=1, source_target_pairs={{0,2},{2,0},{1,3},{3,1},{4,6},{6,4},{5,7},{7,5},{8,10},{10,8},{9,1... | collective-permute-start | bytes 3145736 | tf_op jit(solution)/shard_map/ppermute | solution.py:103
  74.7 23.0 %collective-permute-start.3 = (bf16[256,2048]{1,0:T(8,128)(2,1)S(1)}, bf16[256,2048]{1,0:T(8,128)(2,1)S(1)}, u32[]{:S(2)}, u32[]{:S(2)}) collective-permute-start(bf16[256,2048]{1,0:T(8,128)(2,1)S(1)} %pad_maximum_fusion.17), channel_id=1, source_target_pairs={{0,1},{1,0},{2,3},{3,2},{4,5},{5,4},{6,7},{7,6},{8,9},{9,8},{10,11... | collective-permute-start | bytes 3145736 | tf_op jit(solution)/shard_map/ppermute | solution.py:104
  137.9 26.1 %collective-permute-start.4 = (bf16[2,128,2048]{2,1,0:T(8,128)(2,1)S(1)}, bf16[2,128,2048]{2,1,0:T(8,128)(2,1)S(1)}, u32[]{:S(2)}, u32[]{:S(2)}) collective-permute-start(bf16[2,128,2048]{2,1,0:T(8,128)(2,1)S(1)} %bitcast.392), channel_id=1, source_target_pairs={{0,2},{2,0},{1,3},{3,1},{4,6},{6,4},{5,7},{7,5},{8,10},{10,8},{9,1... | collective-permute-start | bytes 3145736 | tf_op jit(solution)/shard_map/ppermute | solution.py:116
  139.3 57.3 %collective-permute-start.14 = (bf16[128,2048]{1,0:T(8,128)(2,1)S(1)}, bf16[128,2048]{1,0:T(8,128)(2,1)S(1)}, u32[]{:S(2)}, u32[]{:S(2)}) collective-permute-start(bf16[128,2048]{1,0:T(8,128)(2,1)S(1)} %get-tuple-element.131), channel_id=1, source_target_pairs={{0,2},{2,0},{1,3},{3,1},{4,6},{6,4},{5,7},{7,5},{8,10},{10,8},{9,1... | collective-permute-start | bytes 1572872 | tf_op jit(solution)/shard_map/ppermute | solution.py:100
  140.3 38.8 %collective-permute-start.12 = (bf16[128,2048]{1,0:T(8,128)(2,1)S(1)}, bf16[128,2048]{1,0:T(8,128)(2,1)S(1)}, u32[]{:S(2)}, u32[]{:S(2)}) collective-permute-start(bf16[128,2048]{1,0:T(8,128)(2,1)S(1)} %get-tuple-element.133), channel_id=1, source_target_pairs={{0,1},{1,0},{2,3},{3,2},{4,5},{5,4},{6,7},{7,6},{8,9},{9,8},{10,11... | collective-permute-start | bytes 1572872 | tf_op jit(solution)/shard_map/ppermute | solution.py:99
  141.8 35.8 %collective-permute-start.6 = (bf16[2,128,2048]{2,1,0:T(8,128)(2,1)S(1)}, bf16[2,128,2048]{2,1,0:T(8,128)(2,1)S(1)}, u32[]{:S(2)}, u32[]{:S(2)}) collective-permute-start(bf16[2,128,2048]{2,1,0:T(8,128)(2,1)S(1)} %bitcast.391), channel_id=1, source_target_pairs={{0,1},{1,0},{2,3},{3,2},{4,5},{5,4},{6,7},{7,6},{8,9},{9,8},{10,11... | collective-permute-start | bytes 3145736 | tf_op jit(solution)/shard_map/ppermute | solution.py:117
  179.2 33.1 %collective-permute-start.13 = (bf16[256,2048]{1,0:T(8,128)(2,1)S(1)}, bf16[256,2048]{1,0:T(8,128)(2,1)S(1)}, u32[]{:S(2)}, u32[]{:S(2)}) collective-permute-start(bf16[256,2048]{1,0:T(8,128)(2,1)S(1)} %pad_maximum_fusion.20), channel_id=1, source_target_pairs={{0,2},{2,0},{1,3},{3,1},{4,6},{6,4},{5,7},{7,5},{8,10},{10,8},{9,1... | collective-permute-start | bytes 3145736 | tf_op jit(solution)/shard_map/ppermute | solution.py:103
  196.7 27.8 %collective-permute-start.15 = (bf16[256,2048]{1,0:T(8,128)(2,1)S(1)}, bf16[256,2048]{1,0:T(8,128)(2,1)S(1)}, u32[]{:S(2)}, u32[]{:S(2)}) collective-permute-start(bf16[256,2048]{1,0:T(8,128)(2,1)S(1)} %pad_maximum_fusion.21), channel_id=1, source_target_pairs={{0,1},{1,0},{2,3},{3,2},{4,5},{5,4},{6,7},{7,6},{8,9},{9,8},{10,11... | collective-permute-start | bytes 3145736 | tf_op jit(solution)/shard_map/ppermute | solution.py:104
  213.6 25.4 %collective-permute-start.9 = (bf16[256,2048]{1,0:T(8,128)(2,1)S(1)}, bf16[256,2048]{1,0:T(8,128)(2,1)S(1)}, u32[]{:S(2)}, u32[]{:S(2)}) collective-permute-start(bf16[256,2048]{1,0:T(8,128)(2,1)S(1)} %pad_maximum_fusion.18), channel_id=1, source_target_pairs={{0,2},{2,0},{1,3},{3,1},{4,6},{6,4},{5,7},{7,5},{8,10},{10,8},{9,1... | collective-permute-start | bytes 3145736 | tf_op jit(solution)/shard_map/ppermute | solution.py:103
  294.0 218.6 %reduce-scatter.7.cloned.1.call-start = ((), (), s32[]{:S(2)}) async-start(), calls=%async_computation.8 | async-start | bytes 10616832 | tf_op jit(solution)/shard_map/reduce_scatter | solution.py:281
  332.0 50.3 %collective-permute-start.22 = (bf16[2,128,2048]{2,1,0:T(8,128)(2,1)}, bf16[2,128,2048]{2,1,0:T(8,128)(2,1)}, u32[]{:S(2)}, u32[]{:S(2)}) collective-permute-start(bf16[2,128,2048]{2,1,0:T(8,128)(2,1)} %bitcast.63), channel_id=1, source_target_pairs={{0,1},{1,0},{2,3},{3,2},{4,5},{5,4},{6,7},{7,6},{8,9},{9,8},{10,11... | collective-permute-start | bytes 3145736 | tf_op jit(solution)/shard_map/ppermute | solution.py:117
  333.5 45.0 %collective-permute-start.20 = (bf16[2,128,2048]{2,1,0:T(8,128)(2,1)}, bf16[2,128,2048]{2,1,0:T(8,128)(2,1)}, u32[]{:S(2)}, u32[]{:S(2)}) collective-permute-start(bf16[2,128,2048]{2,1,0:T(8,128)(2,1)} %bitcast.59), channel_id=1, source_target_pairs={{0,2},{2,0},{1,3},{3,1},{4,6},{6,4},{5,7},{7,5},{8,10},{10,8},{9,1... | collective-permute-start | bytes 3145736 | tf_op jit(solution)/shard_map/ppermute | solution.py:116
  344.7 42.1 %collective-permute-start.18 = (bf16[2,128,2048]{2,1,0:T(8,128)(2,1)}, bf16[2,128,2048]{2,1,0:T(8,128)(2,1)S(1)}, u32[]{:S(2)}, u32[]{:S(2)}) collective-permute-start(bf16[2,128,2048]{2,1,0:T(8,128)(2,1)} %bitcast.55), channel_id=1, source_target_pairs={{0,1},{1,0},{2,3},{3,2},{4,5},{5,4},{6,7},{7,6},{8,9},{9,8},{10,11... | collective-permute-start | bytes 3145736 | tf_op jit(solution)/shard_map/ppermute | solution.py:117
  345.6 39.7 %collective-permute-start.16 = (bf16[2,128,2048]{2,1,0:T(8,128)(2,1)}, bf16[2,128,2048]{2,1,0:T(8,128)(2,1)}, u32[]{:S(2)}, u32[]{:S(2)}) collective-permute-start(bf16[2,128,2048]{2,1,0:T(8,128)(2,1)} %bitcast.51), channel_id=1, source_target_pairs={{0,2},{2,0},{1,3},{3,1},{4,6},{6,4},{5,7},{7,5},{8,10},{10,8},{9,1... | collective-permute-start | bytes 3145736 | tf_op jit(solution)/shard_map/ppermute | solution.py:116
  404.1 144.7 %reduce-scatter.9.cloned.1.call-start = ((), (), s32[]{:S(2)}) async-start(), calls=%async_computation.9 | async-start | bytes 2359296 | tf_op jit(solution)/shard_map/reduce_scatter | solution.py:286
  413.7 26.0 %collective-permute-start.25 = (bf16[256,2048]{1,0:T(8,128)(2,1)S(1)}, bf16[256,2048]{1,0:T(8,128)(2,1)S(1)}, u32[]{:S(2)}, u32[]{:S(2)}) collective-permute-start(bf16[256,2048]{1,0:T(8,128)(2,1)S(1)} %pad_maximum_fusion.22), channel_id=1, source_target_pairs={{0,2},{2,0},{1,3},{3,1},{4,6},{6,4},{5,7},{7,5},{8,10},{10,8},{9,1... | collective-permute-start | bytes 3145736 | tf_op jit(solution)/shard_map/ppermute | solution.py:103
  414.5 24.1 %collective-permute-start.26 = (bf16[128,2048]{1,0:T(8,128)(2,1)S(1)}, bf16[128,2048]{1,0:T(8,128)(2,1)S(1)}, u32[]{:S(2)}, u32[]{:S(2)}) collective-permute-start(bf16[128,2048]{1,0:T(8,128)(2,1)S(1)} %get-tuple-element.128), channel_id=1, source_target_pairs={{0,2},{2,0},{1,3},{3,1},{4,6},{6,4},{5,7},{7,5},{8,10},{10,8},{9,1... | collective-permute-start | bytes 1572872 | tf_op jit(solution)/shard_map/ppermute | solution.py:100
  512.6 92.1 %reduce-scatter.11.cloned.1.call-start = ((), (), s32[]{:S(2)}) async-start(), calls=%async_computation.10 | async-start | bytes 5308416 | tf_op jit(solution)/shard_map/reduce_scatter | solution.py:342
  552.4 22.1 %collective-permute-start.28 = (bf16[2,128,2048]{2,1,0:T(8,128)(2,1)S(1)}, bf16[2,128,2048]{2,1,0:T(8,128)(2,1)S(1)}, u32[]{:S(2)}, u32[]{:S(2)}) collective-permute-start(bf16[2,128,2048]{2,1,0:T(8,128)(2,1)S(1)} %bitcast.394), channel_id=1, source_target_pairs={{0,2},{2,0},{1,3},{3,1},{4,6},{6,4},{5,7},{7,5},{8,10},{10,8},{9,1... | collective-permute-start | bytes 3145736 | tf_op jit(solution)/shard_map/ppermute | solution.py:116
  553.9 23.9 %collective-permute-start.30 = (bf16[2,128,2048]{2,1,0:T(8,128)(2,1)S(1)}, bf16[2,128,2048]{2,1,0:T(8,128)(2,1)S(1)}, u32[]{:S(2)}, u32[]{:S(2)}) collective-permute-start(bf16[2,128,2048]{2,1,0:T(8,128)(2,1)S(1)} %bitcast.393), channel_id=1, source_target_pairs={{0,1},{1,0},{2,3},{3,2},{4,5},{5,4},{6,7},{7,6},{8,9},{9,8},{10,11... | collective-permute-start | bytes 3145736 | tf_op jit(solution)/shard_map/ppermute | solution.py:117
  (105 other events, 949.4 us)
Sparse Core Ops, SparseCore 0:
  15.2 72.2 all-gather.3
  89.6 89.2 all-gather.5
  180.5 89.3 all-gather.7
  294.1 100.0 reduce-scatter.4
  404.2 99.3 reduce-scatter.6
  512.7 36.1 reduce-scatter.8
  551.2 53.4 reduce-scatter.10

commit v10 on v9

--- a/solution.py
+++ b/solution.py
@@ -250,22 +250,25 @@
         up = gate_up[:, ff_half:]
         sigmoid = jax.nn.sigmoid(gate)
         hidden = (gate * sigmoid * up).astype(jnp.bfloat16)
-        part = times_transposed(hidden, down_wt)
-        down_partial = part if down_partial is None else down_partial + part
         d_hidden = jnp.dot(grad_rows, down_wt, preferred_element_type=jnp.float32)
         d_up = (d_hidden * gate * sigmoid).astype(jnp.bfloat16)
         d_gate = (d_hidden * up * sigmoid * (1.0 + gate * (1.0 - sigmoid))).astype(jnp.bfloat16)
         d_gate_up = jnp.concatenate([d_gate, d_up], axis=1)
-        part = times_transposed(d_gate_up, gate_up_w)
-        d_mlp_partial = part if d_mlp_partial is None else d_mlp_partial + part
+        if h == 1:
+            d_mlp_partial = d_mlp_partial + times_transposed(d_gate_up, gate_up_w)
+            down_partial = down_partial + times_transposed(hidden, down_wt)
         g_down_t = contract_rows(grad_rows, hidden)
         g_gate_up = contract_rows(mlp_all, d_gate_up)
         joined = jnp.concatenate(
             [g_gate_up.astype(jnp.bfloat16), g_down_t.astype(jnp.bfloat16)], axis=1
         )
         if h == 0:
-            joined, mlp_sets[1] = lax.optimization_barrier((joined, mlp_sets[1]))
+            joined, mlp_sets[1], hidden, d_gate_up = lax.optimization_barrier(
+                (joined, mlp_sets[1], hidden, d_gate_up)
+            )
             mlp_grads.append(lax.psum_scatter(joined, "wide", scatter_dimension=0, tiled=True))
+            d_mlp_partial = times_transposed(d_gate_up, gate_up_w)
+            down_partial = times_transposed(hidden, down_wt)
         else:
             last_joined = joined
 
@@ -278,12 +281,13 @@
     )
     p_probs = jnp.where(allowed, jnp.exp(p_scores - log_totals[..., None]), 0.0)
     d_resid_low, last_joined = lax.optimization_barrier((d_resid.astype(jnp.bfloat16), last_joined))
-    mlp_grads.append(lax.psum_scatter(last_joined, "wide", scatter_dimension=0, tiled=True))
     branch_rows = narrow_gather(d_resid_low, relative)
     out_grad = contract_rows(branch_rows, attended).astype(jnp.bfloat16)
-    mlp_grads, out_grad = lax.optimization_barrier((mlp_grads, out_grad))
-    mlp_grads = [split_cols(g.astype(jnp.float32), [2 * ff_half, ff_half]) for g in mlp_grads]
-    g_out_t = lax.psum_scatter(out_grad, "wide", scatter_dimension=0, tiled=True).astype(jnp.float32)
+    mlp_grads.append(
+        lax.psum_scatter(
+            jnp.concatenate([last_joined, out_grad], axis=1), "wide", scatter_dimension=0, tiled=True
+        )
+    )
     d_attended = jnp.dot(branch_rows, out_wt, preferred_element_type=jnp.float32).astype(jnp.bfloat16)
     d_mixed = d_attended.reshape(rows_group, groups_here, repeat, HD)
 
@@ -337,7 +341,10 @@
     qkv_grad = jnp.concatenate(
         [contract_rows(normed_all, d_qkv).astype(jnp.bfloat16), gain_block.astype(jnp.bfloat16)], axis=1
     )
-    g_out_t, qkv_grad = lax.optimization_barrier((g_out_t, qkv_grad))
+    mlp_grads, qkv_grad = lax.optimization_barrier((mlp_grads, qkv_grad))
+    mlp_grads = [g.astype(jnp.float32) for g in mlp_grads]
+    g_out_t = mlp_grads[1][:, 3 * ff_half :]
+    mlp_grads = [split_cols(g[:, : 3 * ff_half], [2 * ff_half, ff_half]) for g in mlp_grads]
     g_qkv, g_gains = split_cols(
         lax.psum_scatter(qkv_grad, "wide", scatter_dimension=0, tiled=True).astype(jnp.float32),
         [q_cols + 2 * kv_cols, 128],

time: 622 us -> 669 us (1.076)
  waiting for transfers between devices: 237 us -> 260 us
  local copies, waits for them, and re-layouts: 73.6 us -> 89.2 us
  other arithmetic: 83 us -> 95.1 us
    reduce_scatter x2 -> x1, waiting for transfers between devices: 4.51 us -> 39.9 us  [shards_body(): lax.psum_scatter(jnp.concatenate([last_joined, out_grad], axis=1), 'wide'...]
    concatenate x0 -> x2, other arithmetic: none -> 16.7 us  [the longest x1 14.5 us: shards_body(): jnp.concatenate([last_joined, out_grad], axis=1)]
    unnamed x227 -> x208, local copies, waits for them, and re-layouts: 31.7 us -> 40.8 us
    concatenate x2, other arithmetic: 23 us -> 14.1 us  [shards_body(): jnp.concatenate([g_gate_up.astype(jnp.bfloat16), g_down_t.astype(jnp.bflo...]
  transfers between devices with their start and end apart: 41 -> 40, of which waited for: 26 -> 26; matrix products, arithmetic and copies ran while one was open for 47% -> 46% of each run, Pallas kernels for 0% -> 0%
where the time goes in v10:
time: 669 us; the launch traced here: 664 us
  waiting for transfers between devices  260 us (39%)
  matrix products  162 us (24%)
  other arithmetic  95.1 us (14%)
  local copies, waits for them, and re-layouts  89.2 us (13%)
  starting transfers between devices  41.8 us (6%)
  between operations  16.3 us (2%)
    dot_general x6, matrix products, times_transposed(): lax.dot_general(left, right, (((1,), (1,)), ((), ())), preferred_element_...  43.5 us
    ppermute x4, waiting for transfers between devices, narrow_scatter(): a_got = lax.ppermute(blocks[2:4].astype(jnp.bfloat16), 'narrow', YPERM)  41.3 us
    ppermute x4, waiting for transfers between devices, narrow_gather(): a_pair_y = lax.ppermute(a_pair, 'narrow', YPERM)  41.3 us
    ppermute x4, waiting for transfers between devices, narrow_gather(): b_pair_x = lax.ppermute(b_pair, 'narrow', XPERM)  41.1 us
    unnamed x208, local copies, waits for them, and re-layouts  40.8 us
    reduce_scatter x1, waiting for transfers between devices, shards_body(): lax.psum_scatter(jnp.concatenate([last_joined, out_grad], axis=1), 'wide'...  39.9 us
    dot_general x6, matrix products, contract_rows(): lax.dot_general(left, right, (((0,), (0,)), ((), ())), preferred_element_...  38.1 us
    ppermute x4, waiting for transfers between devices, narrow_gather(): b_y = lax.ppermute(b, 'narrow', YPERM)  35.9 us
  transfers between devices with their start and end apart: 40, of which 26 were waited for; matrix products, arithmetic and copies ran while one was open for 46% of the time, Pallas kernels for 0%

profile of v10, /device:TPU:0, one launch (start us, length us, event | category | flops | bytes accessed | tf_op | source)
XLA Modules:
  0.0 663.8 jit_solution(525854566096869746)
XLA Ops:
  37.7 17.8 %collective-permute-done.1 = bf16[256,2048]{1,0:T(8,128)(2,1)S(1)} collective-permute-done((bf16[256,2048]{1,0:T(8,128)(2,1)S(1)}, bf16[256,2048]{1,0:T(8,128)(2,1)S(1)}, u32[]{:S(2)}, u32[]{:S(2)}) %collective-permute-start.1) | collective-permute-done | bytes 1048608 | tf_op jit(solution)/shard_map/ppermute | solution.py:103
  59.0 10.9 %collective-permute-done.2 = bf16[128,2048]{1,0:T(8,128)(2,1)S(1)} collective-permute-done((bf16[128,2048]{1,0:T(8,128)(2,1)S(1)}, bf16[128,2048]{1,0:T(8,128)(2,1)S(1)}, u32[]{:S(2)}, u32[]{:S(2)}) %collective-permute-start.2) | collective-permute-done | bytes 524320 | tf_op jit(solution)/shard_map/ppermute | solution.py:100
  75.7 17.2 %collective-permute-done.3 = bf16[256,2048]{1,0:T(8,128)(2,1)S(1)} collective-permute-done((bf16[256,2048]{1,0:T(8,128)(2,1)S(1)}, bf16[256,2048]{1,0:T(8,128)(2,1)S(1)}, u32[]{:S(2)}, u32[]{:S(2)}) %collective-permute-start.3) | collective-permute-done | bytes 1048608 | tf_op jit(solution)/shard_map/ppermute | solution.py:104
  156.6 12.6 %collective-permute-done.4 = bf16[2,128,2048]{2,1,0:T(8,128)(2,1)} collective-permute-done((bf16[2,128,2048]{2,1,0:T(8,128)(2,1)}, bf16[2,128,2048]{2,1,0:T(8,128)(2,1)}, u32[]{:S(2)}, u32[]{:S(2)}) %collective-permute-start.4) | collective-permute-done | bytes 1048608 | tf_op jit(solution)/shard_map/ppermute | solution.py:116
  172.1 11.1 %collective-permute-done.6 = bf16[2,128,2048]{2,1,0:T(8,128)(2,1)S(1)} collective-permute-done((bf16[2,128,2048]{2,1,0:T(8,128)(2,1)}, bf16[2,128,2048]{2,1,0:T(8,128)(2,1)S(1)}, u32[]{:S(2)}, u32[]{:S(2)}) %collective-permute-start.6) | collective-permute-done | bytes 1048608 | tf_op jit(solution)/shard_map/ppermute | solution.py:117
  205.8 12.1 %collective-permute-done.13 = bf16[256,2048]{1,0:T(8,128)(2,1)S(1)} collective-permute-done((bf16[256,2048]{1,0:T(8,128)(2,1)S(1)}, bf16[256,2048]{1,0:T(8,128)(2,1)S(1)}, u32[]{:S(2)}, u32[]{:S(2)}) %collective-permute-start.13) | collective-permute-done | bytes 1048608 | tf_op jit(solution)/shard_map/ppermute | solution.py:103
  221.4 10.2 %collective-permute-done.15 = bf16[256,2048]{1,0:T(8,128)(2,1)S(1)} collective-permute-done((bf16[256,2048]{1,0:T(8,128)(2,1)S(1)}, bf16[256,2048]{1,0:T(8,128)(2,1)S(1)}, u32[]{:S(2)}, u32[]{:S(2)}) %collective-permute-start.15) | collective-permute-done | bytes 1048608 | tf_op jit(solution)/shard_map/ppermute | solution.py:104
  234.6 11.3 %collective-permute-done.9 = bf16[256,2048]{1,0:T(8,128)(2,1)S(1)} collective-permute-done((bf16[256,2048]{1,0:T(8,128)(2,1)S(1)}, bf16[256,2048]{1,0:T(8,128)(2,1)S(1)}, u32[]{:S(2)}, u32[]{:S(2)}) %collective-permute-start.9) | collective-permute-done | bytes 1048608 | tf_op jit(solution)/shard_map/ppermute | solution.py:103
  249.7 10.4 %fusion.19 = f32[1024,1536]{0,1:T(8,128)S(1)} fusion(bf16[1024,2048]{1,0:T(8,128)(2,1)} %constant_dynamic-update-slice_fusion.19, bf16[2048,2304]{0,1:T(8,128)(2,1)} %all-gather.6.cloned.1.call-done), kind=kOutput, calls=%fused_computation.32 | convolution fusion | flops 6442450944 | bytes 16777216 | tf_op jit(solution)/shard_map/dot_general | solution.py:248
  272.5 10.6 %convolution_convert_fusion.1 = bf16[2048,1536]{0,1:T(8,128)(2,1)S(1)} fusion(bf16[1024,2048]{1,0:T(8,128)(2,1)} %constant_dynamic-update-slice_fusion.19, bf16[1024,768]{0,1:T(8,128)(2,1)S(1)} %get-tuple-element.86, bf16[1024,768]{0,1:T(8,128)(2,1)S(1)} %get-tuple-element.85), kind=kOutput, calls=%fused_computation.29 | convolution fusion | flops 6451888128 | bytes 13631488 | tf_op jit(solution)/shard_map/dot_general | solution.py:61
  283.1 11.9 %pad_maximum_fusion.1 = bf16[2048,2304]{0,1:T(8,128)(2,1)} fusion(bf16[2048,768]{0,1:T(8,128)(2,1)S(1)} %convolution_convert_fusion.4, bf16[2048,1536]{0,1:T(8,128)(2,1)S(1)} %convolution_convert_fusion.1), kind=kLoop, calls=%fused_computation.17 | loop fusion | flops 18874368 | bytes 18874368 | tf_op jit(solution)/shard_map/concatenate | solution.py:262
  303.8 10.2 %fusion.162 = f32[1024,1536]{0,1:T(8,128)S(1)} fusion(bf16[1024,2048]{1,0:T(8,128)(2,1)} %constant_dynamic-update-slice_fusion.19, bf16[2048,1536]{0,1:T(8,128)(2,1)} %slice.573), kind=kOutput, calls=%fused_computation.378 | convolution fusion | flops 6442450944 | bytes 16777216 | tf_op jit(solution)/shard_map/dot_general | solution.py:248
  327.4 11.4 %fusion.160 = (bf16[1024,2048]{1,0:T(8,128)(2,1)S(1)}, f32[1024,2048]{1,0:T(8,128)}) fusion(f32[1024,2048]{1,0:T(8,128)S(1)} %fusion.48, bf16[1024,1536]{0,1:T(8,128)(2,1)S(1)} %copy-done.27, bf16[2048,2304]{0,1:T(8,128)(2,1)} %all-gather.6.cloned.1.call-done), kind=kOutput, calls=%fused_computation.376 | convolution fusion | flops 6446645248 | bytes 30408704 | tf_op jit(solution)/shard_map/dot_general | solution.py:67
  360.9 9.8 %convolution_convert_fusion = bf16[2048,1536]{0,1:T(8,128)(2,1)S(1)} fusion(bf16[1024,2048]{1,0:T(8,128)(2,1)} %constant_dynamic-update-slice_fusion.19, bf16[1024,768]{0,1:T(8,128)(2,1)} %copy-done.71, bf16[1024,768]{0,1:T(8,128)(2,1)S(1)} %copy-done.70), kind=kOutput, calls=%fused_computation.28 | convolution fusion | flops 6451888128 | bytes 13631488 | tf_op jit(solution)/shard_map/dot_general | solution.py:61
  378.1 11.4 %collective-permute-done.16 = bf16[2,128,2048]{2,1,0:T(8,128)(2,1)S(1)} collective-permute-done((bf16[2,128,2048]{2,1,0:T(8,128)(2,1)S(1)}, bf16[2,128,2048]{2,1,0:T(8,128)(2,1)S(1)}, u32[]{:S(2)}, u32[]{:S(2)}) %collective-permute-start.16) | collective-permute-done | bytes 1048608 | tf_op jit(solution)/shard_map/ppermute | solution.py:116
  408.7 8.7 %collective-permute-done.24 = bf16[128,2048]{1,0:T(8,128)(2,1)S(1)} collective-permute-done((bf16[128,2048]{1,0:T(8,128)(2,1)S(1)}, bf16[128,2048]{1,0:T(8,128)(2,1)S(1)}, u32[]{:S(2)}, u32[]{:S(2)}) %collective-permute-start.24) | collective-permute-done | bytes 524320 | tf_op jit(solution)/shard_map/ppermute | solution.py:99
  419.6 23.8 %collective-permute-done.26 = bf16[128,2048]{1,0:T(8,128)(2,1)S(1)} collective-permute-done((bf16[128,2048]{1,0:T(8,128)(2,1)S(1)}, bf16[128,2048]{1,0:T(8,128)(2,1)S(1)}, u32[]{:S(2)}, u32[]{:S(2)}) %collective-permute-start.26) | collective-permute-done | bytes 524320 | tf_op jit(solution)/shard_map/ppermute | solution.py:100
  444.7 13.7 %collective-permute-done.27 = bf16[256,2048]{1,0:T(8,128)(2,1)S(1)} collective-permute-done((bf16[256,2048]{1,0:T(8,128)(2,1)S(1)}, bf16[256,2048]{1,0:T(8,128)(2,1)S(1)}, u32[]{:S(2)}, u32[]{:S(2)}) %collective-permute-start.27) | collective-permute-done | bytes 1048608 | tf_op jit(solution)/shard_map/ppermute | solution.py:104
  460.9 14.5 %pad_maximum_fusion = bf16[2048,2816]{0,1:T(8,128)(2,1)} fusion(bf16[2048,512]{0,1:T(8,128)(2,1)S(1)} %convolution_convert_fusion.5, bf16[2048,2304]{0,1:T(8,128)(2,1)S(1)} %pad_maximum_fusion.2), kind=kLoop, calls=%fused_computation.16 | loop fusion | flops 23068672 | bytes 23068672 | tf_op jit(solution)/shard_map/concatenate | solution.py:288
  481.5 12.9 %fusion = (f32[2,2,1024]{2,1,0:T(2,128)S(1)}, f32[2,1024,1024,2]{2,1,3,0:T(8,128)}) fusion(f32[2,1024,1024,2]{2,1,3,0:T(8,128)} %copy-done, f32[2,2,1024]{2,1,0:T(2,128)S(1)} %log_add_fusion, pred[1024,1024]{0,1:T(8,128)(4,1)S(1)} %copy-done.8, bf16[1024,2,128,1]{0,2,3,1:T(8,128)(2,1)S(1)} %bitcast.384, bf16[1024,2,2,128]{0,3,2,1:T(8,128)(2,1)S(1)} %bitcast.395), kind=kOutput, calls=%fused_computation.2 | convolution fusion | flops 1094709248 | bytes 36208640 | tf_op jit(solution)/shard_map/qgrd,kgd->grqk/dot_general | solution.py:294
  494.4 12.5 %fusion.2 = bf16[2,2,1024,1024]{2,3,1,0:T(8,128)(2,1)S(1)} fusion(f32[2,1024,1024,2]{2,1,3,0:T(8,128)} %get-tuple-element.188, f32[2,1024,1024,2]{2,1,3,0:T(8,128)} %copy-done, f32[2,2,1024]{2,1,0:T(2,128)S(1)} %get-tuple-element.187, f32[2,2,1024]{2,1,0:T(2,128)S(1)} %log_add_fusion, pred[1024,1024]{0,1:T(8,128)(4,1)S(1)} %copy-done.8), kind=kLoop, calls=%fused_computation.4 | loop fusion | flops 25165824 | bytes 43024384 | tf_op jit(solution)/shard_map/convert_element_type | solution.py:296
  525.8 10.3 %fusion.12 = (f32[2048]{0:T(1024)S(1)}, bf16[1024,2048]{1,0:T(8,128)(2,1)}, f32[1024,2048]{1,0:T(8,128)}) fusion(bf16[1024,2048]{1,0:T(8,128)(2,1)S(1)} %copy-done.21, f32[1024]{0:T(1024)S(1)} %copy-done.66, bf16[2048,1664]{0,1:T(8,128)(2,1)} %all-gather.4.cloned.1.call-done, bf16[1024,256]{0,1:T(8,128)(2,1)S(1)} %bitcast.415, ...), kind=kOutput, calls=%fused_computation.24 | convolution fusion | flops 4311742464 | bytes 23080960 | tf_op jit(solution)/shard_map/dot_general | solution.py:67
  555.4 39.9 %reduce-scatter.6.cloned.1.call-done = bf16[256,2816]{0,1:T(8,128)(2,1)} async-done(((bf16[2048,2816]{0,1:T(8,128)(2,1)}), bf16[256,2816]{0,1:T(8,128)(2,1)}) %reduce-scatter.6.cloned.1.call-update) | async-done | bytes 1441808 | tf_op jit(solution)/shard_map/reduce_scatter | solution.py:287
  602.8 17.3 %collective-permute-done.28 = bf16[2,128,2048]{2,1,0:T(8,128)(2,1)S(1)} collective-permute-done((bf16[2,128,2048]{2,1,0:T(8,128)(2,1)S(1)}, bf16[2,128,2048]{2,1,0:T(8,128)(2,1)S(1)}, u32[]{:S(2)}, u32[]{:S(2)}) %collective-permute-start.28) | collective-permute-done | bytes 1048608 | tf_op jit(solution)/shard_map/ppermute | solution.py:116
  (458 shorter events, 315.0 us)
Async XLA Ops:
  7.2 88.7 %all-gather.4.cloned.1.call-start = ((), (), s32[]{:S(2)}) async-start(), calls=%async_computation.3 | async-start | bytes 7667712 | tf_op jit(solution)/shard_map/all_gather | solution.py:137
  15.1 234.6 %all-gather.6.cloned.1.call-start = ((), (), s32[]{:S(2)}) async-start(), calls=%async_computation.4 | async-start | bytes 10616832 | tf_op jit(solution)/shard_map/all_gather | solution.py:137
  25.5 269.5 %all-gather.8.cloned.1.call-start = ((), (), s32[]{:S(2)}) async-start(), calls=%async_computation.5 | async-start | bytes 10616832 | tf_op jit(solution)/shard_map/all_gather | solution.py:137
  31.1 24.5 %collective-permute-start.1 = (bf16[256,2048]{1,0:T(8,128)(2,1)S(1)}, bf16[256,2048]{1,0:T(8,128)(2,1)S(1)}, u32[]{:S(2)}, u32[]{:S(2)}) collective-permute-start(bf16[256,2048]{1,0:T(8,128)(2,1)S(1)} %pad_maximum_fusion.15), channel_id=1, source_target_pairs={{0,2},{2,0},{1,3},{3,1},{4,6},{6,4},{5,7},{7,5},{8,10},{10,8},{9,1... | collective-permute-start | bytes 3145736 | tf_op jit(solution)/shard_map/ppermute | solution.py:103
  70.0 22.9 %collective-permute-start.3 = (bf16[256,2048]{1,0:T(8,128)(2,1)S(1)}, bf16[256,2048]{1,0:T(8,128)(2,1)S(1)}, u32[]{:S(2)}, u32[]{:S(2)}) collective-permute-start(bf16[256,2048]{1,0:T(8,128)(2,1)S(1)} %pad_maximum_fusion.16), channel_id=1, source_target_pairs={{0,1},{1,0},{2,3},{3,2},{4,5},{5,4},{6,7},{7,6},{8,9},{9,8},{10,11... | collective-permute-start | bytes 3145736 | tf_op jit(solution)/shard_map/ppermute | solution.py:104
  142.9 26.4 %collective-permute-start.4 = (bf16[2,128,2048]{2,1,0:T(8,128)(2,1)}, bf16[2,128,2048]{2,1,0:T(8,128)(2,1)}, u32[]{:S(2)}, u32[]{:S(2)}) collective-permute-start(bf16[2,128,2048]{2,1,0:T(8,128)(2,1)} %bitcast.41), channel_id=1, source_target_pairs={{0,2},{2,0},{1,3},{3,1},{4,6},{6,4},{5,7},{7,5},{8,10},{10,8},{9,1... | collective-permute-start | bytes 3145736 | tf_op jit(solution)/shard_map/ppermute | solution.py:116
  145.1 57.1 %collective-permute-start.14 = (bf16[128,2048]{1,0:T(8,128)(2,1)S(1)}, bf16[128,2048]{1,0:T(8,128)(2,1)}, u32[]{:S(2)}, u32[]{:S(2)}) collective-permute-start(bf16[128,2048]{1,0:T(8,128)(2,1)S(1)} %get-tuple-element.131), channel_id=1, source_target_pairs={{0,2},{2,0},{1,3},{3,1},{4,6},{6,4},{5,7},{7,5},{8,10},{10,8},{9,1... | collective-permute-start | bytes 1572872 | tf_op jit(solution)/shard_map/ppermute | solution.py:100
  145.9 38.1 %collective-permute-start.12 = (bf16[128,2048]{1,0:T(8,128)(2,1)S(1)}, bf16[128,2048]{1,0:T(8,128)(2,1)}, u32[]{:S(2)}, u32[]{:S(2)}) collective-permute-start(bf16[128,2048]{1,0:T(8,128)(2,1)S(1)} %get-tuple-element.133), channel_id=1, source_target_pairs={{0,1},{1,0},{2,3},{3,2},{4,5},{5,4},{6,7},{7,6},{8,9},{9,8},{10,11... | collective-permute-start | bytes 1572872 | tf_op jit(solution)/shard_map/ppermute | solution.py:99
  153.2 402.1 %reduce-scatter.4.cloned.1.call-start = ((), (), s32[]{:S(2)}) async-start(), calls=%async_computation.6 | async-start | bytes 10616832 | tf_op jit(solution)/shard_map/reduce_scatter | solution.py:269
  153.3 29.9 %collective-permute-start.6 = (bf16[2,128,2048]{2,1,0:T(8,128)(2,1)}, bf16[2,128,2048]{2,1,0:T(8,128)(2,1)S(1)}, u32[]{:S(2)}, u32[]{:S(2)}) collective-permute-start(bf16[2,128,2048]{2,1,0:T(8,128)(2,1)} %bitcast.391), channel_id=1, source_target_pairs={{0,1},{1,0},{2,3},{3,2},{4,5},{5,4},{6,7},{7,6},{8,9},{9,8},{10,11... | collective-permute-start | bytes 3145736 | tf_op jit(solution)/shard_map/ppermute | solution.py:117
  185.1 32.8 %collective-permute-start.13 = (bf16[256,2048]{1,0:T(8,128)(2,1)S(1)}, bf16[256,2048]{1,0:T(8,128)(2,1)S(1)}, u32[]{:S(2)}, u32[]{:S(2)}) collective-permute-start(bf16[256,2048]{1,0:T(8,128)(2,1)S(1)} %pad_maximum_fusion.17), channel_id=1, source_target_pairs={{0,2},{2,0},{1,3},{3,1},{4,6},{6,4},{5,7},{7,5},{8,10},{10,8},{9,1... | collective-permute-start | bytes 3145736 | tf_op jit(solution)/shard_map/ppermute | solution.py:103
  203.3 28.2 %collective-permute-start.15 = (bf16[256,2048]{1,0:T(8,128)(2,1)S(1)}, bf16[256,2048]{1,0:T(8,128)(2,1)S(1)}, u32[]{:S(2)}, u32[]{:S(2)}) collective-permute-start(bf16[256,2048]{1,0:T(8,128)(2,1)S(1)} %pad_maximum_fusion.18), channel_id=1, source_target_pairs={{0,1},{1,0},{2,3},{3,2},{4,5},{5,4},{6,7},{7,6},{8,9},{9,8},{10,11... | collective-permute-start | bytes 3145736 | tf_op jit(solution)/shard_map/ppermute | solution.py:104
  218.6 27.3 %collective-permute-start.9 = (bf16[256,2048]{1,0:T(8,128)(2,1)S(1)}, bf16[256,2048]{1,0:T(8,128)(2,1)S(1)}, u32[]{:S(2)}, u32[]{:S(2)}) collective-permute-start(bf16[256,2048]{1,0:T(8,128)(2,1)S(1)} %pad_maximum_fusion.19), channel_id=1, source_target_pairs={{0,2},{2,0},{1,3},{3,1},{4,6},{6,4},{5,7},{7,5},{8,10},{10,8},{9,1... | collective-permute-start | bytes 3145736 | tf_op jit(solution)/shard_map/ppermute | solution.py:103
  303.7 291.5 %reduce-scatter.6.cloned.1.call-start = ((), (), s32[]{:S(2)}) async-start(), calls=%async_computation.7 | async-start | bytes 12976128 | tf_op jit(solution)/shard_map/reduce_scatter | solution.py:287
  340.3 35.5 %collective-permute-start.22 = (bf16[2,128,2048]{2,1,0:T(8,128)(2,1)}, bf16[2,128,2048]{2,1,0:T(8,128)(2,1)}, u32[]{:S(2)}, u32[]{:S(2)}) collective-permute-start(bf16[2,128,2048]{2,1,0:T(8,128)(2,1)} %bitcast.63), channel_id=1, source_target_pairs={{0,1},{1,0},{2,3},{3,2},{4,5},{5,4},{6,7},{7,6},{8,9},{9,8},{10,11... | collective-permute-start | bytes 3145736 | tf_op jit(solution)/shard_map/ppermute | solution.py:117
  341.2 32.0 %collective-permute-start.20 = (bf16[2,128,2048]{2,1,0:T(8,128)(2,1)}, bf16[2,128,2048]{2,1,0:T(8,128)(2,1)}, u32[]{:S(2)}, u32[]{:S(2)}) collective-permute-start(bf16[2,128,2048]{2,1,0:T(8,128)(2,1)} %bitcast.59), channel_id=1, source_target_pairs={{0,2},{2,0},{1,3},{3,1},{4,6},{6,4},{5,7},{7,5},{8,10},{10,8},{9,1... | collective-permute-start | bytes 3145736 | tf_op jit(solution)/shard_map/ppermute | solution.py:116
  351.2 38.6 %collective-permute-start.18 = (bf16[2,128,2048]{2,1,0:T(8,128)(2,1)S(1)}, bf16[2,128,2048]{2,1,0:T(8,128)(2,1)S(1)}, u32[]{:S(2)}, u32[]{:S(2)}) collective-permute-start(bf16[2,128,2048]{2,1,0:T(8,128)(2,1)S(1)} %bitcast.390), channel_id=1, source_target_pairs={{0,1},{1,0},{2,3},{3,2},{4,5},{5,4},{6,7},{7,6},{8,9},{9,8},{10,11... | collective-permute-start | bytes 3145736 | tf_op jit(solution)/shard_map/ppermute | solution.py:117
  352.8 36.7 %collective-permute-start.16 = (bf16[2,128,2048]{2,1,0:T(8,128)(2,1)S(1)}, bf16[2,128,2048]{2,1,0:T(8,128)(2,1)S(1)}, u32[]{:S(2)}, u32[]{:S(2)}) collective-permute-start(bf16[2,128,2048]{2,1,0:T(8,128)(2,1)S(1)} %bitcast.392), channel_id=1, source_target_pairs={{0,2},{2,0},{1,3},{3,1},{4,6},{6,4},{5,7},{7,5},{8,10},{10,8},{9,1... | collective-permute-start | bytes 3145736 | tf_op jit(solution)/shard_map/ppermute | solution.py:116
  374.8 21.1 %collective-permute-start.21 = (bf16[128,2048]{1,0:T(8,128)(2,1)S(1)}, bf16[128,2048]{1,0:T(8,128)(2,1)S(1)}, u32[]{:S(2)}, u32[]{:S(2)}) collective-permute-start(bf16[128,2048]{1,0:T(8,128)(2,1)S(1)} %fusion.84), channel_id=1, source_target_pairs={{0,1},{1,0},{2,3},{3,2},{4,5},{5,4},{6,7},{7,6},{8,9},{9,8},{10,11... | collective-permute-start | bytes 1572872 | tf_op jit(solution)/shard_map/ppermute | solution.py:120
  417.5 27.0 %collective-permute-start.25 = (bf16[256,2048]{1,0:T(8,128)(2,1)S(1)}, bf16[256,2048]{1,0:T(8,128)(2,1)S(1)}, u32[]{:S(2)}, u32[]{:S(2)}) collective-permute-start(bf16[256,2048]{1,0:T(8,128)(2,1)S(1)} %pad_maximum_fusion.21), channel_id=1, source_target_pairs={{0,2},{2,0},{1,3},{3,1},{4,6},{6,4},{5,7},{7,5},{8,10},{10,8},{9,1... | collective-permute-start | bytes 3145736 | tf_op jit(solution)/shard_map/ppermute | solution.py:103
  419.1 24.4 %collective-permute-start.26 = (bf16[128,2048]{1,0:T(8,128)(2,1)S(1)}, bf16[128,2048]{1,0:T(8,128)(2,1)S(1)}, u32[]{:S(2)}, u32[]{:S(2)}) collective-permute-start(bf16[128,2048]{1,0:T(8,128)(2,1)S(1)} %get-tuple-element.128), channel_id=1, source_target_pairs={{0,2},{2,0},{1,3},{3,1},{4,6},{6,4},{5,7},{7,5},{8,10},{10,8},{9,1... | collective-permute-start | bytes 1572872 | tf_op jit(solution)/shard_map/ppermute | solution.py:100
  475.4 175.4 %reduce-scatter.8.cloned.1.call-start = ((), (), s32[]{:S(2)}) async-start(), calls=%async_computation.8 | async-start | bytes 5308416 | tf_op jit(solution)/shard_map/reduce_scatter | solution.py:349
  597.0 23.1 %collective-permute-start.28 = (bf16[2,128,2048]{2,1,0:T(8,128)(2,1)S(1)}, bf16[2,128,2048]{2,1,0:T(8,128)(2,1)S(1)}, u32[]{:S(2)}, u32[]{:S(2)}) collective-permute-start(bf16[2,128,2048]{2,1,0:T(8,128)(2,1)S(1)} %bitcast.394), channel_id=1, source_target_pairs={{0,2},{2,0},{1,3},{3,1},{4,6},{6,4},{5,7},{7,5},{8,10},{10,8},{9,1... | collective-permute-start | bytes 3145736 | tf_op jit(solution)/shard_map/ppermute | solution.py:116
  598.5 23.7 %collective-permute-start.30 = (bf16[2,128,2048]{2,1,0:T(8,128)(2,1)S(1)}, bf16[2,128,2048]{2,1,0:T(8,128)(2,1)S(1)}, u32[]{:S(2)}, u32[]{:S(2)}) collective-permute-start(bf16[2,128,2048]{2,1,0:T(8,128)(2,1)S(1)} %bitcast.393), channel_id=1, source_target_pairs={{0,1},{1,0},{2,3},{3,2},{4,5},{5,4},{6,7},{7,6},{8,9},{9,8},{10,11... | collective-permute-start | bytes 3145736 | tf_op jit(solution)/shard_map/ppermute | solution.py:117
  (95 other events, 758.0 us)
Sparse Core Ops, SparseCore 0:
  15.2 72.1 all-gather.3
  89.6 89.3 all-gather.5
  181.1 89.3 all-gather.7
  303.8 99.5 reduce-scatter.3
  475.5 119.6 reduce-scatter.5
  597.4 53.3 reduce-scatter.7

commit v11 on v10

--- a/solution.py
+++ b/solution.py
@@ -250,25 +250,22 @@
         up = gate_up[:, ff_half:]
         sigmoid = jax.nn.sigmoid(gate)
         hidden = (gate * sigmoid * up).astype(jnp.bfloat16)
+        part = times_transposed(hidden, down_wt)
+        down_partial = part if down_partial is None else down_partial + part
         d_hidden = jnp.dot(grad_rows, down_wt, preferred_element_type=jnp.float32)
         d_up = (d_hidden * gate * sigmoid).astype(jnp.bfloat16)
         d_gate = (d_hidden * up * sigmoid * (1.0 + gate * (1.0 - sigmoid))).astype(jnp.bfloat16)
         d_gate_up = jnp.concatenate([d_gate, d_up], axis=1)
-        if h == 1:
-            d_mlp_partial = d_mlp_partial + times_transposed(d_gate_up, gate_up_w)
-            down_partial = down_partial + times_transposed(hidden, down_wt)
+        part = times_transposed(d_gate_up, gate_up_w)
+        d_mlp_partial = part if d_mlp_partial is None else d_mlp_partial + part
         g_down_t = contract_rows(grad_rows, hidden)
         g_gate_up = contract_rows(mlp_all, d_gate_up)
         joined = jnp.concatenate(
             [g_gate_up.astype(jnp.bfloat16), g_down_t.astype(jnp.bfloat16)], axis=1
         )
         if h == 0:
-            joined, mlp_sets[1], hidden, d_gate_up = lax.optimization_barrier(
-                (joined, mlp_sets[1], hidden, d_gate_up)
-            )
+            joined, mlp_sets[1] = lax.optimization_barrier((joined, mlp_sets[1]))
             mlp_grads.append(lax.psum_scatter(joined, "wide", scatter_dimension=0, tiled=True))
-            d_mlp_partial = times_transposed(d_gate_up, gate_up_w)
-            down_partial = times_transposed(hidden, down_wt)
         else:
             last_joined = joined
 

time: 669 us -> 659 us (0.985)
  local copies, waits for them, and re-layouts: 89.2 us -> 70.7 us
  waiting for transfers between devices: 260 us -> 277 us
  other arithmetic: 95.1 us -> 84.4 us
    unnamed x208 -> x206, local copies, waits for them, and re-layouts: 40.8 us -> 31.2 us
  transfers between devices with their start and end apart: 40 -> 40, of which waited for: 26 -> 28; matrix products, arithmetic and copies ran while one was open for 46% -> 43% of each run, Pallas kernels for 0% -> 0%
where the time goes in v11:
time: 659 us; the launch traced here: 655 us
  waiting for transfers between devices  277 us (42%)
  matrix products  161 us (24%)
  other arithmetic  84.4 us (13%)
  local copies, waits for them, and re-layouts  70.7 us (11%)
  starting transfers between devices  44.9 us (7%)
  between operations  16.5 us (3%)
    ppermute x4, waiting for transfers between devices, narrow_scatter(): a_got = lax.ppermute(blocks[2:4].astype(jnp.bfloat16), 'narrow', YPERM)  47.1 us
    ppermute x4, waiting for transfers between devices, narrow_gather(): a_pair_y = lax.ppermute(a_pair, 'narrow', YPERM)  45.9 us
    dot_general x6, matrix products, times_transposed(): lax.dot_general(left, right, (((1,), (1,)), ((), ())), preferred_element_...  43.3 us
    ppermute x4, waiting for transfers between devices, narrow_gather(): b_pair_x = lax.ppermute(b_pair, 'narrow', XPERM)  40.8 us
    reduce_scatter x1, waiting for transfers between devices, shards_body(): lax.psum_scatter(jnp.concatenate([last_joined, out_grad], axis=1), 'wide'...  40.2 us
    ppermute x4, waiting for transfers between devices, narrow_gather(): b_y = lax.ppermute(b, 'narrow', YPERM)  37.6 us
    dot_general x6, matrix products, contract_rows(): lax.dot_general(left, right, (((0,), (0,)), ((), ())), preferred_element_...  37.2 us
    unnamed x206, local copies, waits for them, and re-layouts  31.2 us
  transfers between devices with their start and end apart: 40, of which 28 were waited for; matrix products, arithmetic and copies ran while one was open for 43% of the time, Pallas kernels for 0%

profile of v11, /device:TPU:0, one launch (start us, length us, event | category | flops | bytes accessed | tf_op | source)
XLA Modules:
  0.0 654.7 jit_solution(1641831277483602659)
XLA Ops:
  38.6 21.7 %collective-permute-done.1 = bf16[256,2048]{1,0:T(8,128)(2,1)S(1)} collective-permute-done((bf16[256,2048]{1,0:T(8,128)(2,1)S(1)}, bf16[256,2048]{1,0:T(8,128)(2,1)S(1)}, u32[]{:S(2)}, u32[]{:S(2)}) %collective-permute-start.1) | collective-permute-done | bytes 1048608 | tf_op jit(solution)/shard_map/ppermute | solution.py:103
  63.8 10.9 %collective-permute-done.2 = bf16[128,2048]{1,0:T(8,128)(2,1)S(1)} collective-permute-done((bf16[128,2048]{1,0:T(8,128)(2,1)S(1)}, bf16[128,2048]{1,0:T(8,128)(2,1)S(1)}, u32[]{:S(2)}, u32[]{:S(2)}) %collective-permute-start.2) | collective-permute-done | bytes 524320 | tf_op jit(solution)/shard_map/ppermute | solution.py:100
  80.3 17.4 %collective-permute-done.3 = bf16[256,2048]{1,0:T(8,128)(2,1)S(1)} collective-permute-done((bf16[256,2048]{1,0:T(8,128)(2,1)S(1)}, bf16[256,2048]{1,0:T(8,128)(2,1)S(1)}, u32[]{:S(2)}, u32[]{:S(2)}) %collective-permute-start.3) | collective-permute-done | bytes 1048608 | tf_op jit(solution)/shard_map/ppermute | solution.py:104
  142.7 21.2 %collective-permute-done.4 = bf16[2,128,2048]{2,1,0:T(8,128)(2,1)S(1)} collective-permute-done((bf16[2,128,2048]{2,1,0:T(8,128)(2,1)S(1)}, bf16[2,128,2048]{2,1,0:T(8,128)(2,1)S(1)}, u32[]{:S(2)}, u32[]{:S(2)}) %collective-permute-start.4) | collective-permute-done | bytes 1048608 | tf_op jit(solution)/shard_map/ppermute | solution.py:116
  165.5 12.0 %collective-permute-done.6 = bf16[2,128,2048]{2,1,0:T(8,128)(2,1)S(1)} collective-permute-done((bf16[2,128,2048]{2,1,0:T(8,128)(2,1)S(1)}, bf16[2,128,2048]{2,1,0:T(8,128)(2,1)S(1)}, u32[]{:S(2)}, u32[]{:S(2)}) %collective-permute-start.6) | collective-permute-done | bytes 1048608 | tf_op jit(solution)/shard_map/ppermute | solution.py:117
  197.3 14.9 %collective-permute-done.13 = bf16[256,2048]{1,0:T(8,128)(2,1)S(1)} collective-permute-done((bf16[256,2048]{1,0:T(8,128)(2,1)S(1)}, bf16[256,2048]{1,0:T(8,128)(2,1)S(1)}, u32[]{:S(2)}, u32[]{:S(2)}) %collective-permute-start.13) | collective-permute-done | bytes 1048608 | tf_op jit(solution)/shard_map/ppermute | solution.py:103
  214.6 9.9 %collective-permute-done.15 = bf16[256,2048]{1,0:T(8,128)(2,1)S(1)} collective-permute-done((bf16[256,2048]{1,0:T(8,128)(2,1)S(1)}, bf16[256,2048]{1,0:T(8,128)(2,1)S(1)}, u32[]{:S(2)}, u32[]{:S(2)}) %collective-permute-start.15) | collective-permute-done | bytes 1048608 | tf_op jit(solution)/shard_map/ppermute | solution.py:104
  229.7 9.3 %collective-permute-done.9 = bf16[256,2048]{1,0:T(8,128)(2,1)S(1)} collective-permute-done((bf16[256,2048]{1,0:T(8,128)(2,1)S(1)}, bf16[256,2048]{1,0:T(8,128)(2,1)S(1)}, u32[]{:S(2)}, u32[]{:S(2)}) %collective-permute-start.9) | collective-permute-done | bytes 1048608 | tf_op jit(solution)/shard_map/ppermute | solution.py:103
  243.2 10.8 %fusion.19 = f32[1024,1536]{1,0:T(8,128)S(1)} fusion(bf16[1024,2048]{1,0:T(8,128)(2,1)} %constant_dynamic-update-slice_fusion.13, bf16[2048,2304]{0,1:T(8,128)(2,1)} %all-gather.6.cloned.1.call-done), kind=kOutput, calls=%fused_computation.32 | convolution fusion | flops 6442450944 | bytes 16777216 | tf_op jit(solution)/shard_map/dot_general | solution.py:248
  264.2 9.7 %convolution_convert_fusion.1 = bf16[2048,1536]{0,1:T(8,128)(2,1)S(1)} fusion(bf16[1024,2048]{1,0:T(8,128)(2,1)} %constant_dynamic-update-slice_fusion.13, bf16[1024,768]{1,0:T(8,128)(2,1)S(1)} %get-tuple-element.82, bf16[1024,768]{1,0:T(8,128)(2,1)S(1)} %get-tuple-element.81), kind=kOutput, calls=%fused_computation.29 | convolution fusion | flops 6451888128 | bytes 13631488 | tf_op jit(solution)/shard_map/dot_general | solution.py:61
  273.9 11.3 %pad_maximum_fusion.1 = bf16[2048,2304]{0,1:T(8,128)(2,1)} fusion(bf16[2048,768]{0,1:T(8,128)(2,1)S(1)} %convolution_convert_fusion.4, bf16[2048,1536]{0,1:T(8,128)(2,1)S(1)} %convolution_convert_fusion.1), kind=kLoop, calls=%fused_computation.17 | loop fusion | flops 18874368 | bytes 18874368 | tf_op jit(solution)/shard_map/concatenate | solution.py:263
  294.0 10.4 %fusion.164 = f32[1024,1536]{1,0:T(8,128)S(1)} fusion(bf16[1024,2048]{1,0:T(8,128)(2,1)} %constant_dynamic-update-slice_fusion.13, bf16[2048,1536]{0,1:T(8,128)(2,1)} %slice.573), kind=kOutput, calls=%fused_computation.380 | convolution fusion | flops 6442450944 | bytes 16777216 | tf_op jit(solution)/shard_map/dot_general | solution.py:248
  308.9 8.9 %fusion.48 = f32[1024,2048]{1,0:T(8,128)} fusion(bf16[2048,1536]{0,1:T(8,128)(2,1)S(1)} %bitcast.381, bf16[1024,768]{1,0:T(8,128)(2,1)S(1)} %get-tuple-element.80, bf16[1024,768]{1,0:T(8,128)(2,1)S(1)} %get-tuple-element.79), kind=kOutput, calls=%fused_computation.108 | convolution fusion | flops 6448742400 | bytes 17825792 | tf_op jit(solution)/shard_map/dot_general | solution.py:67
  317.7 12.9 %fusion.162 = (bf16[1024,2048]{1,0:T(8,128)(2,1)S(1)}, f32[1024,2048]{1,0:T(8,128)}) fusion(f32[1024,2048]{1,0:T(8,128)} %fusion.48, bf16[2048,2304]{0,1:T(8,128)(2,1)} %all-gather.6.cloned.1.call-done, bf16[1024,768]{1,0:T(8,128)(2,1)} %copy-done.70, bf16[1024,768]{1,0:T(8,128)(2,1)S(1)} %copy-done.69), kind=kOutput, calls=%fused_computation.378 | convolution fusion | flops 6452936704 | bytes 30408704 | tf_op jit(solution)/shard_map/dot_general | solution.py:67
  352.8 9.5 %convolution_convert_fusion = bf16[2048,1536]{0,1:T(8,128)(2,1)S(1)} fusion(bf16[1024,2048]{1,0:T(8,128)(2,1)} %constant_dynamic-update-slice_fusion.13, bf16[1024,768]{1,0:T(8,128)(2,1)} %copy-done.67, bf16[1024,768]{1,0:T(8,128)(2,1)} %copy-done.66), kind=kOutput, calls=%fused_computation.28 | convolution fusion | flops 6451888128 | bytes 13631488 | tf_op jit(solution)/shard_map/dot_general | solution.py:61
  409.3 24.2 %collective-permute-done.26 = bf16[128,2048]{1,0:T(8,128)(2,1)S(1)} collective-permute-done((bf16[128,2048]{1,0:T(8,128)(2,1)S(1)}, bf16[128,2048]{1,0:T(8,128)(2,1)S(1)}, u32[]{:S(2)}, u32[]{:S(2)}) %collective-permute-start.26) | collective-permute-done | bytes 524320 | tf_op jit(solution)/shard_map/ppermute | solution.py:100
  435.5 13.1 %collective-permute-done.27 = bf16[256,2048]{1,0:T(8,128)(2,1)S(1)} collective-permute-done((bf16[256,2048]{1,0:T(8,128)(2,1)S(1)}, bf16[256,2048]{1,0:T(8,128)(2,1)S(1)}, u32[]{:S(2)}, u32[]{:S(2)}) %collective-permute-start.27) | collective-permute-done | bytes 1048608 | tf_op jit(solution)/shard_map/ppermute | solution.py:104
  451.0 14.5 %pad_maximum_fusion = bf16[2048,2816]{0,1:T(8,128)(2,1)} fusion(bf16[2048,512]{0,1:T(8,128)(2,1)S(1)} %convolution_convert_fusion.5, bf16[2048,2304]{0,1:T(8,128)(2,1)S(1)} %pad_maximum_fusion.2), kind=kLoop, calls=%fused_computation.16 | loop fusion | flops 23068672 | bytes 23068672 | tf_op jit(solution)/shard_map/concatenate | solution.py:285
  471.7 13.5 %fusion = (f32[2,2,1024]{2,1,0:T(2,128)S(1)}, f32[2,1024,1024,2]{2,1,3,0:T(8,128)}) fusion(f32[2,1024,1024,2]{2,1,3,0:T(8,128)} %copy-done, f32[2,2,1024]{2,1,0:T(2,128)S(1)} %log_add_fusion, pred[1024,1024]{0,1:T(8,128)(4,1)S(1)} %copy-done.8, bf16[1024,2,128,1]{0,2,3,1:T(8,128)(2,1)S(1)} %bitcast.385, bf16[1024,2,2,128]{0,3,2,1:T(8,128)(2,1)S(1)} %bitcast.397), kind=kOutput, calls=%fused_computation.2 | convolution fusion | flops 1094709248 | bytes 36208640 | tf_op jit(solution)/shard_map/qgrd,kgd->grqk/dot_general | solution.py:291
  485.2 12.5 %fusion.2 = bf16[2,2,1024,1024]{2,3,1,0:T(8,128)(2,1)S(1)} fusion(f32[2,1024,1024,2]{2,1,3,0:T(8,128)} %get-tuple-element.184, f32[2,1024,1024,2]{2,1,3,0:T(8,128)} %copy-done, f32[2,2,1024]{2,1,0:T(2,128)S(1)} %get-tuple-element.183, f32[2,2,1024]{2,1,0:T(2,128)S(1)} %log_add_fusion, pred[1024,1024]{0,1:T(8,128)(4,1)S(1)} %copy-done.8), kind=kLoop, calls=%fused_computation.4 | loop fusion | flops 25165824 | bytes 43024384 | tf_op jit(solution)/shard_map/convert_element_type | solution.py:293
  516.6 10.3 %fusion.12 = (f32[2048]{0:T(1024)S(1)}, bf16[1024,2048]{1,0:T(8,128)(2,1)}, f32[1024,2048]{1,0:T(8,128)}) fusion(bf16[1024,2048]{1,0:T(8,128)(2,1)S(1)} %copy-done.20, f32[1024]{0:T(1024)S(1)} %copy-done.63, bf16[2048,1664]{0,1:T(8,128)(2,1)} %all-gather.4.cloned.1.call-done, bf16[1024,256]{0,1:T(8,128)(2,1)S(1)} %bitcast.417, ...), kind=kOutput, calls=%fused_computation.24 | convolution fusion | flops 4311742464 | bytes 23080960 | tf_op jit(solution)/shard_map/dot_general | solution.py:67
  545.9 40.2 %reduce-scatter.6.cloned.1.call-done = bf16[256,2816]{0,1:T(8,128)(2,1)} async-done(((bf16[2048,2816]{0,1:T(8,128)(2,1)}), bf16[256,2816]{0,1:T(8,128)(2,1)}) %reduce-scatter.6.cloned.1.call-update) | async-done | bytes 1441808 | tf_op jit(solution)/shard_map/reduce_scatter | solution.py:284
  593.6 17.3 %collective-permute-done.28 = bf16[2,128,2048]{2,1,0:T(8,128)(2,1)S(1)} collective-permute-done((bf16[2,128,2048]{2,1,0:T(8,128)(2,1)S(1)}, bf16[2,128,2048]{2,1,0:T(8,128)(2,1)S(1)}, u32[]{:S(2)}, u32[]{:S(2)}) %collective-permute-start.28) | collective-permute-done | bytes 1048608 | tf_op jit(solution)/shard_map/ppermute | solution.py:116
  614.7 8.7 %collective-permute-done.29 = bf16[128,2048]{1,0:T(8,128)(2,1)S(1)} collective-permute-done((bf16[128,2048]{1,0:T(8,128)(2,1)S(1)}, bf16[128,2048]{1,0:T(8,128)(2,1)S(1)}, u32[]{:S(2)}, u32[]{:S(2)}) %collective-permute-start.29) | collective-permute-done | bytes 524320 | tf_op jit(solution)/shard_map/ppermute | solution.py:120
  (456 shorter events, 293.1 us)
Async XLA Ops:
  7.2 93.6 %all-gather.4.cloned.1.call-start = ((), (), s32[]{:S(2)}) async-start(), calls=%async_computation.3 | async-start | bytes 7667712 | tf_op jit(solution)/shard_map/all_gather | solution.py:137
  15.0 228.1 %all-gather.6.cloned.1.call-start = ((), (), s32[]{:S(2)}) async-start(), calls=%async_computation.4 | async-start | bytes 10616832 | tf_op jit(solution)/shard_map/all_gather | solution.py:137
  19.8 265.4 %all-gather.8.cloned.1.call-start = ((), (), s32[]{:S(2)}) async-start(), calls=%async_computation.5 | async-start | bytes 10616832 | tf_op jit(solution)/shard_map/all_gather | solution.py:137
  26.3 519.6 %reduce-scatter.4.cloned.1.call-start = ((), (), s32[]{:S(2)}) async-start(), calls=%async_computation.6 | async-start | bytes 10616832 | tf_op jit(solution)/shard_map/reduce_scatter | solution.py:268
  35.8 24.5 %collective-permute-start.1 = (bf16[256,2048]{1,0:T(8,128)(2,1)S(1)}, bf16[256,2048]{1,0:T(8,128)(2,1)S(1)}, u32[]{:S(2)}, u32[]{:S(2)}) collective-permute-start(bf16[256,2048]{1,0:T(8,128)(2,1)S(1)} %pad_maximum_fusion.17), channel_id=1, source_target_pairs={{0,2},{2,0},{1,3},{3,1},{4,6},{6,4},{5,7},{7,5},{8,10},{10,8},{9,1... | collective-permute-start | bytes 3145736 | tf_op jit(solution)/shard_map/ppermute | solution.py:103
  74.7 23.0 %collective-permute-start.3 = (bf16[256,2048]{1,0:T(8,128)(2,1)S(1)}, bf16[256,2048]{1,0:T(8,128)(2,1)S(1)}, u32[]{:S(2)}, u32[]{:S(2)}) collective-permute-start(bf16[256,2048]{1,0:T(8,128)(2,1)S(1)} %pad_maximum_fusion.18), channel_id=1, source_target_pairs={{0,1},{1,0},{2,3},{3,2},{4,5},{5,4},{6,7},{7,6},{8,9},{9,8},{10,11... | collective-permute-start | bytes 3145736 | tf_op jit(solution)/shard_map/ppermute | solution.py:104
  137.8 26.1 %collective-permute-start.4 = (bf16[2,128,2048]{2,1,0:T(8,128)(2,1)S(1)}, bf16[2,128,2048]{2,1,0:T(8,128)(2,1)S(1)}, u32[]{:S(2)}, u32[]{:S(2)}) collective-permute-start(bf16[2,128,2048]{2,1,0:T(8,128)(2,1)S(1)} %bitcast.394), channel_id=1, source_target_pairs={{0,2},{2,0},{1,3},{3,1},{4,6},{6,4},{5,7},{7,5},{8,10},{10,8},{9,1... | collective-permute-start | bytes 3145736 | tf_op jit(solution)/shard_map/ppermute | solution.py:116
  139.3 57.3 %collective-permute-start.14 = (bf16[128,2048]{1,0:T(8,128)(2,1)S(1)}, bf16[128,2048]{1,0:T(8,128)(2,1)S(1)}, u32[]{:S(2)}, u32[]{:S(2)}) collective-permute-start(bf16[128,2048]{1,0:T(8,128)(2,1)S(1)} %get-tuple-element.127), channel_id=1, source_target_pairs={{0,2},{2,0},{1,3},{3,1},{4,6},{6,4},{5,7},{7,5},{8,10},{10,8},{9,1... | collective-permute-start | bytes 1572872 | tf_op jit(solution)/shard_map/ppermute | solution.py:100
  140.2 38.8 %collective-permute-start.12 = (bf16[128,2048]{1,0:T(8,128)(2,1)S(1)}, bf16[128,2048]{1,0:T(8,128)(2,1)S(1)}, u32[]{:S(2)}, u32[]{:S(2)}) collective-permute-start(bf16[128,2048]{1,0:T(8,128)(2,1)S(1)} %get-tuple-element.129), channel_id=1, source_target_pairs={{0,1},{1,0},{2,3},{3,2},{4,5},{5,4},{6,7},{7,6},{8,9},{9,8},{10,11... | collective-permute-start | bytes 1572872 | tf_op jit(solution)/shard_map/ppermute | solution.py:99
  141.7 35.8 %collective-permute-start.6 = (bf16[2,128,2048]{2,1,0:T(8,128)(2,1)S(1)}, bf16[2,128,2048]{2,1,0:T(8,128)(2,1)S(1)}, u32[]{:S(2)}, u32[]{:S(2)}) collective-permute-start(bf16[2,128,2048]{2,1,0:T(8,128)(2,1)S(1)} %bitcast.393), channel_id=1, source_target_pairs={{0,1},{1,0},{2,3},{3,2},{4,5},{5,4},{6,7},{7,6},{8,9},{9,8},{10,11... | collective-permute-start | bytes 3145736 | tf_op jit(solution)/shard_map/ppermute | solution.py:117
  164.3 19.9 %collective-permute-start.5 = (bf16[128,2048]{1,0:T(8,128)(2,1)S(1)}, bf16[128,2048]{1,0:T(8,128)(2,1)S(1)}, u32[]{:S(2)}, u32[]{:S(2)}) collective-permute-start(bf16[128,2048]{1,0:T(8,128)(2,1)S(1)} %fusion.80), channel_id=1, source_target_pairs={{0,1},{1,0},{2,3},{3,2},{4,5},{5,4},{6,7},{7,6},{8,9},{9,8},{10,11... | collective-permute-start | bytes 1572872 | tf_op jit(solution)/shard_map/ppermute | solution.py:120
  179.1 33.1 %collective-permute-start.13 = (bf16[256,2048]{1,0:T(8,128)(2,1)S(1)}, bf16[256,2048]{1,0:T(8,128)(2,1)S(1)}, u32[]{:S(2)}, u32[]{:S(2)}) collective-permute-start(bf16[256,2048]{1,0:T(8,128)(2,1)S(1)} %pad_maximum_fusion.21), channel_id=1, source_target_pairs={{0,2},{2,0},{1,3},{3,1},{4,6},{6,4},{5,7},{7,5},{8,10},{10,8},{9,1... | collective-permute-start | bytes 3145736 | tf_op jit(solution)/shard_map/ppermute | solution.py:103
  196.7 27.9 %collective-permute-start.15 = (bf16[256,2048]{1,0:T(8,128)(2,1)S(1)}, bf16[256,2048]{1,0:T(8,128)(2,1)S(1)}, u32[]{:S(2)}, u32[]{:S(2)}) collective-permute-start(bf16[256,2048]{1,0:T(8,128)(2,1)S(1)} %pad_maximum_fusion.22), channel_id=1, source_target_pairs={{0,1},{1,0},{2,3},{3,2},{4,5},{5,4},{6,7},{7,6},{8,9},{9,8},{10,11... | collective-permute-start | bytes 3145736 | tf_op jit(solution)/shard_map/ppermute | solution.py:104
  213.6 25.4 %collective-permute-start.9 = (bf16[256,2048]{1,0:T(8,128)(2,1)S(1)}, bf16[256,2048]{1,0:T(8,128)(2,1)S(1)}, u32[]{:S(2)}, u32[]{:S(2)}) collective-permute-start(bf16[256,2048]{1,0:T(8,128)(2,1)S(1)} %pad_maximum_fusion.19), channel_id=1, source_target_pairs={{0,2},{2,0},{1,3},{3,1},{4,6},{6,4},{5,7},{7,5},{8,10},{10,8},{9,1... | collective-permute-start | bytes 3145736 | tf_op jit(solution)/shard_map/ppermute | solution.py:103
  293.9 292.2 %reduce-scatter.6.cloned.1.call-start = ((), (), s32[]{:S(2)}) async-start(), calls=%async_computation.7 | async-start | bytes 12976128 | tf_op jit(solution)/shard_map/reduce_scatter | solution.py:284
  332.2 36.4 %collective-permute-start.22 = (bf16[2,128,2048]{2,1,0:T(8,128)(2,1)}, bf16[2,128,2048]{2,1,0:T(8,128)(2,1)}, u32[]{:S(2)}, u32[]{:S(2)}) collective-permute-start(bf16[2,128,2048]{2,1,0:T(8,128)(2,1)} %bitcast.63), channel_id=1, source_target_pairs={{0,1},{1,0},{2,3},{3,2},{4,5},{5,4},{6,7},{7,6},{8,9},{9,8},{10,11... | collective-permute-start | bytes 3145736 | tf_op jit(solution)/shard_map/ppermute | solution.py:117
  333.7 31.7 %collective-permute-start.20 = (bf16[2,128,2048]{2,1,0:T(8,128)(2,1)}, bf16[2,128,2048]{2,1,0:T(8,128)(2,1)}, u32[]{:S(2)}, u32[]{:S(2)}) collective-permute-start(bf16[2,128,2048]{2,1,0:T(8,128)(2,1)} %bitcast.59), channel_id=1, source_target_pairs={{0,2},{2,0},{1,3},{3,1},{4,6},{6,4},{5,7},{7,5},{8,10},{10,8},{9,1... | collective-permute-start | bytes 3145736 | tf_op jit(solution)/shard_map/ppermute | solution.py:116
  343.6 36.8 %collective-permute-start.18 = (bf16[2,128,2048]{2,1,0:T(8,128)(2,1)S(1)}, bf16[2,128,2048]{2,1,0:T(8,128)(2,1)S(1)}, u32[]{:S(2)}, u32[]{:S(2)}) collective-permute-start(bf16[2,128,2048]{2,1,0:T(8,128)(2,1)S(1)} %bitcast.391), channel_id=1, source_target_pairs={{0,1},{1,0},{2,3},{3,2},{4,5},{5,4},{6,7},{7,6},{8,9},{9,8},{10,11... | collective-permute-start | bytes 3145736 | tf_op jit(solution)/shard_map/ppermute | solution.py:117
  344.5 35.4 %collective-permute-start.16 = (bf16[2,128,2048]{2,1,0:T(8,128)(2,1)S(1)}, bf16[2,128,2048]{2,1,0:T(8,128)(2,1)S(1)}, u32[]{:S(2)}, u32[]{:S(2)}) collective-permute-start(bf16[2,128,2048]{2,1,0:T(8,128)(2,1)S(1)} %bitcast.392), channel_id=1, source_target_pairs={{0,2},{2,0},{1,3},{3,1},{4,6},{6,4},{5,7},{7,5},{8,10},{10,8},{9,1... | collective-permute-start | bytes 3145736 | tf_op jit(solution)/shard_map/ppermute | solution.py:116
  407.0 28.3 %collective-permute-start.25 = (bf16[256,2048]{1,0:T(8,128)(2,1)S(1)}, bf16[256,2048]{1,0:T(8,128)(2,1)S(1)}, u32[]{:S(2)}, u32[]{:S(2)}) collective-permute-start(bf16[256,2048]{1,0:T(8,128)(2,1)S(1)} %pad_maximum_fusion.23), channel_id=1, source_target_pairs={{0,2},{2,0},{1,3},{3,1},{4,6},{6,4},{5,7},{7,5},{8,10},{10,8},{9,1... | collective-permute-start | bytes 3145736 | tf_op jit(solution)/shard_map/ppermute | solution.py:103
  409.3 24.3 %collective-permute-start.26 = (bf16[128,2048]{1,0:T(8,128)(2,1)S(1)}, bf16[128,2048]{1,0:T(8,128)(2,1)S(1)}, u32[]{:S(2)}, u32[]{:S(2)}) collective-permute-start(bf16[128,2048]{1,0:T(8,128)(2,1)S(1)} %get-tuple-element.124), channel_id=1, source_target_pairs={{0,2},{2,0},{1,3},{3,1},{4,6},{6,4},{5,7},{7,5},{8,10},{10,8},{9,1... | collective-permute-start | bytes 1572872 | tf_op jit(solution)/shard_map/ppermute | solution.py:100
  465.6 176.1 %reduce-scatter.8.cloned.1.call-start = ((), (), s32[]{:S(2)}) async-start(), calls=%async_computation.8 | async-start | bytes 5308416 | tf_op jit(solution)/shard_map/reduce_scatter | solution.py:346
  587.8 23.1 %collective-permute-start.28 = (bf16[2,128,2048]{2,1,0:T(8,128)(2,1)S(1)}, bf16[2,128,2048]{2,1,0:T(8,128)(2,1)S(1)}, u32[]{:S(2)}, u32[]{:S(2)}) collective-permute-start(bf16[2,128,2048]{2,1,0:T(8,128)(2,1)S(1)} %bitcast.396), channel_id=1, source_target_pairs={{0,2},{2,0},{1,3},{3,1},{4,6},{6,4},{5,7},{7,5},{8,10},{10,8},{9,1... | collective-permute-start | bytes 3145736 | tf_op jit(solution)/shard_map/ppermute | solution.py:116
  589.4 23.8 %collective-permute-start.30 = (bf16[2,128,2048]{2,1,0:T(8,128)(2,1)S(1)}, bf16[2,128,2048]{2,1,0:T(8,128)(2,1)S(1)}, u32[]{:S(2)}, u32[]{:S(2)}) collective-permute-start(bf16[2,128,2048]{2,1,0:T(8,128)(2,1)S(1)} %bitcast.395), channel_id=1, source_target_pairs={{0,1},{1,0},{2,3},{3,2},{4,5},{5,4},{6,7},{7,6},{8,9},{9,8},{10,11... | collective-permute-start | bytes 3145736 | tf_op jit(solution)/shard_map/ppermute | solution.py:117
  (94 other events, 818.7 us)
Sparse Core Ops, SparseCore 0:
  15.2 72.2 all-gather.3
  89.6 89.2 all-gather.5
  180.5 89.3 all-gather.7
  294.0 99.9 reduce-scatter.3
  465.7 120.3 reduce-scatter.5
  588.3 53.3 reduce-scatter.7

commit v12 on v9

--- a/solution.py
+++ b/solution.py
@@ -167,7 +167,9 @@
     q_cols = w_query.shape[1]
     kv_cols = w_key.shape[1]
     ff_cols = w_gate.shape[1]
-    ff_half = ff_cols // 2
+    ff_first = max(128, (2 * ff_cols // 3) // 128 * 128)
+    ff_parts = (ff_first, ff_cols - ff_first)
+    ff_starts = (0, ff_first)
     relative = relative_ok(seq_count)
 
     tokens_all = narrow_gather(tokens, relative)
@@ -191,7 +193,7 @@
     down_t = w_down.T
     mlp_sets = []
     for h in range(2):
-        cols = slice(h * ff_half, (h + 1) * ff_half)
+        cols = slice(ff_starts[h], ff_starts[h] + ff_parts[h])
         mlp_sets.append(
             wide_gather([jnp.concatenate([w_gate[:, cols], w_up[:, cols]], axis=1), down_t[:, cols]])
         )
@@ -246,8 +248,8 @@
     for h in range(2):
         gate_up_w, down_wt = mlp_sets[h]
         gate_up = jnp.dot(mlp_all, gate_up_w, preferred_element_type=jnp.float32)
-        gate = gate_up[:, :ff_half]
-        up = gate_up[:, ff_half:]
+        gate = gate_up[:, : ff_parts[h]]
+        up = gate_up[:, ff_parts[h] :]
         sigmoid = jax.nn.sigmoid(gate)
         hidden = (gate * sigmoid * up).astype(jnp.bfloat16)
         part = times_transposed(hidden, down_wt)
@@ -282,7 +284,9 @@
     branch_rows = narrow_gather(d_resid_low, relative)
     out_grad = contract_rows(branch_rows, attended).astype(jnp.bfloat16)
     mlp_grads, out_grad = lax.optimization_barrier((mlp_grads, out_grad))
-    mlp_grads = [split_cols(g.astype(jnp.float32), [2 * ff_half, ff_half]) for g in mlp_grads]
+    mlp_grads = [
+        split_cols(g.astype(jnp.float32), [2 * ff_parts[h], ff_parts[h]]) for h, g in enumerate(mlp_grads)
+    ]
     g_out_t = lax.psum_scatter(out_grad, "wide", scatter_dimension=0, tiled=True).astype(jnp.float32)
     d_attended = jnp.dot(branch_rows, out_wt, preferred_element_type=jnp.float32).astype(jnp.bfloat16)
     d_mixed = d_attended.reshape(rows_group, groups_here, repeat, HD)
@@ -353,8 +357,8 @@
     g_query = g_qkv[:, :q_cols]
     g_key = g_qkv[:, q_cols : q_cols + kv_cols]
     g_value = g_qkv[:, q_cols + kv_cols :]
-    g_gate = jnp.concatenate([mlp_grads[h][0][:, :ff_half] for h in range(2)], axis=1)
-    g_up = jnp.concatenate([mlp_grads[h][0][:, ff_half:] for h in range(2)], axis=1)
+    g_gate = jnp.concatenate([mlp_grads[h][0][:, : ff_parts[h]] for h in range(2)], axis=1)
+    g_up = jnp.concatenate([mlp_grads[h][0][:, ff_parts[h] :] for h in range(2)], axis=1)
     g_down = jnp.concatenate([mlp_grads[h][1] for h in range(2)], axis=1).T
     output = (resid + narrow_scatter(down_partial, relative)).astype(jnp.bfloat16)
     return (

time: 622 us -> 762 us (1.23)
  waiting for transfers between devices: 237 us -> 357 us
  matrix products: 168 us -> 177 us
    reduce_scatter x1, waiting for transfers between devices: 0.01 us -> 70.2 us  [shards_body(): lax.psum_scatter(joined, 'wide', scatter_dimension=0, tiled=True)]
    ppermute x4, waiting for transfers between devices: 13.3 us -> 55.4 us  [narrow_scatter(): b_got = lax.ppermute(blocks[6:8].astype(jnp.bfloat16), 'narrow', XPERM)]
    ppermute x4, waiting for transfers between devices: 37.7 us -> 13.9 us  [narrow_scatter(): a_got = lax.ppermute(blocks[2:4].astype(jnp.bfloat16), 'narrow', YPERM)]
    ppermute x4, waiting for transfers between devices: 21.7 us -> 0.01 us  [narrow_scatter(): a_got2 = lax.ppermute(a_sum[1].astype(jnp.bfloat16), 'narrow', XPERM)]
    all_gather x3, waiting for transfers between devices: 0.02 us -> 21.5 us  [wide_gather(): lax.all_gather(jnp.concatenate(blocks, axis=1), 'wide', axis=0, tiled=True)]
    ppermute x4, waiting for transfers between devices: 11.8 us -> 32.3 us  [narrow_scatter(): b_got2 = lax.ppermute(b_sum[1].astype(jnp.bfloat16), 'narrow', YPERM)]
    unnamed x227 -> x215, local copies, waits for them, and re-layouts: 31.7 us -> 35.7 us
  transfers between devices with their start and end apart: 41 -> 41, of which waited for: 26 -> 26; matrix products, arithmetic and copies ran while one was open for 47% -> 27% of each run, Pallas kernels for 0% -> 0%
where the time goes in v12:
time: 762 us; the launch traced here: 757 us
  waiting for transfers between devices  357 us (47%)
  matrix products  177 us (23%)
  other arithmetic  85.8 us (11%)
  local copies, waits for them, and re-layouts  78 us (10%)
  starting transfers between devices  42.3 us (6%)
  between operations  16.4 us (2%)
    reduce_scatter x1, waiting for transfers between devices, shards_body(): lax.psum_scatter(joined, 'wide', scatter_dimension=0, tiled=True)  70.2 us
    ppermute x4, waiting for transfers between devices, narrow_scatter(): b_got = lax.ppermute(blocks[6:8].astype(jnp.bfloat16), 'narrow', XPERM)  55.4 us
    dot_general x6, matrix products, times_transposed(): lax.dot_general(left, right, (((1,), (1,)), ((), ())), preferred_element_...  49.2 us
    ppermute x4, waiting for transfers between devices, narrow_gather(): b_pair_x = lax.ppermute(b_pair, 'narrow', XPERM)  48.3 us
    dot_general x6, matrix products, contract_rows(): lax.dot_general(left, right, (((0,), (0,)), ((), ())), preferred_element_...  44.3 us
    ppermute x4, waiting for transfers between devices, narrow_gather(): a_pair_y = lax.ppermute(a_pair, 'narrow', YPERM)  43.5 us
    ppermute x4, waiting for transfers between devices, narrow_gather(): b_y = lax.ppermute(b, 'narrow', YPERM)  43.5 us
    unnamed x215, local copies, waits for them, and re-layouts  35.7 us
  transfers between devices with their start and end apart: 41, of which 26 were waited for; matrix products, arithmetic and copies ran while one was open for 27% of the time, Pallas kernels for 0%

profile of v12, /device:TPU:0, one launch (start us, length us, event | category | flops | bytes accessed | tf_op | source)
XLA Modules:
  0.0 757.3 jit_solution(2899141907086606992)
XLA Ops:
  36.2 21.7 %collective-permute-done.1 = bf16[256,2048]{1,0:T(8,128)(2,1)S(1)} collective-permute-done((bf16[256,2048]{1,0:T(8,128)(2,1)S(1)}, bf16[256,2048]{1,0:T(8,128)(2,1)S(1)}, u32[]{:S(2)}, u32[]{:S(2)}) %collective-permute-start.1) | collective-permute-done | bytes 1048608 | tf_op jit(solution)/shard_map/ppermute | solution.py:103
  61.3 10.9 %collective-permute-done.2 = bf16[128,2048]{1,0:T(8,128)(2,1)S(1)} collective-permute-done((bf16[128,2048]{1,0:T(8,128)(2,1)S(1)}, bf16[128,2048]{1,0:T(8,128)(2,1)S(1)}, u32[]{:S(2)}, u32[]{:S(2)}) %collective-permute-start.2) | collective-permute-done | bytes 524320 | tf_op jit(solution)/shard_map/ppermute | solution.py:100
  78.2 17.2 %collective-permute-done.3 = bf16[256,2048]{1,0:T(8,128)(2,1)S(1)} collective-permute-done((bf16[256,2048]{1,0:T(8,128)(2,1)S(1)}, bf16[256,2048]{1,0:T(8,128)(2,1)S(1)}, u32[]{:S(2)}, u32[]{:S(2)}) %collective-permute-start.3) | collective-permute-done | bytes 1048608 | tf_op jit(solution)/shard_map/ppermute | solution.py:104
  143.4 20.4 %collective-permute-done.6 = bf16[2,128,2048]{2,1,0:T(8,128)(2,1)S(1)} collective-permute-done((bf16[2,128,2048]{2,1,0:T(8,128)(2,1)S(1)}, bf16[2,128,2048]{2,1,0:T(8,128)(2,1)S(1)}, u32[]{:S(2)}, u32[]{:S(2)}) %collective-permute-start.6) | collective-permute-done | bytes 1048608 | tf_op jit(solution)/shard_map/ppermute | solution.py:117
  165.2 13.0 %collective-permute-done.4 = bf16[2,128,2048]{2,1,0:T(8,128)(2,1)S(1)} collective-permute-done((bf16[2,128,2048]{2,1,0:T(8,128)(2,1)S(1)}, bf16[2,128,2048]{2,1,0:T(8,128)(2,1)S(1)}, u32[]{:S(2)}, u32[]{:S(2)}) %collective-permute-start.4) | collective-permute-done | bytes 1048608 | tf_op jit(solution)/shard_map/ppermute | solution.py:116
  195.1 12.7 %collective-permute-done.13 = bf16[256,2048]{1,0:T(8,128)(2,1)S(1)} collective-permute-done((bf16[256,2048]{1,0:T(8,128)(2,1)S(1)}, bf16[256,2048]{1,0:T(8,128)(2,1)S(1)}, u32[]{:S(2)}, u32[]{:S(2)}) %collective-permute-start.13) | collective-permute-done | bytes 1048608 | tf_op jit(solution)/shard_map/ppermute | solution.py:103
  232.3 9.1 %collective-permute-done.9 = bf16[256,2048]{1,0:T(8,128)(2,1)} collective-permute-done((bf16[256,2048]{1,0:T(8,128)(2,1)}, bf16[256,2048]{1,0:T(8,128)(2,1)}, u32[]{:S(2)}, u32[]{:S(2)}) %collective-permute-start.9) | collective-permute-done | bytes 1048608 | tf_op jit(solution)/shard_map/ppermute | solution.py:103
  249.1 21.5 %all-gather.6.cloned.1.call-done = bf16[2048,3072]{0,1:T(8,128)(2,1)} async-done(((bf16[256,3072]{0,1:T(8,128)(2,1)}), bf16[2048,3072]{0,1:T(8,128)(2,1)}) %all-gather.6.cloned.1.call-update) | async-done | bytes 12582928 | tf_op jit(solution)/shard_map/all_gather | solution.py:137
  270.5 12.6 %fusion.19 = f32[1024,2048]{1,0:T(8,128)S(1)} fusion(bf16[1024,2048]{1,0:T(8,128)(2,1)} %constant_dynamic-update-slice_fusion.13, bf16[2048,3072]{0,1:T(8,128)(2,1)} %all-gather.6.cloned.1.call-done), kind=kOutput, calls=%fused_computation.29 | convolution fusion | flops 8589934592 | bytes 20971520 | tf_op jit(solution)/shard_map/dot_general | solution.py:250
  283.1 10.6 %multiply_convert_fusion.1 = (bf16[1024,1024]{1,0:T(8,128)(2,1)S(1)}, bf16[1024,1024]{1,0:T(8,128)(2,1)}, bf16[1024,1024]{1,0:T(8,128)(2,1)S(1)}) fusion(f32[1024,2048]{1,0:T(8,128)S(1)} %fusion.19, bf16[1024,2048]{1,0:T(8,128)(2,1)} %constant_dynamic-update-slice_fusion.19, bf16[2048,3072]{0,1:T(8,128)(2,1)} %all-gather.6.cloned.1.call-done), kind=kOutput, calls=%fused_computation.36 | convolution fusion | flops 4311744512 | bytes 23068672 | tf_op jit(solution)/shard_map/dot_general | solution.py:257
  302.2 11.6 %convolution_convert_fusion = bf16[2048,2048]{0,1:T(8,128)(2,1)S(1)} fusion(bf16[1024,2048]{1,0:T(8,128)(2,1)} %constant_dynamic-update-slice_fusion.13, bf16[1024,1024]{1,0:T(8,128)(2,1)} %get-tuple-element.84, bf16[1024,1024]{1,0:T(8,128)(2,1)S(1)} %get-tuple-element.83), kind=kOutput, calls=%fused_computation.26 | convolution fusion | flops 8602517504 | bytes 16777216 | tf_op jit(solution)/shard_map/dot_general | solution.py:61
  313.8 15.1 %pad_maximum_fusion = bf16[2048,3072]{0,1:T(8,128)(2,1)} fusion(bf16[2048,1024]{0,1:T(8,128)(2,1)S(1)} %convolution_convert_fusion.3, bf16[2048,2048]{0,1:T(8,128)(2,1)S(1)} %convolution_convert_fusion), kind=kLoop, calls=%fused_computation.13 | loop fusion | flops 25165824 | bytes 25165824 | tf_op jit(solution)/shard_map/concatenate | solution.py:265
  356.6 16.9 %fusion.159 = (bf16[1024,2048]{1,0:T(8,128)(2,1)}, f32[1024,2048]{1,0:T(8,128)}) fusion(f32[1024,2048]{1,0:T(8,128)} %fusion.59, bf16[2048,3072]{0,1:T(8,128)(2,1)} %all-gather.6.cloned.1.call-done, bf16[1024,1024]{1,0:T(8,128)(2,1)} %get-tuple-element.84, bf16[1024,1024]{1,0:T(8,128)(2,1)} %copy-done.74), kind=kOutput, calls=%fused_computation.373 | convolution fusion | flops 8602517504 | bytes 33554432 | tf_op jit(solution)/shard_map/dot_general | solution.py:67
  411.8 16.9 %collective-permute-done.18 = bf16[2,128,2048]{2,1,0:T(8,128)(2,1)} collective-permute-done((bf16[2,128,2048]{2,1,0:T(8,128)(2,1)}, bf16[2,128,2048]{2,1,0:T(8,128)(2,1)}, u32[]{:S(2)}, u32[]{:S(2)}) %collective-permute-start.18) | collective-permute-done | bytes 1048608 | tf_op jit(solution)/shard_map/ppermute | solution.py:117
  442.2 9.3 %collective-permute-done.19 = bf16[128,2048]{1,0:T(8,128)(2,1)S(1)} collective-permute-done((bf16[128,2048]{1,0:T(8,128)(2,1)S(1)}, bf16[128,2048]{1,0:T(8,128)(2,1)S(1)}, u32[]{:S(2)}, u32[]{:S(2)}) %collective-permute-start.19) | collective-permute-done | bytes 524320 | tf_op jit(solution)/shard_map/ppermute | solution.py:121
  455.0 12.4 %collective-permute-done.24 = bf16[128,2048]{1,0:T(8,128)(2,1)S(1)} collective-permute-done((bf16[128,2048]{1,0:T(8,128)(2,1)S(1)}, bf16[128,2048]{1,0:T(8,128)(2,1)S(1)}, u32[]{:S(2)}, u32[]{:S(2)}) %collective-permute-start.24) | collective-permute-done | bytes 524320 | tf_op jit(solution)/shard_map/ppermute | solution.py:99
  469.7 32.6 %collective-permute-done.26 = bf16[128,2048]{1,0:T(8,128)(2,1)S(1)} collective-permute-done((bf16[128,2048]{1,0:T(8,128)(2,1)S(1)}, bf16[128,2048]{1,0:T(8,128)(2,1)S(1)}, u32[]{:S(2)}, u32[]{:S(2)}) %collective-permute-start.26) | collective-permute-done | bytes 524320 | tf_op jit(solution)/shard_map/ppermute | solution.py:100
  503.2 21.9 %collective-permute-done.27 = bf16[256,2048]{1,0:T(8,128)(2,1)S(1)} collective-permute-done((bf16[256,2048]{1,0:T(8,128)(2,1)S(1)}, bf16[256,2048]{1,0:T(8,128)(2,1)S(1)}, u32[]{:S(2)}, u32[]{:S(2)}) %collective-permute-start.27) | collective-permute-done | bytes 1048608 | tf_op jit(solution)/shard_map/ppermute | solution.py:104
  527.8 13.1 %fusion = (f32[2,2,1024]{2,1,0:T(2,128)S(1)}, f32[2,1024,1024,2]{2,1,3,0:T(8,128)}) fusion(f32[2,1024,1024,2]{2,1,3,0:T(8,128)} %copy-done, f32[2,2,1024]{2,1,0:T(2,128)S(1)} %log_add_fusion, pred[1024,1024]{0,1:T(8,128)(4,1)S(1)} %copy-done.8, bf16[1024,2,128,1]{0,2,3,1:T(8,128)(2,1)S(1)} %bitcast.382, bf16[1024,2,2,128]{0,3,2,1:T(8,128)(2,1)S(1)} %bitcast.395), kind=kOutput, calls=%fused_computation.2 | convolution fusion | flops 1094709248 | bytes 36208640 | tf_op jit(solution)/shard_map/qgrd,kgd->grqk/dot_general | solution.py:294
  540.9 12.5 %fusion.2 = bf16[2,2,1024,1024]{2,3,1,0:T(8,128)(2,1)S(1)} fusion(f32[2,1024,1024,2]{2,1,3,0:T(8,128)} %get-tuple-element.182, f32[2,1024,1024,2]{2,1,3,0:T(8,128)} %copy-done, f32[2,2,1024]{2,1,0:T(2,128)S(1)} %get-tuple-element.181, f32[2,2,1024]{2,1,0:T(2,128)S(1)} %log_add_fusion, pred[1024,1024]{0,1:T(8,128)(4,1)S(1)} %copy-done.8), kind=kLoop, calls=%fused_computation.4 | loop fusion | flops 25165824 | bytes 43024384 | tf_op jit(solution)/shard_map/convert_element_type | solution.py:296
  569.8 11.2 %fusion.60 = bf16[2,128,1024]{2,1,0:T(8,128)(2,1)} fusion(bf16[1024,2,2,128]{0,3,2,1:T(8,128)(2,1)} %bitcast.396, f32[2,1024,1024,2]{2,1,3,0:T(8,128)} %copy-done, f32[2,2,1024]{2,1,0:T(2,128)S(1)} %log_add_fusion, pred[1024,1024]{0,1:T(8,128)(4,1)S(1)} %copy-done.8), kind=kOutput, calls=%fused_computation.121 | convolution fusion | flops 1090781184 | bytes 19415040 | tf_op jit(solution)/shard_map/grqk,qgrd->kgd/dot_general | solution.py:299
  581.0 70.2 %reduce-scatter.5.cloned.1.call-done = bf16[256,3072]{0,1:T(8,128)(2,1)} async-done(((bf16[2048,3072]{0,1:T(8,128)(2,1)}), bf16[256,3072]{0,1:T(8,128)(2,1)}) %reduce-scatter.5.cloned.1.call-update) | async-done | bytes 1572880 | tf_op jit(solution)/shard_map/reduce_scatter | solution.py:270
  651.3 13.9 %fusion.12 = (f32[2048]{0:T(1024)S(1)}, bf16[1024,2048]{1,0:T(8,128)(2,1)}, f32[1024,2048]{1,0:T(8,128)}) fusion(bf16[1024,2048]{1,0:T(8,128)(2,1)} %copy-done.22, f32[1024]{0:T(1024)S(1)} %copy-done.70, bf16[2048,1664]{0,1:T(8,128)(2,1)} %all-gather.4.cloned.1.call-done, bf16[1024,256]{0,1:T(8,128)(2,1)} %bitcast.416, bf16[1024,256]{0,1:T(8,128)(2,1)} %bitcast.400, ...), kind=kOutput, calls=%fused_computation.22 | convolution fusion | flops 4311742464 | bytes 23080960 | tf_op jit(solution)/shard_map/dot_general | solution.py:67
  697.6 16.6 %collective-permute-done.30 = bf16[2,128,2048]{2,1,0:T(8,128)(2,1)S(1)} collective-permute-done((bf16[2,128,2048]{2,1,0:T(8,128)(2,1)S(1)}, bf16[2,128,2048]{2,1,0:T(8,128)(2,1)S(1)}, u32[]{:S(2)}, u32[]{:S(2)}) %collective-permute-start.30) | collective-permute-done | bytes 1048608 | tf_op jit(solution)/shard_map/ppermute | solution.py:117
  (473 shorter events, 317.2 us)
Async XLA Ops:
  7.2 91.1 %all-gather.4.cloned.1.call-start = ((), (), s32[]{:S(2)}) async-start(), calls=%async_computation.4 | async-start | bytes 7667712 | tf_op jit(solution)/shard_map/all_gather | solution.py:137
  15.1 207.5 %all-gather.8.cloned.1.call-start = ((), (), s32[]{:S(2)}) async-start(), calls=%async_computation.6 | async-start | bytes 7077888 | tf_op jit(solution)/shard_map/all_gather | solution.py:137
  17.4 253.1 %all-gather.6.cloned.1.call-start = ((), (), s32[]{:S(2)}) async-start(), calls=%async_computation.5 | async-start | bytes 14155776 | tf_op jit(solution)/shard_map/all_gather | solution.py:137
  27.0 553.9 %reduce-scatter.7.cloned.1.call-start = ((), (), s32[]{:S(2)}) async-start(), calls=%async_computation.8 | async-start | bytes 7077888 | tf_op jit(solution)/shard_map/reduce_scatter | solution.py:283
  33.4 24.5 %collective-permute-start.1 = (bf16[256,2048]{1,0:T(8,128)(2,1)S(1)}, bf16[256,2048]{1,0:T(8,128)(2,1)S(1)}, u32[]{:S(2)}, u32[]{:S(2)}) collective-permute-start(bf16[256,2048]{1,0:T(8,128)(2,1)S(1)} %pad_maximum_fusion.15), channel_id=1, source_target_pairs={{0,2},{2,0},{1,3},{3,1},{4,6},{6,4},{5,7},{7,5},{8,10},{10,8},{9,1... | collective-permute-start | bytes 3145736 | tf_op jit(solution)/shard_map/ppermute | solution.py:103
  137.8 26.1 %collective-permute-start.6 = (bf16[2,128,2048]{2,1,0:T(8,128)(2,1)S(1)}, bf16[2,128,2048]{2,1,0:T(8,128)(2,1)S(1)}, u32[]{:S(2)}, u32[]{:S(2)}) collective-permute-start(bf16[2,128,2048]{2,1,0:T(8,128)(2,1)S(1)} %bitcast.392), channel_id=1, source_target_pairs={{0,1},{1,0},{2,3},{3,2},{4,5},{5,4},{6,7},{7,6},{8,9},{9,8},{10,11... | collective-permute-start | bytes 3145736 | tf_op jit(solution)/shard_map/ppermute | solution.py:117
  139.8 39.7 %collective-permute-start.12 = (bf16[128,2048]{1,0:T(8,128)(2,1)S(1)}, bf16[128,2048]{1,0:T(8,128)(2,1)S(1)}, u32[]{:S(2)}, u32[]{:S(2)}) collective-permute-start(bf16[128,2048]{1,0:T(8,128)(2,1)S(1)} %get-tuple-element.130), channel_id=1, source_target_pairs={{0,1},{1,0},{2,3},{3,2},{4,5},{5,4},{6,7},{7,6},{8,9},{9,8},{10,11... | collective-permute-start | bytes 1572872 | tf_op jit(solution)/shard_map/ppermute | solution.py:99
  140.9 52.1 %collective-permute-start.14 = (bf16[128,2048]{1,0:T(8,128)(2,1)S(1)}, bf16[128,2048]{1,0:T(8,128)(2,1)S(1)}, u32[]{:S(2)}, u32[]{:S(2)}) collective-permute-start(bf16[128,2048]{1,0:T(8,128)(2,1)S(1)} %get-tuple-element.128), channel_id=1, source_target_pairs={{0,2},{2,0},{1,3},{3,1},{4,6},{6,4},{5,7},{7,5},{8,10},{10,8},{9,1... | collective-permute-start | bytes 1572872 | tf_op jit(solution)/shard_map/ppermute | solution.py:100
  142.2 36.0 %collective-permute-start.4 = (bf16[2,128,2048]{2,1,0:T(8,128)(2,1)S(1)}, bf16[2,128,2048]{2,1,0:T(8,128)(2,1)S(1)}, u32[]{:S(2)}, u32[]{:S(2)}) collective-permute-start(bf16[2,128,2048]{2,1,0:T(8,128)(2,1)S(1)} %bitcast.391), channel_id=1, source_target_pairs={{0,2},{2,0},{1,3},{3,1},{4,6},{6,4},{5,7},{7,5},{8,10},{10,8},{9,1... | collective-permute-start | bytes 3145736 | tf_op jit(solution)/shard_map/ppermute | solution.py:116
  164.2 25.2 %collective-permute-start.7 = (bf16[128,2048]{1,0:T(8,128)(2,1)S(1)}, bf16[128,2048]{1,0:T(8,128)(2,1)S(1)}, u32[]{:S(2)}, u32[]{:S(2)}) collective-permute-start(bf16[128,2048]{1,0:T(8,128)(2,1)S(1)} %fusion.81), channel_id=1, source_target_pairs={{0,2},{2,0},{1,3},{3,1},{4,6},{6,4},{5,7},{7,5},{8,10},{10,8},{9,1... | collective-permute-start | bytes 1572872 | tf_op jit(solution)/shard_map/ppermute | solution.py:121
  179.6 28.2 %collective-permute-start.13 = (bf16[256,2048]{1,0:T(8,128)(2,1)S(1)}, bf16[256,2048]{1,0:T(8,128)(2,1)S(1)}, u32[]{:S(2)}, u32[]{:S(2)}) collective-permute-start(bf16[256,2048]{1,0:T(8,128)(2,1)S(1)} %pad_maximum_fusion.19), channel_id=1, source_target_pairs={{0,2},{2,0},{1,3},{3,1},{4,6},{6,4},{5,7},{7,5},{8,10},{10,8},{9,1... | collective-permute-start | bytes 3145736 | tf_op jit(solution)/shard_map/ppermute | solution.py:103
  193.1 28.4 %collective-permute-start.15 = (bf16[256,2048]{1,0:T(8,128)(2,1)S(1)}, bf16[256,2048]{1,0:T(8,128)(2,1)S(1)}, u32[]{:S(2)}, u32[]{:S(2)}) collective-permute-start(bf16[256,2048]{1,0:T(8,128)(2,1)S(1)} %pad_maximum_fusion.20), channel_id=1, source_target_pairs={{0,1},{1,0},{2,3},{3,2},{4,5},{5,4},{6,7},{7,6},{8,9},{9,8},{10,11... | collective-permute-start | bytes 3145736 | tf_op jit(solution)/shard_map/ppermute | solution.py:104
  211.3 30.1 %collective-permute-start.9 = (bf16[256,2048]{1,0:T(8,128)(2,1)}, bf16[256,2048]{1,0:T(8,128)(2,1)}, u32[]{:S(2)}, u32[]{:S(2)}) collective-permute-start(bf16[256,2048]{1,0:T(8,128)(2,1)} %pad_maximum_fusion.17), channel_id=1, source_target_pairs={{0,2},{2,0},{1,3},{3,1},{4,6},{6,4},{5,7},{7,5},{8,10},{10,8},{9,1... | collective-permute-start | bytes 3145736 | tf_op jit(solution)/shard_map/ppermute | solution.py:103
  379.8 26.3 %collective-permute-start.22 = (bf16[2,128,2048]{2,1,0:T(8,128)(2,1)}, bf16[2,128,2048]{2,1,0:T(8,128)(2,1)}, u32[]{:S(2)}, u32[]{:S(2)}) collective-permute-start(bf16[2,128,2048]{2,1,0:T(8,128)(2,1)} %bitcast.63), channel_id=1, source_target_pairs={{0,1},{1,0},{2,3},{3,2},{4,5},{5,4},{6,7},{7,6},{8,9},{9,8},{10,11... | collective-permute-start | bytes 3145736 | tf_op jit(solution)/shard_map/ppermute | solution.py:117
  381.3 28.6 %collective-permute-start.20 = (bf16[2,128,2048]{2,1,0:T(8,128)(2,1)}, bf16[2,128,2048]{2,1,0:T(8,128)(2,1)S(1)}, u32[]{:S(2)}, u32[]{:S(2)}) collective-permute-start(bf16[2,128,2048]{2,1,0:T(8,128)(2,1)} %bitcast.59), channel_id=1, source_target_pairs={{0,2},{2,0},{1,3},{3,1},{4,6},{6,4},{5,7},{7,5},{8,10},{10,8},{9,1... | collective-permute-start | bytes 3145736 | tf_op jit(solution)/shard_map/ppermute | solution.py:116
  395.6 33.1 %collective-permute-start.18 = (bf16[2,128,2048]{2,1,0:T(8,128)(2,1)}, bf16[2,128,2048]{2,1,0:T(8,128)(2,1)}, u32[]{:S(2)}, u32[]{:S(2)}) collective-permute-start(bf16[2,128,2048]{2,1,0:T(8,128)(2,1)} %bitcast.55), channel_id=1, source_target_pairs={{0,1},{1,0},{2,3},{3,2},{4,5},{5,4},{6,7},{7,6},{8,9},{9,8},{10,11... | collective-permute-start | bytes 3145736 | tf_op jit(solution)/shard_map/ppermute | solution.py:117
  396.2 35.7 %collective-permute-start.16 = (bf16[2,128,2048]{2,1,0:T(8,128)(2,1)}, bf16[2,128,2048]{2,1,0:T(8,128)(2,1)}, u32[]{:S(2)}, u32[]{:S(2)}) collective-permute-start(bf16[2,128,2048]{2,1,0:T(8,128)(2,1)} %bitcast.51), channel_id=1, source_target_pairs={{0,2},{2,0},{1,3},{3,1},{4,6},{6,4},{5,7},{7,5},{8,10},{10,8},{9,1... | collective-permute-start | bytes 3145736 | tf_op jit(solution)/shard_map/ppermute | solution.py:116
  408.4 32.9 %collective-permute-start.23 = (bf16[128,2048]{1,0:T(8,128)(2,1)S(1)}, bf16[128,2048]{1,0:T(8,128)(2,1)S(1)}, u32[]{:S(2)}, u32[]{:S(2)}) collective-permute-start(bf16[128,2048]{1,0:T(8,128)(2,1)S(1)} %fusion.85), channel_id=1, source_target_pairs={{0,2},{2,0},{1,3},{3,1},{4,6},{6,4},{5,7},{7,5},{8,10},{10,8},{9,1... | collective-permute-start | bytes 1572872 | tf_op jit(solution)/shard_map/ppermute | solution.py:121
  410.3 31.1 %collective-permute-start.21 = (bf16[128,2048]{1,0:T(8,128)(2,1)S(1)}, bf16[128,2048]{1,0:T(8,128)(2,1)S(1)}, u32[]{:S(2)}, u32[]{:S(2)}) collective-permute-start(bf16[128,2048]{1,0:T(8,128)(2,1)S(1)} %fusion.84), channel_id=1, source_target_pairs={{0,1},{1,0},{2,3},{3,2},{4,5},{5,4},{6,7},{7,6},{8,9},{9,8},{10,11... | collective-permute-start | bytes 1572872 | tf_op jit(solution)/shard_map/ppermute | solution.py:120
  453.6 197.5 %reduce-scatter.5.cloned.1.call-start = ((), (), s32[]{:S(2)}) async-start(), calls=%async_computation.7 | async-start | bytes 14155776 | tf_op jit(solution)/shard_map/reduce_scatter | solution.py:270
  454.2 234.1 %reduce-scatter.9.cloned.1.call-start = ((), (), s32[]{:S(2)}) async-start(), calls=%async_computation.9 | async-start | bytes 2359296 | tf_op jit(solution)/shard_map/reduce_scatter | solution.py:290
  467.5 35.5 %collective-permute-start.25 = (bf16[256,2048]{1,0:T(8,128)(2,1)S(1)}, bf16[256,2048]{1,0:T(8,128)(2,1)S(1)}, u32[]{:S(2)}, u32[]{:S(2)}) collective-permute-start(bf16[256,2048]{1,0:T(8,128)(2,1)S(1)} %pad_maximum_fusion.21), channel_id=1, source_target_pairs={{0,2},{2,0},{1,3},{3,1},{4,6},{6,4},{5,7},{7,5},{8,10},{10,8},{9,1... | collective-permute-start | bytes 3145736 | tf_op jit(solution)/shard_map/ppermute | solution.py:103
  469.0 33.2 %collective-permute-start.26 = (bf16[128,2048]{1,0:T(8,128)(2,1)S(1)}, bf16[128,2048]{1,0:T(8,128)(2,1)S(1)}, u32[]{:S(2)}, u32[]{:S(2)}) collective-permute-start(bf16[128,2048]{1,0:T(8,128)(2,1)S(1)} %get-tuple-element.125), channel_id=1, source_target_pairs={{0,2},{2,0},{1,3},{3,1},{4,6},{6,4},{5,7},{7,5},{8,10},{10,8},{9,1... | collective-permute-start | bytes 1572872 | tf_op jit(solution)/shard_map/ppermute | solution.py:100
  651.1 93.1 %reduce-scatter.11.cloned.1.call-start = ((), (), s32[]{:S(2)}) async-start(), calls=%async_computation.10 | async-start | bytes 5308416 | tf_op jit(solution)/shard_map/reduce_scatter | solution.py:346
  (103 other events, 1249.2 us)
Sparse Core Ops, SparseCore 0:
  15.2 72.1 all-gather.3
  89.6 63.3 all-gather.7
  155.2 115.3 all-gather.5
  453.7 67.6 reduce-scatter.6
  523.5 127.5 reduce-scatter.4
  653.8 34.3 reduce-scatter.8
  690.6 53.6 reduce-scatter.10

commit v13 on v12

--- a/solution.py
+++ b/solution.py
@@ -283,22 +283,27 @@
     mlp_grads.append(lax.psum_scatter(last_joined, "wide", scatter_dimension=0, tiled=True))
     branch_rows = narrow_gather(d_resid_low, relative)
     out_grad = contract_rows(branch_rows, attended).astype(jnp.bfloat16)
+    d_attended = jnp.dot(branch_rows, out_wt, preferred_element_type=jnp.float32).astype(jnp.bfloat16)
+    d_mixed = d_attended.reshape(rows_group, groups_here, repeat, HD)
+    d_value = jnp.einsum(
+        "grqk,qgrd->kgd", p_probs.astype(jnp.bfloat16), d_mixed, preferred_element_type=jnp.float32
+    ).astype(jnp.bfloat16)
+    value_grad = contract_rows(normed_all, d_value.reshape(rows_group, groups_here * HD))
+    out_grad = jnp.concatenate([out_grad, value_grad.astype(jnp.bfloat16)], axis=1)
     mlp_grads, out_grad = lax.optimization_barrier((mlp_grads, out_grad))
     mlp_grads = [
         split_cols(g.astype(jnp.float32), [2 * ff_parts[h], ff_parts[h]]) for h, g in enumerate(mlp_grads)
     ]
-    g_out_t = lax.psum_scatter(out_grad, "wide", scatter_dimension=0, tiled=True).astype(jnp.float32)
-    d_attended = jnp.dot(branch_rows, out_wt, preferred_element_type=jnp.float32).astype(jnp.bfloat16)
-    d_mixed = d_attended.reshape(rows_group, groups_here, repeat, HD)
+    g_out_t, g_value = split_cols(
+        lax.psum_scatter(out_grad, "wide", scatter_dimension=0, tiled=True).astype(jnp.float32),
+        [q_cols, kv_cols],
+    )
 
     d_probs = jnp.einsum("qgrd,kgd->grqk", d_mixed, v_use, preferred_element_type=jnp.float32)
     inner = jnp.sum(p_probs * d_probs, axis=-1, keepdims=True)
     d_scores = (p_probs * (d_probs - inner)).astype(jnp.bfloat16)
     d_query = jnp.einsum("grqk,kgd->qgrd", d_scores, k_use, preferred_element_type=jnp.float32) * scale
     d_key = jnp.einsum("grqk,qgrd->kgd", d_scores, q_grouped, preferred_element_type=jnp.float32) * scale
-    d_value = jnp.einsum(
-        "grqk,qgrd->kgd", p_probs.astype(jnp.bfloat16), d_mixed, preferred_element_type=jnp.float32
-    ).astype(jnp.bfloat16)
 
     d_query = d_query.reshape(rows_group, heads_here, HD)
     d_q_norm = d_query * cos_heads + rotate_back(d_query * sin_heads)
@@ -338,13 +343,18 @@
         axis=-1,
     ).reshape(d_full, 4)
     gain_block = jnp.pad(gain_block, ((0, 0), (0, 124)))
+    qk_cols = q_cols + kv_cols
     qkv_grad = jnp.concatenate(
-        [contract_rows(normed_all, d_qkv).astype(jnp.bfloat16), gain_block.astype(jnp.bfloat16)], axis=1
+        [
+            contract_rows(normed_all, d_qkv[:, :qk_cols]).astype(jnp.bfloat16),
+            gain_block.astype(jnp.bfloat16),
+        ],
+        axis=1,
     )
     g_out_t, qkv_grad = lax.optimization_barrier((g_out_t, qkv_grad))
     g_qkv, g_gains = split_cols(
         lax.psum_scatter(qkv_grad, "wide", scatter_dimension=0, tiled=True).astype(jnp.float32),
-        [q_cols + 2 * kv_cols, 128],
+        [qk_cols, 128],
     )
     d_normed = narrow_scatter(d_normed_partial, relative)
     d_input_part, _ = rms_back(inputs, gain_attn, d_normed)
@@ -356,7 +366,6 @@
 
     g_query = g_qkv[:, :q_cols]
     g_key = g_qkv[:, q_cols : q_cols + kv_cols]
-    g_value = g_qkv[:, q_cols + kv_cols :]
     g_gate = jnp.concatenate([mlp_grads[h][0][:, : ff_parts[h]] for h in range(2)], axis=1)
     g_up = jnp.concatenate([mlp_grads[h][0][:, ff_parts[h] :] for h in range(2)], axis=1)
     g_down = jnp.concatenate([mlp_grads[h][1] for h in range(2)], axis=1).T

time: 762 us -> 764 us (level)
  matrix products: 177 us -> 164 us
    dot_general x6 -> x7, matrix products: 44.3 us -> 40.1 us  [contract_rows(): lax.dot_general(left, right, (((0,), (0,)), ((), ())), preferred_element_...]
    unnamed x215 -> x222, local copies, waits for them, and re-layouts: 35.7 us -> 37 us
  transfers between devices with their start and end apart: 41 -> 41, of which waited for: 26 -> 25; matrix products, arithmetic and copies ran while one was open for 27% -> 26% of each run, Pallas kernels for 0% -> 0%
where the time goes in v13:
time: 764 us; the launch traced here: 757 us
  waiting for transfers between devices  363 us (48%)
  matrix products  164 us (21%)
  other arithmetic  88.9 us (12%)
  local copies, waits for them, and re-layouts  81.7 us (11%)
  starting transfers between devices  42.4 us (6%)
  between operations  16.6 us (2%)
    reduce_scatter x1, waiting for transfers between devices, shards_body(): lax.psum_scatter(joined, 'wide', scatter_dimension=0, tiled=True)  77.4 us
    ppermute x4, waiting for transfers between devices, narrow_scatter(): b_got = lax.ppermute(blocks[6:8].astype(jnp.bfloat16), 'narrow', XPERM)  55.7 us
    ppermute x4, waiting for transfers between devices, narrow_gather(): b_pair_x = lax.ppermute(b_pair, 'narrow', XPERM)  48.4 us
    dot_general x6, matrix products, times_transposed(): lax.dot_general(left, right, (((1,), (1,)), ((), ())), preferred_element_...  43.6 us
    ppermute x4, waiting for transfers between devices, narrow_gather(): b_y = lax.ppermute(b, 'narrow', YPERM)  43.5 us
    ppermute x4, waiting for transfers between devices, narrow_gather(): a_pair_y = lax.ppermute(a_pair, 'narrow', YPERM)  43.4 us
    dot_general x7, matrix products, contract_rows(): lax.dot_general(left, right, (((0,), (0,)), ((), ())), preferred_element_...  40.1 us
    unnamed x222, local copies, waits for them, and re-layouts  37 us
  transfers between devices with their start and end apart: 41, of which 25 were waited for; matrix products, arithmetic and copies ran while one was open for 26% of the time, Pallas kernels for 0%

profile of v13, /device:TPU:0, one launch (start us, length us, event | category | flops | bytes accessed | tf_op | source)
XLA Modules:
  0.0 757.1 jit_solution(1369791225649052010)
XLA Ops:
  36.2 21.7 %collective-permute-done.1 = bf16[256,2048]{1,0:T(8,128)(2,1)S(1)} collective-permute-done((bf16[256,2048]{1,0:T(8,128)(2,1)S(1)}, bf16[256,2048]{1,0:T(8,128)(2,1)S(1)}, u32[]{:S(2)}, u32[]{:S(2)}) %collective-permute-start.1) | collective-permute-done | bytes 1048608 | tf_op jit(solution)/shard_map/ppermute | solution.py:103
  61.4 10.9 %collective-permute-done.2 = bf16[128,2048]{1,0:T(8,128)(2,1)S(1)} collective-permute-done((bf16[128,2048]{1,0:T(8,128)(2,1)S(1)}, bf16[128,2048]{1,0:T(8,128)(2,1)S(1)}, u32[]{:S(2)}, u32[]{:S(2)}) %collective-permute-start.2) | collective-permute-done | bytes 524320 | tf_op jit(solution)/shard_map/ppermute | solution.py:100
  78.2 17.2 %collective-permute-done.3 = bf16[256,2048]{1,0:T(8,128)(2,1)S(1)} collective-permute-done((bf16[256,2048]{1,0:T(8,128)(2,1)S(1)}, bf16[256,2048]{1,0:T(8,128)(2,1)S(1)}, u32[]{:S(2)}, u32[]{:S(2)}) %collective-permute-start.3) | collective-permute-done | bytes 1048608 | tf_op jit(solution)/shard_map/ppermute | solution.py:104
  143.5 20.5 %collective-permute-done.6 = bf16[2,128,2048]{2,1,0:T(8,128)(2,1)S(1)} collective-permute-done((bf16[2,128,2048]{2,1,0:T(8,128)(2,1)S(1)}, bf16[2,128,2048]{2,1,0:T(8,128)(2,1)S(1)}, u32[]{:S(2)}, u32[]{:S(2)}) %collective-permute-start.6) | collective-permute-done | bytes 1048608 | tf_op jit(solution)/shard_map/ppermute | solution.py:117
  165.2 13.0 %collective-permute-done.4 = bf16[2,128,2048]{2,1,0:T(8,128)(2,1)S(1)} collective-permute-done((bf16[2,128,2048]{2,1,0:T(8,128)(2,1)S(1)}, bf16[2,128,2048]{2,1,0:T(8,128)(2,1)S(1)}, u32[]{:S(2)}, u32[]{:S(2)}) %collective-permute-start.4) | collective-permute-done | bytes 1048608 | tf_op jit(solution)/shard_map/ppermute | solution.py:116
  195.2 12.7 %collective-permute-done.13 = bf16[256,2048]{1,0:T(8,128)(2,1)S(1)} collective-permute-done((bf16[256,2048]{1,0:T(8,128)(2,1)S(1)}, bf16[256,2048]{1,0:T(8,128)(2,1)S(1)}, u32[]{:S(2)}, u32[]{:S(2)}) %collective-permute-start.13) | collective-permute-done | bytes 1048608 | tf_op jit(solution)/shard_map/ppermute | solution.py:103
  232.3 9.1 %collective-permute-done.9 = bf16[256,2048]{1,0:T(8,128)(2,1)} collective-permute-done((bf16[256,2048]{1,0:T(8,128)(2,1)}, bf16[256,2048]{1,0:T(8,128)(2,1)}, u32[]{:S(2)}, u32[]{:S(2)}) %collective-permute-start.9) | collective-permute-done | bytes 1048608 | tf_op jit(solution)/shard_map/ppermute | solution.py:103
  249.2 21.4 %all-gather.6.cloned.1.call-done = bf16[2048,3072]{0,1:T(8,128)(2,1)} async-done(((bf16[256,3072]{0,1:T(8,128)(2,1)}), bf16[2048,3072]{0,1:T(8,128)(2,1)}) %all-gather.6.cloned.1.call-update) | async-done | bytes 12582928 | tf_op jit(solution)/shard_map/all_gather | solution.py:137
  270.5 12.6 %fusion.19 = f32[1024,2048]{1,0:T(8,128)S(1)} fusion(bf16[1024,2048]{1,0:T(8,128)(2,1)} %constant_dynamic-update-slice_fusion.13, bf16[2048,3072]{0,1:T(8,128)(2,1)} %all-gather.6.cloned.1.call-done), kind=kOutput, calls=%fused_computation.29 | convolution fusion | flops 8589934592 | bytes 20971520 | tf_op jit(solution)/shard_map/dot_general | solution.py:250
  283.1 10.6 %multiply_convert_fusion.1 = (bf16[1024,1024]{1,0:T(8,128)(2,1)S(1)}, bf16[1024,1024]{1,0:T(8,128)(2,1)}, bf16[1024,1024]{1,0:T(8,128)(2,1)S(1)}) fusion(f32[1024,2048]{1,0:T(8,128)S(1)} %fusion.19, bf16[1024,2048]{1,0:T(8,128)(2,1)} %constant_dynamic-update-slice_fusion.19, bf16[2048,3072]{0,1:T(8,128)(2,1)} %all-gather.6.cloned.1.call-done), kind=kOutput, calls=%fused_computation.35 | convolution fusion | flops 4311744512 | bytes 23068672 | tf_op jit(solution)/shard_map/dot_general | solution.py:257
  293.7 8.5 %convolution_convert_fusion.2 = bf16[2048,1024]{0,1:T(8,128)(2,1)S(1)} fusion(bf16[1024,2048]{1,0:T(8,128)(2,1)} %constant_dynamic-update-slice_fusion.19, bf16[1024,1024]{1,0:T(8,128)(2,1)S(1)} %get-tuple-element.95), kind=kOutput, calls=%fused_computation.41 | convolution fusion | flops 4297064448 | bytes 10485760 | tf_op jit(solution)/shard_map/dot_general | solution.py:61
  302.3 11.6 %convolution_convert_fusion = bf16[2048,2048]{0,1:T(8,128)(2,1)S(1)} fusion(bf16[1024,2048]{1,0:T(8,128)(2,1)} %constant_dynamic-update-slice_fusion.13, bf16[1024,1024]{1,0:T(8,128)(2,1)} %get-tuple-element.84, bf16[1024,1024]{1,0:T(8,128)(2,1)S(1)} %get-tuple-element.83), kind=kOutput, calls=%fused_computation.26 | convolution fusion | flops 8602517504 | bytes 16777216 | tf_op jit(solution)/shard_map/dot_general | solution.py:61
  313.9 15.0 %pad_maximum_fusion = bf16[2048,3072]{0,1:T(8,128)(2,1)} fusion(bf16[2048,1024]{0,1:T(8,128)(2,1)S(1)} %convolution_convert_fusion.2, bf16[2048,2048]{0,1:T(8,128)(2,1)S(1)} %convolution_convert_fusion), kind=kLoop, calls=%fused_computation.13 | loop fusion | flops 25165824 | bytes 25165824 | tf_op jit(solution)/shard_map/concatenate | solution.py:265
  356.6 16.9 %fusion.167 = (bf16[1024,2048]{1,0:T(8,128)(2,1)}, f32[1024,2048]{1,0:T(8,128)}) fusion(f32[1024,2048]{1,0:T(8,128)} %fusion.67, bf16[2048,3072]{0,1:T(8,128)(2,1)} %all-gather.6.cloned.1.call-done, bf16[1024,1024]{1,0:T(8,128)(2,1)} %get-tuple-element.84, bf16[1024,1024]{1,0:T(8,128)(2,1)} %copy-done.74), kind=kOutput, calls=%fused_computation.381 | convolution fusion | flops 8602517504 | bytes 33554432 | tf_op jit(solution)/shard_map/dot_general | solution.py:67
  411.8 16.9 %collective-permute-done.18 = bf16[2,128,2048]{2,1,0:T(8,128)(2,1)} collective-permute-done((bf16[2,128,2048]{2,1,0:T(8,128)(2,1)}, bf16[2,128,2048]{2,1,0:T(8,128)(2,1)}, u32[]{:S(2)}, u32[]{:S(2)}) %collective-permute-start.18) | collective-permute-done | bytes 1048608 | tf_op jit(solution)/shard_map/ppermute | solution.py:117
  442.2 9.3 %collective-permute-done.19 = bf16[128,2048]{1,0:T(8,128)(2,1)S(1)} collective-permute-done((bf16[128,2048]{1,0:T(8,128)(2,1)S(1)}, bf16[128,2048]{1,0:T(8,128)(2,1)S(1)}, u32[]{:S(2)}, u32[]{:S(2)}) %collective-permute-start.19) | collective-permute-done | bytes 524320 | tf_op jit(solution)/shard_map/ppermute | solution.py:121
  455.7 12.4 %collective-permute-done.24 = bf16[128,2048]{1,0:T(8,128)(2,1)S(1)} collective-permute-done((bf16[128,2048]{1,0:T(8,128)(2,1)S(1)}, bf16[128,2048]{1,0:T(8,128)(2,1)S(1)}, u32[]{:S(2)}, u32[]{:S(2)}) %collective-permute-start.24) | collective-permute-done | bytes 524320 | tf_op jit(solution)/shard_map/ppermute | solution.py:99
  470.4 32.6 %collective-permute-done.26 = bf16[128,2048]{1,0:T(8,128)(2,1)S(1)} collective-permute-done((bf16[128,2048]{1,0:T(8,128)(2,1)S(1)}, bf16[128,2048]{1,0:T(8,128)(2,1)S(1)}, u32[]{:S(2)}, u32[]{:S(2)}) %collective-permute-start.26) | collective-permute-done | bytes 524320 | tf_op jit(solution)/shard_map/ppermute | solution.py:100
  503.9 21.9 %collective-permute-done.27 = bf16[256,2048]{1,0:T(8,128)(2,1)S(1)} collective-permute-done((bf16[256,2048]{1,0:T(8,128)(2,1)S(1)}, bf16[256,2048]{1,0:T(8,128)(2,1)S(1)}, u32[]{:S(2)}, u32[]{:S(2)}) %collective-permute-start.27) | collective-permute-done | bytes 1048608 | tf_op jit(solution)/shard_map/ppermute | solution.py:104
  528.4 12.8 %fusion = (f32[2,2,1024]{2,1,0:T(2,128)S(1)}, f32[2,1024,1024,2]{2,1,3,0:T(8,128)}) fusion(f32[2,1024,1024,2]{2,1,3,0:T(8,128)} %copy-done, f32[2,2,1024]{2,1,0:T(2,128)S(1)} %log_add_fusion, pred[1024,1024]{0,1:T(8,128)(4,1)S(1)} %copy-done.8, bf16[1024,2,128,1]{0,2,3,1:T(8,128)(2,1)S(1)} %bitcast.385, bf16[1024,2,2,128]{0,3,2,1:T(8,128)(2,1)S(1)} %bitcast.399), kind=kOutput, calls=%fused_computation.2 | convolution fusion | flops 1094709248 | bytes 36208640 | tf_op jit(solution)/shard_map/qgrd,kgd->grqk/dot_general | solution.py:302
  541.3 12.6 %fusion.2 = bf16[2,2,1024,1024]{2,3,1,0:T(8,128)(2,1)S(1)} fusion(f32[2,1024,1024,2]{2,1,3,0:T(8,128)} %get-tuple-element.180, f32[2,1024,1024,2]{2,1,3,0:T(8,128)} %copy-done, f32[2,2,1024]{2,1,0:T(2,128)S(1)} %get-tuple-element.179, f32[2,2,1024]{2,1,0:T(2,128)S(1)} %log_add_fusion, pred[1024,1024]{0,1:T(8,128)(4,1)S(1)} %copy-done.8), kind=kLoop, calls=%fused_computation.4 | loop fusion | flops 25165824 | bytes 43024384 | tf_op jit(solution)/shard_map/convert_element_type | solution.py:304
  574.5 77.4 %reduce-scatter.5.cloned.1.call-done = bf16[256,3072]{0,1:T(8,128)(2,1)} async-done(((bf16[2048,3072]{0,1:T(8,128)(2,1)}), bf16[256,3072]{0,1:T(8,128)(2,1)}) %reduce-scatter.5.cloned.1.call-update) | async-done | bytes 1572880 | tf_op jit(solution)/shard_map/reduce_scatter | solution.py:270
  702.2 16.9 %collective-permute-done.30 = bf16[2,128,2048]{2,1,0:T(8,128)(2,1)S(1)} collective-permute-done((bf16[2,128,2048]{2,1,0:T(8,128)(2,1)S(1)}, bf16[2,128,2048]{2,1,0:T(8,128)(2,1)S(1)}, u32[]{:S(2)}, u32[]{:S(2)}) %collective-permute-start.30) | collective-permute-done | bytes 1048608 | tf_op jit(solution)/shard_map/ppermute | solution.py:117
  722.8 8.8 %collective-permute-done.31 = bf16[128,2048]{1,0:T(8,128)(2,1)S(1)} collective-permute-done((bf16[128,2048]{1,0:T(8,128)(2,1)S(1)}, bf16[128,2048]{1,0:T(8,128)(2,1)S(1)}, u32[]{:S(2)}, u32[]{:S(2)}) %collective-permute-start.31) | collective-permute-done | bytes 524320 | tf_op jit(solution)/shard_map/ppermute | solution.py:121
  (485 shorter events, 317.5 us)
Async XLA Ops:
  7.2 91.2 %all-gather.4.cloned.1.call-start = ((), (), s32[]{:S(2)}) async-start(), calls=%async_computation.4 | async-start | bytes 7667712 | tf_op jit(solution)/shard_map/all_gather | solution.py:137
  15.1 207.5 %all-gather.8.cloned.1.call-start = ((), (), s32[]{:S(2)}) async-start(), calls=%async_computation.6 | async-start | bytes 7077888 | tf_op jit(solution)/shard_map/all_gather | solution.py:137
  17.4 253.1 %all-gather.6.cloned.1.call-start = ((), (), s32[]{:S(2)}) async-start(), calls=%async_computation.5 | async-start | bytes 14155776 | tf_op jit(solution)/shard_map/all_gather | solution.py:137
  27.0 547.4 %reduce-scatter.7.cloned.1.call-start = ((), (), s32[]{:S(2)}) async-start(), calls=%async_computation.8 | async-start | bytes 7077888 | tf_op jit(solution)/shard_map/reduce_scatter | solution.py:283
  33.4 24.5 %collective-permute-start.1 = (bf16[256,2048]{1,0:T(8,128)(2,1)S(1)}, bf16[256,2048]{1,0:T(8,128)(2,1)S(1)}, u32[]{:S(2)}, u32[]{:S(2)}) collective-permute-start(bf16[256,2048]{1,0:T(8,128)(2,1)S(1)} %pad_maximum_fusion.15), channel_id=1, source_target_pairs={{0,2},{2,0},{1,3},{3,1},{4,6},{6,4},{5,7},{7,5},{8,10},{10,8},{9,1... | collective-permute-start | bytes 3145736 | tf_op jit(solution)/shard_map/ppermute | solution.py:103
  137.8 26.1 %collective-permute-start.6 = (bf16[2,128,2048]{2,1,0:T(8,128)(2,1)S(1)}, bf16[2,128,2048]{2,1,0:T(8,128)(2,1)S(1)}, u32[]{:S(2)}, u32[]{:S(2)}) collective-permute-start(bf16[2,128,2048]{2,1,0:T(8,128)(2,1)S(1)} %bitcast.396), channel_id=1, source_target_pairs={{0,1},{1,0},{2,3},{3,2},{4,5},{5,4},{6,7},{7,6},{8,9},{9,8},{10,11... | collective-permute-start | bytes 3145736 | tf_op jit(solution)/shard_map/ppermute | solution.py:117
  139.8 39.7 %collective-permute-start.12 = (bf16[128,2048]{1,0:T(8,128)(2,1)S(1)}, bf16[128,2048]{1,0:T(8,128)(2,1)S(1)}, u32[]{:S(2)}, u32[]{:S(2)}) collective-permute-start(bf16[128,2048]{1,0:T(8,128)(2,1)S(1)} %get-tuple-element.128), channel_id=1, source_target_pairs={{0,1},{1,0},{2,3},{3,2},{4,5},{5,4},{6,7},{7,6},{8,9},{9,8},{10,11... | collective-permute-start | bytes 1572872 | tf_op jit(solution)/shard_map/ppermute | solution.py:99
  140.9 52.1 %collective-permute-start.14 = (bf16[128,2048]{1,0:T(8,128)(2,1)S(1)}, bf16[128,2048]{1,0:T(8,128)(2,1)S(1)}, u32[]{:S(2)}, u32[]{:S(2)}) collective-permute-start(bf16[128,2048]{1,0:T(8,128)(2,1)S(1)} %get-tuple-element.126), channel_id=1, source_target_pairs={{0,2},{2,0},{1,3},{3,1},{4,6},{6,4},{5,7},{7,5},{8,10},{10,8},{9,1... | collective-permute-start | bytes 1572872 | tf_op jit(solution)/shard_map/ppermute | solution.py:100
  142.2 36.0 %collective-permute-start.4 = (bf16[2,128,2048]{2,1,0:T(8,128)(2,1)S(1)}, bf16[2,128,2048]{2,1,0:T(8,128)(2,1)S(1)}, u32[]{:S(2)}, u32[]{:S(2)}) collective-permute-start(bf16[2,128,2048]{2,1,0:T(8,128)(2,1)S(1)} %bitcast.395), channel_id=1, source_target_pairs={{0,2},{2,0},{1,3},{3,1},{4,6},{6,4},{5,7},{7,5},{8,10},{10,8},{9,1... | collective-permute-start | bytes 3145736 | tf_op jit(solution)/shard_map/ppermute | solution.py:116
  164.3 25.2 %collective-permute-start.7 = (bf16[128,2048]{1,0:T(8,128)(2,1)S(1)}, bf16[128,2048]{1,0:T(8,128)(2,1)S(1)}, u32[]{:S(2)}, u32[]{:S(2)}) collective-permute-start(bf16[128,2048]{1,0:T(8,128)(2,1)S(1)} %fusion.87), channel_id=1, source_target_pairs={{0,2},{2,0},{1,3},{3,1},{4,6},{6,4},{5,7},{7,5},{8,10},{10,8},{9,1... | collective-permute-start | bytes 1572872 | tf_op jit(solution)/shard_map/ppermute | solution.py:121
  179.6 28.2 %collective-permute-start.13 = (bf16[256,2048]{1,0:T(8,128)(2,1)S(1)}, bf16[256,2048]{1,0:T(8,128)(2,1)S(1)}, u32[]{:S(2)}, u32[]{:S(2)}) collective-permute-start(bf16[256,2048]{1,0:T(8,128)(2,1)S(1)} %pad_maximum_fusion.19), channel_id=1, source_target_pairs={{0,2},{2,0},{1,3},{3,1},{4,6},{6,4},{5,7},{7,5},{8,10},{10,8},{9,1... | collective-permute-start | bytes 3145736 | tf_op jit(solution)/shard_map/ppermute | solution.py:103
  193.2 28.4 %collective-permute-start.15 = (bf16[256,2048]{1,0:T(8,128)(2,1)S(1)}, bf16[256,2048]{1,0:T(8,128)(2,1)S(1)}, u32[]{:S(2)}, u32[]{:S(2)}) collective-permute-start(bf16[256,2048]{1,0:T(8,128)(2,1)S(1)} %pad_maximum_fusion.20), channel_id=1, source_target_pairs={{0,1},{1,0},{2,3},{3,2},{4,5},{5,4},{6,7},{7,6},{8,9},{9,8},{10,11... | collective-permute-start | bytes 3145736 | tf_op jit(solution)/shard_map/ppermute | solution.py:104
  211.4 30.1 %collective-permute-start.9 = (bf16[256,2048]{1,0:T(8,128)(2,1)}, bf16[256,2048]{1,0:T(8,128)(2,1)}, u32[]{:S(2)}, u32[]{:S(2)}) collective-permute-start(bf16[256,2048]{1,0:T(8,128)(2,1)} %pad_maximum_fusion.17), channel_id=1, source_target_pairs={{0,2},{2,0},{1,3},{3,1},{4,6},{6,4},{5,7},{7,5},{8,10},{10,8},{9,1... | collective-permute-start | bytes 3145736 | tf_op jit(solution)/shard_map/ppermute | solution.py:103
  379.8 26.3 %collective-permute-start.22 = (bf16[2,128,2048]{2,1,0:T(8,128)(2,1)}, bf16[2,128,2048]{2,1,0:T(8,128)(2,1)}, u32[]{:S(2)}, u32[]{:S(2)}) collective-permute-start(bf16[2,128,2048]{2,1,0:T(8,128)(2,1)} %bitcast.63), channel_id=1, source_target_pairs={{0,1},{1,0},{2,3},{3,2},{4,5},{5,4},{6,7},{7,6},{8,9},{9,8},{10,11... | collective-permute-start | bytes 3145736 | tf_op jit(solution)/shard_map/ppermute | solution.py:117
  381.3 28.6 %collective-permute-start.20 = (bf16[2,128,2048]{2,1,0:T(8,128)(2,1)}, bf16[2,128,2048]{2,1,0:T(8,128)(2,1)S(1)}, u32[]{:S(2)}, u32[]{:S(2)}) collective-permute-start(bf16[2,128,2048]{2,1,0:T(8,128)(2,1)} %bitcast.59), channel_id=1, source_target_pairs={{0,2},{2,0},{1,3},{3,1},{4,6},{6,4},{5,7},{7,5},{8,10},{10,8},{9,1... | collective-permute-start | bytes 3145736 | tf_op jit(solution)/shard_map/ppermute | solution.py:116
  395.6 33.0 %collective-permute-start.18 = (bf16[2,128,2048]{2,1,0:T(8,128)(2,1)}, bf16[2,128,2048]{2,1,0:T(8,128)(2,1)}, u32[]{:S(2)}, u32[]{:S(2)}) collective-permute-start(bf16[2,128,2048]{2,1,0:T(8,128)(2,1)} %bitcast.55), channel_id=1, source_target_pairs={{0,1},{1,0},{2,3},{3,2},{4,5},{5,4},{6,7},{7,6},{8,9},{9,8},{10,11... | collective-permute-start | bytes 3145736 | tf_op jit(solution)/shard_map/ppermute | solution.py:117
  396.2 35.7 %collective-permute-start.16 = (bf16[2,128,2048]{2,1,0:T(8,128)(2,1)}, bf16[2,128,2048]{2,1,0:T(8,128)(2,1)}, u32[]{:S(2)}, u32[]{:S(2)}) collective-permute-start(bf16[2,128,2048]{2,1,0:T(8,128)(2,1)} %bitcast.51), channel_id=1, source_target_pairs={{0,2},{2,0},{1,3},{3,1},{4,6},{6,4},{5,7},{7,5},{8,10},{10,8},{9,1... | collective-permute-start | bytes 3145736 | tf_op jit(solution)/shard_map/ppermute | solution.py:116
  408.4 32.9 %collective-permute-start.23 = (bf16[128,2048]{1,0:T(8,128)(2,1)S(1)}, bf16[128,2048]{1,0:T(8,128)(2,1)S(1)}, u32[]{:S(2)}, u32[]{:S(2)}) collective-permute-start(bf16[128,2048]{1,0:T(8,128)(2,1)S(1)} %fusion.91), channel_id=1, source_target_pairs={{0,2},{2,0},{1,3},{3,1},{4,6},{6,4},{5,7},{7,5},{8,10},{10,8},{9,1... | collective-permute-start | bytes 1572872 | tf_op jit(solution)/shard_map/ppermute | solution.py:121
  410.3 31.1 %collective-permute-start.21 = (bf16[128,2048]{1,0:T(8,128)(2,1)S(1)}, bf16[128,2048]{1,0:T(8,128)(2,1)S(1)}, u32[]{:S(2)}, u32[]{:S(2)}) collective-permute-start(bf16[128,2048]{1,0:T(8,128)(2,1)S(1)} %fusion.90), channel_id=1, source_target_pairs={{0,1},{1,0},{2,3},{3,2},{4,5},{5,4},{6,7},{7,6},{8,9},{9,8},{10,11... | collective-permute-start | bytes 1572872 | tf_op jit(solution)/shard_map/ppermute | solution.py:120
  454.3 197.5 %reduce-scatter.5.cloned.1.call-start = ((), (), s32[]{:S(2)}) async-start(), calls=%async_computation.7 | async-start | bytes 14155776 | tf_op jit(solution)/shard_map/reduce_scatter | solution.py:270
  454.9 238.0 %reduce-scatter.9.cloned.1.call-start = ((), (), s32[]{:S(2)}) async-start(), calls=%async_computation.9 | async-start | bytes 3538944 | tf_op jit(solution)/shard_map/reduce_scatter | solution.py:298
  468.2 35.5 %collective-permute-start.25 = (bf16[256,2048]{1,0:T(8,128)(2,1)S(1)}, bf16[256,2048]{1,0:T(8,128)(2,1)S(1)}, u32[]{:S(2)}, u32[]{:S(2)}) collective-permute-start(bf16[256,2048]{1,0:T(8,128)(2,1)S(1)} %pad_maximum_fusion.21), channel_id=1, source_target_pairs={{0,2},{2,0},{1,3},{3,1},{4,6},{6,4},{5,7},{7,5},{8,10},{10,8},{9,1... | collective-permute-start | bytes 3145736 | tf_op jit(solution)/shard_map/ppermute | solution.py:103
  469.8 33.2 %collective-permute-start.26 = (bf16[128,2048]{1,0:T(8,128)(2,1)S(1)}, bf16[128,2048]{1,0:T(8,128)(2,1)S(1)}, u32[]{:S(2)}, u32[]{:S(2)}) collective-permute-start(bf16[128,2048]{1,0:T(8,128)(2,1)S(1)} %get-tuple-element.123), channel_id=1, source_target_pairs={{0,2},{2,0},{1,3},{3,1},{4,6},{6,4},{5,7},{7,5},{8,10},{10,8},{9,1... | collective-permute-start | bytes 1572872 | tf_op jit(solution)/shard_map/ppermute | solution.py:100
  651.9 91.5 %reduce-scatter.11.cloned.1.call-start = ((), (), s32[]{:S(2)}) async-start(), calls=%async_computation.10 | async-start | bytes 4128768 | tf_op jit(solution)/shard_map/reduce_scatter | solution.py:356
  (107 other events, 1211.3 us)
Sparse Core Ops, SparseCore 0:
  15.2 72.1 all-gather.3
  89.6 63.3 all-gather.7
  155.2 115.3 all-gather.5
  454.4 67.6 reduce-scatter.6
  524.2 127.5 reduce-scatter.4
  654.0 38.8 reduce-scatter.8
  695.2 44.2 reduce-scatter.10

commit v14 on v13

--- a/solution.py
+++ b/solution.py
@@ -167,9 +167,7 @@
     q_cols = w_query.shape[1]
     kv_cols = w_key.shape[1]
     ff_cols = w_gate.shape[1]
-    ff_first = max(128, (2 * ff_cols // 3) // 128 * 128)
-    ff_parts = (ff_first, ff_cols - ff_first)
-    ff_starts = (0, ff_first)
+    ff_half = ff_cols // 2
     relative = relative_ok(seq_count)
 
     tokens_all = narrow_gather(tokens, relative)
@@ -193,7 +191,7 @@
     down_t = w_down.T
     mlp_sets = []
     for h in range(2):
-        cols = slice(ff_starts[h], ff_starts[h] + ff_parts[h])
+        cols = slice(h * ff_half, (h + 1) * ff_half)
         mlp_sets.append(
             wide_gather([jnp.concatenate([w_gate[:, cols], w_up[:, cols]], axis=1), down_t[:, cols]])
         )
@@ -248,8 +246,8 @@
     for h in range(2):
         gate_up_w, down_wt = mlp_sets[h]
         gate_up = jnp.dot(mlp_all, gate_up_w, preferred_element_type=jnp.float32)
-        gate = gate_up[:, : ff_parts[h]]
-        up = gate_up[:, ff_parts[h] :]
+        gate = gate_up[:, :ff_half]
+        up = gate_up[:, ff_half:]
         sigmoid = jax.nn.sigmoid(gate)
         hidden = (gate * sigmoid * up).astype(jnp.bfloat16)
         part = times_transposed(hidden, down_wt)
@@ -279,7 +277,7 @@
         jnp.einsum("qgrd,kgd->grqk", q_grouped, k_use, preferred_element_type=jnp.float32) * scale
     )
     p_probs = jnp.where(allowed, jnp.exp(p_scores - log_totals[..., None]), 0.0)
-    d_resid_low, last_joined = lax.optimization_barrier((d_resid.astype(jnp.bfloat16), last_joined))
+    d_resid_low = d_resid.astype(jnp.bfloat16)
     mlp_grads.append(lax.psum_scatter(last_joined, "wide", scatter_dimension=0, tiled=True))
     branch_rows = narrow_gather(d_resid_low, relative)
     out_grad = contract_rows(branch_rows, attended).astype(jnp.bfloat16)
@@ -291,9 +289,7 @@
     value_grad = contract_rows(normed_all, d_value.reshape(rows_group, groups_here * HD))
     out_grad = jnp.concatenate([out_grad, value_grad.astype(jnp.bfloat16)], axis=1)
     mlp_grads, out_grad = lax.optimization_barrier((mlp_grads, out_grad))
-    mlp_grads = [
-        split_cols(g.astype(jnp.float32), [2 * ff_parts[h], ff_parts[h]]) for h, g in enumerate(mlp_grads)
-    ]
+    mlp_grads = [split_cols(g.astype(jnp.float32), [2 * ff_half, ff_half]) for g in mlp_grads]
     g_out_t, g_value = split_cols(
         lax.psum_scatter(out_grad, "wide", scatter_dimension=0, tiled=True).astype(jnp.float32),
         [q_cols, kv_cols],
@@ -366,8 +362,8 @@
 
     g_query = g_qkv[:, :q_cols]
     g_key = g_qkv[:, q_cols : q_cols + kv_cols]
-    g_gate = jnp.concatenate([mlp_grads[h][0][:, : ff_parts[h]] for h in range(2)], axis=1)
-    g_up = jnp.concatenate([mlp_grads[h][0][:, ff_parts[h] :] for h in range(2)], axis=1)
+    g_gate = jnp.concatenate([mlp_grads[h][0][:, :ff_half] for h in range(2)], axis=1)
+    g_up = jnp.concatenate([mlp_grads[h][0][:, ff_half:] for h in range(2)], axis=1)
     g_down = jnp.concatenate([mlp_grads[h][1] for h in range(2)], axis=1).T
     output = (resid + narrow_scatter(down_partial, relative)).astype(jnp.bfloat16)
     return (

time: 764 us -> 616 us (0.81)
  waiting for transfers between devices: 363 us -> 231 us
  other arithmetic: 88.9 us -> 80 us
    reduce_scatter x1, waiting for transfers between devices: 77.4 us -> 0.01 us  [shards_body(): lax.psum_scatter(joined, 'wide', scatter_dimension=0, tiled=True)]
    ppermute x4, waiting for transfers between devices: 55.7 us -> 12.7 us  [narrow_scatter(): b_got = lax.ppermute(blocks[6:8].astype(jnp.bfloat16), 'narrow', XPERM)]
    ppermute x4, waiting for transfers between devices: 13.8 us -> 38.1 us  [narrow_scatter(): a_got = lax.ppermute(blocks[2:4].astype(jnp.bfloat16), 'narrow', YPERM)]
    all_gather x3, waiting for transfers between devices: 21.4 us -> 0.02 us  [wide_gather(): lax.all_gather(jnp.concatenate(blocks, axis=1), 'wide', axis=0, tiled=True)]
    ppermute x4, waiting for transfers between devices: 0.01 us -> 20.8 us  [narrow_scatter(): a_got2 = lax.ppermute(a_sum[1].astype(jnp.bfloat16), 'narrow', XPERM)]
    ppermute x4, waiting for transfers between devices: 32.5 us -> 11.8 us  [narrow_scatter(): b_got2 = lax.ppermute(b_sum[1].astype(jnp.bfloat16), 'narrow', YPERM)]
    ppermute x4, waiting for transfers between devices: 48.4 us -> 40.7 us  [narrow_gather(): b_pair_x = lax.ppermute(b_pair, 'narrow', XPERM)]
    unnamed x222 -> x220, local copies, waits for them, and re-layouts: 37 us -> 34.1 us
  transfers between devices with their start and end apart: 41 -> 41, of which waited for: 25 -> 25; matrix products, arithmetic and copies ran while one was open for 26% -> 46% of each run, Pallas kernels for 0% -> 0%
where the time goes in v14:
time: 616 us; the launch traced here: 610 us
  waiting for transfers between devices  231 us (38%)
  matrix products  163 us (26%)
  other arithmetic  80 us (13%)
  local copies, waits for them, and re-layouts  76 us (12%)
  starting transfers between devices  44 us (7%)
  between operations  16.5 us (3%)
    ppermute x4, waiting for transfers between devices, narrow_gather(): a_pair_y = lax.ppermute(a_pair, 'narrow', YPERM)  45.9 us
    dot_general x6, matrix products, times_transposed(): lax.dot_general(left, right, (((1,), (1,)), ((), ())), preferred_element_...  44.1 us
    ppermute x4, waiting for transfers between devices, narrow_gather(): b_pair_x = lax.ppermute(b_pair, 'narrow', XPERM)  40.7 us
    ppermute x4, waiting for transfers between devices, narrow_scatter(): a_got = lax.ppermute(blocks[2:4].astype(jnp.bfloat16), 'narrow', YPERM)  38.1 us
    ppermute x4, waiting for transfers between devices, narrow_gather(): b_y = lax.ppermute(b, 'narrow', YPERM)  36.7 us
    dot_general x7, matrix products, contract_rows(): lax.dot_general(left, right, (((0,), (0,)), ((), ())), preferred_element_...  34.6 us
    unnamed x220, local copies, waits for them, and re-layouts  34.1 us
    dot_general x2, matrix products, shards_body(): gate_up = jnp.dot(mlp_all, gate_up_w, preferred_element_type=jnp.float32)  22.9 us
  transfers between devices with their start and end apart: 41, of which 25 were waited for; matrix products, arithmetic and copies ran while one was open for 46% of the time, Pallas kernels for 0%

profile of v14, /device:TPU:0, one launch (start us, length us, event | category | flops | bytes accessed | tf_op | source)
XLA Modules:
  0.0 610.3 jit_solution(7734639214104382626)
XLA Ops:
  38.6 21.7 %collective-permute-done.1 = bf16[256,2048]{1,0:T(8,128)(2,1)S(1)} collective-permute-done((bf16[256,2048]{1,0:T(8,128)(2,1)S(1)}, bf16[256,2048]{1,0:T(8,128)(2,1)S(1)}, u32[]{:S(2)}, u32[]{:S(2)}) %collective-permute-start.1) | collective-permute-done | bytes 1048608 | tf_op jit(solution)/shard_map/ppermute | solution.py:103
  63.8 10.9 %collective-permute-done.2 = bf16[128,2048]{1,0:T(8,128)(2,1)S(1)} collective-permute-done((bf16[128,2048]{1,0:T(8,128)(2,1)S(1)}, bf16[128,2048]{1,0:T(8,128)(2,1)S(1)}, u32[]{:S(2)}, u32[]{:S(2)}) %collective-permute-start.2) | collective-permute-done | bytes 524320 | tf_op jit(solution)/shard_map/ppermute | solution.py:100
  80.3 17.5 %collective-permute-done.3 = bf16[256,2048]{1,0:T(8,128)(2,1)S(1)} collective-permute-done((bf16[256,2048]{1,0:T(8,128)(2,1)S(1)}, bf16[256,2048]{1,0:T(8,128)(2,1)S(1)}, u32[]{:S(2)}, u32[]{:S(2)}) %collective-permute-start.3) | collective-permute-done | bytes 1048608 | tf_op jit(solution)/shard_map/ppermute | solution.py:104
  142.7 21.2 %collective-permute-done.4 = bf16[2,128,2048]{2,1,0:T(8,128)(2,1)S(1)} collective-permute-done((bf16[2,128,2048]{2,1,0:T(8,128)(2,1)S(1)}, bf16[2,128,2048]{2,1,0:T(8,128)(2,1)S(1)}, u32[]{:S(2)}, u32[]{:S(2)}) %collective-permute-start.4) | collective-permute-done | bytes 1048608 | tf_op jit(solution)/shard_map/ppermute | solution.py:116
  165.5 12.0 %collective-permute-done.6 = bf16[2,128,2048]{2,1,0:T(8,128)(2,1)S(1)} collective-permute-done((bf16[2,128,2048]{2,1,0:T(8,128)(2,1)S(1)}, bf16[2,128,2048]{2,1,0:T(8,128)(2,1)S(1)}, u32[]{:S(2)}, u32[]{:S(2)}) %collective-permute-start.6) | collective-permute-done | bytes 1048608 | tf_op jit(solution)/shard_map/ppermute | solution.py:117
  184.3 8.4 %collective-permute-done.7 = bf16[128,2048]{1,0:T(8,128)(2,1)S(1)} collective-permute-done((bf16[128,2048]{1,0:T(8,128)(2,1)S(1)}, bf16[128,2048]{1,0:T(8,128)(2,1)S(1)}, u32[]{:S(2)}, u32[]{:S(2)}) %collective-permute-start.7) | collective-permute-done | bytes 524320 | tf_op jit(solution)/shard_map/ppermute | solution.py:121
  197.3 14.9 %collective-permute-done.13 = bf16[256,2048]{1,0:T(8,128)(2,1)S(1)} collective-permute-done((bf16[256,2048]{1,0:T(8,128)(2,1)S(1)}, bf16[256,2048]{1,0:T(8,128)(2,1)S(1)}, u32[]{:S(2)}, u32[]{:S(2)}) %collective-permute-start.13) | collective-permute-done | bytes 1048608 | tf_op jit(solution)/shard_map/ppermute | solution.py:103
  214.6 9.9 %collective-permute-done.15 = bf16[256,2048]{1,0:T(8,128)(2,1)S(1)} collective-permute-done((bf16[256,2048]{1,0:T(8,128)(2,1)S(1)}, bf16[256,2048]{1,0:T(8,128)(2,1)S(1)}, u32[]{:S(2)}, u32[]{:S(2)}) %collective-permute-start.15) | collective-permute-done | bytes 1048608 | tf_op jit(solution)/shard_map/ppermute | solution.py:104
  229.6 9.3 %collective-permute-done.9 = bf16[256,2048]{1,0:T(8,128)(2,1)S(1)} collective-permute-done((bf16[256,2048]{1,0:T(8,128)(2,1)S(1)}, bf16[256,2048]{1,0:T(8,128)(2,1)S(1)}, u32[]{:S(2)}, u32[]{:S(2)}) %collective-permute-start.9) | collective-permute-done | bytes 1048608 | tf_op jit(solution)/shard_map/ppermute | solution.py:103
  243.2 10.8 %fusion.19 = f32[1024,1536]{1,0:T(8,128)S(1)} fusion(bf16[1024,2048]{1,0:T(8,128)(2,1)} %constant_dynamic-update-slice_fusion.13, bf16[2048,2304]{0,1:T(8,128)(2,1)} %all-gather.6.cloned.1.call-done), kind=kOutput, calls=%fused_computation.31 | convolution fusion | flops 6442450944 | bytes 16777216 | tf_op jit(solution)/shard_map/dot_general | solution.py:248
  264.2 9.7 %convolution_convert_fusion.1 = bf16[2048,1536]{0,1:T(8,128)(2,1)S(1)} fusion(bf16[1024,2048]{1,0:T(8,128)(2,1)} %constant_dynamic-update-slice_fusion.13, bf16[1024,768]{1,0:T(8,128)(2,1)S(1)} %get-tuple-element.82, bf16[1024,768]{1,0:T(8,128)(2,1)S(1)} %get-tuple-element.81), kind=kOutput, calls=%fused_computation.28 | convolution fusion | flops 6451888128 | bytes 13631488 | tf_op jit(solution)/shard_map/dot_general | solution.py:61
  273.9 11.3 %pad_maximum_fusion = bf16[2048,2304]{0,1:T(8,128)(2,1)} fusion(bf16[2048,768]{0,1:T(8,128)(2,1)S(1)} %convolution_convert_fusion.4, bf16[2048,1536]{0,1:T(8,128)(2,1)S(1)} %convolution_convert_fusion.1), kind=kLoop, calls=%fused_computation.16 | loop fusion | flops 18874368 | bytes 18874368 | tf_op jit(solution)/shard_map/concatenate | solution.py:263
  294.0 12.1 %fusion.172 = f32[1024,1536]{1,0:T(8,128)} fusion(bf16[1024,2048]{1,0:T(8,128)(2,1)} %constant_dynamic-update-slice_fusion.13, bf16[2048,1536]{0,1:T(8,128)(2,1)} %slice.571), kind=kOutput, calls=%fused_computation.386 | convolution fusion | flops 6442450944 | bytes 16777216 | tf_op jit(solution)/shard_map/dot_general | solution.py:248
  313.0 8.9 %fusion.53 = f32[1024,2048]{1,0:T(8,128)} fusion(bf16[2048,1536]{0,1:T(8,128)(2,1)S(1)} %bitcast.381, bf16[1024,768]{1,0:T(8,128)(2,1)S(1)} %get-tuple-element.80, bf16[1024,768]{1,0:T(8,128)(2,1)S(1)} %get-tuple-element.79), kind=kOutput, calls=%fused_computation.113 | convolution fusion | flops 6448742400 | bytes 17825792 | tf_op jit(solution)/shard_map/dot_general | solution.py:67
  321.9 13.1 %fusion.170 = (bf16[1024,2048]{1,0:T(8,128)(2,1)S(1)}, f32[1024,2048]{1,0:T(8,128)}) fusion(f32[1024,2048]{1,0:T(8,128)} %fusion.53, bf16[2048,2304]{0,1:T(8,128)(2,1)} %all-gather.6.cloned.1.call-done, bf16[1024,768]{1,0:T(8,128)(2,1)} %copy-done.73, bf16[1024,768]{1,0:T(8,128)(2,1)} %copy-done.72), kind=kOutput, calls=%fused_computation.384 | convolution fusion | flops 6452936704 | bytes 30408704 | tf_op jit(solution)/shard_map/dot_general | solution.py:67
  357.0 9.7 %convolution_convert_fusion = bf16[2048,1536]{0,1:T(8,128)(2,1)S(1)} fusion(bf16[1024,2048]{1,0:T(8,128)(2,1)} %constant_dynamic-update-slice_fusion.13, bf16[1024,768]{1,0:T(8,128)(2,1)S(1)} %get-tuple-element.80, bf16[1024,768]{1,0:T(8,128)(2,1)S(1)} %get-tuple-element.79), kind=kOutput, calls=%fused_computation.27 | convolution fusion | flops 6451888128 | bytes 13631488 | tf_op jit(solution)/shard_map/dot_general | solution.py:61
  366.7 11.3 %pad_maximum_fusion.1 = bf16[2048,2304]{0,1:T(8,128)(2,1)} fusion(bf16[2048,768]{0,1:T(8,128)(2,1)S(1)} %convolution_convert_fusion.3, bf16[2048,1536]{0,1:T(8,128)(2,1)S(1)} %convolution_convert_fusion), kind=kLoop, calls=%fused_computation.17 | loop fusion | flops 18874368 | bytes 18874368 | tf_op jit(solution)/shard_map/concatenate | solution.py:263
  418.6 23.4 %collective-permute-done.26 = bf16[128,2048]{1,0:T(8,128)(2,1)S(1)} collective-permute-done((bf16[128,2048]{1,0:T(8,128)(2,1)S(1)}, bf16[128,2048]{1,0:T(8,128)(2,1)S(1)}, u32[]{:S(2)}, u32[]{:S(2)}) %collective-permute-start.26) | collective-permute-done | bytes 524320 | tf_op jit(solution)/shard_map/ppermute | solution.py:100
  443.8 13.0 %collective-permute-done.27 = bf16[256,2048]{1,0:T(8,128)(2,1)S(1)} collective-permute-done((bf16[256,2048]{1,0:T(8,128)(2,1)S(1)}, bf16[256,2048]{1,0:T(8,128)(2,1)S(1)}, u32[]{:S(2)}, u32[]{:S(2)}) %collective-permute-start.27) | collective-permute-done | bytes 1048608 | tf_op jit(solution)/shard_map/ppermute | solution.py:104
  459.5 12.5 %fusion = (f32[2,2,1024]{2,1,0:T(2,128)S(1)}, f32[2,1024,1024,2]{2,1,3,0:T(8,128)}) fusion(f32[2,1024,1024,2]{2,1,3,0:T(8,128)} %copy-done, f32[2,2,1024]{2,1,0:T(2,128)S(1)} %log_add_fusion, pred[1024,1024]{0,1:T(8,128)(4,1)S(1)} %copy-done.9, bf16[1024,2,128,1]{0,2,3,1:T(8,128)(2,1)S(1)} %bitcast.385, bf16[1024,2,2,128]{0,3,2,1:T(8,128)(2,1)S(1)} %bitcast.400), kind=kOutput, calls=%fused_computation.2 | convolution fusion | flops 1094709248 | bytes 36208640 | tf_op jit(solution)/shard_map/qgrd,kgd->grqk/dot_general | solution.py:298
  472.0 12.4 %fusion.2 = bf16[2,2,1024,1024]{2,3,1,0:T(8,128)(2,1)S(1)} fusion(f32[2,1024,1024,2]{2,1,3,0:T(8,128)} %get-tuple-element.182, f32[2,1024,1024,2]{2,1,3,0:T(8,128)} %copy-done, f32[2,2,1024]{2,1,0:T(2,128)S(1)} %get-tuple-element.181, f32[2,2,1024]{2,1,0:T(2,128)S(1)} %log_add_fusion, pred[1024,1024]{0,1:T(8,128)(4,1)S(1)} %copy-done.9), kind=kLoop, calls=%fused_computation.4 | loop fusion | flops 25165824 | bytes 43024384 | tf_op jit(solution)/shard_map/convert_element_type | solution.py:300
  489.6 8.2 %fusion.68 = bf16[2,128,1024]{2,1,0:T(8,128)(2,1)S(1)} fusion(bf16[1024,2,2,128]{0,3,2,1:T(8,128)(2,1)S(1)} %bitcast.401, f32[2,1024,1024,2]{2,1,3,0:T(8,128)} %copy-done, f32[2,2,1024]{2,1,0:T(2,128)S(1)} %log_add_fusion, pred[1024,1024]{0,1:T(8,128)(4,1)S(1)} %copy-done.9), kind=kOutput, calls=%fused_computation.129 | convolution fusion | flops 1090781184 | bytes 19415040 | tf_op jit(solution)/shard_map/grqk,qgrd->kgd/dot_general | solution.py:286
  555.7 16.9 %collective-permute-done.28 = bf16[2,128,2048]{2,1,0:T(8,128)(2,1)S(1)} collective-permute-done((bf16[2,128,2048]{2,1,0:T(8,128)(2,1)S(1)}, bf16[2,128,2048]{2,1,0:T(8,128)(2,1)S(1)}, u32[]{:S(2)}, u32[]{:S(2)}) %collective-permute-start.28) | collective-permute-done | bytes 1048608 | tf_op jit(solution)/shard_map/ppermute | solution.py:116
  576.3 8.7 %collective-permute-done.29 = bf16[128,2048]{1,0:T(8,128)(2,1)S(1)} collective-permute-done((bf16[128,2048]{1,0:T(8,128)(2,1)S(1)}, bf16[128,2048]{1,0:T(8,128)(2,1)S(1)}, u32[]{:S(2)}, u32[]{:S(2)}) %collective-permute-start.29) | collective-permute-done | bytes 524320 | tf_op jit(solution)/shard_map/ppermute | solution.py:120
  (476 shorter events, 286.1 us)
Async XLA Ops:
  7.2 93.5 %all-gather.4.cloned.1.call-start = ((), (), s32[]{:S(2)}) async-start(), calls=%async_computation.4 | async-start | bytes 7667712 | tf_op jit(solution)/shard_map/all_gather | solution.py:137
  15.0 228.1 %all-gather.6.cloned.1.call-start = ((), (), s32[]{:S(2)}) async-start(), calls=%async_computation.5 | async-start | bytes 10616832 | tf_op jit(solution)/shard_map/all_gather | solution.py:137
  19.8 265.5 %all-gather.8.cloned.1.call-start = ((), (), s32[]{:S(2)}) async-start(), calls=%async_computation.6 | async-start | bytes 10616832 | tf_op jit(solution)/shard_map/all_gather | solution.py:137
  26.3 478.7 %reduce-scatter.5.cloned.1.call-start = ((), (), s32[]{:S(2)}) async-start(), calls=%async_computation.7 | async-start | bytes 10616832 | tf_op jit(solution)/shard_map/reduce_scatter | solution.py:268
  35.8 24.5 %collective-permute-start.1 = (bf16[256,2048]{1,0:T(8,128)(2,1)S(1)}, bf16[256,2048]{1,0:T(8,128)(2,1)S(1)}, u32[]{:S(2)}, u32[]{:S(2)}) collective-permute-start(bf16[256,2048]{1,0:T(8,128)(2,1)S(1)} %pad_maximum_fusion.16), channel_id=1, source_target_pairs={{0,2},{2,0},{1,3},{3,1},{4,6},{6,4},{5,7},{7,5},{8,10},{10,8},{9,1... | collective-permute-start | bytes 3145736 | tf_op jit(solution)/shard_map/ppermute | solution.py:103
  74.7 23.0 %collective-permute-start.3 = (bf16[256,2048]{1,0:T(8,128)(2,1)S(1)}, bf16[256,2048]{1,0:T(8,128)(2,1)S(1)}, u32[]{:S(2)}, u32[]{:S(2)}) collective-permute-start(bf16[256,2048]{1,0:T(8,128)(2,1)S(1)} %pad_maximum_fusion.17), channel_id=1, source_target_pairs={{0,1},{1,0},{2,3},{3,2},{4,5},{5,4},{6,7},{7,6},{8,9},{9,8},{10,11... | collective-permute-start | bytes 3145736 | tf_op jit(solution)/shard_map/ppermute | solution.py:104
  137.8 26.1 %collective-permute-start.4 = (bf16[2,128,2048]{2,1,0:T(8,128)(2,1)S(1)}, bf16[2,128,2048]{2,1,0:T(8,128)(2,1)S(1)}, u32[]{:S(2)}, u32[]{:S(2)}) collective-permute-start(bf16[2,128,2048]{2,1,0:T(8,128)(2,1)S(1)} %bitcast.397), channel_id=1, source_target_pairs={{0,2},{2,0},{1,3},{3,1},{4,6},{6,4},{5,7},{7,5},{8,10},{10,8},{9,1... | collective-permute-start | bytes 3145736 | tf_op jit(solution)/shard_map/ppermute | solution.py:116
  139.3 57.3 %collective-permute-start.14 = (bf16[128,2048]{1,0:T(8,128)(2,1)S(1)}, bf16[128,2048]{1,0:T(8,128)(2,1)S(1)}, u32[]{:S(2)}, u32[]{:S(2)}) collective-permute-start(bf16[128,2048]{1,0:T(8,128)(2,1)S(1)} %get-tuple-element.125), channel_id=1, source_target_pairs={{0,2},{2,0},{1,3},{3,1},{4,6},{6,4},{5,7},{7,5},{8,10},{10,8},{9,1... | collective-permute-start | bytes 1572872 | tf_op jit(solution)/shard_map/ppermute | solution.py:100
  140.2 38.8 %collective-permute-start.12 = (bf16[128,2048]{1,0:T(8,128)(2,1)S(1)}, bf16[128,2048]{1,0:T(8,128)(2,1)S(1)}, u32[]{:S(2)}, u32[]{:S(2)}) collective-permute-start(bf16[128,2048]{1,0:T(8,128)(2,1)S(1)} %get-tuple-element.127), channel_id=1, source_target_pairs={{0,1},{1,0},{2,3},{3,2},{4,5},{5,4},{6,7},{7,6},{8,9},{9,8},{10,11... | collective-permute-start | bytes 1572872 | tf_op jit(solution)/shard_map/ppermute | solution.py:99
  141.7 35.8 %collective-permute-start.6 = (bf16[2,128,2048]{2,1,0:T(8,128)(2,1)S(1)}, bf16[2,128,2048]{2,1,0:T(8,128)(2,1)S(1)}, u32[]{:S(2)}, u32[]{:S(2)}) collective-permute-start(bf16[2,128,2048]{2,1,0:T(8,128)(2,1)S(1)} %bitcast.396), channel_id=1, source_target_pairs={{0,1},{1,0},{2,3},{3,2},{4,5},{5,4},{6,7},{7,6},{8,9},{9,8},{10,11... | collective-permute-start | bytes 3145736 | tf_op jit(solution)/shard_map/ppermute | solution.py:117
  179.1 33.1 %collective-permute-start.13 = (bf16[256,2048]{1,0:T(8,128)(2,1)S(1)}, bf16[256,2048]{1,0:T(8,128)(2,1)S(1)}, u32[]{:S(2)}, u32[]{:S(2)}) collective-permute-start(bf16[256,2048]{1,0:T(8,128)(2,1)S(1)} %pad_maximum_fusion.20), channel_id=1, source_target_pairs={{0,2},{2,0},{1,3},{3,1},{4,6},{6,4},{5,7},{7,5},{8,10},{10,8},{9,1... | collective-permute-start | bytes 3145736 | tf_op jit(solution)/shard_map/ppermute | solution.py:103
  196.6 27.9 %collective-permute-start.15 = (bf16[256,2048]{1,0:T(8,128)(2,1)S(1)}, bf16[256,2048]{1,0:T(8,128)(2,1)S(1)}, u32[]{:S(2)}, u32[]{:S(2)}) collective-permute-start(bf16[256,2048]{1,0:T(8,128)(2,1)S(1)} %pad_maximum_fusion.21), channel_id=1, source_target_pairs={{0,1},{1,0},{2,3},{3,2},{4,5},{5,4},{6,7},{7,6},{8,9},{9,8},{10,11... | collective-permute-start | bytes 3145736 | tf_op jit(solution)/shard_map/ppermute | solution.py:104
  213.6 25.4 %collective-permute-start.9 = (bf16[256,2048]{1,0:T(8,128)(2,1)S(1)}, bf16[256,2048]{1,0:T(8,128)(2,1)S(1)}, u32[]{:S(2)}, u32[]{:S(2)}) collective-permute-start(bf16[256,2048]{1,0:T(8,128)(2,1)S(1)} %pad_maximum_fusion.18), channel_id=1, source_target_pairs={{0,2},{2,0},{1,3},{3,1},{4,6},{6,4},{5,7},{7,5},{8,10},{10,8},{9,1... | collective-permute-start | bytes 3145736 | tf_op jit(solution)/shard_map/ppermute | solution.py:103
  293.9 211.1 %reduce-scatter.7.cloned.1.call-start = ((), (), s32[]{:S(2)}) async-start(), calls=%async_computation.8 | async-start | bytes 10616832 | tf_op jit(solution)/shard_map/reduce_scatter | solution.py:281
  336.4 49.9 %collective-permute-start.22 = (bf16[2,128,2048]{2,1,0:T(8,128)(2,1)}, bf16[2,128,2048]{2,1,0:T(8,128)(2,1)}, u32[]{:S(2)}, u32[]{:S(2)}) collective-permute-start(bf16[2,128,2048]{2,1,0:T(8,128)(2,1)} %bitcast.63), channel_id=1, source_target_pairs={{0,1},{1,0},{2,3},{3,2},{4,5},{5,4},{6,7},{7,6},{8,9},{9,8},{10,11... | collective-permute-start | bytes 3145736 | tf_op jit(solution)/shard_map/ppermute | solution.py:117
  338.0 45.1 %collective-permute-start.20 = (bf16[2,128,2048]{2,1,0:T(8,128)(2,1)}, bf16[2,128,2048]{2,1,0:T(8,128)(2,1)}, u32[]{:S(2)}, u32[]{:S(2)}) collective-permute-start(bf16[2,128,2048]{2,1,0:T(8,128)(2,1)} %bitcast.59), channel_id=1, source_target_pairs={{0,2},{2,0},{1,3},{3,1},{4,6},{6,4},{5,7},{7,5},{8,10},{10,8},{9,1... | collective-permute-start | bytes 3145736 | tf_op jit(solution)/shard_map/ppermute | solution.py:116
  351.6 37.9 %collective-permute-start.18 = (bf16[2,128,2048]{2,1,0:T(8,128)(2,1)S(1)}, bf16[2,128,2048]{2,1,0:T(8,128)(2,1)S(1)}, u32[]{:S(2)}, u32[]{:S(2)}) collective-permute-start(bf16[2,128,2048]{2,1,0:T(8,128)(2,1)S(1)} %bitcast.395), channel_id=1, source_target_pairs={{0,1},{1,0},{2,3},{3,2},{4,5},{5,4},{6,7},{7,6},{8,9},{9,8},{10,11... | collective-permute-start | bytes 3145736 | tf_op jit(solution)/shard_map/ppermute | solution.py:117
  352.3 36.7 %collective-permute-start.16 = (bf16[2,128,2048]{2,1,0:T(8,128)(2,1)}, bf16[2,128,2048]{2,1,0:T(8,128)(2,1)S(1)}, u32[]{:S(2)}, u32[]{:S(2)}) collective-permute-start(bf16[2,128,2048]{2,1,0:T(8,128)(2,1)} %bitcast.51), channel_id=1, source_target_pairs={{0,2},{2,0},{1,3},{3,1},{4,6},{6,4},{5,7},{7,5},{8,10},{10,8},{9,1... | collective-permute-start | bytes 3145736 | tf_op jit(solution)/shard_map/ppermute | solution.py:116
  378.0 168.3 %reduce-scatter.9.cloned.1.call-start = ((), (), s32[]{:S(2)}) async-start(), calls=%async_computation.9 | async-start | bytes 3538944 | tf_op jit(solution)/shard_map/reduce_scatter | solution.py:294
  416.4 27.2 %collective-permute-start.25 = (bf16[256,2048]{1,0:T(8,128)(2,1)S(1)}, bf16[256,2048]{1,0:T(8,128)(2,1)S(1)}, u32[]{:S(2)}, u32[]{:S(2)}) collective-permute-start(bf16[256,2048]{1,0:T(8,128)(2,1)S(1)} %pad_maximum_fusion.22), channel_id=1, source_target_pairs={{0,2},{2,0},{1,3},{3,1},{4,6},{6,4},{5,7},{7,5},{8,10},{10,8},{9,1... | collective-permute-start | bytes 3145736 | tf_op jit(solution)/shard_map/ppermute | solution.py:103
  418.2 23.7 %collective-permute-start.26 = (bf16[128,2048]{1,0:T(8,128)(2,1)S(1)}, bf16[128,2048]{1,0:T(8,128)(2,1)S(1)}, u32[]{:S(2)}, u32[]{:S(2)}) collective-permute-start(bf16[128,2048]{1,0:T(8,128)(2,1)S(1)} %get-tuple-element.122), channel_id=1, source_target_pairs={{0,2},{2,0},{1,3},{3,1},{4,6},{6,4},{5,7},{7,5},{8,10},{10,8},{9,1... | collective-permute-start | bytes 1572872 | tf_op jit(solution)/shard_map/ppermute | solution.py:100
  505.1 93.2 %reduce-scatter.11.cloned.1.call-start = ((), (), s32[]{:S(2)}) async-start(), calls=%async_computation.10 | async-start | bytes 4128768 | tf_op jit(solution)/shard_map/reduce_scatter | solution.py:352
  549.8 22.7 %collective-permute-start.28 = (bf16[2,128,2048]{2,1,0:T(8,128)(2,1)S(1)}, bf16[2,128,2048]{2,1,0:T(8,128)(2,1)S(1)}, u32[]{:S(2)}, u32[]{:S(2)}) collective-permute-start(bf16[2,128,2048]{2,1,0:T(8,128)(2,1)S(1)} %bitcast.399), channel_id=1, source_target_pairs={{0,2},{2,0},{1,3},{3,1},{4,6},{6,4},{5,7},{7,5},{8,10},{10,8},{9,1... | collective-permute-start | bytes 3145736 | tf_op jit(solution)/shard_map/ppermute | solution.py:116
  551.4 23.9 %collective-permute-start.30 = (bf16[2,128,2048]{2,1,0:T(8,128)(2,1)S(1)}, bf16[2,128,2048]{2,1,0:T(8,128)(2,1)S(1)}, u32[]{:S(2)}, u32[]{:S(2)}) collective-permute-start(bf16[2,128,2048]{2,1,0:T(8,128)(2,1)S(1)} %bitcast.398), channel_id=1, source_target_pairs={{0,1},{1,0},{2,3},{3,2},{4,5},{5,4},{6,7},{7,6},{8,9},{9,8},{10,11... | collective-permute-start | bytes 3145736 | tf_op jit(solution)/shard_map/ppermute | solution.py:117
  (102 other events, 967.6 us)
Sparse Core Ops, SparseCore 0:
  15.2 72.1 all-gather.3
  89.6 89.3 all-gather.5
  180.6 89.3 all-gather.7
  294.0 99.8 reduce-scatter.4
  396.1 97.8 reduce-scatter.6
  505.2 41.1 reduce-scatter.8
  548.7 44.2 reduce-scatter.10

commit v15 on v14

--- a/solution.py
+++ b/solution.py
@@ -288,12 +288,9 @@
     ).astype(jnp.bfloat16)
     value_grad = contract_rows(normed_all, d_value.reshape(rows_group, groups_here * HD))
     out_grad = jnp.concatenate([out_grad, value_grad.astype(jnp.bfloat16)], axis=1)
-    mlp_grads, out_grad = lax.optimization_barrier((mlp_grads, out_grad))
     mlp_grads = [split_cols(g.astype(jnp.float32), [2 * ff_half, ff_half]) for g in mlp_grads]
-    g_out_t, g_value = split_cols(
-        lax.psum_scatter(out_grad, "wide", scatter_dimension=0, tiled=True).astype(jnp.float32),
-        [q_cols, kv_cols],
-    )
+    out_summed = lax.psum_scatter(out_grad, "wide", scatter_dimension=0, tiled=True)
+    g_out_t, g_value = split_cols(out_summed.astype(jnp.float32), [q_cols, kv_cols])
 
     d_probs = jnp.einsum("qgrd,kgd->grqk", d_mixed, v_use, preferred_element_type=jnp.float32)
     inner = jnp.sum(p_probs * d_probs, axis=-1, keepdims=True)

time: 616 us -> 808 us (1.31)
  waiting for transfers between devices: 231 us -> 439 us
    reduce_scatter x1, waiting for transfers between devices: 0.01 us -> 97.9 us  [shards_body(): lax.psum_scatter(last_joined, 'wide', scatter_dimension=0, tiled=True)]
    reduce_scatter x1, waiting for transfers between devices: 0.01 us -> 73.7 us  [shards_body(): lax.psum_scatter(joined, 'wide', scatter_dimension=0, tiled=True)]
    ppermute x4, waiting for transfers between devices: 38.1 us -> 76.8 us  [narrow_scatter(): a_got = lax.ppermute(blocks[2:4].astype(jnp.bfloat16), 'narrow', YPERM)]
    unnamed x220 -> x216, local copies, waits for them, and re-layouts: 34.1 us -> 32.7 us
  transfers between devices with their start and end apart: 41 -> 41, of which waited for: 25 -> 28; matrix products, arithmetic and copies ran while one was open for 46% -> 23% of each run, Pallas kernels for 0% -> 0%
where the time goes in v15:
time: 808 us; the launch traced here: 804 us
  waiting for transfers between devices  439 us (54%)
  matrix products  164 us (20%)
  other arithmetic  73.5 us (9%)
  local copies, waits for them, and re-layouts  71.2 us (9%)
  starting transfers between devices  39.8 us (5%)
  between operations  16.5 us (2%)
    reduce_scatter x1, waiting for transfers between devices, shards_body(): lax.psum_scatter(last_joined, 'wide', scatter_dimension=0, tiled=True)  97.9 us
    ppermute x4, waiting for transfers between devices, narrow_scatter(): a_got = lax.ppermute(blocks[2:4].astype(jnp.bfloat16), 'narrow', YPERM)  76.8 us
    reduce_scatter x1, waiting for transfers between devices, shards_body(): lax.psum_scatter(joined, 'wide', scatter_dimension=0, tiled=True)  73.7 us
    ppermute x4, waiting for transfers between devices, narrow_gather(): a_pair_y = lax.ppermute(a_pair, 'narrow', YPERM)  46.7 us
    dot_general x6, matrix products, times_transposed(): lax.dot_general(left, right, (((1,), (1,)), ((), ())), preferred_element_...  43.8 us
    ppermute x4, waiting for transfers between devices, narrow_gather(): b_pair_x = lax.ppermute(b_pair, 'narrow', XPERM)  40 us
    dot_general x7, matrix products, contract_rows(): lax.dot_general(left, right, (((0,), (0,)), ((), ())), preferred_element_...  38.3 us
    ppermute x4, waiting for transfers between devices, narrow_gather(): b_y = lax.ppermute(b, 'narrow', YPERM)  36.8 us
  transfers between devices with their start and end apart: 41, of which 28 were waited for; matrix products, arithmetic and copies ran while one was open for 23% of the time, Pallas kernels for 0%

profile of v15, /device:TPU:0, one launch (start us, length us, event | category | flops | bytes accessed | tf_op | source)
XLA Modules:
  0.0 803.6 jit_solution(14229747685128943776)
XLA Ops:
  38.6 21.7 %collective-permute-done.1 = bf16[256,2048]{1,0:T(8,128)(2,1)S(1)} collective-permute-done((bf16[256,2048]{1,0:T(8,128)(2,1)S(1)}, bf16[256,2048]{1,0:T(8,128)(2,1)S(1)}, u32[]{:S(2)}, u32[]{:S(2)}) %collective-permute-start.1) | collective-permute-done | bytes 1048608 | tf_op jit(solution)/shard_map/ppermute | solution.py:103
  63.8 10.9 %collective-permute-done.2 = bf16[128,2048]{1,0:T(8,128)(2,1)S(1)} collective-permute-done((bf16[128,2048]{1,0:T(8,128)(2,1)S(1)}, bf16[128,2048]{1,0:T(8,128)(2,1)S(1)}, u32[]{:S(2)}, u32[]{:S(2)}) %collective-permute-start.2) | collective-permute-done | bytes 524320 | tf_op jit(solution)/shard_map/ppermute | solution.py:100
  80.3 17.4 %collective-permute-done.3 = bf16[256,2048]{1,0:T(8,128)(2,1)S(1)} collective-permute-done((bf16[256,2048]{1,0:T(8,128)(2,1)S(1)}, bf16[256,2048]{1,0:T(8,128)(2,1)S(1)}, u32[]{:S(2)}, u32[]{:S(2)}) %collective-permute-start.3) | collective-permute-done | bytes 1048608 | tf_op jit(solution)/shard_map/ppermute | solution.py:104
  142.8 21.2 %collective-permute-done.4 = bf16[2,128,2048]{2,1,0:T(8,128)(2,1)S(1)} collective-permute-done((bf16[2,128,2048]{2,1,0:T(8,128)(2,1)S(1)}, bf16[2,128,2048]{2,1,0:T(8,128)(2,1)S(1)}, u32[]{:S(2)}, u32[]{:S(2)}) %collective-permute-start.4) | collective-permute-done | bytes 1048608 | tf_op jit(solution)/shard_map/ppermute | solution.py:116
  165.5 12.0 %collective-permute-done.6 = bf16[2,128,2048]{2,1,0:T(8,128)(2,1)S(1)} collective-permute-done((bf16[2,128,2048]{2,1,0:T(8,128)(2,1)S(1)}, bf16[2,128,2048]{2,1,0:T(8,128)(2,1)S(1)}, u32[]{:S(2)}, u32[]{:S(2)}) %collective-permute-start.6) | collective-permute-done | bytes 1048608 | tf_op jit(solution)/shard_map/ppermute | solution.py:117
  196.7 15.5 %collective-permute-done.13 = bf16[256,2048]{1,0:T(8,128)(2,1)S(1)} collective-permute-done((bf16[256,2048]{1,0:T(8,128)(2,1)S(1)}, bf16[256,2048]{1,0:T(8,128)(2,1)S(1)}, u32[]{:S(2)}, u32[]{:S(2)}) %collective-permute-start.13) | collective-permute-done | bytes 1048608 | tf_op jit(solution)/shard_map/ppermute | solution.py:103
  243.2 10.9 %fusion.19 = f32[1024,1536]{1,0:T(8,128)S(1)} fusion(bf16[1024,2048]{1,0:T(8,128)(2,1)} %constant_dynamic-update-slice_fusion.13, bf16[2048,2304]{0,1:T(8,128)(2,1)} %all-gather.6.cloned.1.call-done), kind=kOutput, calls=%fused_computation.31 | convolution fusion | flops 6442450944 | bytes 16777216 | tf_op jit(solution)/shard_map/dot_general | solution.py:248
  264.4 9.7 %convolution_convert_fusion.1 = bf16[2048,1536]{0,1:T(8,128)(2,1)S(1)} fusion(bf16[1024,2048]{1,0:T(8,128)(2,1)} %constant_dynamic-update-slice_fusion.13, bf16[1024,768]{1,0:T(8,128)(2,1)S(1)} %get-tuple-element.76, bf16[1024,768]{1,0:T(8,128)(2,1)S(1)} %get-tuple-element.75), kind=kOutput, calls=%fused_computation.28 | convolution fusion | flops 6451888128 | bytes 13631488 | tf_op jit(solution)/shard_map/dot_general | solution.py:61
  274.1 11.3 %pad_maximum_fusion = bf16[2048,2304]{0,1:T(8,128)(2,1)} fusion(bf16[2048,768]{0,1:T(8,128)(2,1)S(1)} %convolution_convert_fusion.4, bf16[2048,1536]{0,1:T(8,128)(2,1)S(1)} %convolution_convert_fusion.1), kind=kLoop, calls=%fused_computation.16 | loop fusion | flops 18874368 | bytes 18874368 | tf_op jit(solution)/shard_map/concatenate | solution.py:263
  290.9 12.7 %fusion.172 = f32[1024,1536]{1,0:T(8,128)} fusion(bf16[1024,2048]{1,0:T(8,128)(2,1)} %constant_dynamic-update-slice_fusion.13, bf16[2048,1536]{0,1:T(8,128)(2,1)S(1)} %slice.571), kind=kOutput, calls=%fused_computation.386 | convolution fusion | flops 6442450944 | bytes 16777216 | tf_op jit(solution)/shard_map/dot_general | solution.py:248
  323.1 10.9 %fusion.53 = f32[1024,2048]{1,0:T(8,128)} fusion(bf16[2048,1536]{0,1:T(8,128)(2,1)} %copy-done.16, bf16[1024,768]{1,0:T(8,128)(2,1)S(1)} %copy-done.69, bf16[1024,768]{1,0:T(8,128)(2,1)S(1)} %copy-done.67), kind=kOutput, calls=%fused_computation.113 | convolution fusion | flops 6448742400 | bytes 17825792 | tf_op jit(solution)/shard_map/dot_general | solution.py:67
  334.0 12.9 %fusion.170 = (bf16[1024,2048]{1,0:T(8,128)(2,1)S(1)}, f32[1024,2048]{1,0:T(8,128)}) fusion(f32[1024,2048]{1,0:T(8,128)} %fusion.53, bf16[2048,2304]{0,1:T(8,128)(2,1)} %all-gather.6.cloned.1.call-done, bf16[1024,768]{1,0:T(8,128)(2,1)} %copy-done.73, bf16[1024,768]{1,0:T(8,128)(2,1)S(1)} %copy-done.72), kind=kOutput, calls=%fused_computation.384 | convolution fusion | flops 6452936704 | bytes 30408704 | tf_op jit(solution)/shard_map/dot_general | solution.py:67
  354.3 20.5 %collective-permute-done.20 = bf16[2,128,2048]{2,1,0:T(8,128)(2,1)S(1)} collective-permute-done((bf16[2,128,2048]{2,1,0:T(8,128)(2,1)S(1)}, bf16[2,128,2048]{2,1,0:T(8,128)(2,1)S(1)}, u32[]{:S(2)}, u32[]{:S(2)}) %collective-permute-start.20) | collective-permute-done | bytes 1048608 | tf_op jit(solution)/shard_map/ppermute | solution.py:116
  377.2 19.2 %collective-permute-done.16 = bf16[2,128,2048]{2,1,0:T(8,128)(2,1)S(1)} collective-permute-done((bf16[2,128,2048]{2,1,0:T(8,128)(2,1)S(1)}, bf16[2,128,2048]{2,1,0:T(8,128)(2,1)S(1)}, u32[]{:S(2)}, u32[]{:S(2)}) %collective-permute-start.16) | collective-permute-done | bytes 1048608 | tf_op jit(solution)/shard_map/ppermute | solution.py:116
  402.9 9.6 %collective-permute-done.17 = bf16[128,2048]{1,0:T(8,128)(2,1)S(1)} collective-permute-done((bf16[128,2048]{1,0:T(8,128)(2,1)S(1)}, bf16[128,2048]{1,0:T(8,128)(2,1)S(1)}, u32[]{:S(2)}, u32[]{:S(2)}) %collective-permute-start.17) | collective-permute-done | bytes 524320 | tf_op jit(solution)/shard_map/ppermute | solution.py:120
  426.9 22.1 %collective-permute-done.26 = bf16[128,2048]{1,0:T(8,128)(2,1)S(1)} collective-permute-done((bf16[128,2048]{1,0:T(8,128)(2,1)S(1)}, bf16[128,2048]{1,0:T(8,128)(2,1)S(1)}, u32[]{:S(2)}, u32[]{:S(2)}) %collective-permute-start.26) | collective-permute-done | bytes 524320 | tf_op jit(solution)/shard_map/ppermute | solution.py:100
  450.3 13.7 %collective-permute-done.27 = bf16[256,2048]{1,0:T(8,128)(2,1)S(1)} collective-permute-done((bf16[256,2048]{1,0:T(8,128)(2,1)S(1)}, bf16[256,2048]{1,0:T(8,128)(2,1)S(1)}, u32[]{:S(2)}, u32[]{:S(2)}) %collective-permute-start.27) | collective-permute-done | bytes 1048608 | tf_op jit(solution)/shard_map/ppermute | solution.py:104
  476.9 12.6 %fusion = (f32[2,2,1024]{2,1,0:T(2,128)S(1)}, f32[2,1024,1024,2]{2,1,3,0:T(8,128)}) fusion(f32[2,1024,1024,2]{2,1,3,0:T(8,128)} %copy-done, f32[2,2,1024]{2,1,0:T(2,128)S(1)} %log_add_fusion, pred[1024,1024]{0,1:T(8,128)(4,1)S(1)} %copy-done.6, bf16[1024,2,128,1]{0,2,3,1:T(8,128)(2,1)S(1)} %bitcast.383, bf16[1024,2,2,128]{0,3,2,1:T(8,128)(2,1)S(1)} %bitcast.402), kind=kOutput, calls=%fused_computation.2 | convolution fusion | flops 1094709248 | bytes 36208640 | tf_op jit(solution)/shard_map/qgrd,kgd->grqk/dot_general | solution.py:295
  493.2 12.6 %fusion.2 = bf16[2,2,1024,1024]{2,3,1,0:T(8,128)(2,1)S(1)} fusion(f32[2,1024,1024,2]{2,1,3,0:T(8,128)} %get-tuple-element.176, f32[2,1024,1024,2]{2,1,3,0:T(8,128)} %copy-done, f32[2,2,1024]{2,1,0:T(2,128)S(1)} %get-tuple-element.175, f32[2,2,1024]{2,1,0:T(2,128)S(1)} %log_add_fusion, pred[1024,1024]{0,1:T(8,128)(4,1)S(1)} %copy-done.6), kind=kLoop, calls=%fused_computation.4 | loop fusion | flops 25165824 | bytes 43024384 | tf_op jit(solution)/shard_map/convert_element_type | solution.py:297
  548.8 9.7 %convolution_convert_fusion = bf16[2048,1536]{0,1:T(8,128)(2,1)S(1)} fusion(bf16[1024,2048]{1,0:T(8,128)(2,1)} %constant_dynamic-update-slice_fusion.13, bf16[1024,768]{1,0:T(8,128)(2,1)S(1)} %copy-done.70, bf16[1024,768]{1,0:T(8,128)(2,1)S(1)} %copy-done.68), kind=kOutput, calls=%fused_computation.27 | convolution fusion | flops 6451888128 | bytes 13631488 | tf_op jit(solution)/shard_map/dot_general | solution.py:61
  558.6 11.3 %pad_maximum_fusion.1 = bf16[2048,2304]{0,1:T(8,128)(2,1)} fusion(bf16[2048,768]{0,1:T(8,128)(2,1)S(1)} %convolution_convert_fusion.3, bf16[2048,1536]{0,1:T(8,128)(2,1)S(1)} %convolution_convert_fusion), kind=kLoop, calls=%fused_computation.17 | loop fusion | flops 18874368 | bytes 18874368 | tf_op jit(solution)/shard_map/concatenate | solution.py:263
  576.2 15.9 %collective-permute-done.28 = bf16[2,128,2048]{2,1,0:T(8,128)(2,1)S(1)} collective-permute-done((bf16[2,128,2048]{2,1,0:T(8,128)(2,1)S(1)}, bf16[2,128,2048]{2,1,0:T(8,128)(2,1)S(1)}, u32[]{:S(2)}, u32[]{:S(2)}) %collective-permute-start.28) | collective-permute-done | bytes 1048608 | tf_op jit(solution)/shard_map/ppermute | solution.py:116
  614.1 73.7 %reduce-scatter.9.cloned.1.call-done = bf16[256,2304]{0,1:T(8,128)(2,1)} async-done(((bf16[2048,2304]{0,1:T(8,128)(2,1)}), bf16[256,2304]{0,1:T(8,128)(2,1)}) %reduce-scatter.9.cloned.1.call-update) | async-done | bytes 1179664 | tf_op jit(solution)/shard_map/reduce_scatter | solution.py:268
  690.1 97.9 %reduce-scatter.11.cloned.1.call-done = bf16[256,2304]{0,1:T(8,128)(2,1)} async-done(((bf16[2048,2304]{0,1:T(8,128)(2,1)}), bf16[256,2304]{0,1:T(8,128)(2,1)}) %reduce-scatter.11.cloned.1.call-update) | async-done | bytes 1179664 | tf_op jit(solution)/shard_map/reduce_scatter | solution.py:281
  (471 shorter events, 301.1 us)
Async XLA Ops:
  7.2 93.7 %all-gather.4.cloned.1.call-start = ((), (), s32[]{:S(2)}) async-start(), calls=%async_computation.4 | async-start | bytes 7667712 | tf_op jit(solution)/shard_map/all_gather | solution.py:137
  15.1 228.1 %all-gather.6.cloned.1.call-start = ((), (), s32[]{:S(2)}) async-start(), calls=%async_computation.5 | async-start | bytes 10616832 | tf_op jit(solution)/shard_map/all_gather | solution.py:137
  19.8 265.5 %all-gather.8.cloned.1.call-start = ((), (), s32[]{:S(2)}) async-start(), calls=%async_computation.6 | async-start | bytes 10616832 | tf_op jit(solution)/shard_map/all_gather | solution.py:137
  26.3 513.3 %reduce-scatter.5.cloned.1.call-start = ((), (), s32[]{:S(2)}) async-start(), calls=%async_computation.7 | async-start | bytes 3538944 | tf_op jit(solution)/shard_map/reduce_scatter | solution.py:292
  35.8 24.5 %collective-permute-start.1 = (bf16[256,2048]{1,0:T(8,128)(2,1)S(1)}, bf16[256,2048]{1,0:T(8,128)(2,1)S(1)}, u32[]{:S(2)}, u32[]{:S(2)}) collective-permute-start(bf16[256,2048]{1,0:T(8,128)(2,1)S(1)} %pad_maximum_fusion.16), channel_id=1, source_target_pairs={{0,2},{2,0},{1,3},{3,1},{4,6},{6,4},{5,7},{7,5},{8,10},{10,8},{9,1... | collective-permute-start | bytes 3145736 | tf_op jit(solution)/shard_map/ppermute | solution.py:103
  137.9 26.1 %collective-permute-start.4 = (bf16[2,128,2048]{2,1,0:T(8,128)(2,1)S(1)}, bf16[2,128,2048]{2,1,0:T(8,128)(2,1)S(1)}, u32[]{:S(2)}, u32[]{:S(2)}) collective-permute-start(bf16[2,128,2048]{2,1,0:T(8,128)(2,1)S(1)} %bitcast.398), channel_id=1, source_target_pairs={{0,2},{2,0},{1,3},{3,1},{4,6},{6,4},{5,7},{7,5},{8,10},{10,8},{9,1... | collective-permute-start | bytes 3145736 | tf_op jit(solution)/shard_map/ppermute | solution.py:116
  139.3 56.7 %collective-permute-start.14 = (bf16[128,2048]{1,0:T(8,128)(2,1)S(1)}, bf16[128,2048]{1,0:T(8,128)(2,1)S(1)}, u32[]{:S(2)}, u32[]{:S(2)}) collective-permute-start(bf16[128,2048]{1,0:T(8,128)(2,1)S(1)} %get-tuple-element.119), channel_id=1, source_target_pairs={{0,2},{2,0},{1,3},{3,1},{4,6},{6,4},{5,7},{7,5},{8,10},{10,8},{9,1... | collective-permute-start | bytes 1572872 | tf_op jit(solution)/shard_map/ppermute | solution.py:100
  140.3 38.8 %collective-permute-start.12 = (bf16[128,2048]{1,0:T(8,128)(2,1)S(1)}, bf16[128,2048]{1,0:T(8,128)(2,1)S(1)}, u32[]{:S(2)}, u32[]{:S(2)}) collective-permute-start(bf16[128,2048]{1,0:T(8,128)(2,1)S(1)} %get-tuple-element.121), channel_id=1, source_target_pairs={{0,1},{1,0},{2,3},{3,2},{4,5},{5,4},{6,7},{7,6},{8,9},{9,8},{10,11... | collective-permute-start | bytes 1572872 | tf_op jit(solution)/shard_map/ppermute | solution.py:99
  141.8 35.8 %collective-permute-start.6 = (bf16[2,128,2048]{2,1,0:T(8,128)(2,1)S(1)}, bf16[2,128,2048]{2,1,0:T(8,128)(2,1)S(1)}, u32[]{:S(2)}, u32[]{:S(2)}) collective-permute-start(bf16[2,128,2048]{2,1,0:T(8,128)(2,1)S(1)} %bitcast.396), channel_id=1, source_target_pairs={{0,1},{1,0},{2,3},{3,2},{4,5},{5,4},{6,7},{7,6},{8,9},{9,8},{10,11... | collective-permute-start | bytes 3145736 | tf_op jit(solution)/shard_map/ppermute | solution.py:117
  179.1 33.1 %collective-permute-start.13 = (bf16[256,2048]{1,0:T(8,128)(2,1)S(1)}, bf16[256,2048]{1,0:T(8,128)(2,1)S(1)}, u32[]{:S(2)}, u32[]{:S(2)}) collective-permute-start(bf16[256,2048]{1,0:T(8,128)(2,1)S(1)} %pad_maximum_fusion.20), channel_id=1, source_target_pairs={{0,2},{2,0},{1,3},{3,1},{4,6},{6,4},{5,7},{7,5},{8,10},{10,8},{9,1... | collective-permute-start | bytes 3145736 | tf_op jit(solution)/shard_map/ppermute | solution.py:103
  196.1 27.3 %collective-permute-start.15 = (bf16[256,2048]{1,0:T(8,128)(2,1)S(1)}, bf16[256,2048]{1,0:T(8,128)(2,1)S(1)}, u32[]{:S(2)}, u32[]{:S(2)}) collective-permute-start(bf16[256,2048]{1,0:T(8,128)(2,1)S(1)} %pad_maximum_fusion.21), channel_id=1, source_target_pairs={{0,1},{1,0},{2,3},{3,2},{4,5},{5,4},{6,7},{7,6},{8,9},{9,8},{10,11... | collective-permute-start | bytes 3145736 | tf_op jit(solution)/shard_map/ppermute | solution.py:104
  213.6 25.6 %collective-permute-start.9 = (bf16[256,2048]{1,0:T(8,128)(2,1)S(1)}, bf16[256,2048]{1,0:T(8,128)(2,1)S(1)}, u32[]{:S(2)}, u32[]{:S(2)}) collective-permute-start(bf16[256,2048]{1,0:T(8,128)(2,1)S(1)} %pad_maximum_fusion.18), channel_id=1, source_target_pairs={{0,2},{2,0},{1,3},{3,1},{4,6},{6,4},{5,7},{7,5},{8,10},{10,8},{9,1... | collective-permute-start | bytes 3145736 | tf_op jit(solution)/shard_map/ppermute | solution.py:103
  347.2 28.5 %collective-permute-start.22 = (bf16[2,128,2048]{2,1,0:T(8,128)(2,1)S(1)}, bf16[2,128,2048]{2,1,0:T(8,128)(2,1)S(1)}, u32[]{:S(2)}, u32[]{:S(2)}) collective-permute-start(bf16[2,128,2048]{2,1,0:T(8,128)(2,1)S(1)} %bitcast.395), channel_id=1, source_target_pairs={{0,1},{1,0},{2,3},{3,2},{4,5},{5,4},{6,7},{7,6},{8,9},{9,8},{10,11... | collective-permute-start | bytes 3145736 | tf_op jit(solution)/shard_map/ppermute | solution.py:117
  348.7 26.0 %collective-permute-start.20 = (bf16[2,128,2048]{2,1,0:T(8,128)(2,1)S(1)}, bf16[2,128,2048]{2,1,0:T(8,128)(2,1)S(1)}, u32[]{:S(2)}, u32[]{:S(2)}) collective-permute-start(bf16[2,128,2048]{2,1,0:T(8,128)(2,1)S(1)} %bitcast.397), channel_id=1, source_target_pairs={{0,2},{2,0},{1,3},{3,1},{4,6},{6,4},{5,7},{7,5},{8,10},{10,8},{9,1... | collective-permute-start | bytes 3145736 | tf_op jit(solution)/shard_map/ppermute | solution.py:116
  349.5 47.2 %collective-permute-start.18 = (bf16[2,128,2048]{2,1,0:T(8,128)(2,1)S(1)}, bf16[2,128,2048]{2,1,0:T(8,128)(2,1)S(1)}, u32[]{:S(2)}, u32[]{:S(2)}) collective-permute-start(bf16[2,128,2048]{2,1,0:T(8,128)(2,1)S(1)} %bitcast.393), channel_id=1, source_target_pairs={{0,1},{1,0},{2,3},{3,2},{4,5},{5,4},{6,7},{7,6},{8,9},{9,8},{10,11... | collective-permute-start | bytes 3145736 | tf_op jit(solution)/shard_map/ppermute | solution.py:117
  350.4 46.0 %collective-permute-start.16 = (bf16[2,128,2048]{2,1,0:T(8,128)(2,1)S(1)}, bf16[2,128,2048]{2,1,0:T(8,128)(2,1)S(1)}, u32[]{:S(2)}, u32[]{:S(2)}) collective-permute-start(bf16[2,128,2048]{2,1,0:T(8,128)(2,1)S(1)} %bitcast.394), channel_id=1, source_target_pairs={{0,2},{2,0},{1,3},{3,1},{4,6},{6,4},{5,7},{7,5},{8,10},{10,8},{9,1... | collective-permute-start | bytes 3145736 | tf_op jit(solution)/shard_map/ppermute | solution.py:116
  375.1 26.2 %collective-permute-start.21 = (bf16[128,2048]{1,0:T(8,128)(2,1)S(1)}, bf16[128,2048]{1,0:T(8,128)(2,1)S(1)}, u32[]{:S(2)}, u32[]{:S(2)}) collective-permute-start(bf16[128,2048]{1,0:T(8,128)(2,1)S(1)} %fusion.90), channel_id=1, source_target_pairs={{0,1},{1,0},{2,3},{3,2},{4,5},{5,4},{6,7},{7,6},{8,9},{9,8},{10,11... | collective-permute-start | bytes 1572872 | tf_op jit(solution)/shard_map/ppermute | solution.py:120
  376.1 26.0 %collective-permute-start.23 = (bf16[128,2048]{1,0:T(8,128)(2,1)S(1)}, bf16[128,2048]{1,0:T(8,128)(2,1)S(1)}, u32[]{:S(2)}, u32[]{:S(2)}) collective-permute-start(bf16[128,2048]{1,0:T(8,128)(2,1)S(1)} %fusion.91), channel_id=1, source_target_pairs={{0,2},{2,0},{1,3},{3,1},{4,6},{6,4},{5,7},{7,5},{8,10},{10,8},{9,1... | collective-permute-start | bytes 1572872 | tf_op jit(solution)/shard_map/ppermute | solution.py:121
  424.8 25.3 %collective-permute-start.25 = (bf16[256,2048]{1,0:T(8,128)(2,1)S(1)}, bf16[256,2048]{1,0:T(8,128)(2,1)S(1)}, u32[]{:S(2)}, u32[]{:S(2)}) collective-permute-start(bf16[256,2048]{1,0:T(8,128)(2,1)S(1)} %pad_maximum_fusion.22), channel_id=1, source_target_pairs={{0,2},{2,0},{1,3},{3,1},{4,6},{6,4},{5,7},{7,5},{8,10},{10,8},{9,1... | collective-permute-start | bytes 3145736 | tf_op jit(solution)/shard_map/ppermute | solution.py:103
  426.0 23.1 %collective-permute-start.26 = (bf16[128,2048]{1,0:T(8,128)(2,1)S(1)}, bf16[128,2048]{1,0:T(8,128)(2,1)S(1)}, u32[]{:S(2)}, u32[]{:S(2)}) collective-permute-start(bf16[128,2048]{1,0:T(8,128)(2,1)S(1)} %get-tuple-element.116), channel_id=1, source_target_pairs={{0,2},{2,0},{1,3},{3,1},{4,6},{6,4},{5,7},{7,5},{8,10},{10,8},{9,1... | collective-permute-start | bytes 1572872 | tf_op jit(solution)/shard_map/ppermute | solution.py:100
  493.1 116.0 %reduce-scatter.7.cloned.1.call-start = ((), (), s32[]{:S(2)}) async-start(), calls=%async_computation.8 | async-start | bytes 4128768 | tf_op jit(solution)/shard_map/reduce_scatter | solution.py:349
  541.4 146.5 %reduce-scatter.9.cloned.1.call-start = ((), (), s32[]{:S(2)}) async-start(), calls=%async_computation.9 | async-start | bytes 10616832 | tf_op jit(solution)/shard_map/reduce_scatter | solution.py:268
  542.0 246.1 %reduce-scatter.11.cloned.1.call-start = ((), (), s32[]{:S(2)}) async-start(), calls=%async_computation.10 | async-start | bytes 10616832 | tf_op jit(solution)/shard_map/reduce_scatter | solution.py:281
  572.9 23.3 %collective-permute-start.30 = (bf16[2,128,2048]{2,1,0:T(8,128)(2,1)S(1)}, bf16[2,128,2048]{2,1,0:T(8,128)(2,1)S(1)}, u32[]{:S(2)}, u32[]{:S(2)}) collective-permute-start(bf16[2,128,2048]{2,1,0:T(8,128)(2,1)S(1)} %bitcast.399), channel_id=1, source_target_pairs={{0,1},{1,0},{2,3},{3,2},{4,5},{5,4},{6,7},{7,6},{8,9},{9,8},{10,11... | collective-permute-start | bytes 3145736 | tf_op jit(solution)/shard_map/ppermute | solution.py:117
  (100 other events, 824.0 us)
Sparse Core Ops, SparseCore 0:
  15.2 72.2 all-gather.3
  89.6 89.3 all-gather.5
  181.1 89.3 all-gather.7
  493.3 41.2 reduce-scatter.4
  541.5 46.2 reduce-scatter.6
  590.0 97.8 reduce-scatter.8
  690.1 97.8 reduce-scatter.10

commit v16 on v15

--- a/solution.py
+++ b/solution.py
@@ -136,6 +136,10 @@
 def wide_gather(blocks):
     joined = lax.all_gather(jnp.concatenate(blocks, axis=1), "wide", axis=0, tiled=True)
     return split_cols(joined, [blk.shape[1] for blk in blocks])
+
+
+def qkv_scatter(grad):
+    return lax.psum_scatter(grad, "wide", scatter_dimension=0, tiled=True)
 
 
 def shards_body(
@@ -344,9 +348,8 @@
         ],
         axis=1,
     )
-    g_out_t, qkv_grad = lax.optimization_barrier((g_out_t, qkv_grad))
     g_qkv, g_gains = split_cols(
-        lax.psum_scatter(qkv_grad, "wide", scatter_dimension=0, tiled=True).astype(jnp.float32),
+        qkv_scatter(qkv_grad).astype(jnp.float32),
         [qk_cols, 128],
     )
     d_normed = narrow_scatter(d_normed_partial, relative)

time: 808 us -> 806 us (level)
    unnamed x216 -> x214, local copies, waits for them, and re-layouts: 32.7 us -> 32.6 us
  transfers between devices with their start and end apart: 41 -> 41, of which waited for: 28 -> 26; matrix products, arithmetic and copies ran while one was open for 23% -> 23% of each run, Pallas kernels for 0% -> 0%
where the time goes in v16:
time: 806 us; the launch traced here: 802 us
  waiting for transfers between devices  436 us (54%)
  matrix products  164 us (20%)
  other arithmetic  74.6 us (9%)
  local copies, waits for them, and re-layouts  71.1 us (9%)
  starting transfers between devices  39.2 us (5%)
  between operations  16.5 us (2%)
    reduce_scatter x1, waiting for transfers between devices, shards_body(): lax.psum_scatter(last_joined, 'wide', scatter_dimension=0, tiled=True)  97.9 us
    ppermute x4, waiting for transfers between devices, narrow_scatter(): a_got = lax.ppermute(blocks[2:4].astype(jnp.bfloat16), 'narrow', YPERM)  76.2 us
    reduce_scatter x1, waiting for transfers between devices, shards_body(): lax.psum_scatter(joined, 'wide', scatter_dimension=0, tiled=True)  74.2 us
    ppermute x4, waiting for transfers between devices, narrow_gather(): a_pair_y = lax.ppermute(a_pair, 'narrow', YPERM)  46.8 us
    dot_general x6, matrix products, times_transposed(): lax.dot_general(left, right, (((1,), (1,)), ((), ())), preferred_element_...  43.8 us
    ppermute x4, waiting for transfers between devices, narrow_gather(): b_pair_x = lax.ppermute(b_pair, 'narrow', XPERM)  39.9 us
    dot_general x7, matrix products, contract_rows(): lax.dot_general(left, right, (((0,), (0,)), ((), ())), preferred_element_...  38.3 us
    ppermute x4, waiting for transfers between devices, narrow_gather(): b_y = lax.ppermute(b, 'narrow', YPERM)  36.8 us
  transfers between devices with their start and end apart: 41, of which 26 were waited for; matrix products, arithmetic and copies ran while one was open for 23% of the time, Pallas kernels for 0%

profile of v16, /device:TPU:0, one launch (start us, length us, event | category | flops | bytes accessed | tf_op | source)
XLA Modules:
  0.0 801.8 jit_solution(519374837654955959)
XLA Ops:
  38.6 21.7 %collective-permute-done.1 = bf16[256,2048]{1,0:T(8,128)(2,1)S(1)} collective-permute-done((bf16[256,2048]{1,0:T(8,128)(2,1)S(1)}, bf16[256,2048]{1,0:T(8,128)(2,1)S(1)}, u32[]{:S(2)}, u32[]{:S(2)}) %collective-permute-start.1) | collective-permute-done | bytes 1048608 | tf_op jit(solution)/shard_map/ppermute | solution.py:103
  63.8 10.9 %collective-permute-done.2 = bf16[128,2048]{1,0:T(8,128)(2,1)S(1)} collective-permute-done((bf16[128,2048]{1,0:T(8,128)(2,1)S(1)}, bf16[128,2048]{1,0:T(8,128)(2,1)S(1)}, u32[]{:S(2)}, u32[]{:S(2)}) %collective-permute-start.2) | collective-permute-done | bytes 524320 | tf_op jit(solution)/shard_map/ppermute | solution.py:100
  80.3 17.4 %collective-permute-done.3 = bf16[256,2048]{1,0:T(8,128)(2,1)S(1)} collective-permute-done((bf16[256,2048]{1,0:T(8,128)(2,1)S(1)}, bf16[256,2048]{1,0:T(8,128)(2,1)S(1)}, u32[]{:S(2)}, u32[]{:S(2)}) %collective-permute-start.3) | collective-permute-done | bytes 1048608 | tf_op jit(solution)/shard_map/ppermute | solution.py:104
  142.8 21.2 %collective-permute-done.4 = bf16[2,128,2048]{2,1,0:T(8,128)(2,1)S(1)} collective-permute-done((bf16[2,128,2048]{2,1,0:T(8,128)(2,1)S(1)}, bf16[2,128,2048]{2,1,0:T(8,128)(2,1)S(1)}, u32[]{:S(2)}, u32[]{:S(2)}) %collective-permute-start.4) | collective-permute-done | bytes 1048608 | tf_op jit(solution)/shard_map/ppermute | solution.py:116
  165.5 12.0 %collective-permute-done.6 = bf16[2,128,2048]{2,1,0:T(8,128)(2,1)S(1)} collective-permute-done((bf16[2,128,2048]{2,1,0:T(8,128)(2,1)S(1)}, bf16[2,128,2048]{2,1,0:T(8,128)(2,1)S(1)}, u32[]{:S(2)}, u32[]{:S(2)}) %collective-permute-start.6) | collective-permute-done | bytes 1048608 | tf_op jit(solution)/shard_map/ppermute | solution.py:117
  196.7 15.6 %collective-permute-done.13 = bf16[256,2048]{1,0:T(8,128)(2,1)S(1)} collective-permute-done((bf16[256,2048]{1,0:T(8,128)(2,1)S(1)}, bf16[256,2048]{1,0:T(8,128)(2,1)S(1)}, u32[]{:S(2)}, u32[]{:S(2)}) %collective-permute-start.13) | collective-permute-done | bytes 1048608 | tf_op jit(solution)/shard_map/ppermute | solution.py:103
  229.7 9.6 %collective-permute-done.9 = bf16[256,2048]{1,0:T(8,128)(2,1)S(1)} collective-permute-done((bf16[256,2048]{1,0:T(8,128)(2,1)S(1)}, bf16[256,2048]{1,0:T(8,128)(2,1)S(1)}, u32[]{:S(2)}, u32[]{:S(2)}) %collective-permute-start.9) | collective-permute-done | bytes 1048608 | tf_op jit(solution)/shard_map/ppermute | solution.py:103
  243.2 10.9 %fusion.19 = f32[1024,1536]{1,0:T(8,128)S(1)} fusion(bf16[1024,2048]{1,0:T(8,128)(2,1)} %constant_dynamic-update-slice_fusion.13, bf16[2048,2304]{0,1:T(8,128)(2,1)} %all-gather.6.cloned.1.call-done), kind=kOutput, calls=%fused_computation.31 | convolution fusion | flops 6442450944 | bytes 16777216 | tf_op jit(solution)/shard_map/dot_general | solution.py:252
  264.3 9.7 %convolution_convert_fusion.1 = bf16[2048,1536]{0,1:T(8,128)(2,1)S(1)} fusion(bf16[1024,2048]{1,0:T(8,128)(2,1)} %constant_dynamic-update-slice_fusion.13, bf16[1024,768]{1,0:T(8,128)(2,1)S(1)} %get-tuple-element.72, bf16[1024,768]{1,0:T(8,128)(2,1)S(1)} %get-tuple-element.71), kind=kOutput, calls=%fused_computation.28 | convolution fusion | flops 6451888128 | bytes 13631488 | tf_op jit(solution)/shard_map/dot_general | solution.py:61
  274.0 11.3 %pad_maximum_fusion = bf16[2048,2304]{0,1:T(8,128)(2,1)} fusion(bf16[2048,768]{0,1:T(8,128)(2,1)S(1)} %convolution_convert_fusion.4, bf16[2048,1536]{0,1:T(8,128)(2,1)S(1)} %convolution_convert_fusion.1), kind=kLoop, calls=%fused_computation.16 | loop fusion | flops 18874368 | bytes 18874368 | tf_op jit(solution)/shard_map/concatenate | solution.py:267
  290.9 12.7 %fusion.172 = f32[1024,1536]{1,0:T(8,128)} fusion(bf16[1024,2048]{1,0:T(8,128)(2,1)} %constant_dynamic-update-slice_fusion.13, bf16[2048,1536]{0,1:T(8,128)(2,1)S(1)} %slice.571), kind=kOutput, calls=%fused_computation.387 | convolution fusion | flops 6442450944 | bytes 16777216 | tf_op jit(solution)/shard_map/dot_general | solution.py:252
  323.1 10.9 %fusion.53 = f32[1024,2048]{1,0:T(8,128)} fusion(bf16[2048,1536]{0,1:T(8,128)(2,1)} %copy-done.16, bf16[1024,768]{1,0:T(8,128)(2,1)S(1)} %copy-done.68, bf16[1024,768]{1,0:T(8,128)(2,1)S(1)} %copy-done.66), kind=kOutput, calls=%fused_computation.113 | convolution fusion | flops 6448742400 | bytes 17825792 | tf_op jit(solution)/shard_map/dot_general | solution.py:67
  334.0 12.9 %fusion.170 = (bf16[1024,2048]{1,0:T(8,128)(2,1)S(1)}, f32[1024,2048]{1,0:T(8,128)}) fusion(f32[1024,2048]{1,0:T(8,128)} %fusion.53, bf16[2048,2304]{0,1:T(8,128)(2,1)} %all-gather.6.cloned.1.call-done, bf16[1024,768]{1,0:T(8,128)(2,1)} %copy-done.72, bf16[1024,768]{1,0:T(8,128)(2,1)S(1)} %copy-done.71), kind=kOutput, calls=%fused_computation.385 | convolution fusion | flops 6452936704 | bytes 30408704 | tf_op jit(solution)/shard_map/dot_general | solution.py:67
  354.3 20.5 %collective-permute-done.20 = bf16[2,128,2048]{2,1,0:T(8,128)(2,1)S(1)} collective-permute-done((bf16[2,128,2048]{2,1,0:T(8,128)(2,1)S(1)}, bf16[2,128,2048]{2,1,0:T(8,128)(2,1)S(1)}, u32[]{:S(2)}, u32[]{:S(2)}) %collective-permute-start.20) | collective-permute-done | bytes 1048608 | tf_op jit(solution)/shard_map/ppermute | solution.py:116
  377.3 19.1 %collective-permute-done.16 = bf16[2,128,2048]{2,1,0:T(8,128)(2,1)S(1)} collective-permute-done((bf16[2,128,2048]{2,1,0:T(8,128)(2,1)S(1)}, bf16[2,128,2048]{2,1,0:T(8,128)(2,1)S(1)}, u32[]{:S(2)}, u32[]{:S(2)}) %collective-permute-start.16) | collective-permute-done | bytes 1048608 | tf_op jit(solution)/shard_map/ppermute | solution.py:116
  426.9 22.1 %collective-permute-done.26 = bf16[128,2048]{1,0:T(8,128)(2,1)S(1)} collective-permute-done((bf16[128,2048]{1,0:T(8,128)(2,1)S(1)}, bf16[128,2048]{1,0:T(8,128)(2,1)S(1)}, u32[]{:S(2)}, u32[]{:S(2)}) %collective-permute-start.26) | collective-permute-done | bytes 524320 | tf_op jit(solution)/shard_map/ppermute | solution.py:100
  450.2 13.8 %collective-permute-done.27 = bf16[256,2048]{1,0:T(8,128)(2,1)S(1)} collective-permute-done((bf16[256,2048]{1,0:T(8,128)(2,1)S(1)}, bf16[256,2048]{1,0:T(8,128)(2,1)S(1)}, u32[]{:S(2)}, u32[]{:S(2)}) %collective-permute-start.27) | collective-permute-done | bytes 1048608 | tf_op jit(solution)/shard_map/ppermute | solution.py:104
  476.9 12.6 %fusion = (f32[2,2,1024]{2,1,0:T(2,128)S(1)}, f32[2,1024,1024,2]{2,1,3,0:T(8,128)}) fusion(f32[2,1024,1024,2]{2,1,3,0:T(8,128)} %copy-done, f32[2,2,1024]{2,1,0:T(2,128)S(1)} %log_add_fusion, pred[1024,1024]{0,1:T(8,128)(4,1)S(1)} %copy-done.6, bf16[1024,2,128,1]{0,2,3,1:T(8,128)(2,1)S(1)} %bitcast.384, bf16[1024,2,2,128]{0,3,2,1:T(8,128)(2,1)S(1)} %bitcast.403), kind=kOutput, calls=%fused_computation.2 | convolution fusion | flops 1094709248 | bytes 36208640 | tf_op jit(solution)/shard_map/qgrd,kgd->grqk/dot_general | solution.py:299
  493.2 12.6 %fusion.2 = bf16[2,2,1024,1024]{2,3,1,0:T(8,128)(2,1)S(1)} fusion(f32[2,1024,1024,2]{2,1,3,0:T(8,128)} %get-tuple-element.172, f32[2,1024,1024,2]{2,1,3,0:T(8,128)} %copy-done, f32[2,2,1024]{2,1,0:T(2,128)S(1)} %get-tuple-element.171, f32[2,2,1024]{2,1,0:T(2,128)S(1)} %log_add_fusion, pred[1024,1024]{0,1:T(8,128)(4,1)S(1)} %copy-done.6), kind=kLoop, calls=%fused_computation.4 | loop fusion | flops 25165824 | bytes 43024384 | tf_op jit(solution)/shard_map/convert_element_type | solution.py:301
  547.1 9.7 %convolution_convert_fusion = bf16[2048,1536]{0,1:T(8,128)(2,1)S(1)} fusion(bf16[1024,2048]{1,0:T(8,128)(2,1)} %constant_dynamic-update-slice_fusion.13, bf16[1024,768]{1,0:T(8,128)(2,1)S(1)} %copy-done.69, bf16[1024,768]{1,0:T(8,128)(2,1)S(1)} %copy-done.67), kind=kOutput, calls=%fused_computation.27 | convolution fusion | flops 6451888128 | bytes 13631488 | tf_op jit(solution)/shard_map/dot_general | solution.py:61
  556.8 11.3 %pad_maximum_fusion.1 = bf16[2048,2304]{0,1:T(8,128)(2,1)} fusion(bf16[2048,768]{0,1:T(8,128)(2,1)S(1)} %convolution_convert_fusion.3, bf16[2048,1536]{0,1:T(8,128)(2,1)S(1)} %convolution_convert_fusion), kind=kLoop, calls=%fused_computation.17 | loop fusion | flops 18874368 | bytes 18874368 | tf_op jit(solution)/shard_map/concatenate | solution.py:267
  574.3 15.4 %collective-permute-done.28 = bf16[2,128,2048]{2,1,0:T(8,128)(2,1)S(1)} collective-permute-done((bf16[2,128,2048]{2,1,0:T(8,128)(2,1)S(1)}, bf16[2,128,2048]{2,1,0:T(8,128)(2,1)S(1)}, u32[]{:S(2)}, u32[]{:S(2)}) %collective-permute-start.28) | collective-permute-done | bytes 1048608 | tf_op jit(solution)/shard_map/ppermute | solution.py:116
  611.9 74.2 %reduce-scatter.9.cloned.1.call-done = bf16[256,2304]{0,1:T(8,128)(2,1)} async-done(((bf16[2048,2304]{0,1:T(8,128)(2,1)}), bf16[256,2304]{0,1:T(8,128)(2,1)}) %reduce-scatter.9.cloned.1.call-update) | async-done | bytes 1179664 | tf_op jit(solution)/shard_map/reduce_scatter | solution.py:272
  688.4 97.9 %reduce-scatter.11.cloned.1.call-done = bf16[256,2304]{0,1:T(8,128)(2,1)} async-done(((bf16[2048,2304]{0,1:T(8,128)(2,1)}), bf16[256,2304]{0,1:T(8,128)(2,1)}) %reduce-scatter.11.cloned.1.call-update) | async-done | bytes 1179664 | tf_op jit(solution)/shard_map/reduce_scatter | solution.py:285
  (470 shorter events, 299.5 us)
Async XLA Ops:
  7.2 93.7 %all-gather.4.cloned.1.call-start = ((), (), s32[]{:S(2)}) async-start(), calls=%async_computation.4 | async-start | bytes 7667712 | tf_op jit(solution)/shard_map/all_gather | solution.py:137
  15.1 228.2 %all-gather.6.cloned.1.call-start = ((), (), s32[]{:S(2)}) async-start(), calls=%async_computation.5 | async-start | bytes 10616832 | tf_op jit(solution)/shard_map/all_gather | solution.py:137
  19.8 265.5 %all-gather.8.cloned.1.call-start = ((), (), s32[]{:S(2)}) async-start(), calls=%async_computation.6 | async-start | bytes 10616832 | tf_op jit(solution)/shard_map/all_gather | solution.py:137
  26.3 577.0 %reduce-scatter.7.cloned.1.call-start = ((), (), s32[]{:S(2)}) async-start(), calls=%async_computation.8 | async-start | bytes 3538944 | tf_op jit(solution)/shard_map/reduce_scatter | solution.py:296
  35.8 24.5 %collective-permute-start.1 = (bf16[256,2048]{1,0:T(8,128)(2,1)S(1)}, bf16[256,2048]{1,0:T(8,128)(2,1)S(1)}, u32[]{:S(2)}, u32[]{:S(2)}) collective-permute-start(bf16[256,2048]{1,0:T(8,128)(2,1)S(1)} %pad_maximum_fusion.16), channel_id=1, source_target_pairs={{0,2},{2,0},{1,3},{3,1},{4,6},{6,4},{5,7},{7,5},{8,10},{10,8},{9,1... | collective-permute-start | bytes 3145736 | tf_op jit(solution)/shard_map/ppermute | solution.py:103
  74.8 23.0 %collective-permute-start.3 = (bf16[256,2048]{1,0:T(8,128)(2,1)S(1)}, bf16[256,2048]{1,0:T(8,128)(2,1)S(1)}, u32[]{:S(2)}, u32[]{:S(2)}) collective-permute-start(bf16[256,2048]{1,0:T(8,128)(2,1)S(1)} %pad_maximum_fusion.17), channel_id=1, source_target_pairs={{0,1},{1,0},{2,3},{3,2},{4,5},{5,4},{6,7},{7,6},{8,9},{9,8},{10,11... | collective-permute-start | bytes 3145736 | tf_op jit(solution)/shard_map/ppermute | solution.py:104
  137.9 26.1 %collective-permute-start.4 = (bf16[2,128,2048]{2,1,0:T(8,128)(2,1)S(1)}, bf16[2,128,2048]{2,1,0:T(8,128)(2,1)S(1)}, u32[]{:S(2)}, u32[]{:S(2)}) collective-permute-start(bf16[2,128,2048]{2,1,0:T(8,128)(2,1)S(1)} %bitcast.399), channel_id=1, source_target_pairs={{0,2},{2,0},{1,3},{3,1},{4,6},{6,4},{5,7},{7,5},{8,10},{10,8},{9,1... | collective-permute-start | bytes 3145736 | tf_op jit(solution)/shard_map/ppermute | solution.py:116
  139.3 56.7 %collective-permute-start.14 = (bf16[128,2048]{1,0:T(8,128)(2,1)S(1)}, bf16[128,2048]{1,0:T(8,128)(2,1)S(1)}, u32[]{:S(2)}, u32[]{:S(2)}) collective-permute-start(bf16[128,2048]{1,0:T(8,128)(2,1)S(1)} %get-tuple-element.115), channel_id=1, source_target_pairs={{0,2},{2,0},{1,3},{3,1},{4,6},{6,4},{5,7},{7,5},{8,10},{10,8},{9,1... | collective-permute-start | bytes 1572872 | tf_op jit(solution)/shard_map/ppermute | solution.py:100
  140.3 38.8 %collective-permute-start.12 = (bf16[128,2048]{1,0:T(8,128)(2,1)S(1)}, bf16[128,2048]{1,0:T(8,128)(2,1)S(1)}, u32[]{:S(2)}, u32[]{:S(2)}) collective-permute-start(bf16[128,2048]{1,0:T(8,128)(2,1)S(1)} %get-tuple-element.117), channel_id=1, source_target_pairs={{0,1},{1,0},{2,3},{3,2},{4,5},{5,4},{6,7},{7,6},{8,9},{9,8},{10,11... | collective-permute-start | bytes 1572872 | tf_op jit(solution)/shard_map/ppermute | solution.py:99
  141.8 35.8 %collective-permute-start.6 = (bf16[2,128,2048]{2,1,0:T(8,128)(2,1)S(1)}, bf16[2,128,2048]{2,1,0:T(8,128)(2,1)S(1)}, u32[]{:S(2)}, u32[]{:S(2)}) collective-permute-start(bf16[2,128,2048]{2,1,0:T(8,128)(2,1)S(1)} %bitcast.397), channel_id=1, source_target_pairs={{0,1},{1,0},{2,3},{3,2},{4,5},{5,4},{6,7},{7,6},{8,9},{9,8},{10,11... | collective-permute-start | bytes 3145736 | tf_op jit(solution)/shard_map/ppermute | solution.py:117
  179.2 33.1 %collective-permute-start.13 = (bf16[256,2048]{1,0:T(8,128)(2,1)S(1)}, bf16[256,2048]{1,0:T(8,128)(2,1)S(1)}, u32[]{:S(2)}, u32[]{:S(2)}) collective-permute-start(bf16[256,2048]{1,0:T(8,128)(2,1)S(1)} %pad_maximum_fusion.20), channel_id=1, source_target_pairs={{0,2},{2,0},{1,3},{3,1},{4,6},{6,4},{5,7},{7,5},{8,10},{10,8},{9,1... | collective-permute-start | bytes 3145736 | tf_op jit(solution)/shard_map/ppermute | solution.py:103
  196.1 27.3 %collective-permute-start.15 = (bf16[256,2048]{1,0:T(8,128)(2,1)S(1)}, bf16[256,2048]{1,0:T(8,128)(2,1)S(1)}, u32[]{:S(2)}, u32[]{:S(2)}) collective-permute-start(bf16[256,2048]{1,0:T(8,128)(2,1)S(1)} %pad_maximum_fusion.21), channel_id=1, source_target_pairs={{0,1},{1,0},{2,3},{3,2},{4,5},{5,4},{6,7},{7,6},{8,9},{9,8},{10,11... | collective-permute-start | bytes 3145736 | tf_op jit(solution)/shard_map/ppermute | solution.py:104
  213.6 25.7 %collective-permute-start.9 = (bf16[256,2048]{1,0:T(8,128)(2,1)S(1)}, bf16[256,2048]{1,0:T(8,128)(2,1)S(1)}, u32[]{:S(2)}, u32[]{:S(2)}) collective-permute-start(bf16[256,2048]{1,0:T(8,128)(2,1)S(1)} %pad_maximum_fusion.18), channel_id=1, source_target_pairs={{0,2},{2,0},{1,3},{3,1},{4,6},{6,4},{5,7},{7,5},{8,10},{10,8},{9,1... | collective-permute-start | bytes 3145736 | tf_op jit(solution)/shard_map/ppermute | solution.py:103
  347.2 28.5 %collective-permute-start.22 = (bf16[2,128,2048]{2,1,0:T(8,128)(2,1)S(1)}, bf16[2,128,2048]{2,1,0:T(8,128)(2,1)S(1)}, u32[]{:S(2)}, u32[]{:S(2)}) collective-permute-start(bf16[2,128,2048]{2,1,0:T(8,128)(2,1)S(1)} %bitcast.396), channel_id=1, source_target_pairs={{0,1},{1,0},{2,3},{3,2},{4,5},{5,4},{6,7},{7,6},{8,9},{9,8},{10,11... | collective-permute-start | bytes 3145736 | tf_op jit(solution)/shard_map/ppermute | solution.py:117
  348.7 26.0 %collective-permute-start.20 = (bf16[2,128,2048]{2,1,0:T(8,128)(2,1)S(1)}, bf16[2,128,2048]{2,1,0:T(8,128)(2,1)S(1)}, u32[]{:S(2)}, u32[]{:S(2)}) collective-permute-start(bf16[2,128,2048]{2,1,0:T(8,128)(2,1)S(1)} %bitcast.398), channel_id=1, source_target_pairs={{0,2},{2,0},{1,3},{3,1},{4,6},{6,4},{5,7},{7,5},{8,10},{10,8},{9,1... | collective-permute-start | bytes 3145736 | tf_op jit(solution)/shard_map/ppermute | solution.py:116
  349.5 47.2 %collective-permute-start.18 = (bf16[2,128,2048]{2,1,0:T(8,128)(2,1)S(1)}, bf16[2,128,2048]{2,1,0:T(8,128)(2,1)S(1)}, u32[]{:S(2)}, u32[]{:S(2)}) collective-permute-start(bf16[2,128,2048]{2,1,0:T(8,128)(2,1)S(1)} %bitcast.394), channel_id=1, source_target_pairs={{0,1},{1,0},{2,3},{3,2},{4,5},{5,4},{6,7},{7,6},{8,9},{9,8},{10,11... | collective-permute-start | bytes 3145736 | tf_op jit(solution)/shard_map/ppermute | solution.py:117
  350.4 46.0 %collective-permute-start.16 = (bf16[2,128,2048]{2,1,0:T(8,128)(2,1)S(1)}, bf16[2,128,2048]{2,1,0:T(8,128)(2,1)S(1)}, u32[]{:S(2)}, u32[]{:S(2)}) collective-permute-start(bf16[2,128,2048]{2,1,0:T(8,128)(2,1)S(1)} %bitcast.395), channel_id=1, source_target_pairs={{0,2},{2,0},{1,3},{3,1},{4,6},{6,4},{5,7},{7,5},{8,10},{10,8},{9,1... | collective-permute-start | bytes 3145736 | tf_op jit(solution)/shard_map/ppermute | solution.py:116
  375.1 26.2 %collective-permute-start.21 = (bf16[128,2048]{1,0:T(8,128)(2,1)S(1)}, bf16[128,2048]{1,0:T(8,128)(2,1)S(1)}, u32[]{:S(2)}, u32[]{:S(2)}) collective-permute-start(bf16[128,2048]{1,0:T(8,128)(2,1)S(1)} %fusion.90), channel_id=1, source_target_pairs={{0,1},{1,0},{2,3},{3,2},{4,5},{5,4},{6,7},{7,6},{8,9},{9,8},{10,11... | collective-permute-start | bytes 1572872 | tf_op jit(solution)/shard_map/ppermute | solution.py:120
  376.0 26.0 %collective-permute-start.23 = (bf16[128,2048]{1,0:T(8,128)(2,1)S(1)}, bf16[128,2048]{1,0:T(8,128)(2,1)S(1)}, u32[]{:S(2)}, u32[]{:S(2)}) collective-permute-start(bf16[128,2048]{1,0:T(8,128)(2,1)S(1)} %fusion.91), channel_id=1, source_target_pairs={{0,2},{2,0},{1,3},{3,1},{4,6},{6,4},{5,7},{7,5},{8,10},{10,8},{9,1... | collective-permute-start | bytes 1572872 | tf_op jit(solution)/shard_map/ppermute | solution.py:121
  424.8 25.3 %collective-permute-start.25 = (bf16[256,2048]{1,0:T(8,128)(2,1)S(1)}, bf16[256,2048]{1,0:T(8,128)(2,1)S(1)}, u32[]{:S(2)}, u32[]{:S(2)}) collective-permute-start(bf16[256,2048]{1,0:T(8,128)(2,1)S(1)} %pad_maximum_fusion.22), channel_id=1, source_target_pairs={{0,2},{2,0},{1,3},{3,1},{4,6},{6,4},{5,7},{7,5},{8,10},{10,8},{9,1... | collective-permute-start | bytes 3145736 | tf_op jit(solution)/shard_map/ppermute | solution.py:103
  426.0 23.0 %collective-permute-start.26 = (bf16[128,2048]{1,0:T(8,128)(2,1)S(1)}, bf16[128,2048]{1,0:T(8,128)(2,1)S(1)}, u32[]{:S(2)}, u32[]{:S(2)}) collective-permute-start(bf16[128,2048]{1,0:T(8,128)(2,1)S(1)} %get-tuple-element.112), channel_id=1, source_target_pairs={{0,2},{2,0},{1,3},{3,1},{4,6},{6,4},{5,7},{7,5},{8,10},{10,8},{9,1... | collective-permute-start | bytes 1572872 | tf_op jit(solution)/shard_map/ppermute | solution.py:100
  493.1 113.8 %reduce-scatter.5.cloned.1.call-start = ((), (), s32[]{:S(2)}) async-start(), calls=%async_computation.7 | async-start | bytes 4128768 | tf_op jit(solution)/shard_map/reduce_scatter | solution.py:142
  539.6 146.5 %reduce-scatter.9.cloned.1.call-start = ((), (), s32[]{:S(2)}) async-start(), calls=%async_computation.9 | async-start | bytes 10616832 | tf_op jit(solution)/shard_map/reduce_scatter | solution.py:272
  540.2 246.1 %reduce-scatter.11.cloned.1.call-start = ((), (), s32[]{:S(2)}) async-start(), calls=%async_computation.10 | async-start | bytes 10616832 | tf_op jit(solution)/shard_map/reduce_scatter | solution.py:285
  (99 other events, 816.1 us)
Sparse Core Ops, SparseCore 0:
  15.2 72.2 all-gather.3
  89.6 89.2 all-gather.5
  181.1 89.3 all-gather.7
  493.2 41.3 reduce-scatter.6
  539.8 46.2 reduce-scatter.4
  588.2 97.8 reduce-scatter.8
  688.4 97.8 reduce-scatter.10
